TPU v7x, 8 devices: a whole 2x2x1 slice. The times are simulated.
8 devices in a mesh: fsdp: 8 (over z, y, x, core).
Axes of the slice: x: 2, y: 2, z: 1, core: 2. Of those that a mesh axis runs over, the one named last changes fastest.
Arguments:
- tokens_x: bfloat16 [48, 256, 640], P('fsdp')
- context: bfloat16 [48, 77, 2048], P('fsdp')
- cot_out: bfloat16 [48, 256, 640], P('fsdp')
- w_qkv: bfloat16 [2, 1228800], P(None, 'fsdp')
- w_out: bfloat16 [2, 409600], P(None, 'fsdp')
- w_q2: bfloat16 [2, 409600], P(None, 'fsdp')
- w_kv2: bfloat16 [2, 2621440], P(None, 'fsdp')
- w_out2: bfloat16 [2, 409600], P(None, 'fsdp')
- w_ff1: bfloat16 [2, 3276800], P(None, 'fsdp')
- w_ff2: bfloat16 [2, 1638400], P(None, 'fsdp')
- w_vecs: bfloat16 [2, 10880], P(None, 'fsdp')
Outputs:
- output 1: bfloat16 [48, 256, 640], P('fsdp')
- output 2: bfloat16 [48, 256, 640], P('fsdp')
- output 3: float32 [2, 1228800], P(None, 'fsdp')
- output 4: float32 [2, 409600], P(None, 'fsdp')
- output 5: float32 [2, 409600], P(None, 'fsdp')
- output 6: float32 [2, 2621440], P(None, 'fsdp')
- output 7: float32 [2, 409600], P(None, 'fsdp')
- output 8: float32 [2, 3276800], P(None, 'fsdp')
- output 9: float32 [2, 1638400], P(None, 'fsdp')
- output 10: float32 [2, 10880], P(None, 'fsdp')
All inputs are finite; a program needn't handle non-finite values.
Results may differ from a plain program's by a relative error of at most 0.0199541.
Values are sent between devices in bfloat16 or wider.
A program may use at most 1 GiB of HBM per device.

v0:
```python
import functools
import math
import jax
import jax.numpy as jnp
from jax import lax
from jax.experimental import pallas as pl
from jax.experimental.pallas import tpu as pltpu
from jax.sharding import PartitionSpec as P


HEAD = 64
AXIS = 'fsdp'
CHUNK = 512
STEP = 512
VMEM_LIMIT = 60 * 1024 * 1024
FORWARD_UNROLL = 10
BACKWARD_UNROLL = 5

F32 = jnp.float32
BF16 = jnp.bfloat16


def gather_perms(n_dev):
    near = [(i, i ^ (4 if i % 2 == 0 else 2)) for i in range(n_dev)]
    far = [(i, i ^ (2 if i % 2 == 0 else 4)) for i in range(n_dev)]
    core = [(i, i ^ 1) for i in range(n_dev)]
    return near, far, core


def pack_kernel(*refs):
    ins, out = refs[:-1], refs[-1]
    width, row = out.shape[1], 0
    for ref in ins:
        depth = ref.shape[-2]
        for col in range(0, ref.shape[-1], width):
            piece = ref[0, :, col:col + width] if len(ref.shape) == 3 else ref[:, col:col + width]
            out[row:row + depth, :] = piece
            row += depth


def pack(views, layer, extra, width):
    rows = sum(v.shape[1] * v.shape[2] // width for v in views) + sum(e.shape[0] for e in extra)
    specs = [pl.BlockSpec((1,) + v.shape[1:], lambda i: (layer, 0, 0)) for v in views]
    specs += [pl.BlockSpec(e.shape, lambda i: (0, 0)) for e in extra]
    return pl.pallas_call(
        pack_kernel, grid=(1,), in_specs=specs, out_specs=pl.BlockSpec((rows, width), lambda i: (0, 0)),
        out_shape=jax.ShapeDtypeStruct((rows, width), BF16),
        cost_estimate=pl.CostEstimate(flops=rows * width, bytes_accessed=rows * width * 4, transcendentals=0),
        name='pack')(*views, *extra)


def permute(array, perm):
    return lax.ppermute(array, AXIS, perm)


def gather_group(shard, n_dev):
    near, far, core = gather_perms(n_dev)
    first = permute(shard, near)
    mine = permute(shard, core)
    second = permute(jnp.concatenate([shard, first], 0), far)
    other_first = permute(first, core)
    other_second = permute(second, core)
    return [shard, first, second, mine, other_first, other_second]


def piece_table(me, rows):
    core = lax.rem(me, 2)
    one, two = 4 - 2 * core, 2 + 2 * core
    mate = jnp.bitwise_xor(me, 1)
    x = jnp.bitwise_xor
    return [(0, 0, me), (1, 0, x(me, one)), (2, 0, x(me, two)), (2, rows, x(me, 6)),
            (3, 0, mate), (4, 0, x(mate, two)), (5, 0, x(mate, one)), (5, rows, x(mate, 6))]


def start_loads(pieces, group_rows, width, targets, sems):
    me = lax.axis_index(AXIS)
    table = piece_table(me, group_rows)
    for which, (ref, offset) in enumerate(targets):
        depth = ref.shape[0] // 8
        for block in range(ref.shape[1] // width):
            for array, start, device in table:
                src = pieces[array].at[pl.ds(start + offset + block * depth, depth), :]
                dst = ref.at[pl.ds(pl.multiple_of(device * depth, 16), depth), pl.ds(block * width, width)]
                pltpu.make_async_copy(src, dst, sems.at[which]).start()


def wait_load(ref, sem):
    pltpu.make_async_copy(ref, ref, sem).wait()


def dot_nn(a, b):
    return lax.dot_general(a, b, (((1,), (0,)), ((), ())), preferred_element_type=F32)


def dot_nt(a, b):
    return lax.dot_general(a, b, (((1,), (1,)), ((), ())), preferred_element_type=F32)


def norm_stats(x):
    average = jnp.mean(x, axis=-1, keepdims=True)
    centered = x - average
    variance = jnp.mean(centered * centered, axis=-1, keepdims=True)
    scale = lax.rsqrt(variance + 1e-5)
    return centered * scale, scale


def norm_back(x, gain, d_norm):
    unit, scale = norm_stats(x)
    d_unit = d_norm * gain
    inner = d_unit - jnp.mean(d_unit, axis=-1, keepdims=True) - unit * jnp.mean(d_unit * unit, axis=-1, keepdims=True)
    return scale * inner, jnp.sum(d_norm * unit, axis=0, keepdims=True), jnp.sum(d_norm, axis=0, keepdims=True)


def softmax_rows(scores):
    top = jnp.max(scores, axis=-1, keepdims=True)
    raised = jnp.exp(scores - top)
    return raised * (1.0 / jnp.sum(raised, axis=-1, keepdims=True))


def low_lanes(rows):
    return lax.broadcasted_iota(jnp.int32, (rows, 2 * HEAD), 1) < HEAD


def pair_scores(query, key, low, head, valid):
    q_head = jnp.where(low if head == 0 else jnp.logical_not(low), query, jnp.zeros_like(query))
    scores = dot_nt(q_head, key) * HEAD ** -0.5
    if valid is not None:
        column = lax.broadcasted_iota(jnp.int32, scores.shape, 1)
        scores = jnp.where(column < valid, scores, -1e30)
    return q_head, softmax_rows(scores)


def pair_forward(query, key, value, valid=None):
    low = low_lanes(query.shape[0])
    mixed = []
    for head in range(2):
        _, probs = pair_scores(query, key, low, head, valid)
        mixed.append(dot_nn(probs.astype(BF16), value))
    return jnp.where(low, mixed[0], mixed[1]).astype(BF16)


def pair_probs(key, query, low, head, valid):
    q_head = jnp.where(low if head == 0 else jnp.logical_not(low), query, jnp.zeros_like(query))
    scores = dot_nt(key, q_head) * HEAD ** -0.5
    if valid is not None:
        row = lax.broadcasted_iota(jnp.int32, scores.shape, 0)
        scores = jnp.where(row < valid, scores, -1e30)
    top = jnp.max(scores, axis=0, keepdims=True)
    raised = jnp.exp(scores - top)
    return q_head, raised * (1.0 / jnp.sum(raised, axis=0, keepdims=True))


def pair_backward(query, key, value, d_out, valid=None):
    low = low_lanes(query.shape[0])
    turned = key.T
    d_query, d_key, d_value = [], None, None
    for head in range(2):
        q_head, probs = pair_probs(key, query, low, head, valid)
        d_head = jnp.where(low if head == 0 else jnp.logical_not(low), d_out, jnp.zeros_like(d_out))
        d_probs = dot_nt(value, d_head).astype(BF16).astype(F32)
        inner = jnp.sum(d_probs * probs, axis=0, keepdims=True)
        d_scores = ((probs * (d_probs - inner)) * HEAD ** -0.5).astype(BF16)
        d_query.append(dot_nn(turned[head * HEAD:(head + 1) * HEAD, :], d_scores))
        dk, dv = dot_nn(d_scores, q_head), dot_nn(probs.astype(BF16), d_head)
        d_key = dk if d_key is None else d_key + dk
        d_value = dv if d_value is None else d_value + dv
    return jnp.concatenate(d_query, 0).T.astype(BF16), d_key.astype(BF16), d_value.astype(BF16)


def add_rows(ref, step, rows):
    @pl.when(step == 0)
    def _():
        ref[...] = jnp.zeros_like(ref)

    for index, row in enumerate(rows):
        ref[pl.ds(index, 1), :] += row


def self_forward_kernel(samples, tokens, h_ref, rows_ref, *refs):
    pieces, (norm_ref, qkv_ref, mix_ref, out_ref, w_qkv, w_out, sems) = refs[:6], refs[6:]
    width = h_ref.shape[1]
    step = pl.program_id(0)

    @pl.when(step == 0)
    def _():
        depth = width // 8
        start_loads(pieces, pieces[0].shape[0], width, [(w_qkv, 0), (w_out, 3 * depth)], sems)

    x = h_ref[...].astype(F32)
    unit, _ = norm_stats(x)
    normed = (unit * rows_ref[0:1, :] + rows_ref[1:2, :]).astype(BF16)
    norm_ref[...] = normed

    @pl.when(step == 0)
    def _():
        wait_load(w_qkv, sems.at[0])
        wait_load(w_out, sems.at[1])

    qkv_ref[...] = dot_nn(normed, w_qkv[...]).astype(BF16)
    pairs = width // (2 * HEAD)

    def body(index, carry):
        row = pl.multiple_of((index // pairs) * tokens, tokens)
        col = pl.multiple_of((index % pairs) * 2 * HEAD, 2 * HEAD)
        part = lambda which: qkv_ref[pl.ds(row, tokens), pl.ds(which * width + col, 2 * HEAD)]
        mix_ref[pl.ds(row, tokens), pl.ds(col, 2 * HEAD)] = pair_forward(part(0), part(1), part(2))
        return carry

    lax.fori_loop(0, samples * pairs, body, 0, unroll=FORWARD_UNROLL)
    out_ref[...] = x + dot_nn(mix_ref[...], w_out[...]) + rows_ref[6:7, :]


def cross_forward_kernel(samples, tokens, valid, h_ref, rows_ref, ctx_ref, *refs):
    pieces, (norm_ref, query_ref, kv_ref, mix_ref, out_ref, w_kv, w_query, w_out, sems) = refs[:6], refs[6:]
    width = h_ref.shape[1]
    step = pl.program_id(0)
    padded = ctx_ref.shape[0] // (samples * pl.num_programs(0))

    @pl.when(step == 0)
    def _():
        deep, depth = w_kv.shape[0] // 8, width // 8
        start_loads(pieces, pieces[0].shape[0], width,
                    [(w_kv, 0), (w_query, 2 * deep), (w_out, 2 * deep + depth)], sems)

    x = h_ref[...]
    unit, _ = norm_stats(x)
    normed = (unit * rows_ref[2:3, :] + rows_ref[3:4, :]).astype(BF16)
    norm_ref[...] = normed

    @pl.when(step == 0)
    def _():
        wait_load(w_kv, sems.at[0])
        wait_load(w_query, sems.at[1])
        wait_load(w_out, sems.at[2])
        kv_ref[...] = dot_nn(ctx_ref[...], w_kv[...]).astype(BF16)

    query_ref[...] = dot_nn(normed, w_query[...]).astype(BF16)
    pairs = width // (2 * HEAD)

    def body(index, carry):
        sample = index // pairs
        row = pl.multiple_of(sample * tokens, tokens)
        kv_row = pl.multiple_of((step * samples + sample) * padded, 16)
        col = pl.multiple_of((index % pairs) * 2 * HEAD, 2 * HEAD)
        query = query_ref[pl.ds(row, tokens), pl.ds(col, 2 * HEAD)]
        key = kv_ref[pl.ds(kv_row, padded), pl.ds(col, 2 * HEAD)]
        value = kv_ref[pl.ds(kv_row, padded), pl.ds(width + col, 2 * HEAD)]
        mix_ref[pl.ds(row, tokens), pl.ds(col, 2 * HEAD)] = pair_forward(query, key, value, valid)
        return carry

    lax.fori_loop(0, samples * pairs, body, 0, unroll=FORWARD_UNROLL)
    out_ref[...] = x + dot_nn(mix_ref[...], w_out[...]) + rows_ref[7:8, :]


def ff_loads(pieces, w_ff1, w_ff2, sems):
    width = w_ff1.shape[0]
    start_loads(pieces, pieces[0].shape[0], width, [(w_ff1, 0), (w_ff2, w_ff1.shape[1] // width * (width // 8))], sems)


def ff_forward_kernel(h_ref, rows_ref, bias_ref, *refs):
    pieces, (norm_ref, gated_ref, save_a, save_g, out_ref, w_ff1, w_ff2, sems) = refs[:6], refs[6:]
    half = w_ff2.shape[0]
    step = pl.program_id(0)

    @pl.when(step == 0)
    def _():
        ff_loads(pieces, w_ff1, w_ff2, sems)

    x = h_ref[...]
    unit, _ = norm_stats(x)
    normed = (unit * rows_ref[4:5, :] + rows_ref[5:6, :]).astype(BF16)
    norm_ref[...] = normed

    @pl.when(step == 0)
    def _():
        wait_load(w_ff1, sems.at[0])
        wait_load(w_ff2, sems.at[1])

    total = x + rows_ref[8:9, :]
    for start in range(0, half, CHUNK):
        u_a = dot_nn(normed, w_ff1[:, start:start + CHUNK]) + bias_ref[:, start:start + CHUNK]
        u_g = dot_nn(normed, w_ff1[:, half + start:half + start + CHUNK]) + bias_ref[:, half + start:half + start + CHUNK]
        cumulative = 0.5 * (1.0 + lax.erf(u_g * math.sqrt(0.5)))
        gate = u_g * cumulative
        slope = cumulative + u_g * (jnp.exp(-0.5 * u_g * u_g) * (1.0 / math.sqrt(2.0 * math.pi)))
        gated = (u_a * gate).astype(BF16)
        gated_ref[:, start:start + CHUNK] = gated
        save_a[:, start:start + CHUNK] = gate
        save_g[:, start:start + CHUNK] = u_a * slope
        total = total + dot_nn(gated, w_ff2[start:start + CHUNK, :])
    out_ref[...] = total.astype(out_ref.dtype)


def ff_backward_kernel(grad_ref, save_a, save_g, h_ref, rows_ref, *refs):
    pieces, (d_hidden_ref, out_ref, vec_ref, bias_ref, w_ff1, w_ff2, sems) = refs[:6], refs[6:]
    half = w_ff2.shape[0]
    step = pl.program_id(0)

    @pl.when(step == 0)
    def _():
        ff_loads(pieces, w_ff1, w_ff2, sems)
        bias_ref[...] = jnp.zeros_like(bias_ref)

    grad = grad_ref[...].astype(F32)
    grad_bf = grad.astype(BF16)

    @pl.when(step == 0)
    def _():
        wait_load(w_ff1, sems.at[0])
        wait_load(w_ff2, sems.at[1])

    d_norm = jnp.zeros(grad.shape, F32)
    for start in range(0, half, CHUNK):
        d_gated = dot_nt(grad_bf, w_ff2[start:start + CHUNK, :]).astype(BF16).astype(F32)
        for base, saved in ((0, save_a), (half, save_g)):
            d_part = d_gated * saved[:, start:start + CHUNK]
            columns = slice(base + start, base + start + CHUNK)
            bias_ref[0:1, columns] += jnp.sum(d_part, axis=0, keepdims=True)
            d_part = d_part.astype(BF16)
            d_hidden_ref[:, columns] = d_part
            d_norm = d_norm + dot_nt(d_part, w_ff1[:, columns])
    d_res, g_gain, g_shift = norm_back(h_ref[...], rows_ref[4:5, :], d_norm)
    out_ref[...] = grad + d_res
    add_rows(vec_ref, step, [g_gain, g_shift, jnp.sum(grad, axis=0, keepdims=True)])


def cross_backward_kernel(samples, tokens, valid, grad_ref, query_ref, kv_ref, h_ref, rows_ref, *refs):
    pieces, (grad_bf_ref, d_query_ref, d_kv_ref, out_ref, vec_ref, d_mix, w_query, w_out, sems) = refs[:6], refs[6:]
    width = h_ref.shape[1]
    step = pl.program_id(0)
    padded = kv_ref.shape[0] // samples

    @pl.when(step == 0)
    def _():
        depth = width // 8
        base = pieces[0].shape[0] - 2 * depth
        start_loads(pieces, pieces[0].shape[0], width, [(w_query, base), (w_out, base + depth)], sems)

    grad = grad_ref[...]
    grad_bf = grad.astype(BF16)
    grad_bf_ref[...] = grad_bf

    @pl.when(step == 0)
    def _():
        wait_load(w_query, sems.at[0])
        wait_load(w_out, sems.at[1])

    d_mix[...] = dot_nt(grad_bf, w_out[...]).astype(BF16)
    pairs = width // (2 * HEAD)

    def body(index, carry):
        sample = index // pairs
        row = pl.multiple_of(sample * tokens, tokens)
        kv_row = pl.multiple_of(sample * padded, 16)
        col = pl.multiple_of((index % pairs) * 2 * HEAD, 2 * HEAD)
        at = (pl.ds(row, tokens), pl.ds(col, 2 * HEAD))
        at_key = (pl.ds(kv_row, padded), pl.ds(col, 2 * HEAD))
        at_value = (pl.ds(kv_row, padded), pl.ds(width + col, 2 * HEAD))
        dq, dk, dv = pair_backward(query_ref[at], kv_ref[at_key], kv_ref[at_value], d_mix[at], valid)
        d_query_ref[at] = dq
        d_kv_ref[at_key] = dk
        d_kv_ref[at_value] = dv
        return carry

    lax.fori_loop(0, samples * pairs, body, 0, unroll=BACKWARD_UNROLL)
    d_norm = dot_nt(d_query_ref[...], w_query[...])
    d_res, g_gain, g_shift = norm_back(h_ref[...], rows_ref[2:3, :], d_norm)
    out_ref[...] = grad + d_res
    add_rows(vec_ref, step, [g_gain, g_shift, jnp.sum(grad, axis=0, keepdims=True)])


def self_backward_kernel(samples, tokens, grad_ref, qkv_ref, h_ref, rows_ref, *refs):
    pieces, (grad_bf_ref, d_qkv_ref, out_ref, vec_ref, d_mix, w_qkv, w_out, sems) = refs[:6], refs[6:]
    width = h_ref.shape[1]
    step = pl.program_id(0)

    @pl.when(step == 0)
    def _():
        depth = width // 8
        start_loads(pieces, pieces[0].shape[0], width, [(w_qkv, 0), (w_out, 3 * depth)], sems)

    grad = grad_ref[...]
    grad_bf = grad.astype(BF16)
    grad_bf_ref[...] = grad_bf

    @pl.when(step == 0)
    def _():
        wait_load(w_qkv, sems.at[0])
        wait_load(w_out, sems.at[1])

    d_mix[...] = dot_nt(grad_bf, w_out[...]).astype(BF16)
    pairs = width // (2 * HEAD)

    def body(index, carry):
        row = pl.multiple_of((index // pairs) * tokens, tokens)
        col = pl.multiple_of((index % pairs) * 2 * HEAD, 2 * HEAD)
        at = lambda which: (pl.ds(row, tokens), pl.ds(which * width + col, 2 * HEAD))
        d_parts = pair_backward(qkv_ref[at(0)], qkv_ref[at(1)], qkv_ref[at(2)], d_mix[at(0)])
        for which in range(3):
            d_qkv_ref[at(which)] = d_parts[which]
        return carry

    lax.fori_loop(0, samples * pairs, body, 0, unroll=BACKWARD_UNROLL)
    d_norm = dot_nt(d_qkv_ref[...], w_qkv[...])
    d_res, g_gain, g_shift = norm_back(h_ref[...].astype(F32), rows_ref[0:1, :], d_norm)
    out_ref[...] = (grad + d_res).astype(out_ref.dtype)
    add_rows(vec_ref, step, [g_gain, g_shift, jnp.sum(grad, axis=0, keepdims=True)])


ANY = pl.BlockSpec(memory_space=pl.ANY)


def by_step(rows, columns):
    return pl.BlockSpec((rows, columns), lambda i: (i, 0))


def whole(rows, columns):
    return pl.BlockSpec((rows, columns), lambda i: (0, 0))


def shape(rows, columns, dtype):
    return jax.ShapeDtypeStruct((rows, columns), dtype)


def call(kernel, steps, in_specs, out_specs, out_shapes, scratch, flops, moved):
    return pl.pallas_call(
        kernel, grid=(steps,), in_specs=in_specs, out_specs=out_specs, out_shape=out_shapes, scratch_shapes=scratch,
        cost_estimate=pl.CostEstimate(flops=int(flops), bytes_accessed=int(moved), transcendentals=0),
        compiler_params=pltpu.CompilerParams(dimension_semantics=('arbitrary',), vmem_limit_bytes=VMEM_LIMIT))


def self_forward(h, rows, pieces, tokens):
    count, width = h.shape
    return call(
        functools.partial(self_forward_kernel, STEP // tokens, tokens), count // STEP,
        [by_step(STEP, width), whole(*rows.shape)] + [ANY] * 6,
        [by_step(STEP, width), by_step(STEP, 3 * width), by_step(STEP, width), by_step(STEP, width)],
        [shape(count, width, BF16), shape(count, 3 * width, BF16), shape(count, width, BF16), shape(count, width, F32)],
        [pltpu.VMEM((width, 3 * width), BF16), pltpu.VMEM((width, width), BF16), pltpu.SemaphoreType.DMA((2,))],
        count * width * width * 8 + count * tokens * width * 4, 2e7)(h, rows, *pieces)


def cross_forward(h, rows, ctx, pieces, tokens, valid):
    count, width = h.shape
    ctx_rows, ctx_width = ctx.shape
    return call(
        functools.partial(cross_forward_kernel, STEP // tokens, tokens, valid), count // STEP,
        [by_step(STEP, width), whole(*rows.shape), whole(ctx_rows, ctx_width)] + [ANY] * 6,
        [by_step(STEP, width), by_step(STEP, width), whole(ctx_rows, 2 * width), by_step(STEP, width), by_step(STEP, width)],
        [shape(count, width, BF16), shape(count, width, BF16), shape(ctx_rows, 2 * width, BF16), shape(count, width, BF16),
         shape(count, width, F32)],
        [pltpu.VMEM((ctx_width, 2 * width), BF16), pltpu.VMEM((width, width), BF16), pltpu.VMEM((width, width), BF16),
         pltpu.SemaphoreType.DMA((3,))],
        count * width * width * 4 + ctx_rows * ctx_width * width * 4 + count * 128 * width * 4, 2e7)(h, rows, ctx, *pieces)


def ff_forward(h, rows, bias, pieces, out_dtype):
    count, width = h.shape
    half = bias.shape[1] // 2
    return call(
        ff_forward_kernel, count // STEP,
        [by_step(STEP, width), whole(*rows.shape), whole(1, 2 * half)] + [ANY] * 6,
        [by_step(STEP, width), by_step(STEP, half), by_step(STEP, half), by_step(STEP, half), by_step(STEP, width)],
        [shape(count, width, BF16), shape(count, half, BF16), shape(count, half, F32), shape(count, half, F32),
         shape(count, width, out_dtype)],
        [pltpu.VMEM((width, 2 * half), BF16), pltpu.VMEM((half, width), BF16), pltpu.SemaphoreType.DMA((2,))],
        count * width * half * 6, 6e7)(h, rows, bias, *pieces)


def ff_backward(grad, save_a, save_g, h, rows, pieces):
    count, width = h.shape
    half = save_a.shape[1]
    return call(
        ff_backward_kernel, count // STEP,
        [by_step(STEP, width), by_step(STEP, half), by_step(STEP, half), by_step(STEP, width), whole(*rows.shape)] + [ANY] * 6,
        [by_step(STEP, 2 * half), by_step(STEP, width), whole(8, width), whole(8, 2 * half)],
        [shape(count, 2 * half, BF16), shape(count, width, F32), shape(8, width, F32),
         shape(8, 2 * half, F32)],
        [pltpu.VMEM((width, 2 * half), BF16), pltpu.VMEM((half, width), BF16), pltpu.SemaphoreType.DMA((2,))],
        count * width * half * 6, 6e7)(grad, save_a, save_g, h, rows, *pieces)


def cross_backward(grad, query, kv, h, rows, pieces, tokens, valid):
    count, width = h.shape
    ctx_rows = kv.shape[0]
    steps = count // STEP
    return call(
        functools.partial(cross_backward_kernel, STEP // tokens, tokens, valid), steps,
        [by_step(STEP, width), by_step(STEP, width), by_step(ctx_rows // steps, 2 * width), by_step(STEP, width),
         whole(*rows.shape)] + [ANY] * 6,
        [by_step(STEP, width), by_step(STEP, width), by_step(ctx_rows // steps, 2 * width), by_step(STEP, width), whole(8, width)],
        [shape(count, width, BF16), shape(count, width, BF16), shape(ctx_rows, 2 * width, BF16), shape(count, width, F32),
         shape(8, width, F32)],
        [pltpu.VMEM((STEP, width), BF16), pltpu.VMEM((width, width), BF16), pltpu.VMEM((width, width), BF16),
         pltpu.SemaphoreType.DMA((2,))],
        count * width * width * 4 + count * 128 * width * 10, 2e7)(grad, query, kv, h, rows, *pieces)


def self_backward(grad, qkv, h, rows, pieces, tokens, out_dtype):
    count, width = h.shape
    return call(
        functools.partial(self_backward_kernel, STEP // tokens, tokens), count // STEP,
        [by_step(STEP, width), by_step(STEP, 3 * width), by_step(STEP, width), whole(*rows.shape)] + [ANY] * 6,
        [by_step(STEP, width), by_step(STEP, 3 * width), by_step(STEP, width), whole(8, width)],
        [shape(count, width, BF16), shape(count, 3 * width, BF16), shape(count, width, out_dtype), shape(8, width, F32)],
        [pltpu.VMEM((STEP, width), BF16), pltpu.VMEM((width, 3 * width), BF16), pltpu.VMEM((width, width), BF16),
         pltpu.SemaphoreType.DMA((2,))],
        count * width * width * 8 + count * tokens * width * 10, 3e7)(grad, qkv, h, rows, *pieces)


def scatter_sum(full, n_dev):
    near, far, core_perm = gather_perms(n_dev)
    me = lax.axis_index(AXIS)
    core, chip = me % 2, me // 2
    one, two = 1 + core, 2 - core
    by_chip = full.reshape((n_dev // 2, 2) + full.shape[1:])
    pick = lambda array, index: lax.dynamic_index_in_dim(array, index, 0, keepdims=False)
    ours = lambda index: lax.dynamic_slice(by_chip, (index, core) + (0,) * (full.ndim - 1),
                                           (1, 1) + full.shape[1:]).reshape(full.shape[1:])
    got = permute(lax.dynamic_index_in_dim(by_chip, 1 - core, 1, keepdims=False), core_perm)
    part = lambda index: ours(index) + pick(got, index)
    x = jnp.bitwise_xor
    second = permute(jnp.stack([part(x(chip, one)), part(x(x(chip, one), two))]), far)
    third = permute(part(x(chip, two)) + second[1], near)
    return part(chip) + second[0] + third


def weight_grad(inputs, grads):
    grad = lax.dot_general(inputs, grads, (((0,), (0,)), ((), ())), preferred_element_type=F32)
    return grad.reshape(8, grad.shape[0] // 8, grad.shape[1])


def solution(mesh):
    n_dev = mesh.shape[AXIS]

    def inner(tokens_x, context, cot_out, *shards):
        batch, tokens, width = tokens_x.shape
        _, valid, ctx_width = context.shape
        blocks = shards[0].shape[0]
        total = batch * n_dev
        depth = width // n_dev
        count = batch * tokens
        half = 4 * width

        views = []
        for shard, rows in zip(shards[:7], (depth, depth, depth, ctx_width // n_dev, depth, depth, half // n_dev)):
            views.append(shard.reshape(blocks, rows, -1))
        qkv_s, out_s, q2_s, kv2_s, out2_s, ff1_s, ff2_s = lax.optimization_barrier(views)
        me = lax.axis_index(AXIS)
        vec_len = shards[7].shape[1]
        vec_each = 17
        vec_rows = (blocks * vec_each + 15) // 16 * 16
        vec_block = lax.dynamic_update_slice(jnp.zeros((blocks, n_dev * vec_len), BF16), shards[7], (0, me * vec_len))
        vec_block = vec_block[:, :vec_each * width].reshape(blocks * vec_each, width)
        vec_block = jnp.pad(vec_block, ((0, vec_rows - blocks * vec_each), (0, 0)))

        groups = []
        for layer in range(blocks):
            extra = [vec_block] if layer == 0 else []
            for index, members in enumerate(([qkv_s, out_s], [kv2_s, q2_s, out2_s], [ff1_s, ff2_s])):
                block = pack(members, layer, extra if index == 0 else [], width)
                groups.append(gather_group(block, n_dev))

        group_rows = groups[0][0].shape[0]
        vecs = jnp.zeros((vec_rows, width), F32)
        for array, start, _ in piece_table(me, group_rows):
            vecs = vecs + groups[0][array][start + group_rows - vec_rows:start + group_rows].astype(F32)
        vecs = vecs[:blocks * vec_each].reshape(blocks, vec_each, width)
        rows_all = jnp.pad(vecs[:, :9], ((0, 0), (0, 7), (0, 0)))
        bias_all = vecs[:, 9:].reshape(blocks, 1, 8 * width)

        padded = (valid + 15) // 16 * 16
        ctx = jnp.pad(context, ((0, 0), (0, padded - valid), (0, 0))).reshape(batch * padded, ctx_width)

        h = tokens_x.reshape(count, width)
        saved = []
        for layer in range(blocks):
            rows, bias = rows_all[layer], bias_all[layer]
            group = groups[3 * layer:3 * layer + 3]
            norm1, qkv, mix1, h1 = self_forward(h, rows, group[0], tokens)
            norm2, query, kv, mix2, h2 = cross_forward(h1, rows, ctx, group[1], tokens, valid)
            last = layer == blocks - 1
            norm3, gated, save_a, save_g, h3 = ff_forward(h2, rows, bias, group[2], BF16 if last else F32)
            saved.append((h, norm1, qkv, mix1, h1, norm2, query, kv, mix2, h2, norm3, gated, save_a, save_g))
            h = h3
        out_tokens = h

        grad = cot_out.reshape(count, width)
        results, vec_grads = [None] * blocks, [None] * blocks
        for layer in reversed(range(blocks)):
            rows, group = rows_all[layer], groups[3 * layer:3 * layer + 3]
            h0, norm1, qkv, mix1, h1, norm2, query, kv, mix2, h2, norm3, gated, save_a, save_g = saved[layer]
            g_ff2 = scatter_sum(weight_grad(gated, grad.astype(BF16)), n_dev)
            d_hidden, grad, vec3, vec_b1 = ff_backward(grad, save_a, save_g, h2, rows, group[2])
            g_ff1 = scatter_sum(weight_grad(norm3, d_hidden), n_dev)
            grad_bf, d_query, d_kv, grad, vec2 = cross_backward(grad, query, kv, h1, rows, group[1], tokens, valid)
            g_out2 = scatter_sum(weight_grad(mix2, grad_bf), n_dev)
            g_q2 = scatter_sum(weight_grad(norm2, d_query), n_dev)
            g_kv2 = scatter_sum(weight_grad(ctx, d_kv), n_dev)
            grad_bf, d_qkv, grad, vec1 = self_backward(grad, qkv, h0, rows, group[0], tokens, BF16 if layer == 0 else F32)
            g_out = scatter_sum(weight_grad(mix1, grad_bf), n_dev)
            g_qkv = scatter_sum(weight_grad(norm1, d_qkv), n_dev)
            results[layer] = [g_qkv, g_out, g_q2, g_kv2, g_out2, g_ff1, g_ff2]
            vec_grads[layer] = jnp.concatenate([vec1[0], vec1[1], vec2[0], vec2[1], vec3[0], vec3[1],
                                                vec1[2], vec2[2], vec3[2], vec_b1[0]])
        vec_full = jnp.stack([jnp.pad(g, (0, vec_len * n_dev - g.shape[0])).reshape(n_dev, vec_len) for g in vec_grads], 1)
        vec_out = scatter_sum(vec_full, n_dev)
        outs = []
        for index in range(7):
            stacked = jnp.stack([results[layer][index] for layer in range(blocks)]) / total
            stacked = lax.optimization_barrier(stacked)
            outs.append(stacked.reshape(blocks, -1))
        outs.append(vec_out / total)
        return tuple([out_tokens.reshape(tokens_x.shape), grad.reshape(tokens_x.shape)] + outs)

    param_spec = P(None, AXIS)
    in_specs = (P(AXIS), P(AXIS), P(AXIS)) + (param_spec,) * 8
    out_specs = (P(AXIS), P(AXIS)) + (param_spec,) * 8
    return jax.shard_map(inner, mesh=mesh, in_specs=in_specs, out_specs=out_specs, check_vma=False)
```

profile of v0, /device:TPU:0, one launch (start us, length us, event | category | flops | bytes accessed | tf_op | source)
XLA Modules:
  0.0 1029.6 jit_solution(14049378537138759392)
XLA Ops:
  0.7 3.0 copy.57
  10.9 3.3 collective-permute-start.10
  23.8 9.7 collective-permute-done.15.refs_1_
  36.9 3.3 pad_maximum_fusion.4
  40.2 7.6 collective-permute-done.refs_1_
  56.9 12.5 %collective-permute-done.20.refs_1_ = bf16[672,640]{1,0:T(8,128)(2,1)S(1)} collective-permute-done((bf16[672,640]{1,0:T(8,128)(2,1)S(1)}, bf16[672,640]{1,0:T(8,128)(2,1)S(1)}, u32[]{:S(2)}, u32[]{:S(2)}) %collective-permute-start.20) | collective-permute-done | bytes 860192 | tf_op jit(solution)/shard_map/ppermute | solution.py:53
  72.7 2.5 collective-permute-start.25
  77.7 2.8 dot_general.57
  83.7 43.4 %collective-permute-done.1.refs_2_ = bf16[736,640]{1,0:T(8,128)(2,1)} collective-permute-done((bf16[736,640]{1,0:T(8,128)(2,1)}, bf16[736,640]{1,0:T(8,128)(2,1)}, u32[]{:S(2)}, u32[]{:S(2)}) %collective-permute-start.1) | collective-permute-done | bytes 942112 | tf_op jit(solution)/shard_map/ppermute | solution.py:53
  132.9 2.9 pad_maximum_fusion.5
  138.1 5.5 collective-permute-done.16.refs_2_
  148.1 20.2 %shard_map.186 = (bf16[1536,640]{1,0:T(8,128)(2,1)}, bf16[1536,1920]{1,0:T(8,128)(2,1)}, bf16[1536,640]{1,0:T(8,128)(2,1)}, f32[1536,640]{1,0:T(8,128)}) custom-call(bf16[1536,640]{1,0:T(8,128)(2,1)} %bitcast.679, f32[16,640]{1,0:T(8,128)} %get-tuple-element.187.rows_ref, bf16[368,640]{1,0:T(8,128)(2,1)} %pack.6.refs_0_, ...), custom_call_target="tpu_custom_call" | custom-call | flops 6039797760 | bytes 20000000 | tf_op jit(solution)/shard_map/pallas_call | solution.py:434
  168.3 19.6 %shard_map.187 = (bf16[1536,640]{1,0:T(8,128)(2,1)}, bf16[1536,640]{1,0:T(8,128)(2,1)}, bf16[480,1280]{1,0:T(8,128)(2,1)}, bf16[1536,640]{1,0:T(8,128)(2,1)}, f32[1536,640]{1,0:T(8,128)}) custom-call(f32[1536,640]{1,0:T(8,128)} %get-tuple-element.73.h_ref, f32[16,640]{1,0:T(8,128)} %get-tuple-element.187.rows_ref, bf16[480,2048]{1,0:T(8,128)(2,1)} %bitcast.612, ...), custom_call_target="tpu_custom_call" | custom-call | flops 5536481280 | bytes 20000000 | tf_op jit(solution)/shard_map/pallas_call | solution.py:446
  189.0 36.1 %shard_map.188 = (bf16[1536,640]{1,0:T(8,128)(2,1)}, bf16[1536,2560]{1,0:T(8,128)(2,1)}, f32[1536,2560]{1,0:T(8,128)}, f32[1536,2560]{1,0:T(8,128)}, f32[1536,640]{1,0:T(8,128)}) custom-call(f32[1536,640]{1,0:T(8,128)} %get-tuple-element.77.h_ref, f32[16,640]{1,0:T(8,128)} %get-tuple-element.187.rows_ref, f32[1,5120]{1,0:T(1,128)} %bitcast.678, ...), custom_call_target="tpu_custom_call" | custom-call | flops 15099494400 | bytes 60000000 | tf_op jit(solution)/shard_map/pallas_call | solution.py:460
  225.1 21.0 %shard_map.189 = (bf16[1536,640]{1,0:T(8,128)(2,1)}, bf16[1536,1920]{1,0:T(8,128)(2,1)}, bf16[1536,640]{1,0:T(8,128)(2,1)}, f32[1536,640]{1,0:T(8,128)}) custom-call(f32[1536,640]{1,0:T(8,128)} %get-tuple-element.80.h_ref, f32[16,640]{1,0:T(8,128)} %get-tuple-element.186.rows_ref, bf16[320,640]{1,0:T(8,128)(2,1)} %pack.9.refs_0_, ...), custom_call_target="tpu_custom_call" | custom-call | flops 6039797760 | bytes 20000000 | tf_op jit(solution)/shard_map/pallas_call | solution.py:434
  247.1 19.3 %shard_map.190 = (bf16[1536,640]{1,0:T(8,128)(2,1)}, bf16[1536,640]{1,0:T(8,128)(2,1)}, bf16[480,1280]{1,0:T(8,128)(2,1)}, bf16[1536,640]{1,0:T(8,128)(2,1)}, f32[1536,640]{1,0:T(8,128)}) custom-call(f32[1536,640]{1,0:T(8,128)} %get-tuple-element.81.h_ref, f32[16,640]{1,0:T(8,128)} %get-tuple-element.186.rows_ref, bf16[480,2048]{1,0:T(8,128)(2,1)} %bitcast.613, ...), custom_call_target="tpu_custom_call" | custom-call | flops 5536481280 | bytes 20000000 | tf_op jit(solution)/shard_map/pallas_call | solution.py:446
  266.4 35.8 %shard_map.191 = (bf16[1536,640]{1,0:T(8,128)(2,1)}, bf16[1536,2560]{1,0:T(8,128)(2,1)}, f32[1536,2560]{1,0:T(8,128)}, f32[1536,2560]{1,0:T(8,128)}, bf16[1536,640]{1,0:T(8,128)(2,1)}) custom-call(f32[1536,640]{1,0:T(8,128)} %get-tuple-element.82.h_ref, f32[16,640]{1,0:T(8,128)} %get-tuple-element.186.rows_ref, f32[1,5120]{1,0:T(1,128)} %bitcast.677, ...), custom_call_target="tpu_custom_call" | custom-call | flops 15099494400 | bytes 60000000 | tf_op jit(solution)/shard_map/pallas_call | solution.py:460
  302.3 37.0 %shard_map.192 = (bf16[1536,5120]{1,0:T(8,128)(2,1)}, f32[1536,640]{1,0:T(8,128)}, f32[8,640]{1,0:T(8,128)}, f32[8,5120]{1,0:T(8,128)}) custom-call(bf16[1536,640]{1,0:T(8,128)(2,1)} %bitcast.681, f32[1536,2560]{1,0:T(8,128)} %get-tuple-element.84.save_a, f32[1536,2560]{1,0:T(8,128)} %get-tuple-element.85.save_g, f32[1536,640]{1,0:T(8,128)} %get-tuple-element.82.h_ref, ...), custom_call_target="tpu_custom_call" | custom-call | flops 15099494400 | bytes 60000000 | tf_op jit(solution)/shard_map/pallas_call | solution.py:473
  339.3 27.8 %shard_map.193 = (bf16[1536,640]{1,0:T(8,128)(2,1)}, bf16[1536,640]{1,0:T(8,128)(2,1)}, bf16[480,1280]{1,0:T(8,128)(2,1)}, f32[1536,640]{1,0:T(8,128)}, f32[8,640]{1,0:T(8,128)}) custom-call(f32[1536,640]{1,0:T(8,128)} %get-tuple-element.86.grad_ref, bf16[1536,640]{1,0:T(8,128)(2,1)} %get-tuple-element.87.query_ref, ...), custom_call_target="tpu_custom_call" | custom-call | flops 3774873600 | bytes 20000000 | tf_op jit(solution)/shard_map/pallas_call | solution.py:487
  367.1 42.1 %shard_map.194 = (bf16[1536,640]{1,0:T(8,128)(2,1)}, bf16[1536,1920]{1,0:T(8,128)(2,1)}, f32[1536,640]{1,0:T(8,128)}, f32[8,640]{1,0:T(8,128)}) custom-call(f32[1536,640]{1,0:T(8,128)} %get-tuple-element.89.grad_ref, bf16[1536,1920]{1,0:T(8,128)(2,1)} %get-tuple-element.90.qkv_ref, f32[1536,640]{1,0:T(8,128)} %get-tuple-element.80.h_ref, ...), custom_call_target="tpu_custom_call" | custom-call | flops 7549747200 | bytes 30000000 | tf_op jit(solution)/shard_map/pallas_call | solution.py:501
  413.0 37.6 %shard_map.195 = (bf16[1536,5120]{1,0:T(8,128)(2,1)}, f32[1536,640]{1,0:T(8,128)}, f32[8,640]{1,0:T(8,128)}, f32[8,5120]{1,0:T(8,128)}) custom-call(f32[1536,640]{1,0:T(8,128)} %get-tuple-element.91.grad_ref, f32[1536,2560]{1,0:T(8,128)} %get-tuple-element.92.save_a, f32[1536,2560]{1,0:T(8,128)} %get-tuple-element.93.save_g, ...), custom_call_target="tpu_custom_call" | custom-call | flops 15099494400 | bytes 60000000 | tf_op jit(solution)/shard_map/pallas_call | solution.py:473
  450.6 27.8 %shard_map.196 = (bf16[1536,640]{1,0:T(8,128)(2,1)}, bf16[1536,640]{1,0:T(8,128)(2,1)}, bf16[480,1280]{1,0:T(8,128)(2,1)}, f32[1536,640]{1,0:T(8,128)}, f32[8,640]{1,0:T(8,128)}) custom-call(f32[1536,640]{1,0:T(8,128)} %get-tuple-element.94.grad_ref, bf16[1536,640]{1,0:T(8,128)(2,1)} %get-tuple-element.95.query_ref, ...), custom_call_target="tpu_custom_call" | custom-call | flops 3774873600 | bytes 20000000 | tf_op jit(solution)/shard_map/pallas_call | solution.py:487
  478.4 41.8 %shard_map.197 = (bf16[1536,640]{1,0:T(8,128)(2,1)}, bf16[1536,1920]{1,0:T(8,128)(2,1)}, bf16[1536,640]{1,0:T(8,128)(2,1)}, f32[8,640]{1,0:T(8,128)}) custom-call(f32[1536,640]{1,0:T(8,128)} %get-tuple-element.97.grad_ref, bf16[1536,1920]{1,0:T(8,128)(2,1)} %get-tuple-element.98.qkv_ref, bf16[1536,640]{1,0:T(8,128)(2,1)} %bitcast.680, ...), custom_call_target="tpu_custom_call" | custom-call | flops 7549747200 | bytes 30000000 | tf_op jit(solution)/shard_map/pallas_call | solution.py:501
  524.5 10.0 fusion
  538.2 10.8 %copy.26 = bf16[2560,1536]{1,0:T(8,128)(2,1)} copy(bf16[2560,1536]{0,1:T(8,128)(2,1)} %bitcast.609) | data formatting | bytes 15728640 | tf_op jit(solution)/shard_map/dot_general | solution.py:529
  549.0 8.8 fusion.97
  561.6 14.8 %fusion.95 = f32[640,5120]{1,0:T(8,128)S(1)} fusion(bf16[1536,640]{1,0:T(8,128)(2,1)S(1)} %copy-done.91, bf16[1536,5120]{1,0:T(8,128)(2,1)} %get-tuple-element.119), kind=kOutput, calls=%fused_computation.290 | convolution fusion | flops 10066329600 | bytes 30801920 | tf_op jit(solution)/shard_map/dot_general | solution.py:529
  576.5 3.5 dynamic-slice_bitcast_fusion.1
  586.2 3.0 fusion.4
  589.2 3.0 dynamic-slice_bitcast_fusion.3
  594.6 4.9 fusion.2
  599.5 3.0 dynamic-slice_bitcast_fusion.2
  607.9 6.7 fusion.87
  617.9 4.4 fusion.88
  625.2 17.3 %fusion.96 = f32[640,5120]{1,0:T(8,128)} fusion(bf16[1536,640]{1,0:T(8,128)(2,1)} %get-tuple-element.120, bf16[1536,5120]{1,0:T(8,128)(2,1)} %get-tuple-element.121), kind=kOutput, calls=%fused_computation.291 | convolution fusion | flops 10066329600 | bytes 30801920 | tf_op jit(solution)/shard_map/dot_general | solution.py:529
  642.5 4.0 fusion.92
  666.1 4.0 collective-permute-done.55
  671.3 3.3 collective-permute-done.58
  682.4 3.3 collective-permute-done.43
  691.7 2.8 collective-permute-done.37
  697.2 14.8 %collective-permute-done.40 = f32[2,80,640]{2,1,0:T(8,128)S(1)} collective-permute-done((f32[2,80,640]{2,1,0:T(8,128)}, f32[2,80,640]{2,1,0:T(8,128)S(1)}, u32[]{:S(2)}, u32[]{:S(2)}) %collective-permute-start.40) | collective-permute-done | bytes 409632 | tf_op jit(solution)/shard_map/ppermute | solution.py:53
  713.2 6.7 collective-permute-done.56
  721.9 5.7 collective-permute-done.59
  730.4 3.6 collective-permute-done.44
  751.2 6.3 dynamic-slice_bitcast_fusion
  760.3 4.5 collective-permute-done.35
  773.9 12.1 %collective-permute-done.67 = f32[2,320,640]{2,1,0:T(8,128)S(1)} collective-permute-done((f32[2,320,640]{2,1,0:T(8,128)S(1)}, f32[2,320,640]{2,1,0:T(8,128)S(1)}, u32[]{:S(2)}, u32[]{:S(2)}) %collective-permute-start.67) | collective-permute-done | bytes 1638432 | tf_op jit(solution)/shard_map/ppermute | solution.py:53
  792.8 2.5 fusion.35
  797.8 9.3 collective-permute-done.70
  821.4 3.6 bitcast_add_fusion.6
  825.0 3.5 pad_maximum_fusion
  829.2 4.5 bitcast_add_fusion.2
  835.4 18.2 %collective-permute-done.49 = f32[2,256,1280]{2,1,0:T(8,128)} collective-permute-done((f32[2,256,1280]{2,1,0:T(8,128)}, f32[2,256,1280]{2,1,0:T(8,128)}, u32[]{:S(2)}, u32[]{:S(2)}) %collective-permute-start.49) | collective-permute-done | bytes 2621472 | tf_op jit(solution)/shard_map/ppermute | solution.py:53
  854.1 3.0 fusion.18
  867.1 28.5 %collective-permute-done.52 = f32[2,256,1280]{2,1,0:T(8,128)} collective-permute-done((f32[2,256,1280]{2,1,0:T(8,128)}, f32[2,256,1280]{2,1,0:T(8,128)}, u32[]{:S(2)}, u32[]{:S(2)}) %collective-permute-start.52) | collective-permute-done | bytes 2621472 | tf_op jit(solution)/shard_map/ppermute | solution.py:53
  898.9 2.4 fusion.21
  901.3 43.5 %collective-permute-done.61 = f32[2,80,5120]{2,1,0:T(8,128)} collective-permute-done((f32[2,80,5120]{2,1,0:T(8,128)}, f32[2,80,5120]{2,1,0:T(8,128)}, u32[]{:S(2)}, u32[]{:S(2)}) %collective-permute-start.61) | collective-permute-done | bytes 3276832 | tf_op jit(solution)/shard_map/ppermute | solution.py:53
  948.3 49.2 %collective-permute-done.64 = f32[2,80,5120]{2,1,0:T(8,128)} collective-permute-done((f32[2,80,5120]{2,1,0:T(8,128)S(1)}, f32[2,80,5120]{2,1,0:T(8,128)}, u32[]{:S(2)}, u32[]{:S(2)}) %collective-permute-start.64) | collective-permute-done | bytes 3276832 | tf_op jit(solution)/shard_map/ppermute | solution.py:53
  997.5 2.7 fusion.6
  1003.7 3.5 copy.42
  1007.2 2.8 fusion.13
  1010.0 11.4 %collective-permute-done.65 = f32[80,5120]{1,0:T(8,128)} collective-permute-done((f32[80,5120]{1,0:T(8,128)S(1)}, f32[80,5120]{1,0:T(8,128)}, u32[]{:S(2)}, u32[]{:S(2)}) %collective-permute-start.65) | collective-permute-done | bytes 1638432 | tf_op jit(solution)/shard_map/ppermute | solution.py:53
  1021.4 3.2 fusion.9
  1025.0 4.2 copy.44
  (467 shorter events, 206.8 us)
Async XLA Ops:
  10.9 25.6 %collective-permute-start.10 = (bf16[960,640]{1,0:T(8,128)(2,1)}, bf16[960,640]{1,0:T(8,128)(2,1)}, u32[]{:S(2)}, u32[]{:S(2)}) collective-permute-start(bf16[960,640]{1,0:T(8,128)(2,1)} %pack.8.refs_0_), channel_id=1, source_target_pairs={{0,4},{1,3},{2,6},{3,1},{4,0},{5,7},{6,2},{7,5}} | collective-permute-start | bytes 3686408 | tf_op jit(solution)/shard_map/ppermute | solution.py:53
  16.0 17.5 %collective-permute-start.15 = (bf16[320,640]{1,0:T(8,128)(2,1)}, bf16[320,640]{1,0:T(8,128)(2,1)S(1)}, u32[]{:S(2)}, u32[]{:S(2)}) collective-permute-start(bf16[320,640]{1,0:T(8,128)(2,1)} %pack.9.refs_0_), channel_id=1, source_target_pairs={{0,4},{1,3},{2,6},{3,1},{4,0},{5,7},{6,2},{7,5}} | collective-permute-start | bytes 1228808 | tf_op jit(solution)/shard_map/ppermute | solution.py:53
  18.2 31.7 %collective-permute-start.5 = (bf16[672,640]{1,0:T(8,128)(2,1)}, bf16[672,640]{1,0:T(8,128)(2,1)S(1)}, u32[]{:S(2)}, u32[]{:S(2)}) collective-permute-start(bf16[672,640]{1,0:T(8,128)(2,1)} %pack.7.refs_0_), channel_id=1, source_target_pairs={{0,4},{1,3},{2,6},{3,1},{4,0},{5,7},{6,2},{7,5}} | collective-permute-start | bytes 2580488 | tf_op jit(solution)/shard_map/ppermute | solution.py:53
  20.2 16.2 %collective-permute-start.17 = (bf16[320,640]{1,0:T(8,128)(2,1)S(1)}, bf16[320,640]{1,0:T(8,128)(2,1)}, u32[]{:S(2)}, u32[]{:S(2)}) collective-permute-start(bf16[320,640]{1,0:T(8,128)(2,1)S(1)} %copy-done.42), channel_id=1, source_target_pairs={{0,1},{1,0},{2,3},{3,2},{4,5},{5,4},{6,7},{7,6}} | collective-permute-start | bytes 1228808 | tf_op jit(solution)/shard_map/ppermute | solution.py:53
  23.2 24.7 %collective-permute-start = (bf16[368,640]{1,0:T(8,128)(2,1)}, bf16[368,640]{1,0:T(8,128)(2,1)}, u32[]{:S(2)}, u32[]{:S(2)}) collective-permute-start(bf16[368,640]{1,0:T(8,128)(2,1)} %pack.6.refs_0_), channel_id=1, source_target_pairs={{0,4},{1,3},{2,6},{3,1},{4,0},{5,7},{6,2},{7,5}} | collective-permute-start | bytes 1413128 | tf_op jit(solution)/shard_map/ppermute | solution.py:53
  33.5 16.4 %collective-permute-start.2 = (bf16[368,640]{1,0:T(8,128)(2,1)}, bf16[368,640]{1,0:T(8,128)(2,1)}, u32[]{:S(2)}, u32[]{:S(2)}) collective-permute-start(bf16[368,640]{1,0:T(8,128)(2,1)} %pack.6.refs_0_), channel_id=1, source_target_pairs={{0,1},{1,0},{2,3},{3,2},{4,5},{5,4},{6,7},{7,6}} | collective-permute-start | bytes 1413128 | tf_op jit(solution)/shard_map/ppermute | solution.py:53
  36.4 19.0 %collective-permute-start.7 = (bf16[672,640]{1,0:T(8,128)(2,1)S(1)}, bf16[672,640]{1,0:T(8,128)(2,1)S(1)}, u32[]{:S(2)}, u32[]{:S(2)}) collective-permute-start(bf16[672,640]{1,0:T(8,128)(2,1)S(1)} %copy-done.2), channel_id=1, source_target_pairs={{0,1},{1,0},{2,3},{3,2},{4,5},{5,4},{6,7},{7,6}} | collective-permute-start | bytes 2580488 | tf_op jit(solution)/shard_map/ppermute | solution.py:53
  36.4 16.3 %collective-permute-start.18 = (bf16[320,640]{1,0:T(8,128)(2,1)}, bf16[320,640]{1,0:T(8,128)(2,1)S(1)}, u32[]{:S(2)}, u32[]{:S(2)}) collective-permute-start(bf16[320,640]{1,0:T(8,128)(2,1)} %copy-done.62), channel_id=1, source_target_pairs={{0,1},{1,0},{2,3},{3,2},{4,5},{5,4},{6,7},{7,6}} | collective-permute-start | bytes 1228808 | tf_op jit(solution)/shard_map/ppermute | solution.py:53
  47.9 21.5 %collective-permute-start.20 = (bf16[672,640]{1,0:T(8,128)(2,1)S(1)}, bf16[672,640]{1,0:T(8,128)(2,1)S(1)}, u32[]{:S(2)}, u32[]{:S(2)}) collective-permute-start(bf16[672,640]{1,0:T(8,128)(2,1)S(1)} %copy-done.3), channel_id=1, source_target_pairs={{0,4},{1,3},{2,6},{3,1},{4,0},{5,7},{6,2},{7,5}} | collective-permute-start | bytes 2580488 | tf_op jit(solution)/shard_map/ppermute | solution.py:53
  49.9 22.8 %collective-permute-start.22 = (bf16[672,640]{1,0:T(8,128)(2,1)S(1)}, bf16[672,640]{1,0:T(8,128)(2,1)}, u32[]{:S(2)}, u32[]{:S(2)}) collective-permute-start(bf16[672,640]{1,0:T(8,128)(2,1)S(1)} %copy-done.3), channel_id=1, source_target_pairs={{0,1},{1,0},{2,3},{3,2},{4,5},{5,4},{6,7},{7,6}} | collective-permute-start | bytes 2580488 | tf_op jit(solution)/shard_map/ppermute | solution.py:53
  49.9 86.0 %collective-permute-start.11 = (bf16[1920,640]{1,0:T(8,128)(2,1)}, bf16[1920,640]{1,0:T(8,128)(2,1)}, u32[]{:S(2)}, u32[]{:S(2)}) collective-permute-start(bf16[1920,640]{1,0:T(8,128)(2,1)} %pad_maximum_fusion.4), channel_id=1, source_target_pairs={{0,2},{1,5},{2,0},{3,7},{4,6},{5,1},{6,4},{7,3}} | collective-permute-start | bytes 7372808 | tf_op jit(solution)/shard_map/ppermute | solution.py:53
  52.8 76.7 %collective-permute-start.6 = (bf16[1344,640]{1,0:T(8,128)(2,1)}, bf16[1344,640]{1,0:T(8,128)(2,1)}, u32[]{:S(2)}, u32[]{:S(2)}) collective-permute-start(bf16[1344,640]{1,0:T(8,128)(2,1)} %pad_maximum_fusion.6), channel_id=1, source_target_pairs={{0,2},{1,5},{2,0},{3,7},{4,6},{5,1},{6,4},{7,3}} | collective-permute-start | bytes 5160968 | tf_op jit(solution)/shard_map/ppermute | solution.py:53
  55.4 71.7 %collective-permute-start.1 = (bf16[736,640]{1,0:T(8,128)(2,1)}, bf16[736,640]{1,0:T(8,128)(2,1)}, u32[]{:S(2)}, u32[]{:S(2)}) collective-permute-start(bf16[736,640]{1,0:T(8,128)(2,1)} %pad_maximum_fusion.12), channel_id=1, source_target_pairs={{0,2},{1,5},{2,0},{3,7},{4,6},{5,1},{6,4},{7,3}} | collective-permute-start | bytes 2826248 | tf_op jit(solution)/shard_map/ppermute | solution.py:53
  72.7 58.2 %collective-permute-start.25 = (bf16[960,640]{1,0:T(8,128)(2,1)}, bf16[960,640]{1,0:T(8,128)(2,1)}, u32[]{:S(2)}, u32[]{:S(2)}) collective-permute-start(bf16[960,640]{1,0:T(8,128)(2,1)} %pack.11.refs_0_), channel_id=1, source_target_pairs={{0,4},{1,3},{2,6},{3,1},{4,0},{5,7},{6,2},{7,5}} | collective-permute-start | bytes 3686408 | tf_op jit(solution)/shard_map/ppermute | solution.py:53
  75.2 60.6 %collective-permute-start.12 = (bf16[960,640]{1,0:T(8,128)(2,1)}, bf16[960,640]{1,0:T(8,128)(2,1)}, u32[]{:S(2)}, u32[]{:S(2)}) collective-permute-start(bf16[960,640]{1,0:T(8,128)(2,1)} %pack.8.refs_0_), channel_id=1, source_target_pairs={{0,1},{1,0},{2,3},{3,2},{4,5},{5,4},{6,7},{7,6}} | collective-permute-start | bytes 3686408 | tf_op jit(solution)/shard_map/ppermute | solution.py:53
  127.0 10.0 collective-permute-start.4
  129.5 18.2 %collective-permute-start.9 = (bf16[1344,640]{1,0:T(8,128)(2,1)}, bf16[1344,640]{1,0:T(8,128)(2,1)}, u32[]{:S(2)}, u32[]{:S(2)}) collective-permute-start(bf16[1344,640]{1,0:T(8,128)(2,1)} %collective-permute-done.6.refs_2_), channel_id=1, source_target_pairs={{0,1},{1,0},{2,3},{3,2},{4,5},{5,4},{6,7},{7,6}} | collective-permute-start | bytes 5160968 | tf_op jit(solution)/shard_map/ppermute | solution.py:53
  130.9 12.7 %collective-permute-start.16 = (bf16[640,640]{1,0:T(8,128)(2,1)}, bf16[640,640]{1,0:T(8,128)(2,1)}, u32[]{:S(2)}, u32[]{:S(2)}) collective-permute-start(bf16[640,640]{1,0:T(8,128)(2,1)} %pad_maximum_fusion.13), channel_id=1, source_target_pairs={{0,2},{1,5},{2,0},{3,7},{4,6},{5,1},{6,4},{7,3}} | collective-permute-start | bytes 2457608 | tf_op jit(solution)/shard_map/ppermute | solution.py:53
  135.8 52.7 %collective-permute-start.26 = (bf16[1920,640]{1,0:T(8,128)(2,1)}, bf16[1920,640]{1,0:T(8,128)(2,1)}, u32[]{:S(2)}, u32[]{:S(2)}) collective-permute-start(bf16[1920,640]{1,0:T(8,128)(2,1)} %pad_maximum_fusion.5), channel_id=1, source_target_pairs={{0,2},{1,5},{2,0},{3,7},{4,6},{5,1},{6,4},{7,3}} | collective-permute-start | bytes 7372808 | tf_op jit(solution)/shard_map/ppermute | solution.py:53
  135.9 53.0 %collective-permute-start.14 = (bf16[1920,640]{1,0:T(8,128)(2,1)}, bf16[1920,640]{1,0:T(8,128)(2,1)}, u32[]{:S(2)}, u32[]{:S(2)}) collective-permute-start(bf16[1920,640]{1,0:T(8,128)(2,1)} %collective-permute-done.11.refs_2_), channel_id=1, source_target_pairs={{0,1},{1,0},{2,3},{3,2},{4,5},{5,4},{6,7},{7,6}} | collective-permute-start | bytes 7372808 | tf_op jit(solution)/shard_map/ppermute | solution.py:53
  137.1 9.8 collective-permute-start.8
  143.6 44.9 %collective-permute-start.21 = (bf16[1344,640]{1,0:T(8,128)(2,1)}, bf16[1344,640]{1,0:T(8,128)(2,1)}, u32[]{:S(2)}, u32[]{:S(2)}) collective-permute-start(bf16[1344,640]{1,0:T(8,128)(2,1)} %pad_maximum_fusion.7), channel_id=1, source_target_pairs={{0,2},{1,5},{2,0},{3,7},{4,6},{5,1},{6,4},{7,3}} | collective-permute-start | bytes 5160968 | tf_op jit(solution)/shard_map/ppermute | solution.py:53
  146.9 41.1 %collective-permute-start.13 = (bf16[960,640]{1,0:T(8,128)(2,1)}, bf16[960,640]{1,0:T(8,128)(2,1)}, u32[]{:S(2)}, u32[]{:S(2)}) collective-permute-start(bf16[960,640]{1,0:T(8,128)(2,1)} %collective-permute-done.10.refs_1_), channel_id=1, source_target_pairs={{0,1},{1,0},{2,3},{3,2},{4,5},{5,4},{6,7},{7,6}} | collective-permute-start | bytes 3686408 | tf_op jit(solution)/shard_map/ppermute | solution.py:53
  147.7 40.2 %collective-permute-start.19 = (bf16[640,640]{1,0:T(8,128)(2,1)}, bf16[640,640]{1,0:T(8,128)(2,1)}, u32[]{:S(2)}, u32[]{:S(2)}) collective-permute-start(bf16[640,640]{1,0:T(8,128)(2,1)} %collective-permute-done.16.refs_2_), channel_id=1, source_target_pairs={{0,1},{1,0},{2,3},{3,2},{4,5},{5,4},{6,7},{7,6}} | collective-permute-start | bytes 2457608 | tf_op jit(solution)/shard_map/ppermute | solution.py:53
  187.9 78.5 %collective-permute-start.27 = (bf16[960,640]{1,0:T(8,128)(2,1)S(1)}, bf16[960,640]{1,0:T(8,128)(2,1)}, u32[]{:S(2)}, u32[]{:S(2)}) collective-permute-start(bf16[960,640]{1,0:T(8,128)(2,1)S(1)} %copy-done.16), channel_id=1, source_target_pairs={{0,1},{1,0},{2,3},{3,2},{4,5},{5,4},{6,7},{7,6}} | collective-permute-start | bytes 3686408 | tf_op jit(solution)/shard_map/ppermute | solution.py:53
  188.0 58.1 %collective-permute-start.23 = (bf16[672,640]{1,0:T(8,128)(2,1)S(1)}, bf16[672,640]{1,0:T(8,128)(2,1)S(1)}, u32[]{:S(2)}, u32[]{:S(2)}) collective-permute-start(bf16[672,640]{1,0:T(8,128)(2,1)S(1)} %copy-done.21), channel_id=1, source_target_pairs={{0,1},{1,0},{2,3},{3,2},{4,5},{5,4},{6,7},{7,6}} | collective-permute-start | bytes 2580488 | tf_op jit(solution)/shard_map/ppermute | solution.py:53
  188.4 78.0 %collective-permute-start.28 = (bf16[960,640]{1,0:T(8,128)(2,1)}, bf16[960,640]{1,0:T(8,128)(2,1)}, u32[]{:S(2)}, u32[]{:S(2)}) collective-permute-start(bf16[960,640]{1,0:T(8,128)(2,1)} %collective-permute-done.25.refs_1_), channel_id=1, source_target_pairs={{0,1},{1,0},{2,3},{3,2},{4,5},{5,4},{6,7},{7,6}} | collective-permute-start | bytes 3686408 | tf_op jit(solution)/shard_map/ppermute | solution.py:53
  188.5 57.6 %collective-permute-start.24 = (bf16[1344,640]{1,0:T(8,128)(2,1)}, bf16[1344,640]{1,0:T(8,128)(2,1)}, u32[]{:S(2)}, u32[]{:S(2)}) collective-permute-start(bf16[1344,640]{1,0:T(8,128)(2,1)} %collective-permute-done.21.refs_2_), channel_id=1, source_target_pairs={{0,1},{1,0},{2,3},{3,2},{4,5},{5,4},{6,7},{7,6}} | collective-permute-start | bytes 5160968 | tf_op jit(solution)/shard_map/ppermute | solution.py:53
  188.9 77.5 %collective-permute-start.29 = (bf16[1920,640]{1,0:T(8,128)(2,1)}, bf16[1920,640]{1,0:T(8,128)(2,1)}, u32[]{:S(2)}, u32[]{:S(2)}) collective-permute-start(bf16[1920,640]{1,0:T(8,128)(2,1)} %collective-permute-done.26.refs_2_), channel_id=1, source_target_pairs={{0,1},{1,0},{2,3},{3,2},{4,5},{5,4},{6,7},{7,6}} | collective-permute-start | bytes 7372808 | tf_op jit(solution)/shard_map/ppermute | solution.py:53
  524.1 127.2 %collective-permute-start.72 = (f32[4,2,1360]{2,1,0:T(2,128)S(1)}, f32[4,2,1360]{2,1,0:T(2,128)S(1)}, u32[]{:S(2)}, u32[]{:S(2)}) collective-permute-start(f32[4,2,1360]{2,1,0:T(2,128)S(1)} %fusion.70), channel_id=1, source_target_pairs={{0,1},{1,0},{2,3},{3,2},{4,5},{5,4},{6,7},{7,6}} | collective-permute-start | bytes 130568 | tf_op jit(solution)/shard_map/ppermute | solution.py:53
  582.8 72.3 %collective-permute-start.54 = (f32[4,80,640]{2,1,0:T(8,128)}, f32[4,80,640]{2,1,0:T(8,128)}, u32[]{:S(2)}, u32[]{:S(2)}) collective-permute-start(f32[4,80,640]{2,1,0:T(8,128)} %dynamic-slice_bitcast_fusion.9), channel_id=1, source_target_pairs={{0,1},{1,0},{2,3},{3,2},{4,5},{5,4},{6,7},{7,6}} | collective-permute-start | bytes 2457608 | tf_op jit(solution)/shard_map/ppermute | solution.py:53
  585.8 71.0 %collective-permute-start.57 = (f32[4,80,640]{2,1,0:T(8,128)}, f32[4,80,640]{2,1,0:T(8,128)}, u32[]{:S(2)}, u32[]{:S(2)}) collective-permute-start(f32[4,80,640]{2,1,0:T(8,128)} %dynamic-slice_bitcast_fusion.8), channel_id=1, source_target_pairs={{0,1},{1,0},{2,3},{3,2},{4,5},{5,4},{6,7},{7,6}} | collective-permute-start | bytes 2457608 | tf_op jit(solution)/shard_map/ppermute | solution.py:53
  607.6 50.6 %collective-permute-start.42 = (f32[4,80,640]{2,1,0:T(8,128)}, f32[4,80,640]{2,1,0:T(8,128)}, u32[]{:S(2)}, u32[]{:S(2)}) collective-permute-start(f32[4,80,640]{2,1,0:T(8,128)} %dynamic-slice_bitcast_fusion.11), channel_id=1, source_target_pairs={{0,1},{1,0},{2,3},{3,2},{4,5},{5,4},{6,7},{7,6}} | collective-permute-start | bytes 2457608 | tf_op jit(solution)/shard_map/ppermute | solution.py:53
  617.7 59.8 %collective-permute-start.30 = (f32[4,80,1920]{2,1,0:T(8,128)}, f32[4,80,1920]{2,1,0:T(8,128)}, u32[]{:S(2)}, u32[]{:S(2)}) collective-permute-start(f32[4,80,1920]{2,1,0:T(8,128)} %dynamic-slice_bitcast_fusion.7), channel_id=1, source_target_pairs={{0,1},{1,0},{2,3},{3,2},{4,5},{5,4},{6,7},{7,6}} | collective-permute-start | bytes 7372808 | tf_op jit(solution)/shard_map/ppermute | solution.py:53
  655.2 32.1 %collective-permute-start.33 = (f32[4,80,1920]{2,1,0:T(8,128)S(1)}, f32[4,80,1920]{2,1,0:T(8,128)}, u32[]{:S(2)}, u32[]{:S(2)}) collective-permute-start(f32[4,80,1920]{2,1,0:T(8,128)S(1)} %copy-done.27), channel_id=1, source_target_pairs={{0,1},{1,0},{2,3},{3,2},{4,5},{5,4},{6,7},{7,6}} | collective-permute-start | bytes 7372808 | tf_op jit(solution)/shard_map/ppermute | solution.py:53
  660.8 87.0 %collective-permute-start.66 = (f32[4,320,640]{2,1,0:T(8,128)S(1)}, f32[4,320,640]{2,1,0:T(8,128)S(1)}, u32[]{:S(2)}, u32[]{:S(2)}) collective-permute-start(f32[4,320,640]{2,1,0:T(8,128)S(1)} %copy-done.23), channel_id=1, source_target_pairs={{0,1},{1,0},{2,3},{3,2},{4,5},{5,4},{6,7},{7,6}} | collective-permute-start | bytes 9830408 | tf_op jit(solution)/shard_map/ppermute | solution.py:53
  662.2 8.0 collective-permute-start.55
  664.9 9.6 collective-permute-start.58
  670.1 78.8 %collective-permute-start.69 = (f32[4,320,640]{2,1,0:T(8,128)S(1)}, f32[4,320,640]{2,1,0:T(8,128)S(1)}, u32[]{:S(2)}, u32[]{:S(2)}) collective-permute-start(f32[4,320,640]{2,1,0:T(8,128)S(1)} %copy-done.22), channel_id=1, source_target_pairs={{0,1},{1,0},{2,3},{3,2},{4,5},{5,4},{6,7},{7,6}} | collective-permute-start | bytes 9830408 | tf_op jit(solution)/shard_map/ppermute | solution.py:53
  677.5 8.3 collective-permute-start.43
  680.7 9.4 collective-permute-start.46
  685.8 8.8 collective-permute-start.37
  687.3 47.9 %collective-permute-start.31 = (f32[2,80,1920]{2,1,0:T(8,128)}, f32[2,80,1920]{2,1,0:T(8,128)S(1)}, u32[]{:S(2)}, u32[]{:S(2)}) collective-permute-start(f32[2,80,1920]{2,1,0:T(8,128)} %pad_maximum_fusion.10), channel_id=1, source_target_pairs={{0,2},{1,5},{2,0},{3,7},{4,6},{5,1},{6,4},{7,3}} | collective-permute-start | bytes 3686408 | tf_op jit(solution)/shard_map/ppermute | solution.py:53
  690.2 21.8 %collective-permute-start.40 = (f32[2,80,640]{2,1,0:T(8,128)}, f32[2,80,640]{2,1,0:T(8,128)S(1)}, u32[]{:S(2)}, u32[]{:S(2)}) collective-permute-start(f32[2,80,640]{2,1,0:T(8,128)} %pad_maximum_fusion.15), channel_id=1, source_target_pairs={{0,2},{1,5},{2,0},{3,7},{4,6},{5,1},{6,4},{7,3}} | collective-permute-start | bytes 1228808 | tf_op jit(solution)/shard_map/ppermute | solution.py:53
  694.5 47.4 %collective-permute-start.34 = (f32[2,80,1920]{2,1,0:T(8,128)S(1)}, f32[2,80,1920]{2,1,0:T(8,128)S(1)}, u32[]{:S(2)}, u32[]{:S(2)}) collective-permute-start(f32[2,80,1920]{2,1,0:T(8,128)S(1)} %pad_maximum_fusion.11), channel_id=1, source_target_pairs={{0,2},{1,5},{2,0},{3,7},{4,6},{5,1},{6,4},{7,3}} | collective-permute-start | bytes 3686408 | tf_op jit(solution)/shard_map/ppermute | solution.py:53
  712.0 7.9 collective-permute-start.56
  739.8 80.3 %collective-permute-start.60 = (f32[4,80,5120]{2,1,0:T(8,128)}, f32[4,80,5120]{2,1,0:T(8,128)}, u32[]{:S(2)}, u32[]{:S(2)}) collective-permute-start(f32[4,80,5120]{2,1,0:T(8,128)} %dynamic-slice_bitcast_fusion.1), channel_id=1, source_target_pairs={{0,1},{1,0},{2,3},{3,2},{4,5},{5,4},{6,7},{7,6}} | collective-permute-start | bytes 19660808 | tf_op jit(solution)/shard_map/ppermute | solution.py:53
  741.9 68.6 %collective-permute-start.48 = (f32[4,256,1280]{2,1,0:T(8,128)}, f32[4,256,1280]{2,1,0:T(8,128)}, u32[]{:S(2)}, u32[]{:S(2)}) collective-permute-start(f32[4,256,1280]{2,1,0:T(8,128)} %dynamic-slice_bitcast_fusion.3), channel_id=1, source_target_pairs={{0,1},{1,0},{2,3},{3,2},{4,5},{5,4},{6,7},{7,6}} | collective-permute-start | bytes 15728648 | tf_op jit(solution)/shard_map/ppermute | solution.py:53
  747.8 67.5 %collective-permute-start.51 = (f32[4,256,1280]{2,1,0:T(8,128)}, f32[4,256,1280]{2,1,0:T(8,128)}, u32[]{:S(2)}, u32[]{:S(2)}) collective-permute-start(f32[4,256,1280]{2,1,0:T(8,128)} %dynamic-slice_bitcast_fusion.2), channel_id=1, source_target_pairs={{0,1},{1,0},{2,3},{3,2},{4,5},{5,4},{6,7},{7,6}} | collective-permute-start | bytes 15728648 | tf_op jit(solution)/shard_map/ppermute | solution.py:53
  747.8 12.0 %collective-permute-start.32 = (f32[80,1920]{1,0:T(8,128)}, f32[80,1920]{1,0:T(8,128)S(1)}, u32[]{:S(2)}, u32[]{:S(2)}) collective-permute-start(f32[80,1920]{1,0:T(8,128)} %fusion.36), channel_id=1, source_target_pairs={{0,4},{1,3},{2,6},{3,1},{4,0},{5,7},{6,2},{7,5}} | collective-permute-start | bytes 1843208 | tf_op jit(solution)/shard_map/ppermute | solution.py:53
  749.5 15.4 %collective-permute-start.35 = (f32[80,1920]{1,0:T(8,128)}, f32[80,1920]{1,0:T(8,128)}, u32[]{:S(2)}, u32[]{:S(2)}) collective-permute-start(f32[80,1920]{1,0:T(8,128)} %fusion.32), channel_id=1, source_target_pairs={{0,4},{1,3},{2,6},{3,1},{4,0},{5,7},{6,2},{7,5}} | collective-permute-start | bytes 1843208 | tf_op jit(solution)/shard_map/ppermute | solution.py:53
  759.8 68.6 %collective-permute-start.63 = (f32[4,80,5120]{2,1,0:T(8,128)}, f32[4,80,5120]{2,1,0:T(8,128)}, u32[]{:S(2)}, u32[]{:S(2)}) collective-permute-start(f32[4,80,5120]{2,1,0:T(8,128)} %dynamic-slice_bitcast_fusion), channel_id=1, source_target_pairs={{0,1},{1,0},{2,3},{3,2},{4,5},{5,4},{6,7},{7,6}} | collective-permute-start | bytes 19660808 | tf_op jit(solution)/shard_map/ppermute | solution.py:53
  764.8 21.1 %collective-permute-start.67 = (f32[2,320,640]{2,1,0:T(8,128)S(1)}, f32[2,320,640]{2,1,0:T(8,128)S(1)}, u32[]{:S(2)}, u32[]{:S(2)}) collective-permute-start(f32[2,320,640]{2,1,0:T(8,128)S(1)} %pad_maximum_fusion.8), channel_id=1, source_target_pairs={{0,2},{1,5},{2,0},{3,7},{4,6},{5,1},{6,4},{7,3}} | collective-permute-start | bytes 4915208 | tf_op jit(solution)/shard_map/ppermute | solution.py:53
  786.0 21.1 %collective-permute-start.70 = (f32[2,320,640]{2,1,0:T(8,128)S(1)}, f32[2,320,640]{2,1,0:T(8,128)S(1)}, u32[]{:S(2)}, u32[]{:S(2)}) collective-permute-start(f32[2,320,640]{2,1,0:T(8,128)S(1)} %pad_maximum_fusion.9), channel_id=1, source_target_pairs={{0,2},{1,5},{2,0},{3,7},{4,6},{5,1},{6,4},{7,3}} | collective-permute-start | bytes 4915208 | tf_op jit(solution)/shard_map/ppermute | solution.py:53
  807.1 50.1 %collective-permute-start.68 = (f32[320,640]{1,0:T(8,128)}, f32[320,640]{1,0:T(8,128)}, u32[]{:S(2)}, u32[]{:S(2)}) collective-permute-start(f32[320,640]{1,0:T(8,128)} %fusion.28), channel_id=1, source_target_pairs={{0,4},{1,3},{2,6},{3,1},{4,0},{5,7},{6,2},{7,5}} | collective-permute-start | bytes 2457608 | tf_op jit(solution)/shard_map/ppermute | solution.py:53
  810.5 52.0 %collective-permute-start.71 = (f32[320,640]{1,0:T(8,128)}, f32[320,640]{1,0:T(8,128)}, u32[]{:S(2)}, u32[]{:S(2)}) collective-permute-start(f32[320,640]{1,0:T(8,128)} %fusion.24), channel_id=1, source_target_pairs={{0,4},{1,3},{2,6},{3,1},{4,0},{5,7},{6,2},{7,5}} | collective-permute-start | bytes 2457608 | tf_op jit(solution)/shard_map/ppermute | solution.py:53
  815.3 38.3 %collective-permute-start.49 = (f32[2,256,1280]{2,1,0:T(8,128)}, f32[2,256,1280]{2,1,0:T(8,128)}, u32[]{:S(2)}, u32[]{:S(2)}) collective-permute-start(f32[2,256,1280]{2,1,0:T(8,128)} %pad_maximum_fusion.2), channel_id=1, source_target_pairs={{0,2},{1,5},{2,0},{3,7},{4,6},{5,1},{6,4},{7,3}} | collective-permute-start | bytes 7864328 | tf_op jit(solution)/shard_map/ppermute | solution.py:53
  820.1 75.6 %collective-permute-start.52 = (f32[2,256,1280]{2,1,0:T(8,128)}, f32[2,256,1280]{2,1,0:T(8,128)}, u32[]{:S(2)}, u32[]{:S(2)}) collective-permute-start(f32[2,256,1280]{2,1,0:T(8,128)} %pad_maximum_fusion.3), channel_id=1, source_target_pairs={{0,2},{1,5},{2,0},{3,7},{4,6},{5,1},{6,4},{7,3}} | collective-permute-start | bytes 7864328 | tf_op jit(solution)/shard_map/ppermute | solution.py:53
  828.5 116.4 %collective-permute-start.61 = (f32[2,80,5120]{2,1,0:T(8,128)}, f32[2,80,5120]{2,1,0:T(8,128)}, u32[]{:S(2)}, u32[]{:S(2)}) collective-permute-start(f32[2,80,5120]{2,1,0:T(8,128)} %pad_maximum_fusion), channel_id=1, source_target_pairs={{0,2},{1,5},{2,0},{3,7},{4,6},{5,1},{6,4},{7,3}} | collective-permute-start | bytes 9830408 | tf_op jit(solution)/shard_map/ppermute | solution.py:53
  853.5 144.0 %collective-permute-start.64 = (f32[2,80,5120]{2,1,0:T(8,128)S(1)}, f32[2,80,5120]{2,1,0:T(8,128)}, u32[]{:S(2)}, u32[]{:S(2)}) collective-permute-start(f32[2,80,5120]{2,1,0:T(8,128)S(1)} %pad_maximum_fusion.1), channel_id=1, source_target_pairs={{0,2},{1,5},{2,0},{3,7},{4,6},{5,1},{6,4},{7,3}} | collective-permute-start | bytes 9830408 | tf_op jit(solution)/shard_map/ppermute | solution.py:53
  857.2 41.7 %collective-permute-start.50 = (f32[256,1280]{1,0:T(8,128)}, f32[256,1280]{1,0:T(8,128)}, u32[]{:S(2)}, u32[]{:S(2)}) collective-permute-start(f32[256,1280]{1,0:T(8,128)} %fusion.18), channel_id=1, source_target_pairs={{0,4},{1,3},{2,6},{3,1},{4,0},{5,7},{6,2},{7,5}} | collective-permute-start | bytes 3932168 | tf_op jit(solution)/shard_map/ppermute | solution.py:53
  897.6 103.7 %collective-permute-start.53 = (f32[256,1280]{1,0:T(8,128)S(1)}, f32[256,1280]{1,0:T(8,128)S(1)}, u32[]{:S(2)}, u32[]{:S(2)}) collective-permute-start(f32[256,1280]{1,0:T(8,128)S(1)} %fusion.14), channel_id=1, source_target_pairs={{0,4},{1,3},{2,6},{3,1},{4,0},{5,7},{6,2},{7,5}} | collective-permute-start | bytes 3932168 | tf_op jit(solution)/shard_map/ppermute | solution.py:53
  947.1 60.1 %collective-permute-start.62 = (f32[80,5120]{1,0:T(8,128)S(1)}, f32[80,5120]{1,0:T(8,128)}, u32[]{:S(2)}, u32[]{:S(2)}) collective-permute-start(f32[80,5120]{1,0:T(8,128)S(1)} %fusion.10), channel_id=1, source_target_pairs={{0,4},{1,3},{2,6},{3,1},{4,0},{5,7},{6,2},{7,5}} | collective-permute-start | bytes 4915208 | tf_op jit(solution)/shard_map/ppermute | solution.py:53
  1000.2 21.2 %collective-permute-start.65 = (f32[80,5120]{1,0:T(8,128)S(1)}, f32[80,5120]{1,0:T(8,128)}, u32[]{:S(2)}, u32[]{:S(2)}) collective-permute-start(f32[80,5120]{1,0:T(8,128)S(1)} %fusion.6), channel_id=1, source_target_pairs={{0,4},{1,3},{2,6},{3,1},{4,0},{5,7},{6,2},{7,5}} | collective-permute-start | bytes 4915208 | tf_op jit(solution)/shard_map/ppermute | solution.py:53
  (109 other events, 1011.5 us)
where the time goes:
time: 1040 us; the launch traced here: 1030 us
  Pallas kernels  379 us (36%)
  waiting for transfers between devices  309 us (30%)
  other arithmetic  104 us (10%)
  local copies, waits for them, and re-layouts  93.9 us (9%)
  matrix products  82.7 us (8%)
  starting transfers between devices  57.5 us (6%)
    ppermute x75, waiting for transfers between devices, permute(): return lax.ppermute(array, AXIS, perm)  309 us
    pallas_call x2, Pallas kernels, self_backward(): call(functools.partial(self_backward_kernel, STEP // tokens, tokens), cou...  83.9 us
    dot_general x14, matrix products, weight_grad(): lax.dot_general(inputs, grads, (((0,), (0,)), ((), ())), preferred_elemen...  82.7 us
    pallas_call x2, Pallas kernels, ff_backward(): call(ff_backward_kernel, count // STEP, [by_step(STEP, width), by_step(ST...  74.5 us
    pallas_call x2, Pallas kernels, ff_forward(): call(ff_forward_kernel, count // STEP, [by_step(STEP, width), whole(*rows...  71.9 us
    ppermute x75, starting transfers between devices, permute(): return lax.ppermute(array, AXIS, perm)  57.5 us
    pallas_call x2, Pallas kernels, cross_backward(): call(functools.partial(cross_backward_kernel, STEP // tokens, tokens, val...  55.6 us
    unnamed x227, local copies, waits for them, and re-layouts  41.4 us
  transfers between devices with their start and end apart: 75, of which 27 were waited for; matrix products, arithmetic and copies ran while one was open for 23% of the time, Pallas kernels for 12%

commit v1 on v0

--- a/solution.py
+++ b/solution.py
@@ -10,7 +10,8 @@
 
 HEAD = 64
 AXIS = 'fsdp'
-CHUNK = 512
+CHUNK = 1280
+FF_STEP = 256
 STEP = 512
 VMEM_LIMIT = 60 * 1024 * 1024
 FORWARD_UNROLL = 10
@@ -56,32 +57,29 @@
 def gather_group(shard, n_dev):
     near, far, core = gather_perms(n_dev)
     first = permute(shard, near)
-    mine = permute(shard, core)
-    second = permute(jnp.concatenate([shard, first], 0), far)
-    other_first = permute(first, core)
-    other_second = permute(second, core)
-    return [shard, first, second, mine, other_first, other_second]
-
-
-def piece_table(me, rows):
+    second = permute(shard, far)
+    third = permute(first, far)
+    mine = [shard, first, second, third]
+    return mine + [permute(piece, core) for piece in mine]
+
+
+def piece_devices(me):
     core = lax.rem(me, 2)
     one, two = 4 - 2 * core, 2 + 2 * core
-    mate = jnp.bitwise_xor(me, 1)
     x = jnp.bitwise_xor
-    return [(0, 0, me), (1, 0, x(me, one)), (2, 0, x(me, two)), (2, rows, x(me, 6)),
-            (3, 0, mate), (4, 0, x(mate, two)), (5, 0, x(mate, one)), (5, rows, x(mate, 6))]
-
-
-def start_loads(pieces, group_rows, width, targets, sems):
-    me = lax.axis_index(AXIS)
-    table = piece_table(me, group_rows)
-    for which, (ref, offset) in enumerate(targets):
-        depth = ref.shape[0] // 8
-        for block in range(ref.shape[1] // width):
-            for array, start, device in table:
-                src = pieces[array].at[pl.ds(start + offset + block * depth, depth), :]
-                dst = ref.at[pl.ds(pl.multiple_of(device * depth, 16), depth), pl.ds(block * width, width)]
-                pltpu.make_async_copy(src, dst, sems.at[which]).start()
+    mate = x(me, 1)
+    return [me, x(me, one), x(me, two), x(me, 6), mate, x(mate, two), x(mate, one), x(mate, 6)]
+
+
+def start_load(pieces, offset, ref, sem):
+    width = pieces[0].shape[1]
+    depth = ref.shape[0] // 8
+    devices = piece_devices(lax.axis_index(AXIS))
+    for block in range(ref.shape[1] // width):
+        for piece, device in zip(pieces, devices):
+            src = piece.at[pl.ds(offset + block * depth, depth), :]
+            dst = ref.at[pl.ds(pl.multiple_of(device * depth, 16), depth), pl.ds(block * width, width)]
+            pltpu.make_async_copy(src, dst, sem).start()
 
 
 def wait_load(ref, sem):
@@ -177,14 +175,14 @@
 
 
 def self_forward_kernel(samples, tokens, h_ref, rows_ref, *refs):
-    pieces, (norm_ref, qkv_ref, mix_ref, out_ref, w_qkv, w_out, sems) = refs[:6], refs[6:]
+    pieces, (norm_ref, qkv_ref, mix_ref, out_ref, w_qkv, w_out, sems) = refs[:8], refs[8:]
     width = h_ref.shape[1]
     step = pl.program_id(0)
 
     @pl.when(step == 0)
     def _():
-        depth = width // 8
-        start_loads(pieces, pieces[0].shape[0], width, [(w_qkv, 0), (w_out, 3 * depth)], sems)
+        start_load(pieces, 0, w_qkv, sems.at[0])
+        start_load(pieces, 3 * (width // 8), w_out, sems.at[1])
 
     x = h_ref[...].astype(F32)
     unit, _ = norm_stats(x)
@@ -211,7 +209,7 @@
 
 
 def cross_forward_kernel(samples, tokens, valid, h_ref, rows_ref, ctx_ref, *refs):
-    pieces, (norm_ref, query_ref, kv_ref, mix_ref, out_ref, w_kv, w_query, w_out, sems) = refs[:6], refs[6:]
+    pieces, (norm_ref, query_ref, kv_ref, mix_ref, out_ref, w_kv, w_query, w_out, sems) = refs[:8], refs[8:]
     width = h_ref.shape[1]
     step = pl.program_id(0)
     padded = ctx_ref.shape[0] // (samples * pl.num_programs(0))
@@ -219,8 +217,9 @@
     @pl.when(step == 0)
     def _():
         deep, depth = w_kv.shape[0] // 8, width // 8
-        start_loads(pieces, pieces[0].shape[0], width,
-                    [(w_kv, 0), (w_query, 2 * deep), (w_out, 2 * deep + depth)], sems)
+        start_load(pieces, 0, w_kv, sems.at[0])
+        start_load(pieces, 2 * deep, w_query, sems.at[1])
+        start_load(pieces, 2 * deep + depth, w_out, sems.at[2])
 
     x = h_ref[...]
     unit, _ = norm_stats(x)
@@ -252,19 +251,32 @@
     out_ref[...] = x + dot_nn(mix_ref[...], w_out[...]) + rows_ref[7:8, :]
 
 
-def ff_loads(pieces, w_ff1, w_ff2, sems):
-    width = w_ff1.shape[0]
-    start_loads(pieces, pieces[0].shape[0], width, [(w_ff1, 0), (w_ff2, w_ff1.shape[1] // width * (width // 8))], sems)
-
-
-def ff_forward_kernel(h_ref, rows_ref, bias_ref, *refs):
-    pieces, (norm_ref, gated_ref, save_a, save_g, out_ref, w_ff1, w_ff2, sems) = refs[:6], refs[6:]
+def ff_loads(pieces, offset, w_ff1, w_ff2, sems):
+    start_load(pieces[:8], 0, w_ff1, sems.at[0])
+    start_load(pieces[8:], offset, w_ff2, sems.at[1])
+
+
+def ff_up(normed, bias_ref, w_ff1, half, start, gated_ref, save_a, save_g):
+    u_a = dot_nn(normed, w_ff1[:, start:start + CHUNK]) + bias_ref[:, start:start + CHUNK]
+    u_g = dot_nn(normed, w_ff1[:, half + start:half + start + CHUNK]) + bias_ref[:, half + start:half + start + CHUNK]
+    cumulative = 0.5 * (1.0 + lax.erf(u_g * math.sqrt(0.5)))
+    gate = u_g * cumulative
+    slope = cumulative + u_g * (jnp.exp(-0.5 * u_g * u_g) * (1.0 / math.sqrt(2.0 * math.pi)))
+    gated = (u_a * gate).astype(BF16)
+    gated_ref[:, start:start + CHUNK] = gated
+    save_a[:, start:start + CHUNK] = gate
+    save_g[:, start:start + CHUNK] = u_a * slope
+    return gated
+
+
+def ff_forward_kernel(offset, h_ref, rows_ref, bias_ref, *refs):
+    pieces, (norm_ref, gated_ref, save_a, save_g, out_ref, w_ff1, w_ff2, sems) = refs[:16], refs[16:]
     half = w_ff2.shape[0]
     step = pl.program_id(0)
 
     @pl.when(step == 0)
     def _():
-        ff_loads(pieces, w_ff1, w_ff2, sems)
+        ff_loads(pieces, offset, w_ff1, w_ff2, sems)
 
     x = h_ref[...]
     unit, _ = norm_stats(x)
@@ -278,27 +290,52 @@
 
     total = x + rows_ref[8:9, :]
     for start in range(0, half, CHUNK):
-        u_a = dot_nn(normed, w_ff1[:, start:start + CHUNK]) + bias_ref[:, start:start + CHUNK]
-        u_g = dot_nn(normed, w_ff1[:, half + start:half + start + CHUNK]) + bias_ref[:, half + start:half + start + CHUNK]
-        cumulative = 0.5 * (1.0 + lax.erf(u_g * math.sqrt(0.5)))
-        gate = u_g * cumulative
-        slope = cumulative + u_g * (jnp.exp(-0.5 * u_g * u_g) * (1.0 / math.sqrt(2.0 * math.pi)))
-        gated = (u_a * gate).astype(BF16)
-        gated_ref[:, start:start + CHUNK] = gated
-        save_a[:, start:start + CHUNK] = gate
-        save_g[:, start:start + CHUNK] = u_a * slope
+        gated = ff_up(normed, bias_ref, w_ff1, half, start, gated_ref, save_a, save_g)
         total = total + dot_nn(gated, w_ff2[start:start + CHUNK, :])
-    out_ref[...] = total.astype(out_ref.dtype)
-
-
-def ff_backward_kernel(grad_ref, save_a, save_g, h_ref, rows_ref, *refs):
-    pieces, (d_hidden_ref, out_ref, vec_ref, bias_ref, w_ff1, w_ff2, sems) = refs[:6], refs[6:]
+    out_ref[...] = total
+
+
+def ff_up_kernel(h_ref, rows_ref, bias_ref, *refs):
+    pieces, (norm_ref, gated_ref, save_a, save_g, w_ff1, sems) = refs[:8], refs[8:]
+    half = w_ff1.shape[1] // 2
+    step = pl.program_id(0)
+
+    @pl.when(step == 0)
+    def _():
+        start_load(pieces, 0, w_ff1, sems.at[0])
+
+    unit, _ = norm_stats(h_ref[...])
+    normed = (unit * rows_ref[4:5, :] + rows_ref[5:6, :]).astype(BF16)
+    norm_ref[...] = normed
+
+    @pl.when(step == 0)
+    def _():
+        wait_load(w_ff1, sems.at[0])
+
+    for start in range(0, half, CHUNK):
+        ff_up(normed, bias_ref, w_ff1, half, start, gated_ref, save_a, save_g)
+
+
+def ff_down_kernel(h_ref, rows_ref, gated_ref, *refs):
+    pieces, (out_ref, w_ff2, sems) = refs[:8], refs[8:]
+    step = pl.program_id(0)
+
+    @pl.when(step == 0)
+    def _():
+        start_load(pieces, 0, w_ff2, sems.at[0])
+        wait_load(w_ff2, sems.at[0])
+
+    out_ref[...] = (h_ref[...] + rows_ref[8:9, :] + dot_nn(gated_ref[...], w_ff2[...])).astype(BF16)
+
+
+def ff_backward_kernel(offset, grad_ref, save_a, save_g, h_ref, rows_ref, *refs):
+    pieces, (d_hidden_ref, out_ref, vec_ref, bias_ref, w_ff1, w_ff2, sems) = refs[:16], refs[16:]
     half = w_ff2.shape[0]
     step = pl.program_id(0)
 
     @pl.when(step == 0)
     def _():
-        ff_loads(pieces, w_ff1, w_ff2, sems)
+        ff_loads(pieces, offset, w_ff1, w_ff2, sems)
         bias_ref[...] = jnp.zeros_like(bias_ref)
 
     grad = grad_ref[...].astype(F32)
@@ -325,7 +362,7 @@
 
 
 def cross_backward_kernel(samples, tokens, valid, grad_ref, query_ref, kv_ref, h_ref, rows_ref, *refs):
-    pieces, (grad_bf_ref, d_query_ref, d_kv_ref, out_ref, vec_ref, d_mix, w_query, w_out, sems) = refs[:6], refs[6:]
+    pieces, (grad_bf_ref, d_query_ref, d_kv_ref, out_ref, vec_ref, d_mix, w_query, w_out, sems) = refs[:8], refs[8:]
     width = h_ref.shape[1]
     step = pl.program_id(0)
     padded = kv_ref.shape[0] // samples
@@ -334,7 +371,8 @@
     def _():
         depth = width // 8
         base = pieces[0].shape[0] - 2 * depth
-        start_loads(pieces, pieces[0].shape[0], width, [(w_query, base), (w_out, base + depth)], sems)
+        start_load(pieces, base, w_query, sems.at[0])
+        start_load(pieces, base + depth, w_out, sems.at[1])
 
     grad = grad_ref[...]
     grad_bf = grad.astype(BF16)
@@ -370,14 +408,14 @@
 
 
 def self_backward_kernel(samples, tokens, grad_ref, qkv_ref, h_ref, rows_ref, *refs):
-    pieces, (grad_bf_ref, d_qkv_ref, out_ref, vec_ref, d_mix, w_qkv, w_out, sems) = refs[:6], refs[6:]
+    pieces, (grad_bf_ref, d_qkv_ref, out_ref, vec_ref, d_mix, w_qkv, w_out, sems) = refs[:8], refs[8:]
     width = h_ref.shape[1]
     step = pl.program_id(0)
 
     @pl.when(step == 0)
     def _():
-        depth = width // 8
-        start_loads(pieces, pieces[0].shape[0], width, [(w_qkv, 0), (w_out, 3 * depth)], sems)
+        start_load(pieces, 0, w_qkv, sems.at[0])
+        start_load(pieces, 3 * (width // 8), w_out, sems.at[1])
 
     grad = grad_ref[...]
     grad_bf = grad.astype(BF16)
@@ -433,7 +471,7 @@
     count, width = h.shape
     return call(
         functools.partial(self_forward_kernel, STEP // tokens, tokens), count // STEP,
-        [by_step(STEP, width), whole(*rows.shape)] + [ANY] * 6,
+        [by_step(STEP, width), whole(*rows.shape)] + [ANY] * 8,
         [by_step(STEP, width), by_step(STEP, 3 * width), by_step(STEP, width), by_step(STEP, width)],
         [shape(count, width, BF16), shape(count, 3 * width, BF16), shape(count, width, BF16), shape(count, width, F32)],
         [pltpu.VMEM((width, 3 * width), BF16), pltpu.VMEM((width, width), BF16), pltpu.SemaphoreType.DMA((2,))],
@@ -445,7 +483,7 @@
     ctx_rows, ctx_width = ctx.shape
     return call(
         functools.partial(cross_forward_kernel, STEP // tokens, tokens, valid), count // STEP,
-        [by_step(STEP, width), whole(*rows.shape), whole(ctx_rows, ctx_width)] + [ANY] * 6,
+        [by_step(STEP, width), whole(*rows.shape), whole(ctx_rows, ctx_width)] + [ANY] * 8,
         [by_step(STEP, width), by_step(STEP, width), whole(ctx_rows, 2 * width), by_step(STEP, width), by_step(STEP, width)],
         [shape(count, width, BF16), shape(count, width, BF16), shape(ctx_rows, 2 * width, BF16), shape(count, width, BF16),
          shape(count, width, F32)],
@@ -454,28 +492,51 @@
         count * width * width * 4 + ctx_rows * ctx_width * width * 4 + count * 128 * width * 4, 2e7)(h, rows, ctx, *pieces)
 
 
-def ff_forward(h, rows, bias, pieces, out_dtype):
+def ff_forward(h, rows, bias, pieces, offset):
     count, width = h.shape
     half = bias.shape[1] // 2
     return call(
-        ff_forward_kernel, count // STEP,
-        [by_step(STEP, width), whole(*rows.shape), whole(1, 2 * half)] + [ANY] * 6,
-        [by_step(STEP, width), by_step(STEP, half), by_step(STEP, half), by_step(STEP, half), by_step(STEP, width)],
+        functools.partial(ff_forward_kernel, offset), count // FF_STEP,
+        [by_step(FF_STEP, width), whole(*rows.shape), whole(1, 2 * half)] + [ANY] * 16,
+        [by_step(FF_STEP, width), by_step(FF_STEP, half), by_step(FF_STEP, half), by_step(FF_STEP, half), by_step(FF_STEP, width)],
         [shape(count, width, BF16), shape(count, half, BF16), shape(count, half, F32), shape(count, half, F32),
-         shape(count, width, out_dtype)],
+         shape(count, width, F32)],
         [pltpu.VMEM((width, 2 * half), BF16), pltpu.VMEM((half, width), BF16), pltpu.SemaphoreType.DMA((2,))],
         count * width * half * 6, 6e7)(h, rows, bias, *pieces)
 
 
-def ff_backward(grad, save_a, save_g, h, rows, pieces):
+def ff_up_forward(h, rows, bias, pieces):
+    count, width = h.shape
+    half = bias.shape[1] // 2
+    return call(
+        ff_up_kernel, count // FF_STEP,
+        [by_step(FF_STEP, width), whole(*rows.shape), whole(1, 2 * half)] + [ANY] * 8,
+        [by_step(FF_STEP, width), by_step(FF_STEP, half), by_step(FF_STEP, half), by_step(FF_STEP, half)],
+        [shape(count, width, BF16), shape(count, half, BF16), shape(count, half, F32), shape(count, half, F32)],
+        [pltpu.VMEM((width, 2 * half), BF16), pltpu.SemaphoreType.DMA((1,))],
+        count * width * half * 4, 5e7)(h, rows, bias, *pieces)
+
+
+def ff_down_forward(h, rows, gated, pieces):
+    count, width = h.shape
+    half = gated.shape[1]
+    return call(
+        ff_down_kernel, count // STEP,
+        [by_step(STEP, width), whole(*rows.shape), by_step(STEP, half)] + [ANY] * 8,
+        by_step(STEP, width), shape(count, width, BF16),
+        [pltpu.VMEM((half, width), BF16), pltpu.SemaphoreType.DMA((1,))],
+        count * width * half * 2, 2e7)(h, rows, gated, *pieces)
+
+
+def ff_backward(grad, save_a, save_g, h, rows, pieces, offset):
     count, width = h.shape
     half = save_a.shape[1]
     return call(
-        ff_backward_kernel, count // STEP,
-        [by_step(STEP, width), by_step(STEP, half), by_step(STEP, half), by_step(STEP, width), whole(*rows.shape)] + [ANY] * 6,
-        [by_step(STEP, 2 * half), by_step(STEP, width), whole(8, width), whole(8, 2 * half)],
-        [shape(count, 2 * half, BF16), shape(count, width, F32), shape(8, width, F32),
-         shape(8, 2 * half, F32)],
+        functools.partial(ff_backward_kernel, offset), count // FF_STEP,
+        [by_step(FF_STEP, width), by_step(FF_STEP, half), by_step(FF_STEP, half), by_step(FF_STEP, width), whole(*rows.shape)]
+        + [ANY] * 16,
+        [by_step(FF_STEP, 2 * half), by_step(FF_STEP, width), whole(8, width), whole(8, 2 * half)],
+        [shape(count, 2 * half, BF16), shape(count, width, F32), shape(8, width, F32), shape(8, 2 * half, F32)],
         [pltpu.VMEM((width, 2 * half), BF16), pltpu.VMEM((half, width), BF16), pltpu.SemaphoreType.DMA((2,))],
         count * width * half * 6, 6e7)(grad, save_a, save_g, h, rows, *pieces)
 
@@ -487,7 +548,7 @@
     return call(
         functools.partial(cross_backward_kernel, STEP // tokens, tokens, valid), steps,
         [by_step(STEP, width), by_step(STEP, width), by_step(ctx_rows // steps, 2 * width), by_step(STEP, width),
-         whole(*rows.shape)] + [ANY] * 6,
+         whole(*rows.shape)] + [ANY] * 8,
         [by_step(STEP, width), by_step(STEP, width), by_step(ctx_rows // steps, 2 * width), by_step(STEP, width), whole(8, width)],
         [shape(count, width, BF16), shape(count, width, BF16), shape(ctx_rows, 2 * width, BF16), shape(count, width, F32),
          shape(8, width, F32)],
@@ -500,7 +561,7 @@
     count, width = h.shape
     return call(
         functools.partial(self_backward_kernel, STEP // tokens, tokens), count // STEP,
-        [by_step(STEP, width), by_step(STEP, 3 * width), by_step(STEP, width), whole(*rows.shape)] + [ANY] * 6,
+        [by_step(STEP, width), by_step(STEP, 3 * width), by_step(STEP, width), whole(*rows.shape)] + [ANY] * 8,
         [by_step(STEP, width), by_step(STEP, 3 * width), by_step(STEP, width), whole(8, width)],
         [shape(count, width, BF16), shape(count, 3 * width, BF16), shape(count, width, out_dtype), shape(8, width, F32)],
         [pltpu.VMEM((STEP, width), BF16), pltpu.VMEM((width, 3 * width), BF16), pltpu.VMEM((width, width), BF16),
@@ -525,9 +586,147 @@
     return part(chip) + second[0] + third
 
 
-def weight_grad(inputs, grads):
-    grad = lax.dot_general(inputs, grads, (((0,), (0,)), ((), ())), preferred_element_type=F32)
-    return grad.reshape(8, grad.shape[0] // 8, grad.shape[1])
+def grad_kernel(tiles, group_rows, inputs, *refs):
+    ins, (far_ref, keep_ref, x_buf, turned, y_buf, tile, own, recv, x_sem, y_sem, send_sem, recv_sem) = refs[:inputs], refs[inputs:]
+    width = tile.shape[1]
+    me = lax.axis_index(AXIS)
+    core, chip = lax.rem(me, 2), me // 2
+    mate = me + 1 - 2 * core
+    chip_x, chip_y = lax.rem(chip, 2), chip // 2
+
+    xs, ys, x_of, y_of = [], [], [], []
+    for x, x_col, y, y_col, *_ in tiles:
+        if not xs or xs[-1] != (x, x_col):
+            xs.append((x, x_col))
+        if not ys or ys[-1] != (y, y_col):
+            ys.append((y, y_col))
+        x_of.append(len(xs) - 1)
+        y_of.append(len(ys) - 1)
+
+    def load(which, sequence, buf, sem):
+        array, col = sequence[which]
+        return pltpu.make_async_copy(ins[array].at[:, pl.ds(col, width)], buf.at[which % 2], sem.at[which % 2])
+
+    for which in range(2):
+        if which < len(xs):
+            load(which, xs, x_buf, x_sem).start()
+        if which < len(ys):
+            load(which, ys, y_buf, y_sem).start()
+
+    barrier = pltpu.get_barrier_semaphore()
+    pl.semaphore_signal(barrier, inc=1, device_id=(mate,), device_id_type=pl.DeviceIdType.MESH)
+    pl.semaphore_wait(barrier, 1)
+
+    def sends(q):
+        *_, first_row, rows, chips = tiles[q]
+        copies = []
+        for index, other in enumerate(chips):
+            d_x, d_y = lax.rem(chip_x + other % 2, 2), lax.rem(chip_y + other // 2, 2)
+            slot = d_x + 2 * d_y + core * (d_x - d_y)
+            start = pl.multiple_of((2 * index + 1 - core) * rows, 16)
+            copies.append(pltpu.make_async_remote_copy(
+                src_ref=tile.at[q % 3, pl.ds(start, rows), :], dst_ref=recv.at[slot, pl.ds(first_row, rows), :],
+                send_sem=send_sem.at[q % 3, index], recv_sem=recv_sem.at[q, index],
+                device_id=(mate,), device_id_type=pl.DeviceIdType.MESH))
+        return copies
+
+    for q, (x, x_col, y, y_col, first_row, rows, chips) in enumerate(tiles):
+        if q == 0 or x_of[q] != x_of[q - 1]:
+            which = x_of[q]
+            load(which, xs, x_buf, x_sem).wait()
+            turned[...] = x_buf[which % 2].T
+            if which + 2 < len(xs):
+                load(which + 2, xs, x_buf, x_sem).start()
+        if q == 0 or y_of[q] != y_of[q - 1]:
+            load(y_of[q], ys, y_buf, y_sem).wait()
+        if q >= 3:
+            for copy in sends(q - 3):
+                copy.wait_send()
+        tile[q % 3] = dot_nn(turned[...], y_buf[y_of[q] % 2])
+        if (q + 1 == len(tiles) or y_of[q + 1] != y_of[q]) and y_of[q] + 2 < len(ys):
+            load(y_of[q] + 2, ys, y_buf, y_sem).start()
+        for index, other in enumerate(chips):
+            d_x, d_y = lax.rem(chip_x + other % 2, 2), lax.rem(chip_y + other // 2, 2)
+            slot = 2 * d_x + d_y + core * (d_y - d_x)
+            start = pl.multiple_of((2 * index + core) * rows, 16)
+            own[slot, first_row:first_row + rows, :] = tile[q % 3, pl.ds(start, rows), :]
+        if q >= 1:
+            for copy in sends(q - 1):
+                copy.start()
+    last = len(tiles) - 1
+    for copy in sends(last):
+        copy.start()
+    for q in range(max(0, last - 2), last + 1):
+        for copy in sends(q):
+            copy.wait_send()
+    for q in range(last + 1):
+        for copy in sends(q):
+            copy.wait_recv()
+    for slot in range(4):
+        ref = keep_ref if slot < 2 else far_ref
+        ref[(slot % 2) * group_rows:(slot % 2 + 1) * group_rows, :] = own[slot] + recv[slot]
+
+
+def weight_grads(kind, arrays, tiles, group_rows):
+    count, width = arrays[0].shape[0], 640
+    chips = max(len(t[-1]) for t in tiles)
+    out = jax.ShapeDtypeStruct((2 * group_rows, width), F32)
+    return pl.pallas_call(
+        functools.partial(grad_kernel, tiles, group_rows, len(arrays)), in_specs=[ANY] * len(arrays),
+        out_specs=[pl.BlockSpec(memory_space=pltpu.VMEM)] * 2, out_shape=[out, out],
+        scratch_shapes=[pltpu.VMEM((2, count, width), BF16), pltpu.VMEM((width, count), BF16), pltpu.VMEM((2, count, width), BF16),
+                        pltpu.VMEM((3, width, width), F32), pltpu.VMEM((4, group_rows, width), F32),
+                        pltpu.VMEM((4, group_rows, width), F32), pltpu.SemaphoreType.DMA((2,)), pltpu.SemaphoreType.DMA((2,)),
+                        pltpu.SemaphoreType.DMA((3, chips)), pltpu.SemaphoreType.DMA((len(tiles), chips))],
+        cost_estimate=pl.CostEstimate(flops=2 * count * width * width * len(tiles), bytes_accessed=int(2e7), transcendentals=0),
+        compiler_params=pltpu.CompilerParams(collective_id=kind, has_side_effects=True, vmem_limit_bytes=VMEM_LIMIT))(*arrays)
+
+
+def context_grad_kernel(ctx_ref, mine_ref, other_ref, far_ref, keep_ref, d_kv):
+    rows, width = mine_ref.shape[0], far_ref.shape[1]
+    d_kv[0:rows, :] = mine_ref[...]
+    d_kv[rows:2 * rows, :] = other_ref[...]
+    depth = ctx_ref.shape[0] // 4
+    for slot in range(4):
+        ref = keep_ref if slot < 2 else far_ref
+        for block in range(2):
+            start = ((slot % 2) * 2 + block) * depth
+            ref[start:start + depth, :] = dot_nn(ctx_ref[slot * depth:(slot + 1) * depth, :], d_kv[:, block * width:(block + 1) * width])
+
+
+def context_grad(turned, mine, other):
+    width = mine.shape[1] // 2
+    out = jax.ShapeDtypeStruct((turned.shape[0], width), F32)
+    vmem = pl.BlockSpec(memory_space=pltpu.VMEM)
+    return pl.pallas_call(
+        context_grad_kernel, in_specs=[vmem] * 3, out_specs=[vmem] * 2, out_shape=[out, out],
+        scratch_shapes=[pltpu.VMEM((2 * mine.shape[0], 2 * width), BF16)],
+        cost_estimate=pl.CostEstimate(flops=2 * turned.size * 2 * width, bytes_accessed=int(2e7), transcendentals=0),
+        compiler_params=pltpu.CompilerParams(vmem_limit_bytes=VMEM_LIMIT), name='context_grad')(turned, mine, other)
+
+
+def context_columns(ctx, n_dev):
+    _, _, core_perm = gather_perms(n_dev)
+    me = lax.axis_index(AXIS)
+    core, chip = me % 2, me // 2
+    each = ctx.shape[1] // n_dev
+    x = jnp.bitwise_xor
+
+    def columns(of_core):
+        one, two = 1 + of_core, 2 - of_core
+        chips = [chip, x(chip, two), x(chip, one), x(chip, 3)]
+        return jnp.concatenate([lax.dynamic_slice(ctx, (0, (2 * c + of_core) * each), (ctx.shape[0], each)) for c in chips], 1)
+
+    other = permute(columns(1 - core), core_perm)
+    return jnp.concatenate([columns(core), other], 0).T
+
+
+def finish_scatter(far, keep, n_dev):
+    near_perm, far_perm, _ = gather_perms(n_dev)
+    rows = keep.shape[0] // 2
+    second = permute(far, far_perm)
+    third = permute(keep[rows:] + second[rows:], near_perm)
+    return keep[:rows] + second[:rows] + third
 
 
 def solution(mesh):
@@ -545,7 +744,9 @@
         views = []
         for shard, rows in zip(shards[:7], (depth, depth, depth, ctx_width // n_dev, depth, depth, half // n_dev)):
             views.append(shard.reshape(blocks, rows, -1))
-        qkv_s, out_s, q2_s, kv2_s, out2_s, ff1_s, ff2_s = lax.optimization_barrier(views)
+        qkv_s, out_s = lax.optimization_barrier(views[:2])
+        q2_s, kv2_s, out2_s = lax.optimization_barrier(views[2:5])
+        ff1_s, ff2_s = lax.optimization_barrier(views[5:])
         me = lax.axis_index(AXIS)
         vec_len = shards[7].shape[1]
         vec_each = 17
@@ -554,53 +755,72 @@
         vec_block = vec_block[:, :vec_each * width].reshape(blocks * vec_each, width)
         vec_block = jnp.pad(vec_block, ((0, vec_rows - blocks * vec_each), (0, 0)))
 
+        members = []
+        for layer in range(blocks):
+            members += [(layer, [qkv_s, out_s]), (layer, [kv2_s, q2_s, out2_s])]
+            members += [(layer, [ff1_s, ff2_s])] if layer < blocks - 1 else [(layer, [ff1_s]), (layer, [ff2_s])]
         groups = []
-        for layer in range(blocks):
-            extra = [vec_block] if layer == 0 else []
-            for index, members in enumerate(([qkv_s, out_s], [kv2_s, q2_s, out2_s], [ff1_s, ff2_s])):
-                block = pack(members, layer, extra if index == 0 else [], width)
-                groups.append(gather_group(block, n_dev))
+        for index, (layer, parts) in enumerate(members):
+            block = pack(parts, layer, [vec_block] if index == 0 else [], width)
+            groups.append(gather_group(block, n_dev))
+        ff_groups = [groups[3 * layer + 2] * 2 if layer < blocks - 1 else groups[-2] + groups[-1] for layer in range(blocks)]
+        ff_offsets = [8 * depth if layer < blocks - 1 else 0 for layer in range(blocks)]
 
         group_rows = groups[0][0].shape[0]
         vecs = jnp.zeros((vec_rows, width), F32)
-        for array, start, _ in piece_table(me, group_rows):
-            vecs = vecs + groups[0][array][start + group_rows - vec_rows:start + group_rows].astype(F32)
+        for piece in groups[0]:
+            vecs = vecs + piece[group_rows - vec_rows:].astype(F32)
         vecs = vecs[:blocks * vec_each].reshape(blocks, vec_each, width)
         rows_all = jnp.pad(vecs[:, :9], ((0, 0), (0, 7), (0, 0)))
         bias_all = vecs[:, 9:].reshape(blocks, 1, 8 * width)
 
         padded = (valid + 15) // 16 * 16
         ctx = jnp.pad(context, ((0, 0), (0, padded - valid), (0, 0))).reshape(batch * padded, ctx_width)
+
+        turned_ctx = context_columns(ctx, n_dev)
 
         h = tokens_x.reshape(count, width)
         saved = []
         for layer in range(blocks):
             rows, bias = rows_all[layer], bias_all[layer]
-            group = groups[3 * layer:3 * layer + 3]
+            group = groups[3 * layer:3 * layer + 2]
             norm1, qkv, mix1, h1 = self_forward(h, rows, group[0], tokens)
             norm2, query, kv, mix2, h2 = cross_forward(h1, rows, ctx, group[1], tokens, valid)
-            last = layer == blocks - 1
-            norm3, gated, save_a, save_g, h3 = ff_forward(h2, rows, bias, group[2], BF16 if last else F32)
+            if layer < blocks - 1:
+                norm3, gated, save_a, save_g, h3 = ff_forward(h2, rows, bias, ff_groups[layer], ff_offsets[layer])
+            else:
+                norm3, gated, save_a, save_g = ff_up_forward(h2, rows, bias, groups[-2])
+                out_tokens = ff_down_forward(h2, rows, gated, groups[-1])
             saved.append((h, norm1, qkv, mix1, h1, norm2, query, kv, mix2, h2, norm3, gated, save_a, save_g))
-            h = h3
-        out_tokens = h
+            h = h3 if layer < blocks - 1 else None
 
         grad = cot_out.reshape(count, width)
         results, vec_grads = [None] * blocks, [None] * blocks
+        every = tuple(range(n_dev // 2))
+        by_column = lambda x, y, columns, first: [(x, 0, y, c * width, first + c * depth, depth, every) for c in range(columns)]
+        _, _, core_perm = gather_perms(n_dev)
         for layer in reversed(range(blocks)):
-            rows, group = rows_all[layer], groups[3 * layer:3 * layer + 3]
+            rows, group = rows_all[layer], groups[3 * layer:3 * layer + 2]
             h0, norm1, qkv, mix1, h1, norm2, query, kv, mix2, h2, norm3, gated, save_a, save_g = saved[layer]
-            g_ff2 = scatter_sum(weight_grad(gated, grad.astype(BF16)), n_dev)
-            d_hidden, grad, vec3, vec_b1 = ff_backward(grad, save_a, save_g, h2, rows, group[2])
-            g_ff1 = scatter_sum(weight_grad(norm3, d_hidden), n_dev)
+
+            def reduce(pair):
+                return finish_scatter(pair[0], pair[1], n_dev)
+
+            r_ff2 = reduce(weight_grads(1, (gated, grad.astype(BF16)),
+                                           [(0, c * width, 1, 0, 0, half // n_dev, (c,)) for c in range(half // width)], half // n_dev))
+            d_hidden, grad, vec3, vec_b1 = ff_backward(grad, save_a, save_g, h2, rows, ff_groups[layer], ff_offsets[layer])
+            r_ff1 = reduce(weight_grads(2, (norm3, d_hidden), by_column(0, 1, 8, 0), 8 * depth))
             grad_bf, d_query, d_kv, grad, vec2 = cross_backward(grad, query, kv, h1, rows, group[1], tokens, valid)
-            g_out2 = scatter_sum(weight_grad(mix2, grad_bf), n_dev)
-            g_q2 = scatter_sum(weight_grad(norm2, d_query), n_dev)
-            g_kv2 = scatter_sum(weight_grad(ctx, d_kv), n_dev)
+            d_kv_other = permute(d_kv, core_perm)
+            r_cross = reduce(weight_grads(3, (norm2, d_query, mix2, grad_bf),
+                                             by_column(0, 1, 1, 0) + by_column(2, 3, 1, depth), 2 * depth))
+            r_kv = reduce(context_grad(turned_ctx, d_kv, d_kv_other))
             grad_bf, d_qkv, grad, vec1 = self_backward(grad, qkv, h0, rows, group[0], tokens, BF16 if layer == 0 else F32)
-            g_out = scatter_sum(weight_grad(mix1, grad_bf), n_dev)
-            g_qkv = scatter_sum(weight_grad(norm1, d_qkv), n_dev)
-            results[layer] = [g_qkv, g_out, g_q2, g_kv2, g_out2, g_ff1, g_ff2]
+            r_self = reduce(weight_grads(4, (norm1, d_qkv, mix1, grad_bf),
+                                            by_column(0, 1, 3, 0) + by_column(2, 3, 1, 3 * depth), 4 * depth))
+            side = lambda array, blocks_of: jnp.concatenate(jnp.split(array, blocks_of, 0), 1)
+            results[layer] = [side(r_self[:3 * depth], 3), r_self[3 * depth:], r_cross[:depth], side(r_kv, 2), r_cross[depth:],
+                              side(r_ff1, 8), r_ff2]
             vec_grads[layer] = jnp.concatenate([vec1[0], vec1[1], vec2[0], vec2[1], vec3[0], vec3[1],
                                                 vec1[2], vec2[2], vec3[2], vec_b1[0]])
         vec_full = jnp.stack([jnp.pad(g, (0, vec_len * n_dev - g.shape[0])).reshape(n_dev, vec_len) for g in vec_grads], 1)

time: 1040 us -> 980 us (0.942)
  Pallas kernels: 379 us -> 538 us
  matrix products: 82.7 us -> 0 us
  other arithmetic: 104 us -> 24.2 us
  local copies, waits for them, and re-layouts: 93.9 us -> 48.3 us
  waiting for transfers between devices: 309 us -> 297 us
    pallas_call x4 -> x15, Pallas kernels: 146 us -> 303 us  [the longest x8 149 us: weight_grads(): pl.pallas_call(functools.partial(grad_kernel, tiles, group_rows, len(arra...]
    dot_general x14 -> x0, matrix products: 82.7 us -> none  [weight_grad(): lax.dot_general(inputs, grads, (((0,), (0,)), ((), ())), preferred_elemen...]
    squeeze x14 -> x0, local copies, waits for them, and re-layouts: 26.5 us -> none  [scatter_sum(): lax.dynamic_index_in_dim(by_chip, 1 - core, 1, keepdims=False)]
    add x15 -> x1, other arithmetic: 25.3 us -> 0.03 us  [scatter_sum(): third = permute(part(x(chip, two)) + second[1], near)]
    add x15 -> x1, other arithmetic: 23.3 us -> 0.04 us  [scatter_sum(): part = lambda index: ours(index) + pick(got, index)]
    another operation x14 -> x6, other arithmetic: 26 us -> 2.83 us  [inner(): jnp.stack([results[layer][index] for layer in range(blocks)]) / total]
    dot_general x2 -> x0, local copies, waits for them, and re-layouts: 13.6 us -> none  [weight_grad(): lax.dot_general(inputs, grads, (((0,), (0,)), ((), ())), preferred_elemen...]
    concatenate x6 -> x1, other arithmetic: 13.2 us -> 0.12 us  [columns(): jnp.concatenate([lax.dynamic_slice(ctx, (0, (2 * c + of_core) * each), (c...]
  transfers between devices with their start and end apart: 75 -> 75, of which waited for: 27 -> 23; matrix products, arithmetic and copies ran while one was open for 23% -> 5% of each run, Pallas kernels for 12% -> 34%
where the time goes in v1:
time: 980 us; the launch traced here: 971 us
  Pallas kernels  538 us (55%)
  waiting for transfers between devices  297 us (30%)
  starting transfers between devices  61.3 us (6%)
  local copies, waits for them, and re-layouts  48.3 us (5%)
  other arithmetic  24.2 us (2%)
    ppermute x75, waiting for transfers between devices, permute(): return lax.ppermute(array, AXIS, perm)  297 us
    pallas_call x8, Pallas kernels, weight_grads(): pl.pallas_call(functools.partial(grad_kernel, tiles, group_rows, len(arra...  149 us
    pallas_call x2, Pallas kernels, self_backward(): call(functools.partial(self_backward_kernel, STEP // tokens, tokens), cou...  84.1 us
    pallas_call x2, Pallas kernels, ff_backward(): call(functools.partial(ff_backward_kernel, offset), count // FF_STEP, [by...  67.3 us
    ppermute x75, starting transfers between devices, permute(): return lax.ppermute(array, AXIS, perm)  61.3 us
    pallas_call x2, Pallas kernels, cross_backward(): call(functools.partial(cross_backward_kernel, STEP // tokens, tokens, val...  55.9 us
    pallas_call x2, Pallas kernels, self_forward(): call(functools.partial(self_forward_kernel, STEP // tokens, tokens), coun...  41 us
    pallas_call x2, Pallas kernels, cross_forward(): call(functools.partial(cross_forward_kernel, STEP // tokens, tokens, vali...  39.2 us
  transfers between devices with their start and end apart: 75, of which 23 were waited for; matrix products, arithmetic and copies ran while one was open for 5% of the time, Pallas kernels for 34%

profile of v1, /device:TPU:0, one launch (start us, length us, event | category | flops | bytes accessed | tf_op | source)
XLA Modules:
  0.0 970.9 jit_solution(3717168611540382445)
XLA Ops:
  0.7 2.1 copy.67
  4.4 1.8 pack.10.refs_0_
  6.1 3.3 collective-permute-start.21
  13.4 1.8 pack.13.refs_0_.refs_8_
  16.8 1.9 pack.7.refs_0_
  21.0 1.7 collective-permute-start.43
  22.8 4.1 collective-permute-done.42.refs_1_.refs_9_
  27.7 2.1 pack.12.refs_0_
  29.8 8.2 collective-permute-done.43.refs_2_.refs_10_
  38.0 1.8 collective-permute-start.35
  43.4 2.1 pack.8.refs_0_
  48.7 2.1 pack.11.refs_0_
  50.8 8.7 collective-permute-done.35.refs_1_
  59.4 1.8 collective-permute-start.28
  61.2 1.9 collective-permute-start.29
  63.1 1.7 pad.14
  64.8 3.1 pack.9.refs_0_.refs_8_
  67.9 9.9 %collective-permute-done.7.refs_1_ = bf16[672,640]{1,0:T(8,128)(2,1)} collective-permute-done((bf16[672,640]{1,0:T(8,128)(2,1)}, bf16[672,640]{1,0:T(8,128)(2,1)}, u32[]{:S(2)}, u32[]{:S(2)}) %collective-permute-start.7) | collective-permute-done | bytes 860192 | tf_op jit(solution)/shard_map/ppermute | solution.py:54
  77.9 1.8 collective-permute-start.14
  82.4 13.9 %collective-permute-done.28.refs_1_ = bf16[672,640]{1,0:T(8,128)(2,1)} collective-permute-done((bf16[672,640]{1,0:T(8,128)(2,1)}, bf16[672,640]{1,0:T(8,128)(2,1)}, u32[]{:S(2)}, u32[]{:S(2)}) %collective-permute-start.28) | collective-permute-done | bytes 860192 | tf_op jit(solution)/shard_map/ppermute | solution.py:54
  96.3 1.8 collective-permute-done.29.refs_2_
  99.4 8.8 collective-permute-done.2.refs_3_
  115.8 3.3 collective-permute-done.14.refs_1_.refs_9_
  129.9 3.2 maximum_bitcast_fusion.ctx_ref
  135.4 2.0 collective-permute-done.15.refs_2_.refs_10_
  139.0 11.6 %collective-permute-done.16.refs_3_.refs_11_ = bf16[960,640]{1,0:T(8,128)(2,1)} collective-permute-done((bf16[960,640]{1,0:T(8,128)(2,1)}, bf16[960,640]{1,0:T(8,128)(2,1)}, u32[]{:S(2)}, u32[]{:S(2)}) %collective-permute-start.16) | collective-permute-done | bytes 1228832 | tf_op jit(solution)/shard_map/ppermute | solution.py:54
  153.2 20.3 %shard_map.186 = (bf16[1536,640]{1,0:T(8,128)(2,1)}, bf16[1536,1920]{1,0:T(8,128)(2,1)}, bf16[1536,640]{1,0:T(8,128)(2,1)}, f32[1536,640]{1,0:T(8,128)}) custom-call(bf16[1536,640]{1,0:T(8,128)(2,1)} %bitcast.155, f32[16,640]{1,0:T(8,128)} %get-tuple-element.217.rows_ref, bf16[368,640]{1,0:T(8,128)(2,1)} %pack.7.refs_0_, bf16[368,640]{1,0:T(8,128)(2,1)} %copy-done.36, ...), custom_call_target="tpu_custom_call" | custom-call | flops 6039797760 | bytes 20000000 | tf_op jit(solution)/shard_map/pallas_call | solution.py:472
  173.5 19.8 %shard_map.187 = (bf16[1536,640]{1,0:T(8,128)(2,1)}, bf16[1536,640]{1,0:T(8,128)(2,1)}, bf16[480,1280]{1,0:T(8,128)(2,1)}, bf16[1536,640]{1,0:T(8,128)(2,1)}, f32[1536,640]{1,0:T(8,128)}) custom-call(f32[1536,640]{1,0:T(8,128)} %get-tuple-element.92.h_ref, f32[16,640]{1,0:T(8,128)} %get-tuple-element.217.rows_ref, bf16[480,2048]{1,0:T(8,128)(2,1)} %bitcast.122, ...), custom_call_target="tpu_custom_call" | custom-call | flops 5536481280 | bytes 20000000 | tf_op jit(solution)/shard_map/pallas_call | solution.py:484
  195.6 31.8 %shard_map.188 = (bf16[1536,640]{1,0:T(8,128)(2,1)}, bf16[1536,2560]{1,0:T(8,128)(2,1)}, f32[1536,2560]{1,0:T(8,128)}, f32[1536,2560]{1,0:T(8,128)}, f32[1536,640]{1,0:T(8,128)}) custom-call(f32[1536,640]{1,0:T(8,128)} %get-tuple-element.96.h_ref, f32[16,640]{1,0:T(8,128)} %get-tuple-element.217.rows_ref, f32[1,5120]{1,0:T(1,128)} %bitcast.154, ...), custom_call_target="tpu_custom_call" | custom-call | flops 15099494400 | bytes 60000000 | tf_op jit(solution)/shard_map/pallas_call | solution.py:498
  228.4 20.7 %shard_map.189 = (bf16[1536,640]{1,0:T(8,128)(2,1)}, bf16[1536,1920]{1,0:T(8,128)(2,1)}, bf16[1536,640]{1,0:T(8,128)(2,1)}, f32[1536,640]{1,0:T(8,128)}) custom-call(f32[1536,640]{1,0:T(8,128)} %get-tuple-element.99.h_ref, f32[16,640]{1,0:T(8,128)} %get-tuple-element.216.rows_ref, bf16[320,640]{1,0:T(8,128)(2,1)} %pack.10.refs_0_, ...), custom_call_target="tpu_custom_call" | custom-call | flops 6039797760 | bytes 20000000 | tf_op jit(solution)/shard_map/pallas_call | solution.py:472
  250.6 19.4 %shard_map.190 = (bf16[1536,640]{1,0:T(8,128)(2,1)}, bf16[1536,640]{1,0:T(8,128)(2,1)}, bf16[480,1280]{1,0:T(8,128)(2,1)}, bf16[1536,640]{1,0:T(8,128)(2,1)}, f32[1536,640]{1,0:T(8,128)}) custom-call(f32[1536,640]{1,0:T(8,128)} %get-tuple-element.100.h_ref, f32[16,640]{1,0:T(8,128)} %get-tuple-element.216.rows_ref, bf16[480,2048]{1,0:T(8,128)(2,1)} %bitcast.123, ...), custom_call_target="tpu_custom_call" | custom-call | flops 5536481280 | bytes 20000000 | tf_op jit(solution)/shard_map/pallas_call | solution.py:484
  271.1 28.4 %shard_map.191 = (bf16[1536,640]{1,0:T(8,128)(2,1)}, bf16[1536,2560]{1,0:T(8,128)(2,1)}, f32[1536,2560]{1,0:T(8,128)}, f32[1536,2560]{1,0:T(8,128)}) custom-call(f32[1536,640]{1,0:T(8,128)} %get-tuple-element.101.h_ref, f32[16,640]{1,0:T(8,128)} %get-tuple-element.216.rows_ref, f32[1,5120]{1,0:T(1,128)} %bitcast.153, bf16[640,640]{1,0:T(8,128)(2,1)} %pack.12.refs_0_, ...), custom_call_target="tpu_custom_call" | custom-call | flops 10066329600 | bytes 50000000 | tf_op jit(solution)/shard_map/pallas_call | solution.py:511
  300.7 33.7 %shard_map.193 = (bf16[1536,5120]{1,0:T(8,128)(2,1)}, f32[1536,640]{1,0:T(8,128)}, f32[8,640]{1,0:T(8,128)}, f32[8,5120]{1,0:T(8,128)}) custom-call(bf16[1536,640]{1,0:T(8,128)(2,1)} %bitcast.157, f32[1536,2560]{1,0:T(8,128)} %get-tuple-element.103.save_a, f32[1536,2560]{1,0:T(8,128)} %get-tuple-element.104.save_g, f32[1536,640]{1,0:T(8,128)} %get-tuple-element.101.h_ref, ...), custom_call_target="tpu_custom_call" | custom-call | flops 15099494400 | bytes 60000000 | tf_op jit(solution)/shard_map/pallas_call | solution.py:534
  334.4 27.8 %shard_map.194 = (bf16[1536,640]{1,0:T(8,128)(2,1)}, bf16[1536,640]{1,0:T(8,128)(2,1)}, bf16[480,1280]{1,0:T(8,128)(2,1)}, f32[1536,640]{1,0:T(8,128)}, f32[8,640]{1,0:T(8,128)}) custom-call(f32[1536,640]{1,0:T(8,128)} %get-tuple-element.105.grad_ref, bf16[1536,640]{1,0:T(8,128)(2,1)} %get-tuple-element.106.query_ref, ...), custom_call_target="tpu_custom_call" | custom-call | flops 3774873600 | bytes 20000000 | tf_op jit(solution)/shard_map/pallas_call | solution.py:548
  362.2 42.3 %shard_map.195 = (bf16[1536,640]{1,0:T(8,128)(2,1)}, bf16[1536,1920]{1,0:T(8,128)(2,1)}, f32[1536,640]{1,0:T(8,128)}, f32[8,640]{1,0:T(8,128)}) custom-call(f32[1536,640]{1,0:T(8,128)} %get-tuple-element.108.grad_ref, bf16[1536,1920]{1,0:T(8,128)(2,1)} %get-tuple-element.109.qkv_ref, f32[1536,640]{1,0:T(8,128)} %get-tuple-element.99.h_ref, ...), custom_call_target="tpu_custom_call" | custom-call | flops 7549747200 | bytes 30000000 | tf_op jit(solution)/shard_map/pallas_call | solution.py:562
  408.3 3.6 convert_element_type.41.refs_1_
  411.9 33.7 %shard_map.196 = (bf16[1536,5120]{1,0:T(8,128)(2,1)}, f32[1536,640]{1,0:T(8,128)}, f32[8,640]{1,0:T(8,128)}, f32[8,5120]{1,0:T(8,128)}) custom-call(f32[1536,640]{1,0:T(8,128)} %get-tuple-element.110.grad_ref, f32[1536,2560]{1,0:T(8,128)} %get-tuple-element.111.save_a, f32[1536,2560]{1,0:T(8,128)} %get-tuple-element.112.save_g, ...), custom_call_target="tpu_custom_call" | custom-call | flops 15099494400 | bytes 60000000 | tf_op jit(solution)/shard_map/pallas_call | solution.py:534
  445.6 28.1 %shard_map.197 = (bf16[1536,640]{1,0:T(8,128)(2,1)}, bf16[1536,640]{1,0:T(8,128)(2,1)}, bf16[480,1280]{1,0:T(8,128)(2,1)}, f32[1536,640]{1,0:T(8,128)}, f32[8,640]{1,0:T(8,128)}) custom-call(f32[1536,640]{1,0:T(8,128)} %get-tuple-element.113.grad_ref, bf16[1536,640]{1,0:T(8,128)(2,1)} %get-tuple-element.114.query_ref, ...), custom_call_target="tpu_custom_call" | custom-call | flops 3774873600 | bytes 20000000 | tf_op jit(solution)/shard_map/pallas_call | solution.py:548
  473.7 41.8 %shard_map.198 = (bf16[1536,640]{1,0:T(8,128)(2,1)}, bf16[1536,1920]{1,0:T(8,128)(2,1)}, bf16[1536,640]{1,0:T(8,128)(2,1)}, f32[8,640]{1,0:T(8,128)}) custom-call(f32[1536,640]{1,0:T(8,128)} %get-tuple-element.116.grad_ref, bf16[1536,1920]{1,0:T(8,128)(2,1)} %get-tuple-element.117.qkv_ref, bf16[1536,640]{1,0:T(8,128)(2,1)} %bitcast.156, ...), custom_call_target="tpu_custom_call" | custom-call | flops 7549747200 | bytes 30000000 | tf_op jit(solution)/shard_map/pallas_call | solution.py:562
  519.4 17.6 %shard_map.205 = (f32[640,640]{1,0:T(8,128)}, f32[640,640]{1,0:T(8,128)}) custom-call(bf16[1536,2560]{1,0:T(8,128)(2,1)} %get-tuple-element.157.refs_0_, bf16[1536,640]{1,0:T(8,128)(2,1)} %convert_element_type.41.refs_1_), custom_call_target="tpu_custom_call" | custom-call | flops 5033164800 | bytes 20000000 | tf_op jit(solution)/shard_map/pallas_call | solution.py:674
  537.9 17.5 %shard_map.206 = (f32[640,640]{1,0:T(8,128)}, f32[640,640]{1,0:T(8,128)}) custom-call(bf16[1536,2560]{1,0:T(8,128)(2,1)} %get-tuple-element.102.gated_ref.refs_0_, bf16[1536,640]{1,0:T(8,128)(2,1)} %bitcast.158), custom_call_target="tpu_custom_call" | custom-call | flops 5033164800 | bytes 20000000 | tf_op jit(solution)/shard_map/pallas_call | solution.py:674
  556.5 11.8 %shard_map.201 = (f32[320,640]{1,0:T(8,128)}, f32[320,640]{1,0:T(8,128)}) custom-call(bf16[1536,640]{1,0:T(8,128)(2,1)} %get-tuple-element.131.refs_0_, bf16[1536,640]{1,0:T(8,128)(2,1)} %get-tuple-element.132.refs_1_, bf16[1536,640]{1,0:T(8,128)(2,1)} %get-tuple-element.133.refs_2_, bf16[1536,640]{1,0:T(8,128)(2,1)} %get-tuple-element.134.refs_3_), custom_call_target="tpu_custom_call" | custom-call | flops 2516582400 | bytes 20000000 | tf_op jit(solution)/shard_map/pallas_call | solution.py:674
  569.2 11.8 %shard_map.202 = (f32[320,640]{1,0:T(8,128)}, f32[320,640]{1,0:T(8,128)}) custom-call(bf16[1536,640]{1,0:T(8,128)(2,1)} %get-tuple-element.137.refs_0_, bf16[1536,640]{1,0:T(8,128)(2,1)} %get-tuple-element.138.refs_1_, bf16[1536,640]{1,0:T(8,128)(2,1)} %get-tuple-element.139.refs_2_, bf16[1536,640]{1,0:T(8,128)(2,1)} %get-tuple-element.140.refs_3_), custom_call_target="tpu_custom_call" | custom-call | flops 2516582400 | bytes 20000000 | tf_op jit(solution)/shard_map/pallas_call | solution.py:674
  582.2 27.7 %shard_map.203 = (f32[1280,640]{1,0:T(8,128)}, f32[1280,640]{1,0:T(8,128)}) custom-call(bf16[1536,640]{1,0:T(8,128)(2,1)} %get-tuple-element.149.refs_0_, bf16[1536,5120]{1,0:T(8,128)(2,1)} %get-tuple-element.150.refs_1_), custom_call_target="tpu_custom_call" | custom-call | flops 10066329600 | bytes 20000000 | tf_op jit(solution)/shard_map/pallas_call | solution.py:674
  609.8 27.8 %shard_map.204 = (f32[1280,640]{1,0:T(8,128)}, f32[1280,640]{1,0:T(8,128)}) custom-call(bf16[1536,640]{1,0:T(8,128)(2,1)} %get-tuple-element.153.refs_0_, bf16[1536,5120]{1,0:T(8,128)(2,1)} %get-tuple-element.154.refs_1_), custom_call_target="tpu_custom_call" | custom-call | flops 10066329600 | bytes 20000000 | tf_op jit(solution)/shard_map/pallas_call | solution.py:674
  637.6 17.5 %shard_map.199 = (f32[640,640]{1,0:T(8,128)}, f32[640,640]{1,0:T(8,128)}) custom-call(bf16[1536,640]{1,0:T(8,128)(2,1)} %get-tuple-element.119.refs_0_, bf16[1536,1920]{1,0:T(8,128)(2,1)} %get-tuple-element.120.refs_1_, bf16[1536,640]{1,0:T(8,128)(2,1)} %get-tuple-element.121.refs_2_, bf16[1536,640]{1,0:T(8,128)(2,1)} %get-tuple-element.122.refs_3_), custom_call_target="tpu_custom_call" | custom-call | flops 5033164800 | bytes 20000000 | tf_op jit(solution)/shard_map/pallas_call | solution.py:674
  655.1 17.1 %shard_map.200 = (f32[640,640]{1,0:T(8,128)}, f32[640,640]{1,0:T(8,128)}) custom-call(bf16[1536,640]{1,0:T(8,128)(2,1)} %get-tuple-element.125.refs_0_, bf16[1536,1920]{1,0:T(8,128)(2,1)} %get-tuple-element.126.refs_1_, bf16[1536,640]{1,0:T(8,128)(2,1)} %get-tuple-element.127.refs_2_, bf16[1536,640]{1,0:T(8,128)(2,1)} %get-tuple-element.128.refs_3_), custom_call_target="tpu_custom_call" | custom-call | flops 5033164800 | bytes 20000000 | tf_op jit(solution)/shard_map/pallas_call | solution.py:674
  673.2 12.2 %shard_map.192 = bf16[1536,640]{1,0:T(8,128)(2,1)} custom-call(f32[1536,640]{1,0:T(8,128)} %get-tuple-element.101.h_ref, f32[16,640]{1,0:T(8,128)} %get-tuple-element.216.rows_ref, bf16[1536,2560]{1,0:T(8,128)(2,1)} %get-tuple-element.102.gated_ref.refs_0_, bf16[320,640]{1,0:T(8,128)(2,1)} %pack.13.refs_0_.refs_8_, ...), custom_call_target="tpu_custom_call" | custom-call | flops 5033164800 | bytes 20000000 | tf_op jit(solution)/shard_map/pallas_call | solution.py:523
  691.0 3.7 collective-permute-done.54
  694.8 4.3 collective-permute-done.56
  703.3 7.3 context_grad.2
  711.5 7.2 context_grad.3
  726.0 27.8 %collective-permute-done.51 = f32[640,640]{1,0:T(8,128)} collective-permute-done((f32[640,640]{1,0:T(8,128)}, f32[640,640]{1,0:T(8,128)}, u32[]{:S(2)}, u32[]{:S(2)}) %collective-permute-start.51) | collective-permute-done | bytes 1638432 | tf_op jit(solution)/shard_map/ppermute | solution.py:54
  758.4 1.7 collective-permute-done.71
  762.4 2.4 copy.56
  764.9 12.8 %collective-permute-done.50 = f32[320,640]{1,0:T(8,128)S(1)} collective-permute-done((f32[320,640]{1,0:T(8,128)S(1)}, f32[320,640]{1,0:T(8,128)S(1)}, u32[]{:S(2)}, u32[]{:S(2)}) %collective-permute-start.50) | collective-permute-done | bytes 819232 | tf_op jit(solution)/shard_map/ppermute | solution.py:54
  779.9 15.3 %collective-permute-done.52 = f32[320,640]{1,0:T(8,128)S(1)} collective-permute-done((f32[320,640]{1,0:T(8,128)S(1)}, f32[320,640]{1,0:T(8,128)S(1)}, u32[]{:S(2)}, u32[]{:S(2)}) %collective-permute-start.52) | collective-permute-done | bytes 819232 | tf_op jit(solution)/shard_map/ppermute | solution.py:54
  797.6 10.6 %collective-permute-done.64 = f32[1280,640]{1,0:T(8,128)S(1)} collective-permute-done((f32[1280,640]{1,0:T(8,128)}, f32[1280,640]{1,0:T(8,128)S(1)}, u32[]{:S(2)}, u32[]{:S(2)}) %collective-permute-start.64) | collective-permute-done | bytes 3276832 | tf_op jit(solution)/shard_map/ppermute | solution.py:54
  811.1 49.7 %collective-permute-done.66 = f32[1280,640]{1,0:T(8,128)S(1)} collective-permute-done((f32[1280,640]{1,0:T(8,128)}, f32[1280,640]{1,0:T(8,128)S(1)}, u32[]{:S(2)}, u32[]{:S(2)}) %collective-permute-start.66) | collective-permute-done | bytes 3276832 | tf_op jit(solution)/shard_map/ppermute | solution.py:54
  861.9 44.6 %collective-permute-done.59 = f32[1024,640]{1,0:T(8,128)S(1)} collective-permute-done((f32[1024,640]{1,0:T(8,128)}, f32[1024,640]{1,0:T(8,128)S(1)}, u32[]{:S(2)}, u32[]{:S(2)}) %collective-permute-start.59) | collective-permute-done | bytes 2621472 | tf_op jit(solution)/shard_map/ppermute | solution.py:54
  907.8 40.9 %collective-permute-done.62 = f32[1024,640]{1,0:T(8,128)S(1)} collective-permute-done((f32[1024,640]{1,0:T(8,128)S(1)}, f32[1024,640]{1,0:T(8,128)S(1)}, u32[]{:S(2)}, u32[]{:S(2)}) %collective-permute-start.62) | collective-permute-done | bytes 2621472 | tf_op jit(solution)/shard_map/ppermute | solution.py:54
  950.9 4.2 copy.55
  955.4 11.0 %collective-permute-done.63 = f32[512,640]{1,0:T(8,128)S(1)} collective-permute-done((f32[512,640]{1,0:T(8,128)S(1)}, f32[512,640]{1,0:T(8,128)S(1)}, u32[]{:S(2)}, u32[]{:S(2)}) %collective-permute-start.63) | collective-permute-done | bytes 1310752 | tf_op jit(solution)/shard_map/ppermute | solution.py:54
  967.1 3.5 copy.53
  (348 shorter events, 103.0 us)
Async XLA Ops:
  6.1 14.2 %collective-permute-start.21 = (bf16[320,640]{1,0:T(8,128)(2,1)}, bf16[320,640]{1,0:T(8,128)(2,1)}, u32[]{:S(2)}, u32[]{:S(2)}) collective-permute-start(bf16[320,640]{1,0:T(8,128)(2,1)} %pack.10.refs_0_), channel_id=1, source_target_pairs={{0,4},{1,3},{2,6},{3,1},{4,0},{5,7},{6,2},{7,5}} | collective-permute-start | bytes 1228808 | tf_op jit(solution)/shard_map/ppermute | solution.py:54
  18.7 21.1 %collective-permute-start = (bf16[368,640]{1,0:T(8,128)(2,1)}, bf16[368,640]{1,0:T(8,128)(2,1)S(1)}, u32[]{:S(2)}, u32[]{:S(2)}) collective-permute-start(bf16[368,640]{1,0:T(8,128)(2,1)} %pack.7.refs_0_), channel_id=1, source_target_pairs={{0,4},{1,3},{2,6},{3,1},{4,0},{5,7},{6,2},{7,5}} | collective-permute-start | bytes 1413128 | tf_op jit(solution)/shard_map/ppermute | solution.py:54
  20.4 20.9 %collective-permute-start.1 = (bf16[368,640]{1,0:T(8,128)(2,1)}, bf16[368,640]{1,0:T(8,128)(2,1)S(1)}, u32[]{:S(2)}, u32[]{:S(2)}) collective-permute-start(bf16[368,640]{1,0:T(8,128)(2,1)} %pack.7.refs_0_), channel_id=1, source_target_pairs={{0,2},{1,5},{2,0},{3,7},{4,6},{5,1},{6,4},{7,3}} | collective-permute-start | bytes 1413128 | tf_op jit(solution)/shard_map/ppermute | solution.py:54
  21.0 17.0 %collective-permute-start.43 = (bf16[320,640]{1,0:T(8,128)(2,1)}, bf16[320,640]{1,0:T(8,128)(2,1)S(1)}, u32[]{:S(2)}, u32[]{:S(2)}) collective-permute-start(bf16[320,640]{1,0:T(8,128)(2,1)} %pack.13.refs_0_.refs_8_), channel_id=1, source_target_pairs={{0,2},{1,5},{2,0},{3,7},{4,6},{5,1},{6,4},{7,3}} | collective-permute-start | bytes 1228808 | tf_op jit(solution)/shard_map/ppermute | solution.py:54
  22.8 22.7 %collective-permute-start.3 = (bf16[368,640]{1,0:T(8,128)(2,1)}, bf16[368,640]{1,0:T(8,128)(2,1)S(1)}, u32[]{:S(2)}, u32[]{:S(2)}) collective-permute-start(bf16[368,640]{1,0:T(8,128)(2,1)} %pack.7.refs_0_), channel_id=1, source_target_pairs={{0,1},{1,0},{2,3},{3,2},{4,5},{5,4},{6,7},{7,6}} | collective-permute-start | bytes 1413128 | tf_op jit(solution)/shard_map/ppermute | solution.py:54
  26.9 19.1 %collective-permute-start.23 = (bf16[320,640]{1,0:T(8,128)(2,1)}, bf16[320,640]{1,0:T(8,128)(2,1)}, u32[]{:S(2)}, u32[]{:S(2)}) collective-permute-start(bf16[320,640]{1,0:T(8,128)(2,1)} %collective-permute-done.21.refs_1_), channel_id=1, source_target_pairs={{0,2},{1,5},{2,0},{3,7},{4,6},{5,1},{6,4},{7,3}} | collective-permute-start | bytes 1228808 | tf_op jit(solution)/shard_map/ppermute | solution.py:54
  38.0 21.4 %collective-permute-start.35 = (bf16[640,640]{1,0:T(8,128)(2,1)}, bf16[640,640]{1,0:T(8,128)(2,1)}, u32[]{:S(2)}, u32[]{:S(2)}) collective-permute-start(bf16[640,640]{1,0:T(8,128)(2,1)} %pack.12.refs_0_), channel_id=1, source_target_pairs={{0,4},{1,3},{2,6},{3,1},{4,0},{5,7},{6,2},{7,5}} | collective-permute-start | bytes 2457608 | tf_op jit(solution)/shard_map/ppermute | solution.py:54
  39.8 21.4 %collective-permute-start.36 = (bf16[640,640]{1,0:T(8,128)(2,1)}, bf16[640,640]{1,0:T(8,128)(2,1)}, u32[]{:S(2)}, u32[]{:S(2)}) collective-permute-start(bf16[640,640]{1,0:T(8,128)(2,1)} %pack.12.refs_0_), channel_id=1, source_target_pairs={{0,2},{1,5},{2,0},{3,7},{4,6},{5,1},{6,4},{7,3}} | collective-permute-start | bytes 2457608 | tf_op jit(solution)/shard_map/ppermute | solution.py:54
  45.5 32.4 %collective-permute-start.7 = (bf16[672,640]{1,0:T(8,128)(2,1)}, bf16[672,640]{1,0:T(8,128)(2,1)}, u32[]{:S(2)}, u32[]{:S(2)}) collective-permute-start(bf16[672,640]{1,0:T(8,128)(2,1)} %pack.8.refs_0_), channel_id=1, source_target_pairs={{0,4},{1,3},{2,6},{3,1},{4,0},{5,7},{6,2},{7,5}} | collective-permute-start | bytes 2580488 | tf_op jit(solution)/shard_map/ppermute | solution.py:54
  46.6 33.5 %collective-permute-start.8 = (bf16[672,640]{1,0:T(8,128)(2,1)}, bf16[672,640]{1,0:T(8,128)(2,1)}, u32[]{:S(2)}, u32[]{:S(2)}) collective-permute-start(bf16[672,640]{1,0:T(8,128)(2,1)} %pack.8.refs_0_), channel_id=1, source_target_pairs={{0,2},{1,5},{2,0},{3,7},{4,6},{5,1},{6,4},{7,3}} | collective-permute-start | bytes 2580488 | tf_op jit(solution)/shard_map/ppermute | solution.py:54
  48.3 32.7 %collective-permute-start.10 = (bf16[672,640]{1,0:T(8,128)(2,1)}, bf16[672,640]{1,0:T(8,128)(2,1)}, u32[]{:S(2)}, u32[]{:S(2)}) collective-permute-start(bf16[672,640]{1,0:T(8,128)(2,1)} %pack.8.refs_0_), channel_id=1, source_target_pairs={{0,1},{1,0},{2,3},{3,2},{4,5},{5,4},{6,7},{7,6}} | collective-permute-start | bytes 2580488 | tf_op jit(solution)/shard_map/ppermute | solution.py:54
  59.4 36.9 %collective-permute-start.28 = (bf16[672,640]{1,0:T(8,128)(2,1)}, bf16[672,640]{1,0:T(8,128)(2,1)}, u32[]{:S(2)}, u32[]{:S(2)}) collective-permute-start(bf16[672,640]{1,0:T(8,128)(2,1)} %pack.11.refs_0_), channel_id=1, source_target_pairs={{0,4},{1,3},{2,6},{3,1},{4,0},{5,7},{6,2},{7,5}} | collective-permute-start | bytes 2580488 | tf_op jit(solution)/shard_map/ppermute | solution.py:54
  61.2 36.9 %collective-permute-start.29 = (bf16[672,640]{1,0:T(8,128)(2,1)}, bf16[672,640]{1,0:T(8,128)(2,1)}, u32[]{:S(2)}, u32[]{:S(2)}) collective-permute-start(bf16[672,640]{1,0:T(8,128)(2,1)} %pack.11.refs_0_), channel_id=1, source_target_pairs={{0,2},{1,5},{2,0},{3,7},{4,6},{5,1},{6,4},{7,3}} | collective-permute-start | bytes 2580488 | tf_op jit(solution)/shard_map/ppermute | solution.py:54
  77.9 41.2 %collective-permute-start.14 = (bf16[960,640]{1,0:T(8,128)(2,1)}, bf16[960,640]{1,0:T(8,128)(2,1)}, u32[]{:S(2)}, u32[]{:S(2)}) collective-permute-start(bf16[960,640]{1,0:T(8,128)(2,1)} %pack.9.refs_0_.refs_8_), channel_id=1, source_target_pairs={{0,4},{1,3},{2,6},{3,1},{4,0},{5,7},{6,2},{7,5}} | collective-permute-start | bytes 3686408 | tf_op jit(solution)/shard_map/ppermute | solution.py:54
  80.1 35.6 %collective-permute-start.57 = (bf16[480,1024]{1,0:T(8,128)(2,1)S(1)}, bf16[480,1024]{1,0:T(8,128)(2,1)}, u32[]{:S(2)}, u32[]{:S(2)}) collective-permute-start(bf16[480,1024]{1,0:T(8,128)(2,1)S(1)} %pad_maximum_fusion), channel_id=1, source_target_pairs={{0,1},{1,0},{2,3},{3,2},{4,5},{5,4},{6,7},{7,6}} | collective-permute-start | bytes 2949128 | tf_op jit(solution)/shard_map/ppermute | solution.py:54
  81.0 27.2 %collective-permute-start.2 = (bf16[368,640]{1,0:T(8,128)(2,1)S(1)}, bf16[368,640]{1,0:T(8,128)(2,1)}, u32[]{:S(2)}, u32[]{:S(2)}) collective-permute-start(bf16[368,640]{1,0:T(8,128)(2,1)S(1)} %copy-done.37), channel_id=1, source_target_pairs={{0,2},{1,5},{2,0},{3,7},{4,6},{5,1},{6,4},{7,3}} | collective-permute-start | bytes 1413128 | tf_op jit(solution)/shard_map/ppermute | solution.py:54
  96.3 13.2 %collective-permute-start.4 = (bf16[368,640]{1,0:T(8,128)(2,1)S(1)}, bf16[368,640]{1,0:T(8,128)(2,1)S(1)}, u32[]{:S(2)}, u32[]{:S(2)}) collective-permute-start(bf16[368,640]{1,0:T(8,128)(2,1)S(1)} %copy-done.37), channel_id=1, source_target_pairs={{0,1},{1,0},{2,3},{3,2},{4,5},{5,4},{6,7},{7,6}} | collective-permute-start | bytes 1413128 | tf_op jit(solution)/shard_map/ppermute | solution.py:54
  108.2 21.2 %collective-permute-start.31 = (bf16[672,640]{1,0:T(8,128)(2,1)}, bf16[672,640]{1,0:T(8,128)(2,1)}, u32[]{:S(2)}, u32[]{:S(2)}) collective-permute-start(bf16[672,640]{1,0:T(8,128)(2,1)} %pack.11.refs_0_), channel_id=1, source_target_pairs={{0,1},{1,0},{2,3},{3,2},{4,5},{5,4},{6,7},{7,6}} | collective-permute-start | bytes 2580488 | tf_op jit(solution)/shard_map/ppermute | solution.py:54
  109.5 24.4 %collective-permute-start.9 = (bf16[672,640]{1,0:T(8,128)(2,1)}, bf16[672,640]{1,0:T(8,128)(2,1)}, u32[]{:S(2)}, u32[]{:S(2)}) collective-permute-start(bf16[672,640]{1,0:T(8,128)(2,1)} %collective-permute-done.7.refs_1_), channel_id=1, source_target_pairs={{0,2},{1,5},{2,0},{3,7},{4,6},{5,1},{6,4},{7,3}} | collective-permute-start | bytes 2580488 | tf_op jit(solution)/shard_map/ppermute | solution.py:54
  111.1 18.3 %collective-permute-start.6 = (bf16[368,640]{1,0:T(8,128)(2,1)}, bf16[368,640]{1,0:T(8,128)(2,1)}, u32[]{:S(2)}, u32[]{:S(2)}) collective-permute-start(bf16[368,640]{1,0:T(8,128)(2,1)} %collective-permute-done.2.refs_3_), channel_id=1, source_target_pairs={{0,1},{1,0},{2,3},{3,2},{4,5},{5,4},{6,7},{7,6}} | collective-permute-start | bytes 1413128 | tf_op jit(solution)/shard_map/ppermute | solution.py:54
  115.7 21.7 %collective-permute-start.15 = (bf16[960,640]{1,0:T(8,128)(2,1)S(1)}, bf16[960,640]{1,0:T(8,128)(2,1)S(1)}, u32[]{:S(2)}, u32[]{:S(2)}) collective-permute-start(bf16[960,640]{1,0:T(8,128)(2,1)S(1)} %copy-done), channel_id=1, source_target_pairs={{0,2},{1,5},{2,0},{3,7},{4,6},{5,1},{6,4},{7,3}} | collective-permute-start | bytes 3686408 | tf_op jit(solution)/shard_map/ppermute | solution.py:54
  119.0 31.6 %collective-permute-start.16 = (bf16[960,640]{1,0:T(8,128)(2,1)}, bf16[960,640]{1,0:T(8,128)(2,1)}, u32[]{:S(2)}, u32[]{:S(2)}) collective-permute-start(bf16[960,640]{1,0:T(8,128)(2,1)} %collective-permute-done.14.refs_1_.refs_9_), channel_id=1, source_target_pairs={{0,2},{1,5},{2,0},{3,7},{4,6},{5,1},{6,4},{7,3}} | collective-permute-start | bytes 3686408 | tf_op jit(solution)/shard_map/ppermute | solution.py:54
  133.9 18.1 %collective-permute-start.13 = (bf16[672,640]{1,0:T(8,128)(2,1)}, bf16[672,640]{1,0:T(8,128)(2,1)S(1)}, u32[]{:S(2)}, u32[]{:S(2)}) collective-permute-start(bf16[672,640]{1,0:T(8,128)(2,1)} %collective-permute-done.9.refs_3_), channel_id=1, source_target_pairs={{0,1},{1,0},{2,3},{3,2},{4,5},{5,4},{6,7},{7,6}} | collective-permute-start | bytes 2580488 | tf_op jit(solution)/shard_map/ppermute | solution.py:54
  137.4 55.9 %collective-permute-start.17 = (bf16[960,640]{1,0:T(8,128)(2,1)S(1)}, bf16[960,640]{1,0:T(8,128)(2,1)}, u32[]{:S(2)}, u32[]{:S(2)}) collective-permute-start(bf16[960,640]{1,0:T(8,128)(2,1)S(1)} %copy-done), channel_id=1, source_target_pairs={{0,1},{1,0},{2,3},{3,2},{4,5},{5,4},{6,7},{7,6}} | collective-permute-start | bytes 3686408 | tf_op jit(solution)/shard_map/ppermute | solution.py:54
  138.5 56.4 %collective-permute-start.18 = (bf16[960,640]{1,0:T(8,128)(2,1)}, bf16[960,640]{1,0:T(8,128)(2,1)}, u32[]{:S(2)}, u32[]{:S(2)}) collective-permute-start(bf16[960,640]{1,0:T(8,128)(2,1)} %collective-permute-done.14.refs_1_.refs_9_), channel_id=1, source_target_pairs={{0,1},{1,0},{2,3},{3,2},{4,5},{5,4},{6,7},{7,6}} | collective-permute-start | bytes 3686408 | tf_op jit(solution)/shard_map/ppermute | solution.py:54
  138.5 56.5 %collective-permute-start.19 = (bf16[960,640]{1,0:T(8,128)(2,1)S(1)}, bf16[960,640]{1,0:T(8,128)(2,1)}, u32[]{:S(2)}, u32[]{:S(2)}) collective-permute-start(bf16[960,640]{1,0:T(8,128)(2,1)S(1)} %collective-permute-done.15.refs_2_.refs_10_), channel_id=1, source_target_pairs={{0,1},{1,0},{2,3},{3,2},{4,5},{5,4},{6,7},{7,6}} | collective-permute-start | bytes 3686408 | tf_op jit(solution)/shard_map/ppermute | solution.py:54
  150.7 44.8 %collective-permute-start.20 = (bf16[960,640]{1,0:T(8,128)(2,1)}, bf16[960,640]{1,0:T(8,128)(2,1)}, u32[]{:S(2)}, u32[]{:S(2)}) collective-permute-start(bf16[960,640]{1,0:T(8,128)(2,1)} %collective-permute-done.16.refs_3_.refs_11_), channel_id=1, source_target_pairs={{0,1},{1,0},{2,3},{3,2},{4,5},{5,4},{6,7},{7,6}} | collective-permute-start | bytes 3686408 | tf_op jit(solution)/shard_map/ppermute | solution.py:54
  152.0 41.9 %collective-permute-start.30 = (bf16[672,640]{1,0:T(8,128)(2,1)}, bf16[672,640]{1,0:T(8,128)(2,1)}, u32[]{:S(2)}, u32[]{:S(2)}) collective-permute-start(bf16[672,640]{1,0:T(8,128)(2,1)} %collective-permute-done.28.refs_1_), channel_id=1, source_target_pairs={{0,2},{1,5},{2,0},{3,7},{4,6},{5,1},{6,4},{7,3}} | collective-permute-start | bytes 2580488 | tf_op jit(solution)/shard_map/ppermute | solution.py:54
  193.3 34.1 %collective-permute-start.27 = (bf16[320,640]{1,0:T(8,128)(2,1)}, bf16[320,640]{1,0:T(8,128)(2,1)S(1)}, u32[]{:S(2)}, u32[]{:S(2)}) collective-permute-start(bf16[320,640]{1,0:T(8,128)(2,1)} %collective-permute-done.23.refs_3_), channel_id=1, source_target_pairs={{0,1},{1,0},{2,3},{3,2},{4,5},{5,4},{6,7},{7,6}} | collective-permute-start | bytes 1228808 | tf_op jit(solution)/shard_map/ppermute | solution.py:54
  193.9 33.9 %collective-permute-start.37 = (bf16[640,640]{1,0:T(8,128)(2,1)}, bf16[640,640]{1,0:T(8,128)(2,1)}, u32[]{:S(2)}, u32[]{:S(2)}) collective-permute-start(bf16[640,640]{1,0:T(8,128)(2,1)} %collective-permute-done.35.refs_1_), channel_id=1, source_target_pairs={{0,2},{1,5},{2,0},{3,7},{4,6},{5,1},{6,4},{7,3}} | collective-permute-start | bytes 2457608 | tf_op jit(solution)/shard_map/ppermute | solution.py:54
  194.9 33.0 %collective-permute-start.32 = (bf16[672,640]{1,0:T(8,128)(2,1)}, bf16[672,640]{1,0:T(8,128)(2,1)S(1)}, u32[]{:S(2)}, u32[]{:S(2)}) collective-permute-start(bf16[672,640]{1,0:T(8,128)(2,1)} %collective-permute-done.28.refs_1_), channel_id=1, source_target_pairs={{0,1},{1,0},{2,3},{3,2},{4,5},{5,4},{6,7},{7,6}} | collective-permute-start | bytes 2580488 | tf_op jit(solution)/shard_map/ppermute | solution.py:54
  195.1 33.3 %collective-permute-start.33 = (bf16[672,640]{1,0:T(8,128)(2,1)}, bf16[672,640]{1,0:T(8,128)(2,1)S(1)}, u32[]{:S(2)}, u32[]{:S(2)}) collective-permute-start(bf16[672,640]{1,0:T(8,128)(2,1)} %collective-permute-done.29.refs_2_), channel_id=1, source_target_pairs={{0,1},{1,0},{2,3},{3,2},{4,5},{5,4},{6,7},{7,6}} | collective-permute-start | bytes 2580488 | tf_op jit(solution)/shard_map/ppermute | solution.py:54
  195.5 53.7 %collective-permute-start.34 = (bf16[672,640]{1,0:T(8,128)(2,1)}, bf16[672,640]{1,0:T(8,128)(2,1)S(1)}, u32[]{:S(2)}, u32[]{:S(2)}) collective-permute-start(bf16[672,640]{1,0:T(8,128)(2,1)} %collective-permute-done.30.refs_3_), channel_id=1, source_target_pairs={{0,1},{1,0},{2,3},{3,2},{4,5},{5,4},{6,7},{7,6}} | collective-permute-start | bytes 2580488 | tf_op jit(solution)/shard_map/ppermute | solution.py:54
  227.4 42.6 %collective-permute-start.38 = (bf16[640,640]{1,0:T(8,128)(2,1)S(1)}, bf16[640,640]{1,0:T(8,128)(2,1)}, u32[]{:S(2)}, u32[]{:S(2)}) collective-permute-start(bf16[640,640]{1,0:T(8,128)(2,1)S(1)} %copy-done.18), channel_id=1, source_target_pairs={{0,1},{1,0},{2,3},{3,2},{4,5},{5,4},{6,7},{7,6}} | collective-permute-start | bytes 2457608 | tf_op jit(solution)/shard_map/ppermute | solution.py:54
  227.8 42.7 %collective-permute-start.39 = (bf16[640,640]{1,0:T(8,128)(2,1)}, bf16[640,640]{1,0:T(8,128)(2,1)}, u32[]{:S(2)}, u32[]{:S(2)}) collective-permute-start(bf16[640,640]{1,0:T(8,128)(2,1)} %collective-permute-done.35.refs_1_), channel_id=1, source_target_pairs={{0,1},{1,0},{2,3},{3,2},{4,5},{5,4},{6,7},{7,6}} | collective-permute-start | bytes 2457608 | tf_op jit(solution)/shard_map/ppermute | solution.py:54
  227.9 42.7 %collective-permute-start.40 = (bf16[640,640]{1,0:T(8,128)(2,1)}, bf16[640,640]{1,0:T(8,128)(2,1)}, u32[]{:S(2)}, u32[]{:S(2)}) collective-permute-start(bf16[640,640]{1,0:T(8,128)(2,1)} %collective-permute-done.36.refs_2_), channel_id=1, source_target_pairs={{0,1},{1,0},{2,3},{3,2},{4,5},{5,4},{6,7},{7,6}} | collective-permute-start | bytes 2457608 | tf_op jit(solution)/shard_map/ppermute | solution.py:54
  228.3 42.7 %collective-permute-start.41 = (bf16[640,640]{1,0:T(8,128)(2,1)}, bf16[640,640]{1,0:T(8,128)(2,1)}, u32[]{:S(2)}, u32[]{:S(2)}) collective-permute-start(bf16[640,640]{1,0:T(8,128)(2,1)} %collective-permute-done.37.refs_3_), channel_id=1, source_target_pairs={{0,1},{1,0},{2,3},{3,2},{4,5},{5,4},{6,7},{7,6}} | collective-permute-start | bytes 2457608 | tf_op jit(solution)/shard_map/ppermute | solution.py:54
  249.2 20.9 %collective-permute-start.44 = (bf16[320,640]{1,0:T(8,128)(2,1)}, bf16[320,640]{1,0:T(8,128)(2,1)S(1)}, u32[]{:S(2)}, u32[]{:S(2)}) collective-permute-start(bf16[320,640]{1,0:T(8,128)(2,1)} %collective-permute-done.42.refs_1_.refs_9_), channel_id=1, source_target_pairs={{0,2},{1,5},{2,0},{3,7},{4,6},{5,1},{6,4},{7,3}} | collective-permute-start | bytes 1228808 | tf_op jit(solution)/shard_map/ppermute | solution.py:54
  270.0 29.5 %collective-permute-start.45 = (bf16[320,640]{1,0:T(8,128)(2,1)S(1)}, bf16[320,640]{1,0:T(8,128)(2,1)S(1)}, u32[]{:S(2)}, u32[]{:S(2)}) collective-permute-start(bf16[320,640]{1,0:T(8,128)(2,1)S(1)} %copy-done.23), channel_id=1, source_target_pairs={{0,1},{1,0},{2,3},{3,2},{4,5},{5,4},{6,7},{7,6}} | collective-permute-start | bytes 1228808 | tf_op jit(solution)/shard_map/ppermute | solution.py:54
  270.1 29.4 %collective-permute-start.46 = (bf16[320,640]{1,0:T(8,128)(2,1)}, bf16[320,640]{1,0:T(8,128)(2,1)S(1)}, u32[]{:S(2)}, u32[]{:S(2)}) collective-permute-start(bf16[320,640]{1,0:T(8,128)(2,1)} %collective-permute-done.42.refs_1_.refs_9_), channel_id=1, source_target_pairs={{0,1},{1,0},{2,3},{3,2},{4,5},{5,4},{6,7},{7,6}} | collective-permute-start | bytes 1228808 | tf_op jit(solution)/shard_map/ppermute | solution.py:54
  270.5 29.0 %collective-permute-start.47 = (bf16[320,640]{1,0:T(8,128)(2,1)S(1)}, bf16[320,640]{1,0:T(8,128)(2,1)S(1)}, u32[]{:S(2)}, u32[]{:S(2)}) collective-permute-start(bf16[320,640]{1,0:T(8,128)(2,1)S(1)} %copy-done.43), channel_id=1, source_target_pairs={{0,1},{1,0},{2,3},{3,2},{4,5},{5,4},{6,7},{7,6}} | collective-permute-start | bytes 1228808 | tf_op jit(solution)/shard_map/ppermute | solution.py:54
  270.6 29.0 %collective-permute-start.48 = (bf16[320,640]{1,0:T(8,128)(2,1)S(1)}, bf16[320,640]{1,0:T(8,128)(2,1)S(1)}, u32[]{:S(2)}, u32[]{:S(2)}) collective-permute-start(bf16[320,640]{1,0:T(8,128)(2,1)S(1)} %collective-permute-done.44.refs_3_.refs_11_), channel_id=1, source_target_pairs={{0,1},{1,0},{2,3},{3,2},{4,5},{5,4},{6,7},{7,6}} | collective-permute-start | bytes 1228808 | tf_op jit(solution)/shard_map/ppermute | solution.py:54
  519.4 152.9 %collective-permute-start.72 = (f32[4,2,1360]{2,1,0:T(2,128)S(1)}, f32[4,2,1360]{2,1,0:T(2,128)S(1)}, u32[]{:S(2)}, u32[]{:S(2)}) collective-permute-start(f32[4,2,1360]{2,1,0:T(2,128)S(1)} %fusion.18), channel_id=1, source_target_pairs={{0,1},{1,0},{2,3},{3,2},{4,5},{5,4},{6,7},{7,6}} | collective-permute-start | bytes 130568 | tf_op jit(solution)/shard_map/ppermute | solution.py:54
  537.0 181.8 %collective-permute-start.68 = (f32[640,640]{1,0:T(8,128)}, f32[640,640]{1,0:T(8,128)}, u32[]{:S(2)}, u32[]{:S(2)}) collective-permute-start(f32[640,640]{1,0:T(8,128)} %get-tuple-element.159), channel_id=1, source_target_pairs={{0,2},{1,5},{2,0},{3,7},{4,6},{5,1},{6,4},{7,3}} | collective-permute-start | bytes 4915208 | tf_op jit(solution)/shard_map/ppermute | solution.py:54
  555.3 166.1 %collective-permute-start.70 = (f32[640,640]{1,0:T(8,128)}, f32[640,640]{1,0:T(8,128)}, u32[]{:S(2)}, u32[]{:S(2)}) collective-permute-start(f32[640,640]{1,0:T(8,128)} %get-tuple-element.161), channel_id=1, source_target_pairs={{0,2},{1,5},{2,0},{3,7},{4,6},{5,1},{6,4},{7,3}} | collective-permute-start | bytes 4915208 | tf_op jit(solution)/shard_map/ppermute | solution.py:54
  568.3 117.2 %collective-permute-start.53 = (f32[320,640]{1,0:T(8,128)}, f32[320,640]{1,0:T(8,128)S(1)}, u32[]{:S(2)}, u32[]{:S(2)}) collective-permute-start(f32[320,640]{1,0:T(8,128)} %get-tuple-element.136), channel_id=1, source_target_pairs={{0,2},{1,5},{2,0},{3,7},{4,6},{5,1},{6,4},{7,3}} | collective-permute-start | bytes 2457608 | tf_op jit(solution)/shard_map/ppermute | solution.py:54
  581.0 105.7 %collective-permute-start.55 = (f32[320,640]{1,0:T(8,128)}, f32[320,640]{1,0:T(8,128)S(1)}, u32[]{:S(2)}, u32[]{:S(2)}) collective-permute-start(f32[320,640]{1,0:T(8,128)} %get-tuple-element.142), channel_id=1, source_target_pairs={{0,2},{1,5},{2,0},{3,7},{4,6},{5,1},{6,4},{7,3}} | collective-permute-start | bytes 2457608 | tf_op jit(solution)/shard_map/ppermute | solution.py:54
  672.3 13.1 %collective-permute-start.73 = (f32[2,2,1360]{2,1,0:T(2,128)S(1)}, f32[2,2,1360]{2,1,0:T(2,128)S(1)}, u32[]{:S(2)}, u32[]{:S(2)}) collective-permute-start(f32[2,2,1360]{2,1,0:T(2,128)S(1)} %pad_maximum_fusion.1), channel_id=1, source_target_pairs={{0,2},{1,5},{2,0},{3,7},{4,6},{5,1},{6,4},{7,3}} | collective-permute-start | bytes 65288 | tf_op jit(solution)/shard_map/ppermute | solution.py:54
  685.4 14.7 %collective-permute-start.58 = (bf16[480,1280]{1,0:T(8,128)(2,1)}, bf16[480,1280]{1,0:T(8,128)(2,1)S(1)}, u32[]{:S(2)}, u32[]{:S(2)}) collective-permute-start(bf16[480,1280]{1,0:T(8,128)(2,1)} %get-tuple-element.143.mine_ref), channel_id=1, source_target_pairs={{0,1},{1,0},{2,3},{3,2},{4,5},{5,4},{6,7},{7,6}} | collective-permute-start | bytes 3686408 | tf_op jit(solution)/shard_map/ppermute | solution.py:54
  694.7 15.9 %collective-permute-start.61 = (bf16[480,1280]{1,0:T(8,128)(2,1)}, bf16[480,1280]{1,0:T(8,128)(2,1)}, u32[]{:S(2)}, u32[]{:S(2)}) collective-permute-start(bf16[480,1280]{1,0:T(8,128)(2,1)} %get-tuple-element.146.mine_ref), channel_id=1, source_target_pairs={{0,1},{1,0},{2,3},{3,2},{4,5},{5,4},{6,7},{7,6}} | collective-permute-start | bytes 3686408 | tf_op jit(solution)/shard_map/ppermute | solution.py:54
  699.1 24.5 %collective-permute-start.49 = (f32[640,640]{1,0:T(8,128)}, f32[640,640]{1,0:T(8,128)}, u32[]{:S(2)}, u32[]{:S(2)}) collective-permute-start(f32[640,640]{1,0:T(8,128)} %get-tuple-element.124), channel_id=1, source_target_pairs={{0,2},{1,5},{2,0},{3,7},{4,6},{5,1},{6,4},{7,3}} | collective-permute-start | bytes 4915208 | tf_op jit(solution)/shard_map/ppermute | solution.py:54
  700.1 53.7 %collective-permute-start.51 = (f32[640,640]{1,0:T(8,128)}, f32[640,640]{1,0:T(8,128)}, u32[]{:S(2)}, u32[]{:S(2)}) collective-permute-start(f32[640,640]{1,0:T(8,128)} %get-tuple-element.130), channel_id=1, source_target_pairs={{0,2},{1,5},{2,0},{3,7},{4,6},{5,1},{6,4},{7,3}} | collective-permute-start | bytes 4915208 | tf_op jit(solution)/shard_map/ppermute | solution.py:54
  710.6 97.6 %collective-permute-start.64 = (f32[1280,640]{1,0:T(8,128)}, f32[1280,640]{1,0:T(8,128)S(1)}, u32[]{:S(2)}, u32[]{:S(2)}) collective-permute-start(f32[1280,640]{1,0:T(8,128)} %get-tuple-element.152), channel_id=1, source_target_pairs={{0,2},{1,5},{2,0},{3,7},{4,6},{5,1},{6,4},{7,3}} | collective-permute-start | bytes 9830408 | tf_op jit(solution)/shard_map/ppermute | solution.py:54
  718.7 142.1 %collective-permute-start.66 = (f32[1280,640]{1,0:T(8,128)}, f32[1280,640]{1,0:T(8,128)S(1)}, u32[]{:S(2)}, u32[]{:S(2)}) collective-permute-start(f32[1280,640]{1,0:T(8,128)} %get-tuple-element.156), channel_id=1, source_target_pairs={{0,2},{1,5},{2,0},{3,7},{4,6},{5,1},{6,4},{7,3}} | collective-permute-start | bytes 9830408 | tf_op jit(solution)/shard_map/ppermute | solution.py:54
  721.4 34.5 %collective-permute-start.69 = (f32[320,640]{1,0:T(8,128)S(1)}, f32[320,640]{1,0:T(8,128)S(1)}, u32[]{:S(2)}, u32[]{:S(2)}) collective-permute-start(f32[320,640]{1,0:T(8,128)S(1)} %slice_add_fusion.10), channel_id=1, source_target_pairs={{0,4},{1,3},{2,6},{3,1},{4,0},{5,7},{6,2},{7,5}} | collective-permute-start | bytes 2457608 | tf_op jit(solution)/shard_map/ppermute | solution.py:54
  723.6 36.6 %collective-permute-start.71 = (f32[320,640]{1,0:T(8,128)S(1)}, f32[320,640]{1,0:T(8,128)S(1)}, u32[]{:S(2)}, u32[]{:S(2)}) collective-permute-start(f32[320,640]{1,0:T(8,128)S(1)} %slice_add_fusion.8), channel_id=1, source_target_pairs={{0,4},{1,3},{2,6},{3,1},{4,0},{5,7},{6,2},{7,5}} | collective-permute-start | bytes 2457608 | tf_op jit(solution)/shard_map/ppermute | solution.py:54
  753.8 23.9 %collective-permute-start.50 = (f32[320,640]{1,0:T(8,128)S(1)}, f32[320,640]{1,0:T(8,128)S(1)}, u32[]{:S(2)}, u32[]{:S(2)}) collective-permute-start(f32[320,640]{1,0:T(8,128)S(1)} %slice_add_fusion.14), channel_id=1, source_target_pairs={{0,4},{1,3},{2,6},{3,1},{4,0},{5,7},{6,2},{7,5}} | collective-permute-start | bytes 2457608 | tf_op jit(solution)/shard_map/ppermute | solution.py:54
  755.9 150.6 %collective-permute-start.59 = (f32[1024,640]{1,0:T(8,128)}, f32[1024,640]{1,0:T(8,128)S(1)}, u32[]{:S(2)}, u32[]{:S(2)}) collective-permute-start(f32[1024,640]{1,0:T(8,128)} %get-tuple-element.145), channel_id=1, source_target_pairs={{0,2},{1,5},{2,0},{3,7},{4,6},{5,1},{6,4},{7,3}} | collective-permute-start | bytes 7864328 | tf_op jit(solution)/shard_map/ppermute | solution.py:54
  760.1 35.1 %collective-permute-start.52 = (f32[320,640]{1,0:T(8,128)S(1)}, f32[320,640]{1,0:T(8,128)S(1)}, u32[]{:S(2)}, u32[]{:S(2)}) collective-permute-start(f32[320,640]{1,0:T(8,128)S(1)} %slice_add_fusion.12), channel_id=1, source_target_pairs={{0,4},{1,3},{2,6},{3,1},{4,0},{5,7},{6,2},{7,5}} | collective-permute-start | bytes 2457608 | tf_op jit(solution)/shard_map/ppermute | solution.py:54
  777.7 171.0 %collective-permute-start.62 = (f32[1024,640]{1,0:T(8,128)S(1)}, f32[1024,640]{1,0:T(8,128)S(1)}, u32[]{:S(2)}, u32[]{:S(2)}) collective-permute-start(f32[1024,640]{1,0:T(8,128)S(1)} %copy-done.40), channel_id=1, source_target_pairs={{0,2},{1,5},{2,0},{3,7},{4,6},{5,1},{6,4},{7,3}} | collective-permute-start | bytes 7864328 | tf_op jit(solution)/shard_map/ppermute | solution.py:54
  808.4 141.3 %collective-permute-start.65 = (f32[640,640]{1,0:T(8,128)S(1)}, f32[640,640]{1,0:T(8,128)S(1)}, u32[]{:S(2)}, u32[]{:S(2)}) collective-permute-start(f32[640,640]{1,0:T(8,128)S(1)} %slice_add_fusion.2), channel_id=1, source_target_pairs={{0,4},{1,3},{2,6},{3,1},{4,0},{5,7},{6,2},{7,5}} | collective-permute-start | bytes 4915208 | tf_op jit(solution)/shard_map/ppermute | solution.py:54
  861.0 89.1 %collective-permute-start.67 = (f32[640,640]{1,0:T(8,128)S(1)}, f32[640,640]{1,0:T(8,128)S(1)}, u32[]{:S(2)}, u32[]{:S(2)}) collective-permute-start(f32[640,640]{1,0:T(8,128)S(1)} %slice_add_fusion), channel_id=1, source_target_pairs={{0,4},{1,3},{2,6},{3,1},{4,0},{5,7},{6,2},{7,5}} | collective-permute-start | bytes 4915208 | tf_op jit(solution)/shard_map/ppermute | solution.py:54
  906.9 48.3 %collective-permute-start.60 = (f32[512,640]{1,0:T(8,128)S(1)}, f32[512,640]{1,0:T(8,128)S(1)}, u32[]{:S(2)}, u32[]{:S(2)}) collective-permute-start(f32[512,640]{1,0:T(8,128)S(1)} %slice_add_fusion.6), channel_id=1, source_target_pairs={{0,4},{1,3},{2,6},{3,1},{4,0},{5,7},{6,2},{7,5}} | collective-permute-start | bytes 3932168 | tf_op jit(solution)/shard_map/ppermute | solution.py:54
  948.8 17.6 %collective-permute-start.63 = (f32[512,640]{1,0:T(8,128)S(1)}, f32[512,640]{1,0:T(8,128)S(1)}, u32[]{:S(2)}, u32[]{:S(2)}) collective-permute-start(f32[512,640]{1,0:T(8,128)S(1)} %slice_add_fusion.4), channel_id=1, source_target_pairs={{0,4},{1,3},{2,6},{3,1},{4,0},{5,7},{6,2},{7,5}} | collective-permute-start | bytes 3932168 | tf_op jit(solution)/shard_map/ppermute | solution.py:54
  (62 other events, 868.6 us)

commit v2 on v1

--- a/solution.py
+++ b/solution.py
@@ -14,6 +14,7 @@
 FF_STEP = 256
 STEP = 512
 VMEM_LIMIT = 60 * 1024 * 1024
+VMEM_MOST = 67043328
 FORWARD_UNROLL = 10
 BACKWARD_UNROLL = 5
 
@@ -328,39 +329,6 @@
     out_ref[...] = (h_ref[...] + rows_ref[8:9, :] + dot_nn(gated_ref[...], w_ff2[...])).astype(BF16)
 
 
-def ff_backward_kernel(offset, grad_ref, save_a, save_g, h_ref, rows_ref, *refs):
-    pieces, (d_hidden_ref, out_ref, vec_ref, bias_ref, w_ff1, w_ff2, sems) = refs[:16], refs[16:]
-    half = w_ff2.shape[0]
-    step = pl.program_id(0)
-
-    @pl.when(step == 0)
-    def _():
-        ff_loads(pieces, offset, w_ff1, w_ff2, sems)
-        bias_ref[...] = jnp.zeros_like(bias_ref)
-
-    grad = grad_ref[...].astype(F32)
-    grad_bf = grad.astype(BF16)
-
-    @pl.when(step == 0)
-    def _():
-        wait_load(w_ff1, sems.at[0])
-        wait_load(w_ff2, sems.at[1])
-
-    d_norm = jnp.zeros(grad.shape, F32)
-    for start in range(0, half, CHUNK):
-        d_gated = dot_nt(grad_bf, w_ff2[start:start + CHUNK, :]).astype(BF16).astype(F32)
-        for base, saved in ((0, save_a), (half, save_g)):
-            d_part = d_gated * saved[:, start:start + CHUNK]
-            columns = slice(base + start, base + start + CHUNK)
-            bias_ref[0:1, columns] += jnp.sum(d_part, axis=0, keepdims=True)
-            d_part = d_part.astype(BF16)
-            d_hidden_ref[:, columns] = d_part
-            d_norm = d_norm + dot_nt(d_part, w_ff1[:, columns])
-    d_res, g_gain, g_shift = norm_back(h_ref[...], rows_ref[4:5, :], d_norm)
-    out_ref[...] = grad + d_res
-    add_rows(vec_ref, step, [g_gain, g_shift, jnp.sum(grad, axis=0, keepdims=True)])
-
-
 def cross_backward_kernel(samples, tokens, valid, grad_ref, query_ref, kv_ref, h_ref, rows_ref, *refs):
     pieces, (grad_bf_ref, d_query_ref, d_kv_ref, out_ref, vec_ref, d_mix, w_query, w_out, sems) = refs[:8], refs[8:]
     width = h_ref.shape[1]
@@ -526,19 +494,6 @@
         by_step(STEP, width), shape(count, width, BF16),
         [pltpu.VMEM((half, width), BF16), pltpu.SemaphoreType.DMA((1,))],
         count * width * half * 2, 2e7)(h, rows, gated, *pieces)
-
-
-def ff_backward(grad, save_a, save_g, h, rows, pieces, offset):
-    count, width = h.shape
-    half = save_a.shape[1]
-    return call(
-        functools.partial(ff_backward_kernel, offset), count // FF_STEP,
-        [by_step(FF_STEP, width), by_step(FF_STEP, half), by_step(FF_STEP, half), by_step(FF_STEP, width), whole(*rows.shape)]
-        + [ANY] * 16,
-        [by_step(FF_STEP, 2 * half), by_step(FF_STEP, width), whole(8, width), whole(8, 2 * half)],
-        [shape(count, 2 * half, BF16), shape(count, width, F32), shape(8, width, F32), shape(8, 2 * half, F32)],
-        [pltpu.VMEM((width, 2 * half), BF16), pltpu.VMEM((half, width), BF16), pltpu.SemaphoreType.DMA((2,))],
-        count * width * half * 6, 6e7)(grad, save_a, save_g, h, rows, *pieces)
 
 
 def cross_backward(grad, query, kv, h, rows, pieces, tokens, valid):
@@ -682,6 +637,226 @@
         compiler_params=pltpu.CompilerParams(collective_id=kind, has_side_effects=True, vmem_limit_bytes=VMEM_LIMIT))(*arrays)
 
 
+def ff_grad_kernel(offset, with_down, grad_ref, save_a, save_g, norm_ref, h_ref, rows_ref, *refs):
+    gated_ref, refs = (refs[0], refs[1:]) if with_down else (None, refs)
+    pieces, refs = refs[:16], refs[16:]
+    out_ref, vec_ref, bias_ref, far1, keep1 = refs[:5]
+    far2, keep2 = refs[5:7] if with_down else (None, None)
+    (grad, grad_bf, turned, acc, part_a, part_g, d_a, d_g, w_ff1, w_ff2, tile, recv1, obuf,
+     in_sem, part_sem, w1_sem, w2_sem, out_sem, send_sem, recv_sem1) = refs[7 if with_down else 5:][:20]
+    if with_down:
+        z_buf, z_turned, recv2, z_sem, recv_sem2 = refs[-5:]
+    count, width = grad.shape
+    half = w_ff2.shape[0]
+    chunks, each = half // width, STEP
+    steps = count // each
+    depth, deep = width // 8, half // 8
+    me = lax.axis_index(AXIS)
+    core, chip = lax.rem(me, 2), me // 2
+    mate = me + 1 - 2 * core
+    chip_x, chip_y = lax.rem(chip, 2), chip // 2
+
+    def slot_of(other, of_mate):
+        d_x, d_y = lax.rem(chip_x + other % 2, 2), lax.rem(chip_y + other // 2, 2)
+        return d_x + 2 * d_y + core * (d_x - d_y) if of_mate else 2 * d_x + d_y + core * (d_y - d_x)
+
+    def chip_in(slot):
+        one, two = slot // 2, slot % 2
+        d_x, d_y = one + core * (two - one), two + core * (one - two)
+        return 2 * lax.rem(chip_y + d_y, 2) + lax.rem(chip_x + d_x, 2)
+
+    load_grad = pltpu.make_async_copy(grad_ref, grad, in_sem.at[0])
+    load_norm = pltpu.make_async_copy(norm_ref, d_a, in_sem.at[1])
+    load_grad.start()
+    load_norm.start()
+    start_load(pieces[8:], offset, w_ff2, w2_sem)
+
+    def parts(index):
+        chunk, step = divmod(index, steps)
+        at = (pl.ds(step * each, each), pl.ds(chunk * width, width))
+        return [pltpu.make_async_copy(ref.at[at], buf.at[index % 2], part_sem.at[which, index % 2])
+                for which, (ref, buf) in enumerate(((save_a, part_a), (save_g, part_g)))]
+
+    def load_h(step):
+        return pltpu.make_async_copy(h_ref.at[pl.ds(step * each, each), :], part_a.at[step % 2], part_sem.at[0, step % 2])
+
+    for copy in parts(0):
+        copy.start()
+    devices = piece_devices(me)
+    for block in [b + k for b in range(chunks) for k in (0, chunks)]:
+        for piece, device in zip(pieces[:8], devices):
+            pltpu.make_async_copy(piece.at[pl.ds(block * depth, depth), :],
+                                  w_ff1.at[pl.ds(pl.multiple_of(device * depth, 16), depth), pl.ds(block * width, width)],
+                                  w1_sem.at[block]).start()
+    for copy in parts(1):
+        copy.start()
+
+    barrier = pltpu.get_barrier_semaphore()
+    pl.semaphore_signal(barrier, inc=1, device_id=(mate,), device_id_type=pl.DeviceIdType.MESH)
+    pl.semaphore_wait(barrier, 1)
+
+    def load_z(chunk):
+        return pltpu.make_async_copy(gated_ref.at[:, pl.ds(chunk * width, width)], z_buf, z_sem)
+
+    if with_down:
+        load_z(0).start()
+
+    tiles = []
+    for chunk in range(chunks):
+        tiles += [(1, chunk), (1, chunks + chunk)] + ([(2, chunk)] if with_down else [])
+    ring = tile.shape[0]
+
+    def sends(q):
+        which, block = tiles[q]
+        copies = []
+        for index, other in enumerate(range(4) if which == 1 else (block,)):
+            rows = depth if which == 1 else deep
+            start = pl.multiple_of((2 * index + 1 - core) * rows, 16)
+            slot = slot_of(other, True)
+            dst = (recv1.at[block, pl.ds(pl.multiple_of(slot * rows, 16), rows), :] if which == 1 else recv2.at[block])
+            copies.append(pltpu.make_async_remote_copy(
+                src_ref=tile.at[q % ring, pl.ds(start, rows), :], dst_ref=dst, send_sem=send_sem.at[q % ring, index],
+                recv_sem=recv_sem1.at[block, index] if which == 1 else recv_sem2.at[block],
+                device_id=(mate,), device_id_type=pl.DeviceIdType.MESH))
+        return copies
+
+    def writes(q, branch=None):
+        which, block = tiles[q]
+        if which == 1:
+            return [pltpu.make_async_copy(
+                obuf.at[q % 2, pl.ds(slot * depth, depth), :],
+                (keep1 if slot < 2 else far1).at[pl.ds((slot % 2) * 8 * depth + block * depth, depth), :],
+                out_sem.at[q % 2]) for slot in range(4)]
+        slot = slot_of(block, False)
+        ref = keep2 if branch == 0 else far2
+        return [pltpu.make_async_copy(obuf.at[q % 2], ref.at[pl.ds(pl.multiple_of(lax.rem(slot, 2) * deep, 16), deep), :],
+                                      out_sem.at[q % 2])]
+
+    def wait_writes(q):
+        pltpu.make_async_copy(obuf.at[q % 2], obuf.at[q % 2], out_sem.at[q % 2]).wait()
+
+    def finish(q):
+        which, block = tiles[q]
+        for copy in sends(q):
+            copy.wait_recv()
+        if q >= 2:
+            wait_writes(q - 2)
+        if which == 1:
+            for slot in range(4):
+                start = pl.multiple_of((2 * chip_in(slot) + core) * depth, 16)
+                rows = slice(slot * depth, (slot + 1) * depth)
+                obuf[q % 2, rows, :] = tile[q % ring, pl.ds(start, depth), :] + recv1[block, rows, :]
+            for copy in writes(q):
+                copy.start()
+        else:
+            obuf[q % 2] = tile[q % ring, pl.ds(pl.multiple_of(core * deep, 16), deep), :] + recv2[block]
+            slot = slot_of(block, False)
+            for branch in range(2):
+                @pl.when(slot // 2 == branch)
+                def _():
+                    for copy in writes(q, branch):
+                        copy.start()
+        for copy in sends(q):
+            copy.wait_send()
+
+    load_grad.wait()
+    grad_bf[...] = grad[...].astype(BF16)
+    load_norm.wait()
+    turned[...] = d_a[...].T
+    acc[...] = jnp.zeros_like(acc)
+    bias_ref[...] = jnp.zeros_like(bias_ref)
+    vec_ref[...] = jnp.zeros_like(vec_ref)
+    wait_load(w_ff2, w2_sem)
+
+    q = 0
+    for chunk in range(chunks):
+        for block in (chunk, chunks + chunk):
+            ref = w_ff1.at[:, pl.ds(block * width, width)]
+            pltpu.make_async_copy(ref, ref, w1_sem.at[block]).wait()
+        for step in range(steps):
+            index = chunk * steps + step
+            rows = slice(step * each, (step + 1) * each)
+            d_gated = dot_nt(grad_bf[rows, :], w_ff2[chunk * width:(chunk + 1) * width, :]).astype(BF16).astype(F32)
+            for copy in parts(index):
+                copy.wait()
+            total = acc[rows, :]
+            for base, saved, kept in ((0, part_a, d_a), (half, part_g, d_g)):
+                d_part = d_gated * saved[index % 2]
+                columns = slice(base + chunk * width, base + (chunk + 1) * width)
+                bias_ref[0:1, columns] += jnp.sum(d_part, axis=0, keepdims=True)
+                d_part = d_part.astype(BF16)
+                kept[rows, :] = d_part
+                total = total + dot_nt(d_part, w_ff1[:, columns])
+            acc[rows, :] = total
+            if index + 2 < chunks * steps:
+                for copy in parts(index + 2):
+                    copy.start()
+        for kept in (d_a, d_g):
+            tile[q % ring] = dot_nn(turned[...], kept[...])
+            if q >= 1:
+                for copy in sends(q - 1):
+                    copy.start()
+            if q >= 3:
+                finish(q - 3)
+            q += 1
+        if with_down:
+            load_z(chunk).wait()
+            z_turned[...] = z_buf[...].T
+            if chunk + 1 < chunks:
+                load_z(chunk + 1).start()
+            tile[q % ring] = dot_nn(z_turned[...], grad_bf[...])
+            for copy in sends(q - 1):
+                copy.start()
+            if q >= 3:
+                finish(q - 3)
+            q += 1
+    load_h(0).start()
+    load_h(1).start()
+    for copy in sends(q - 1):
+        copy.start()
+    for step in range(steps):
+        rows = slice(step * each, (step + 1) * each)
+        load_h(step).wait()
+        mine = grad[rows, :].astype(F32)
+        d_res, g_gain, g_shift = norm_back(part_a[step % 2], rows_ref[4:5, :], acc[rows, :])
+        if step + 2 < steps:
+            load_h(step + 2).start()
+        acc[rows, :] = mine + d_res
+        pltpu.make_async_copy(acc.at[pl.ds(step * each, each), :], out_ref.at[pl.ds(step * each, each), :], in_sem.at[0]).start()
+        for at, row in enumerate((g_gain, g_shift, jnp.sum(mine, axis=0, keepdims=True))):
+            vec_ref[at:at + 1, :] += row
+    for late in range(max(0, q - 3), q):
+        finish(late)
+    for late in range(max(0, q - 2), q):
+        wait_writes(late)
+    pltpu.make_async_copy(acc, out_ref, in_sem.at[0]).wait()
+
+
+def ff_grads(kind, grad, save_a, save_g, norm, h, rows, gated, pieces, offset):
+    count, width = h.shape
+    half = save_a.shape[1]
+    down = gated is not None
+    vmem = pl.BlockSpec(memory_space=pltpu.VMEM)
+    big, small = shape(2 * width, width, F32), shape(half // 4, width, F32)
+    dma = pltpu.SemaphoreType.DMA
+    scratch = [pltpu.VMEM((count, width), grad.dtype), pltpu.VMEM((count, width), BF16), pltpu.VMEM((width, count), BF16),
+               pltpu.VMEM((count, width), F32), pltpu.VMEM((2, STEP, width), F32), pltpu.VMEM((2, STEP, width), F32),
+               pltpu.VMEM((count, width), BF16), pltpu.VMEM((count, width), BF16), pltpu.VMEM((width, 2 * half), BF16),
+               pltpu.VMEM((half, width), BF16), pltpu.VMEM((4, width, width), F32), pltpu.VMEM((8, width // 2, width), F32),
+               pltpu.VMEM((2, width // 2, width), F32), dma((2,)), dma((2, 2)), dma((8,)), dma, dma((2,)), dma((4, 4)), dma((8, 4))]
+    if down:
+        scratch += [pltpu.VMEM((count, width), BF16), pltpu.VMEM((width, count), BF16), pltpu.VMEM((4, half // 8, width), F32),
+                    dma, dma((4,))]
+    return pl.pallas_call(
+        functools.partial(ff_grad_kernel, offset, down),
+        in_specs=[ANY] * 5 + [vmem] + [ANY] * (16 + down),
+        out_specs=[ANY, vmem, vmem, ANY, ANY] + [ANY, ANY] * down,
+        out_shape=[shape(count, width, F32), shape(8, width, F32), shape(8, 2 * half, F32), big, big] + [small, small] * down,
+        scratch_shapes=scratch,
+        cost_estimate=pl.CostEstimate(flops=count * width * half * (14 if down else 10), bytes_accessed=int(6e7), transcendentals=0),
+        compiler_params=pltpu.CompilerParams(collective_id=kind, has_side_effects=True, vmem_limit_bytes=VMEM_MOST))(grad, save_a, save_g, norm, h, rows, *([gated] if down else []), *pieces)
+
+
 def context_grad_kernel(ctx_ref, mine_ref, other_ref, far_ref, keep_ref, d_kv):
     rows, width = mine_ref.shape[0], far_ref.shape[1]
     d_kv[0:rows, :] = mine_ref[...]
@@ -800,16 +975,21 @@
         by_column = lambda x, y, columns, first: [(x, 0, y, c * width, first + c * depth, depth, every) for c in range(columns)]
         _, _, core_perm = gather_perms(n_dev)
         for layer in reversed(range(blocks)):
+            turn = blocks - 1 - layer
             rows, group = rows_all[layer], groups[3 * layer:3 * layer + 2]
             h0, norm1, qkv, mix1, h1, norm2, query, kv, mix2, h2, norm3, gated, save_a, save_g = saved[layer]
 
             def reduce(pair):
                 return finish_scatter(pair[0], pair[1], n_dev)
 
-            r_ff2 = reduce(weight_grads(1, (gated, grad.astype(BF16)),
-                                           [(0, c * width, 1, 0, 0, half // n_dev, (c,)) for c in range(half // width)], half // n_dev))
-            d_hidden, grad, vec3, vec_b1 = ff_backward(grad, save_a, save_g, h2, rows, ff_groups[layer], ff_offsets[layer])
-            r_ff1 = reduce(weight_grads(2, (norm3, d_hidden), by_column(0, 1, 8, 0), 8 * depth))
+            if turn == 0:
+                r_ff2 = reduce(weight_grads(1, (gated, grad.astype(BF16)),
+                                               [(0, c * width, 1, 0, 0, half // n_dev, (c,)) for c in range(half // width)], half // n_dev))
+            grad, vec3, vec_b1, *pairs = ff_grads(5 + min(turn, 1), grad, save_a, save_g, norm3, h2, rows,
+                                                  gated if turn > 0 else None, ff_groups[layer], ff_offsets[layer])
+            r_ff1 = reduce(pairs[:2])
+            if turn > 0:
+                r_ff2 = reduce(pairs[2:])
             grad_bf, d_query, d_kv, grad, vec2 = cross_backward(grad, query, kv, h1, rows, group[1], tokens, valid)
             d_kv_other = permute(d_kv, core_perm)
             r_cross = reduce(weight_grads(3, (norm2, d_query, mix2, grad_bf),

time: 980 us -> 966 us (0.986)
  Pallas kernels: 538 us -> 525 us
    pallas_call x8 -> x5, Pallas kernels: 149 us -> 75.5 us  [weight_grads(): pl.pallas_call(functools.partial(grad_kernel, tiles, group_rows, len(arra...]
    pallas_call x2, Pallas kernels: 67.3 us -> 128 us  [ff_grads(): pl.pallas_call(functools.partial(ff_grad_kernel, offset, down), in_specs=...]
    unnamed x151 -> x155, local copies, waits for them, and re-layouts: 29.4 us -> 32.7 us
  transfers between devices with their start and end apart: 75 -> 75, of which waited for: 23 -> 23; matrix products, arithmetic and copies ran while one was open for 5% -> 6% of each run, Pallas kernels for 34% -> 27%
where the time goes in v2:
time: 966 us; the launch traced here: 956 us
  Pallas kernels  525 us (54%)
  waiting for transfers between devices  293 us (30%)
  starting transfers between devices  62 us (6%)
  local copies, waits for them, and re-layouts  53 us (5%)
  other arithmetic  21 us (2%)
    ppermute x75, waiting for transfers between devices, permute(): return lax.ppermute(array, AXIS, perm)  293 us
    pallas_call x2, Pallas kernels, ff_grads(): pl.pallas_call(functools.partial(ff_grad_kernel, offset, down), in_specs=...  128 us
    pallas_call x2, Pallas kernels, self_backward(): call(functools.partial(self_backward_kernel, STEP // tokens, tokens), cou...  84.2 us
    pallas_call x5, Pallas kernels, weight_grads(): pl.pallas_call(functools.partial(grad_kernel, tiles, group_rows, len(arra...  75.5 us
    ppermute x75, starting transfers between devices, permute(): return lax.ppermute(array, AXIS, perm)  62 us
    pallas_call x2, Pallas kernels, cross_backward(): call(functools.partial(cross_backward_kernel, STEP // tokens, tokens, val...  56 us
    pallas_call x2, Pallas kernels, self_forward(): call(functools.partial(self_forward_kernel, STEP // tokens, tokens), coun...  41 us
    pallas_call x2, Pallas kernels, cross_forward(): call(functools.partial(cross_forward_kernel, STEP // tokens, tokens, vali...  38.9 us
  transfers between devices with their start and end apart: 75, of which 23 were waited for; matrix products, arithmetic and copies ran while one was open for 6% of the time, Pallas kernels for 27%

profile of v2, /device:TPU:0, one launch (start us, length us, event | category | flops | bytes accessed | tf_op | source)
XLA Modules:
  0.0 956.5 jit_solution(10130581725516058845)
XLA Ops:
  0.7 2.1 copy.67
  2.7 1.6 copy.68
  4.4 1.8 pack.10.refs_0_
  6.1 3.3 collective-permute-start.21
  13.4 1.8 pack.13.refs_0_.refs_8_
  16.8 1.9 pack.7.refs_0_
  18.7 1.7 collective-permute-start
  21.0 1.7 collective-permute-start.43
  22.8 4.1 collective-permute-done.42.refs_1_.refs_9_
  27.7 2.2 pack.12.refs_0_
  29.9 8.2 collective-permute-done.43.refs_2_.refs_10_
  38.1 1.8 collective-permute-start.35
  43.5 2.2 pack.8.refs_0_
  48.7 2.1 pack.11.refs_0_
  50.8 8.7 collective-permute-done.35.refs_1_
  59.5 1.8 collective-permute-start.28
  61.3 1.8 collective-permute-start.29
  63.1 1.7 pad.14
  64.8 3.1 pack.9.refs_0_.refs_8_.refs_1_.refs_9_
  67.9 10.0 %collective-permute-done.7.refs_1_ = bf16[672,640]{1,0:T(8,128)(2,1)} collective-permute-done((bf16[672,640]{1,0:T(8,128)(2,1)}, bf16[672,640]{1,0:T(8,128)(2,1)}, u32[]{:S(2)}, u32[]{:S(2)}) %collective-permute-start.7) | collective-permute-done | bytes 860192 | tf_op jit(solution)/shard_map/ppermute | solution.py:55
  78.0 1.8 collective-permute-start.14
  83.5 12.9 %collective-permute-done.28.refs_1_ = bf16[672,640]{1,0:T(8,128)(2,1)} collective-permute-done((bf16[672,640]{1,0:T(8,128)(2,1)}, bf16[672,640]{1,0:T(8,128)(2,1)}, u32[]{:S(2)}, u32[]{:S(2)}) %collective-permute-start.28) | collective-permute-done | bytes 860192 | tf_op jit(solution)/shard_map/ppermute | solution.py:55
  96.4 1.8 collective-permute-done.29.refs_2_
  99.3 9.0 collective-permute-done.2.refs_3_
  113.3 1.8 copy.38
  115.1 1.8 copy.39
  116.9 1.8 copy.40
  129.6 3.2 maximum_bitcast_fusion.ctx_ref
  135.1 2.4 collective-permute-done.15.refs_2_.refs_10_.refs_3_.refs_11_
  139.0 11.6 %collective-permute-done.16.refs_3_.refs_11_.refs_4_.refs_12_ = bf16[960,640]{1,0:T(8,128)(2,1)} collective-permute-done((bf16[960,640]{1,0:T(8,128)(2,1)}, bf16[960,640]{1,0:T(8,128)(2,1)}, u32[]{:S(2)}, u32[]{:S(2)}) %collective-permute-start.16) | collective-permute-done | bytes 1228832 | tf_op jit(solution)/shard_map/ppermute | solution.py:55
  153.2 20.2 %shard_map.186 = (bf16[1536,640]{1,0:T(8,128)(2,1)}, bf16[1536,1920]{1,0:T(8,128)(2,1)}, bf16[1536,640]{1,0:T(8,128)(2,1)}, f32[1536,640]{1,0:T(8,128)}) custom-call(bf16[1536,640]{1,0:T(8,128)(2,1)} %bitcast.155, f32[16,640]{1,0:T(8,128)} %get-tuple-element.213.rows_ref, bf16[368,640]{1,0:T(8,128)(2,1)} %pack.7.refs_0_, bf16[368,640]{1,0:T(8,128)(2,1)} %copy-done.38, ...), custom_call_target="tpu_custom_call" | custom-call | flops 6039797760 | bytes 20000000 | tf_op jit(solution)/shard_map/pallas_call | solution.py:440
  173.4 19.5 %shard_map.187 = (bf16[1536,640]{1,0:T(8,128)(2,1)}, bf16[1536,640]{1,0:T(8,128)(2,1)}, bf16[480,1280]{1,0:T(8,128)(2,1)}, bf16[1536,640]{1,0:T(8,128)(2,1)}, f32[1536,640]{1,0:T(8,128)}) custom-call(f32[1536,640]{1,0:T(8,128)} %get-tuple-element.90.h_ref, f32[16,640]{1,0:T(8,128)} %get-tuple-element.213.rows_ref, bf16[480,2048]{1,0:T(8,128)(2,1)} %bitcast.122, ...), custom_call_target="tpu_custom_call" | custom-call | flops 5536481280 | bytes 20000000 | tf_op jit(solution)/shard_map/pallas_call | solution.py:452
  195.2 31.9 %shard_map.188 = (bf16[1536,640]{1,0:T(8,128)(2,1)}, bf16[1536,2560]{1,0:T(8,128)(2,1)}, f32[1536,2560]{1,0:T(8,128)}, f32[1536,2560]{1,0:T(8,128)}, f32[1536,640]{1,0:T(8,128)}) custom-call(f32[1536,640]{1,0:T(8,128)} %get-tuple-element.94.h_ref, f32[16,640]{1,0:T(8,128)} %get-tuple-element.213.rows_ref, f32[1,5120]{1,0:T(1,128)} %bitcast.154, ...), custom_call_target="tpu_custom_call" | custom-call | flops 15099494400 | bytes 60000000 | tf_op jit(solution)/shard_map/pallas_call | solution.py:466
  228.2 20.8 %shard_map.189 = (bf16[1536,640]{1,0:T(8,128)(2,1)}, bf16[1536,1920]{1,0:T(8,128)(2,1)}, bf16[1536,640]{1,0:T(8,128)(2,1)}, f32[1536,640]{1,0:T(8,128)}) custom-call(f32[1536,640]{1,0:T(8,128)} %get-tuple-element.97.h_ref, f32[16,640]{1,0:T(8,128)} %get-tuple-element.212.rows_ref, bf16[320,640]{1,0:T(8,128)(2,1)} %pack.10.refs_0_, ...), custom_call_target="tpu_custom_call" | custom-call | flops 6039797760 | bytes 20000000 | tf_op jit(solution)/shard_map/pallas_call | solution.py:440
  250.4 19.4 %shard_map.190 = (bf16[1536,640]{1,0:T(8,128)(2,1)}, bf16[1536,640]{1,0:T(8,128)(2,1)}, bf16[480,1280]{1,0:T(8,128)(2,1)}, bf16[1536,640]{1,0:T(8,128)(2,1)}, f32[1536,640]{1,0:T(8,128)}) custom-call(f32[1536,640]{1,0:T(8,128)} %get-tuple-element.98.h_ref, f32[16,640]{1,0:T(8,128)} %get-tuple-element.212.rows_ref, bf16[480,2048]{1,0:T(8,128)(2,1)} %bitcast.123, ...), custom_call_target="tpu_custom_call" | custom-call | flops 5536481280 | bytes 20000000 | tf_op jit(solution)/shard_map/pallas_call | solution.py:452
  270.9 28.7 %shard_map.191 = (bf16[1536,640]{1,0:T(8,128)(2,1)}, bf16[1536,2560]{1,0:T(8,128)(2,1)}, f32[1536,2560]{1,0:T(8,128)}, f32[1536,2560]{1,0:T(8,128)}) custom-call(f32[1536,640]{1,0:T(8,128)} %get-tuple-element.99.h_ref, f32[16,640]{1,0:T(8,128)} %get-tuple-element.212.rows_ref, f32[1,5120]{1,0:T(1,128)} %bitcast.153, bf16[640,640]{1,0:T(8,128)(2,1)} %pack.12.refs_0_, ...), custom_call_target="tpu_custom_call" | custom-call | flops 10066329600 | bytes 50000000 | tf_op jit(solution)/shard_map/pallas_call | solution.py:479
  301.2 58.0 %shard_map.193 = (f32[1536,640]{1,0:T(8,128)}, f32[8,640]{1,0:T(8,128)}, f32[8,5120]{1,0:T(8,128)}, f32[1280,640]{1,0:T(8,128)}, f32[1280,640]{1,0:T(8,128)}) custom-call(bf16[1536,640]{1,0:T(8,128)(2,1)} %bitcast.157, f32[1536,2560]{1,0:T(8,128)} %get-tuple-element.101.save_a, f32[1536,2560]{1,0:T(8,128)} %get-tuple-element.102.save_g, ...), custom_call_target="tpu_custom_call" | custom-call | flops 25165824000 | bytes 60000000 | tf_op jit(solution)/shard_map/pallas_call | solution.py:850
  359.2 28.2 %shard_map.194 = (bf16[1536,640]{1,0:T(8,128)(2,1)}, bf16[1536,640]{1,0:T(8,128)(2,1)}, bf16[480,1280]{1,0:T(8,128)(2,1)}, f32[1536,640]{1,0:T(8,128)}, f32[8,640]{1,0:T(8,128)}) custom-call(f32[1536,640]{1,0:T(8,128)} %get-tuple-element.104.grad_ref, bf16[1536,640]{1,0:T(8,128)(2,1)} %get-tuple-element.105.query_ref, ...), custom_call_target="tpu_custom_call" | custom-call | flops 3774873600 | bytes 20000000 | tf_op jit(solution)/shard_map/pallas_call | solution.py:503
  387.4 42.1 %shard_map.195 = (bf16[1536,640]{1,0:T(8,128)(2,1)}, bf16[1536,1920]{1,0:T(8,128)(2,1)}, f32[1536,640]{1,0:T(8,128)}, f32[8,640]{1,0:T(8,128)}) custom-call(f32[1536,640]{1,0:T(8,128)} %get-tuple-element.107.grad_ref, bf16[1536,1920]{1,0:T(8,128)(2,1)} %get-tuple-element.108.qkv_ref, f32[1536,640]{1,0:T(8,128)} %get-tuple-element.97.h_ref, ...), custom_call_target="tpu_custom_call" | custom-call | flops 7549747200 | bytes 30000000 | tf_op jit(solution)/shard_map/pallas_call | solution.py:517
  434.0 69.8 %shard_map.196 = (f32[1536,640]{1,0:T(8,128)}, f32[8,640]{1,0:T(8,128)}, f32[8,5120]{1,0:T(8,128)}, f32[1280,640]{1,0:T(8,128)}, f32[1280,640]{1,0:T(8,128)}, /*index=5*/f32[640,640]{1,0:T(8,128)}, f32[640,640]{1,0:T(8,128)}) custom-call(f32[1536,640]{1,0:T(8,128)} %get-tuple-element.109.grad_ref, f32[1536,2560]{1,0:T(8,128)} %get-tuple-element.110.save_a, ...), custom_call_target="tpu_custom_call" | custom-call | flops 35232153600 | bytes 60000000 | tf_op jit(solution)/shard_map/pallas_call | solution.py:850
  503.8 27.8 %shard_map.197 = (bf16[1536,640]{1,0:T(8,128)(2,1)}, bf16[1536,640]{1,0:T(8,128)(2,1)}, bf16[480,1280]{1,0:T(8,128)(2,1)}, f32[1536,640]{1,0:T(8,128)}, f32[8,640]{1,0:T(8,128)}) custom-call(f32[1536,640]{1,0:T(8,128)} %get-tuple-element.114.grad_ref, bf16[1536,640]{1,0:T(8,128)(2,1)} %get-tuple-element.115.query_ref, ...), custom_call_target="tpu_custom_call" | custom-call | flops 3774873600 | bytes 20000000 | tf_op jit(solution)/shard_map/pallas_call | solution.py:503
  531.6 42.0 %shard_map.198 = (bf16[1536,640]{1,0:T(8,128)(2,1)}, bf16[1536,1920]{1,0:T(8,128)(2,1)}, bf16[1536,640]{1,0:T(8,128)(2,1)}, f32[8,640]{1,0:T(8,128)}) custom-call(f32[1536,640]{1,0:T(8,128)} %get-tuple-element.117.grad_ref, bf16[1536,1920]{1,0:T(8,128)(2,1)} %get-tuple-element.118.qkv_ref, bf16[1536,640]{1,0:T(8,128)(2,1)} %bitcast.156, ...), custom_call_target="tpu_custom_call" | custom-call | flops 7549747200 | bytes 30000000 | tf_op jit(solution)/shard_map/pallas_call | solution.py:517
  579.2 17.1 %shard_map.203 = (f32[640,640]{1,0:T(8,128)}, f32[640,640]{1,0:T(8,128)}) custom-call(bf16[1536,2560]{1,0:T(8,128)(2,1)} %get-tuple-element.100.gated_ref.refs_0_, bf16[1536,640]{1,0:T(8,128)(2,1)} %bitcast.158), custom_call_target="tpu_custom_call" | custom-call | flops 5033164800 | bytes 20000000 | tf_op jit(solution)/shard_map/pallas_call | solution.py:629
  597.4 11.9 %shard_map.201 = (f32[320,640]{1,0:T(8,128)}, f32[320,640]{1,0:T(8,128)}) custom-call(bf16[1536,640]{1,0:T(8,128)(2,1)} %get-tuple-element.132.refs_0_, bf16[1536,640]{1,0:T(8,128)(2,1)} %get-tuple-element.133.refs_1_, bf16[1536,640]{1,0:T(8,128)(2,1)} %get-tuple-element.134.refs_2_, bf16[1536,640]{1,0:T(8,128)(2,1)} %get-tuple-element.135.refs_3_), custom_call_target="tpu_custom_call" | custom-call | flops 2516582400 | bytes 20000000 | tf_op jit(solution)/shard_map/pallas_call | solution.py:629
  610.4 11.9 %shard_map.202 = (f32[320,640]{1,0:T(8,128)}, f32[320,640]{1,0:T(8,128)}) custom-call(bf16[1536,640]{1,0:T(8,128)(2,1)} %get-tuple-element.138.refs_0_, bf16[1536,640]{1,0:T(8,128)(2,1)} %get-tuple-element.139.refs_1_, bf16[1536,640]{1,0:T(8,128)(2,1)} %get-tuple-element.140.refs_2_, bf16[1536,640]{1,0:T(8,128)(2,1)} %get-tuple-element.141.refs_3_), custom_call_target="tpu_custom_call" | custom-call | flops 2516582400 | bytes 20000000 | tf_op jit(solution)/shard_map/pallas_call | solution.py:629
  623.3 17.0 %shard_map.199 = (f32[640,640]{1,0:T(8,128)}, f32[640,640]{1,0:T(8,128)}) custom-call(bf16[1536,640]{1,0:T(8,128)(2,1)} %get-tuple-element.120.refs_0_, bf16[1536,1920]{1,0:T(8,128)(2,1)} %get-tuple-element.121.refs_1_, bf16[1536,640]{1,0:T(8,128)(2,1)} %get-tuple-element.122.refs_2_, bf16[1536,640]{1,0:T(8,128)(2,1)} %get-tuple-element.123.refs_3_), custom_call_target="tpu_custom_call" | custom-call | flops 5033164800 | bytes 20000000 | tf_op jit(solution)/shard_map/pallas_call | solution.py:629
  640.3 17.4 %shard_map.200 = (f32[640,640]{1,0:T(8,128)}, f32[640,640]{1,0:T(8,128)}) custom-call(bf16[1536,640]{1,0:T(8,128)(2,1)} %get-tuple-element.126.refs_0_, bf16[1536,1920]{1,0:T(8,128)(2,1)} %get-tuple-element.127.refs_1_, bf16[1536,640]{1,0:T(8,128)(2,1)} %get-tuple-element.128.refs_2_, bf16[1536,640]{1,0:T(8,128)(2,1)} %get-tuple-element.129.refs_3_), custom_call_target="tpu_custom_call" | custom-call | flops 5033164800 | bytes 20000000 | tf_op jit(solution)/shard_map/pallas_call | solution.py:629
  658.9 12.0 %shard_map.192 = bf16[1536,640]{1,0:T(8,128)(2,1)} custom-call(f32[1536,640]{1,0:T(8,128)} %get-tuple-element.99.h_ref, f32[16,640]{1,0:T(8,128)} %get-tuple-element.212.rows_ref, bf16[1536,2560]{1,0:T(8,128)(2,1)} %get-tuple-element.100.gated_ref.refs_0_, bf16[320,640]{1,0:T(8,128)(2,1)} %pack.13.refs_0_.refs_8_, bf16[320,640]{1,0:T(8,128)(2,1)} %copy-done.44, ...), custom_call_target="tpu_custom_call" | custom-call | flops 5033164800 | bytes 20000000 | tf_op jit(solution)/shard_map/pallas_call | solution.py:491
  676.4 3.7 collective-permute-done.54
  680.2 4.3 collective-permute-done.56
  688.7 7.2 context_grad.2
  697.0 7.2 context_grad.3
  711.3 28.0 %collective-permute-done.51 = f32[640,640]{1,0:T(8,128)} collective-permute-done((f32[640,640]{1,0:T(8,128)}, f32[640,640]{1,0:T(8,128)}, u32[]{:S(2)}, u32[]{:S(2)}) %collective-permute-start.51) | collective-permute-done | bytes 1638432 | tf_op jit(solution)/shard_map/ppermute | solution.py:55
  747.9 2.4 copy.56
  750.3 12.6 %collective-permute-done.50 = f32[320,640]{1,0:T(8,128)S(1)} collective-permute-done((f32[320,640]{1,0:T(8,128)S(1)}, f32[320,640]{1,0:T(8,128)S(1)}, u32[]{:S(2)}, u32[]{:S(2)}) %collective-permute-start.50) | collective-permute-done | bytes 819232 | tf_op jit(solution)/shard_map/ppermute | solution.py:55
  765.4 15.1 %collective-permute-done.52 = f32[320,640]{1,0:T(8,128)S(1)} collective-permute-done((f32[320,640]{1,0:T(8,128)S(1)}, f32[320,640]{1,0:T(8,128)S(1)}, u32[]{:S(2)}, u32[]{:S(2)}) %collective-permute-start.52) | collective-permute-done | bytes 819232 | tf_op jit(solution)/shard_map/ppermute | solution.py:55
  782.9 10.7 %collective-permute-done.64 = f32[1280,640]{1,0:T(8,128)S(1)} collective-permute-done((f32[1280,640]{1,0:T(8,128)}, f32[1280,640]{1,0:T(8,128)S(1)}, u32[]{:S(2)}, u32[]{:S(2)}) %collective-permute-start.64) | collective-permute-done | bytes 3276832 | tf_op jit(solution)/shard_map/ppermute | solution.py:55
  795.1 1.7 copy.50
  796.7 49.5 %collective-permute-done.66 = f32[1280,640]{1,0:T(8,128)S(1)} collective-permute-done((f32[1280,640]{1,0:T(8,128)}, f32[1280,640]{1,0:T(8,128)S(1)}, u32[]{:S(2)}, u32[]{:S(2)}) %collective-permute-start.66) | collective-permute-done | bytes 3276832 | tf_op jit(solution)/shard_map/ppermute | solution.py:55
  847.5 44.4 %collective-permute-done.59 = f32[1024,640]{1,0:T(8,128)S(1)} collective-permute-done((f32[1024,640]{1,0:T(8,128)}, f32[1024,640]{1,0:T(8,128)S(1)}, u32[]{:S(2)}, u32[]{:S(2)}) %collective-permute-start.59) | collective-permute-done | bytes 2621472 | tf_op jit(solution)/shard_map/ppermute | solution.py:55
  893.4 40.7 %collective-permute-done.62 = f32[1024,640]{1,0:T(8,128)S(1)} collective-permute-done((f32[1024,640]{1,0:T(8,128)S(1)}, f32[1024,640]{1,0:T(8,128)S(1)}, u32[]{:S(2)}, u32[]{:S(2)}) %collective-permute-start.62) | collective-permute-done | bytes 2621472 | tf_op jit(solution)/shard_map/ppermute | solution.py:55
  936.5 4.2 copy.55
  941.0 10.8 %collective-permute-done.63 = f32[512,640]{1,0:T(8,128)S(1)} collective-permute-done((f32[512,640]{1,0:T(8,128)S(1)}, f32[512,640]{1,0:T(8,128)S(1)}, u32[]{:S(2)}, u32[]{:S(2)}) %collective-permute-start.63) | collective-permute-done | bytes 1310752 | tf_op jit(solution)/shard_map/ppermute | solution.py:55
  952.5 3.5 copy.53
  (348 shorter events, 100.3 us)
Async XLA Ops:
  6.1 14.2 %collective-permute-start.21 = (bf16[320,640]{1,0:T(8,128)(2,1)}, bf16[320,640]{1,0:T(8,128)(2,1)}, u32[]{:S(2)}, u32[]{:S(2)}) collective-permute-start(bf16[320,640]{1,0:T(8,128)(2,1)} %pack.10.refs_0_), channel_id=1, source_target_pairs={{0,4},{1,3},{2,6},{3,1},{4,0},{5,7},{6,2},{7,5}} | collective-permute-start | bytes 1228808 | tf_op jit(solution)/shard_map/ppermute | solution.py:55
  18.7 21.2 %collective-permute-start = (bf16[368,640]{1,0:T(8,128)(2,1)}, bf16[368,640]{1,0:T(8,128)(2,1)S(1)}, u32[]{:S(2)}, u32[]{:S(2)}) collective-permute-start(bf16[368,640]{1,0:T(8,128)(2,1)} %pack.7.refs_0_), channel_id=1, source_target_pairs={{0,4},{1,3},{2,6},{3,1},{4,0},{5,7},{6,2},{7,5}} | collective-permute-start | bytes 1413128 | tf_op jit(solution)/shard_map/ppermute | solution.py:55
  20.4 21.0 %collective-permute-start.1 = (bf16[368,640]{1,0:T(8,128)(2,1)}, bf16[368,640]{1,0:T(8,128)(2,1)S(1)}, u32[]{:S(2)}, u32[]{:S(2)}) collective-permute-start(bf16[368,640]{1,0:T(8,128)(2,1)} %pack.7.refs_0_), channel_id=1, source_target_pairs={{0,2},{1,5},{2,0},{3,7},{4,6},{5,1},{6,4},{7,3}} | collective-permute-start | bytes 1413128 | tf_op jit(solution)/shard_map/ppermute | solution.py:55
  21.0 17.1 %collective-permute-start.43 = (bf16[320,640]{1,0:T(8,128)(2,1)}, bf16[320,640]{1,0:T(8,128)(2,1)}, u32[]{:S(2)}, u32[]{:S(2)}) collective-permute-start(bf16[320,640]{1,0:T(8,128)(2,1)} %pack.13.refs_0_.refs_8_), channel_id=1, source_target_pairs={{0,2},{1,5},{2,0},{3,7},{4,6},{5,1},{6,4},{7,3}} | collective-permute-start | bytes 1228808 | tf_op jit(solution)/shard_map/ppermute | solution.py:55
  22.8 22.9 %collective-permute-start.3 = (bf16[368,640]{1,0:T(8,128)(2,1)}, bf16[368,640]{1,0:T(8,128)(2,1)S(1)}, u32[]{:S(2)}, u32[]{:S(2)}) collective-permute-start(bf16[368,640]{1,0:T(8,128)(2,1)} %pack.7.refs_0_), channel_id=1, source_target_pairs={{0,1},{1,0},{2,3},{3,2},{4,5},{5,4},{6,7},{7,6}} | collective-permute-start | bytes 1413128 | tf_op jit(solution)/shard_map/ppermute | solution.py:55
  26.9 19.3 %collective-permute-start.23 = (bf16[320,640]{1,0:T(8,128)(2,1)}, bf16[320,640]{1,0:T(8,128)(2,1)}, u32[]{:S(2)}, u32[]{:S(2)}) collective-permute-start(bf16[320,640]{1,0:T(8,128)(2,1)} %collective-permute-done.21.refs_1_), channel_id=1, source_target_pairs={{0,2},{1,5},{2,0},{3,7},{4,6},{5,1},{6,4},{7,3}} | collective-permute-start | bytes 1228808 | tf_op jit(solution)/shard_map/ppermute | solution.py:55
  38.1 21.4 %collective-permute-start.35 = (bf16[640,640]{1,0:T(8,128)(2,1)}, bf16[640,640]{1,0:T(8,128)(2,1)}, u32[]{:S(2)}, u32[]{:S(2)}) collective-permute-start(bf16[640,640]{1,0:T(8,128)(2,1)} %pack.12.refs_0_), channel_id=1, source_target_pairs={{0,4},{1,3},{2,6},{3,1},{4,0},{5,7},{6,2},{7,5}} | collective-permute-start | bytes 2457608 | tf_op jit(solution)/shard_map/ppermute | solution.py:55
  39.9 21.4 %collective-permute-start.36 = (bf16[640,640]{1,0:T(8,128)(2,1)}, bf16[640,640]{1,0:T(8,128)(2,1)}, u32[]{:S(2)}, u32[]{:S(2)}) collective-permute-start(bf16[640,640]{1,0:T(8,128)(2,1)} %pack.12.refs_0_), channel_id=1, source_target_pairs={{0,2},{1,5},{2,0},{3,7},{4,6},{5,1},{6,4},{7,3}} | collective-permute-start | bytes 2457608 | tf_op jit(solution)/shard_map/ppermute | solution.py:55
  45.6 32.3 %collective-permute-start.7 = (bf16[672,640]{1,0:T(8,128)(2,1)}, bf16[672,640]{1,0:T(8,128)(2,1)}, u32[]{:S(2)}, u32[]{:S(2)}) collective-permute-start(bf16[672,640]{1,0:T(8,128)(2,1)} %pack.8.refs_0_), channel_id=1, source_target_pairs={{0,4},{1,3},{2,6},{3,1},{4,0},{5,7},{6,2},{7,5}} | collective-permute-start | bytes 2580488 | tf_op jit(solution)/shard_map/ppermute | solution.py:55
  46.6 35.4 %collective-permute-start.8 = (bf16[672,640]{1,0:T(8,128)(2,1)}, bf16[672,640]{1,0:T(8,128)(2,1)}, u32[]{:S(2)}, u32[]{:S(2)}) collective-permute-start(bf16[672,640]{1,0:T(8,128)(2,1)} %pack.8.refs_0_), channel_id=1, source_target_pairs={{0,2},{1,5},{2,0},{3,7},{4,6},{5,1},{6,4},{7,3}} | collective-permute-start | bytes 2580488 | tf_op jit(solution)/shard_map/ppermute | solution.py:55
  48.3 33.6 %collective-permute-start.10 = (bf16[672,640]{1,0:T(8,128)(2,1)}, bf16[672,640]{1,0:T(8,128)(2,1)}, u32[]{:S(2)}, u32[]{:S(2)}) collective-permute-start(bf16[672,640]{1,0:T(8,128)(2,1)} %pack.8.refs_0_), channel_id=1, source_target_pairs={{0,1},{1,0},{2,3},{3,2},{4,5},{5,4},{6,7},{7,6}} | collective-permute-start | bytes 2580488 | tf_op jit(solution)/shard_map/ppermute | solution.py:55
  59.5 36.9 %collective-permute-start.28 = (bf16[672,640]{1,0:T(8,128)(2,1)}, bf16[672,640]{1,0:T(8,128)(2,1)}, u32[]{:S(2)}, u32[]{:S(2)}) collective-permute-start(bf16[672,640]{1,0:T(8,128)(2,1)} %pack.11.refs_0_), channel_id=1, source_target_pairs={{0,4},{1,3},{2,6},{3,1},{4,0},{5,7},{6,2},{7,5}} | collective-permute-start | bytes 2580488 | tf_op jit(solution)/shard_map/ppermute | solution.py:55
  61.3 36.9 %collective-permute-start.29 = (bf16[672,640]{1,0:T(8,128)(2,1)}, bf16[672,640]{1,0:T(8,128)(2,1)}, u32[]{:S(2)}, u32[]{:S(2)}) collective-permute-start(bf16[672,640]{1,0:T(8,128)(2,1)} %pack.11.refs_0_), channel_id=1, source_target_pairs={{0,2},{1,5},{2,0},{3,7},{4,6},{5,1},{6,4},{7,3}} | collective-permute-start | bytes 2580488 | tf_op jit(solution)/shard_map/ppermute | solution.py:55
  78.0 41.2 %collective-permute-start.14 = (bf16[960,640]{1,0:T(8,128)(2,1)}, bf16[960,640]{1,0:T(8,128)(2,1)}, u32[]{:S(2)}, u32[]{:S(2)}) collective-permute-start(bf16[960,640]{1,0:T(8,128)(2,1)} %pack.9.refs_0_.refs_8_.refs_1_.refs_9_), channel_id=1, source_target_pairs={{0,4},{1,3},{2,6},{3,1},{4,0},{5,7},{6,2},{7,5}} | collective-permute-start | bytes 3686408 | tf_op jit(solution)/shard_map/ppermute | solution.py:55
  81.9 36.7 %collective-permute-start.57 = (bf16[480,1024]{1,0:T(8,128)(2,1)}, bf16[480,1024]{1,0:T(8,128)(2,1)S(1)}, u32[]{:S(2)}, u32[]{:S(2)}) collective-permute-start(bf16[480,1024]{1,0:T(8,128)(2,1)} %pad_maximum_fusion), channel_id=1, source_target_pairs={{0,1},{1,0},{2,3},{3,2},{4,5},{5,4},{6,7},{7,6}} | collective-permute-start | bytes 2949128 | tf_op jit(solution)/shard_map/ppermute | solution.py:55
  82.0 26.3 %collective-permute-start.2 = (bf16[368,640]{1,0:T(8,128)(2,1)S(1)}, bf16[368,640]{1,0:T(8,128)(2,1)}, u32[]{:S(2)}, u32[]{:S(2)}) collective-permute-start(bf16[368,640]{1,0:T(8,128)(2,1)S(1)} %copy-done.39), channel_id=1, source_target_pairs={{0,2},{1,5},{2,0},{3,7},{4,6},{5,1},{6,4},{7,3}} | collective-permute-start | bytes 1413128 | tf_op jit(solution)/shard_map/ppermute | solution.py:55
  96.4 13.0 %collective-permute-start.4 = (bf16[368,640]{1,0:T(8,128)(2,1)S(1)}, bf16[368,640]{1,0:T(8,128)(2,1)S(1)}, u32[]{:S(2)}, u32[]{:S(2)}) collective-permute-start(bf16[368,640]{1,0:T(8,128)(2,1)S(1)} %copy-done.39), channel_id=1, source_target_pairs={{0,1},{1,0},{2,3},{3,2},{4,5},{5,4},{6,7},{7,6}} | collective-permute-start | bytes 1413128 | tf_op jit(solution)/shard_map/ppermute | solution.py:55
  108.3 20.7 %collective-permute-start.31 = (bf16[672,640]{1,0:T(8,128)(2,1)S(1)}, bf16[672,640]{1,0:T(8,128)(2,1)}, u32[]{:S(2)}, u32[]{:S(2)}) collective-permute-start(bf16[672,640]{1,0:T(8,128)(2,1)S(1)} %copy-done.1), channel_id=1, source_target_pairs={{0,1},{1,0},{2,3},{3,2},{4,5},{5,4},{6,7},{7,6}} | collective-permute-start | bytes 2580488 | tf_op jit(solution)/shard_map/ppermute | solution.py:55
  109.4 24.2 %collective-permute-start.9 = (bf16[672,640]{1,0:T(8,128)(2,1)}, bf16[672,640]{1,0:T(8,128)(2,1)}, u32[]{:S(2)}, u32[]{:S(2)}) collective-permute-start(bf16[672,640]{1,0:T(8,128)(2,1)} %collective-permute-done.7.refs_1_), channel_id=1, source_target_pairs={{0,2},{1,5},{2,0},{3,7},{4,6},{5,1},{6,4},{7,3}} | collective-permute-start | bytes 2580488 | tf_op jit(solution)/shard_map/ppermute | solution.py:55
  111.0 18.1 %collective-permute-start.6 = (bf16[368,640]{1,0:T(8,128)(2,1)}, bf16[368,640]{1,0:T(8,128)(2,1)}, u32[]{:S(2)}, u32[]{:S(2)}) collective-permute-start(bf16[368,640]{1,0:T(8,128)(2,1)} %collective-permute-done.2.refs_3_), channel_id=1, source_target_pairs={{0,1},{1,0},{2,3},{3,2},{4,5},{5,4},{6,7},{7,6}} | collective-permute-start | bytes 1413128 | tf_op jit(solution)/shard_map/ppermute | solution.py:55
  118.7 18.8 %collective-permute-start.15 = (bf16[960,640]{1,0:T(8,128)(2,1)S(1)}, bf16[960,640]{1,0:T(8,128)(2,1)}, u32[]{:S(2)}, u32[]{:S(2)}) collective-permute-start(bf16[960,640]{1,0:T(8,128)(2,1)S(1)} %copy-done.12), channel_id=1, source_target_pairs={{0,2},{1,5},{2,0},{3,7},{4,6},{5,1},{6,4},{7,3}} | collective-permute-start | bytes 3686408 | tf_op jit(solution)/shard_map/ppermute | solution.py:55
  119.1 31.5 %collective-permute-start.16 = (bf16[960,640]{1,0:T(8,128)(2,1)}, bf16[960,640]{1,0:T(8,128)(2,1)}, u32[]{:S(2)}, u32[]{:S(2)}) collective-permute-start(bf16[960,640]{1,0:T(8,128)(2,1)} %collective-permute-done.14.refs_1_.refs_9_.refs_2_.refs_10_), channel_id=1, source_target_pairs={{0,2},{1,5},{2,0},{3,7},{4,6},{5,1},{6,4},{7,3}} | collective-permute-start | bytes 3686408 | tf_op jit(solution)/shard_map/ppermute | solution.py:55
  133.6 18.4 %collective-permute-start.13 = (bf16[672,640]{1,0:T(8,128)(2,1)}, bf16[672,640]{1,0:T(8,128)(2,1)S(1)}, u32[]{:S(2)}, u32[]{:S(2)}) collective-permute-start(bf16[672,640]{1,0:T(8,128)(2,1)} %collective-permute-done.9.refs_3_), channel_id=1, source_target_pairs={{0,1},{1,0},{2,3},{3,2},{4,5},{5,4},{6,7},{7,6}} | collective-permute-start | bytes 2580488 | tf_op jit(solution)/shard_map/ppermute | solution.py:55
  137.5 55.4 %collective-permute-start.17 = (bf16[960,640]{1,0:T(8,128)(2,1)S(1)}, bf16[960,640]{1,0:T(8,128)(2,1)}, u32[]{:S(2)}, u32[]{:S(2)}) collective-permute-start(bf16[960,640]{1,0:T(8,128)(2,1)S(1)} %copy-done.12), channel_id=1, source_target_pairs={{0,1},{1,0},{2,3},{3,2},{4,5},{5,4},{6,7},{7,6}} | collective-permute-start | bytes 3686408 | tf_op jit(solution)/shard_map/ppermute | solution.py:55
  138.5 56.1 %collective-permute-start.18 = (bf16[960,640]{1,0:T(8,128)(2,1)}, bf16[960,640]{1,0:T(8,128)(2,1)}, u32[]{:S(2)}, u32[]{:S(2)}) collective-permute-start(bf16[960,640]{1,0:T(8,128)(2,1)} %collective-permute-done.14.refs_1_.refs_9_.refs_2_.refs_10_), channel_id=1, source_target_pairs={{0,1},{1,0},{2,3},{3,2},{4,5},{5,4},{6,7},{7,6}} | collective-permute-start | bytes 3686408 | tf_op jit(solution)/shard_map/ppermute | solution.py:55
  138.5 56.2 %collective-permute-start.19 = (bf16[960,640]{1,0:T(8,128)(2,1)}, bf16[960,640]{1,0:T(8,128)(2,1)}, u32[]{:S(2)}, u32[]{:S(2)}) collective-permute-start(bf16[960,640]{1,0:T(8,128)(2,1)} %collective-permute-done.15.refs_2_.refs_10_.refs_3_.refs_11_), channel_id=1, source_target_pairs={{0,1},{1,0},{2,3},{3,2},{4,5},{5,4},{6,7},{7,6}} | collective-permute-start | bytes 3686408 | tf_op jit(solution)/shard_map/ppermute | solution.py:55
  150.7 44.5 %collective-permute-start.20 = (bf16[960,640]{1,0:T(8,128)(2,1)}, bf16[960,640]{1,0:T(8,128)(2,1)}, u32[]{:S(2)}, u32[]{:S(2)}) collective-permute-start(bf16[960,640]{1,0:T(8,128)(2,1)} %collective-permute-done.16.refs_3_.refs_11_.refs_4_.refs_12_), channel_id=1, source_target_pairs={{0,1},{1,0},{2,3},{3,2},{4,5},{5,4},{6,7},{7,6}} | collective-permute-start | bytes 3686408 | tf_op jit(solution)/shard_map/ppermute | solution.py:55
  152.0 41.6 %collective-permute-start.30 = (bf16[672,640]{1,0:T(8,128)(2,1)}, bf16[672,640]{1,0:T(8,128)(2,1)}, u32[]{:S(2)}, u32[]{:S(2)}) collective-permute-start(bf16[672,640]{1,0:T(8,128)(2,1)} %collective-permute-done.28.refs_1_), channel_id=1, source_target_pairs={{0,2},{1,5},{2,0},{3,7},{4,6},{5,1},{6,4},{7,3}} | collective-permute-start | bytes 2580488 | tf_op jit(solution)/shard_map/ppermute | solution.py:55
  192.9 34.2 %collective-permute-start.27 = (bf16[320,640]{1,0:T(8,128)(2,1)}, bf16[320,640]{1,0:T(8,128)(2,1)S(1)}, u32[]{:S(2)}, u32[]{:S(2)}) collective-permute-start(bf16[320,640]{1,0:T(8,128)(2,1)} %collective-permute-done.23.refs_3_), channel_id=1, source_target_pairs={{0,1},{1,0},{2,3},{3,2},{4,5},{5,4},{6,7},{7,6}} | collective-permute-start | bytes 1228808 | tf_op jit(solution)/shard_map/ppermute | solution.py:55
  193.6 34.0 %collective-permute-start.37 = (bf16[640,640]{1,0:T(8,128)(2,1)}, bf16[640,640]{1,0:T(8,128)(2,1)}, u32[]{:S(2)}, u32[]{:S(2)}) collective-permute-start(bf16[640,640]{1,0:T(8,128)(2,1)} %collective-permute-done.35.refs_1_), channel_id=1, source_target_pairs={{0,2},{1,5},{2,0},{3,7},{4,6},{5,1},{6,4},{7,3}} | collective-permute-start | bytes 2457608 | tf_op jit(solution)/shard_map/ppermute | solution.py:55
  194.6 33.1 %collective-permute-start.32 = (bf16[672,640]{1,0:T(8,128)(2,1)}, bf16[672,640]{1,0:T(8,128)(2,1)S(1)}, u32[]{:S(2)}, u32[]{:S(2)}) collective-permute-start(bf16[672,640]{1,0:T(8,128)(2,1)} %collective-permute-done.28.refs_1_), channel_id=1, source_target_pairs={{0,1},{1,0},{2,3},{3,2},{4,5},{5,4},{6,7},{7,6}} | collective-permute-start | bytes 2580488 | tf_op jit(solution)/shard_map/ppermute | solution.py:55
  194.7 33.4 %collective-permute-start.33 = (bf16[672,640]{1,0:T(8,128)(2,1)}, bf16[672,640]{1,0:T(8,128)(2,1)S(1)}, u32[]{:S(2)}, u32[]{:S(2)}) collective-permute-start(bf16[672,640]{1,0:T(8,128)(2,1)} %collective-permute-done.29.refs_2_), channel_id=1, source_target_pairs={{0,1},{1,0},{2,3},{3,2},{4,5},{5,4},{6,7},{7,6}} | collective-permute-start | bytes 2580488 | tf_op jit(solution)/shard_map/ppermute | solution.py:55
  195.1 54.0 %collective-permute-start.34 = (bf16[672,640]{1,0:T(8,128)(2,1)}, bf16[672,640]{1,0:T(8,128)(2,1)S(1)}, u32[]{:S(2)}, u32[]{:S(2)}) collective-permute-start(bf16[672,640]{1,0:T(8,128)(2,1)} %collective-permute-done.30.refs_3_), channel_id=1, source_target_pairs={{0,1},{1,0},{2,3},{3,2},{4,5},{5,4},{6,7},{7,6}} | collective-permute-start | bytes 2580488 | tf_op jit(solution)/shard_map/ppermute | solution.py:55
  227.2 42.6 %collective-permute-start.38 = (bf16[640,640]{1,0:T(8,128)(2,1)S(1)}, bf16[640,640]{1,0:T(8,128)(2,1)}, u32[]{:S(2)}, u32[]{:S(2)}) collective-permute-start(bf16[640,640]{1,0:T(8,128)(2,1)S(1)} %copy-done.21), channel_id=1, source_target_pairs={{0,1},{1,0},{2,3},{3,2},{4,5},{5,4},{6,7},{7,6}} | collective-permute-start | bytes 2457608 | tf_op jit(solution)/shard_map/ppermute | solution.py:55
  227.6 42.8 %collective-permute-start.39 = (bf16[640,640]{1,0:T(8,128)(2,1)}, bf16[640,640]{1,0:T(8,128)(2,1)}, u32[]{:S(2)}, u32[]{:S(2)}) collective-permute-start(bf16[640,640]{1,0:T(8,128)(2,1)} %collective-permute-done.35.refs_1_), channel_id=1, source_target_pairs={{0,1},{1,0},{2,3},{3,2},{4,5},{5,4},{6,7},{7,6}} | collective-permute-start | bytes 2457608 | tf_op jit(solution)/shard_map/ppermute | solution.py:55
  227.7 42.7 %collective-permute-start.40 = (bf16[640,640]{1,0:T(8,128)(2,1)}, bf16[640,640]{1,0:T(8,128)(2,1)}, u32[]{:S(2)}, u32[]{:S(2)}) collective-permute-start(bf16[640,640]{1,0:T(8,128)(2,1)} %collective-permute-done.36.refs_2_), channel_id=1, source_target_pairs={{0,1},{1,0},{2,3},{3,2},{4,5},{5,4},{6,7},{7,6}} | collective-permute-start | bytes 2457608 | tf_op jit(solution)/shard_map/ppermute | solution.py:55
  228.1 42.8 %collective-permute-start.41 = (bf16[640,640]{1,0:T(8,128)(2,1)}, bf16[640,640]{1,0:T(8,128)(2,1)}, u32[]{:S(2)}, u32[]{:S(2)}) collective-permute-start(bf16[640,640]{1,0:T(8,128)(2,1)} %collective-permute-done.37.refs_3_), channel_id=1, source_target_pairs={{0,1},{1,0},{2,3},{3,2},{4,5},{5,4},{6,7},{7,6}} | collective-permute-start | bytes 2457608 | tf_op jit(solution)/shard_map/ppermute | solution.py:55
  249.1 20.8 %collective-permute-start.44 = (bf16[320,640]{1,0:T(8,128)(2,1)S(1)}, bf16[320,640]{1,0:T(8,128)(2,1)S(1)}, u32[]{:S(2)}, u32[]{:S(2)}) collective-permute-start(bf16[320,640]{1,0:T(8,128)(2,1)S(1)} %copy-done.45), channel_id=1, source_target_pairs={{0,2},{1,5},{2,0},{3,7},{4,6},{5,1},{6,4},{7,3}} | collective-permute-start | bytes 1228808 | tf_op jit(solution)/shard_map/ppermute | solution.py:55
  269.8 29.8 %collective-permute-start.45 = (bf16[320,640]{1,0:T(8,128)(2,1)S(1)}, bf16[320,640]{1,0:T(8,128)(2,1)S(1)}, u32[]{:S(2)}, u32[]{:S(2)}) collective-permute-start(bf16[320,640]{1,0:T(8,128)(2,1)S(1)} %copy-done.25), channel_id=1, source_target_pairs={{0,1},{1,0},{2,3},{3,2},{4,5},{5,4},{6,7},{7,6}} | collective-permute-start | bytes 1228808 | tf_op jit(solution)/shard_map/ppermute | solution.py:55
  269.9 29.7 %collective-permute-start.46 = (bf16[320,640]{1,0:T(8,128)(2,1)S(1)}, bf16[320,640]{1,0:T(8,128)(2,1)S(1)}, u32[]{:S(2)}, u32[]{:S(2)}) collective-permute-start(bf16[320,640]{1,0:T(8,128)(2,1)S(1)} %copy-done.45), channel_id=1, source_target_pairs={{0,1},{1,0},{2,3},{3,2},{4,5},{5,4},{6,7},{7,6}} | collective-permute-start | bytes 1228808 | tf_op jit(solution)/shard_map/ppermute | solution.py:55
  270.4 29.3 %collective-permute-start.47 = (bf16[320,640]{1,0:T(8,128)(2,1)}, bf16[320,640]{1,0:T(8,128)(2,1)S(1)}, u32[]{:S(2)}, u32[]{:S(2)}) collective-permute-start(bf16[320,640]{1,0:T(8,128)(2,1)} %collective-permute-done.43.refs_2_.refs_10_), channel_id=1, source_target_pairs={{0,1},{1,0},{2,3},{3,2},{4,5},{5,4},{6,7},{7,6}} | collective-permute-start | bytes 1228808 | tf_op jit(solution)/shard_map/ppermute | solution.py:55
  270.4 29.3 %collective-permute-start.48 = (bf16[320,640]{1,0:T(8,128)(2,1)S(1)}, bf16[320,640]{1,0:T(8,128)(2,1)S(1)}, u32[]{:S(2)}, u32[]{:S(2)}) collective-permute-start(bf16[320,640]{1,0:T(8,128)(2,1)S(1)} %collective-permute-done.44.refs_3_.refs_11_), channel_id=1, source_target_pairs={{0,1},{1,0},{2,3},{3,2},{4,5},{5,4},{6,7},{7,6}} | collective-permute-start | bytes 1228808 | tf_op jit(solution)/shard_map/ppermute | solution.py:55
  577.5 80.2 %collective-permute-start.72 = (f32[4,2,1360]{2,1,0:T(2,128)S(1)}, f32[4,2,1360]{2,1,0:T(2,128)S(1)}, u32[]{:S(2)}, u32[]{:S(2)}) collective-permute-start(f32[4,2,1360]{2,1,0:T(2,128)S(1)} %fusion.18), channel_id=1, source_target_pairs={{0,1},{1,0},{2,3},{3,2},{4,5},{5,4},{6,7},{7,6}} | collective-permute-start | bytes 130568 | tf_op jit(solution)/shard_map/ppermute | solution.py:55
  578.2 126.0 %collective-permute-start.68 = (f32[640,640]{1,0:T(8,128)}, f32[640,640]{1,0:T(8,128)}, u32[]{:S(2)}, u32[]{:S(2)}) collective-permute-start(f32[640,640]{1,0:T(8,128)} %get-tuple-element.155), channel_id=1, source_target_pairs={{0,2},{1,5},{2,0},{3,7},{4,6},{5,1},{6,4},{7,3}} | collective-permute-start | bytes 4915208 | tf_op jit(solution)/shard_map/ppermute | solution.py:55
  596.3 110.4 %collective-permute-start.70 = (f32[640,640]{1,0:T(8,128)}, f32[640,640]{1,0:T(8,128)}, u32[]{:S(2)}, u32[]{:S(2)}) collective-permute-start(f32[640,640]{1,0:T(8,128)} %get-tuple-element.157), channel_id=1, source_target_pairs={{0,2},{1,5},{2,0},{3,7},{4,6},{5,1},{6,4},{7,3}} | collective-permute-start | bytes 4915208 | tf_op jit(solution)/shard_map/ppermute | solution.py:55
  609.3 61.8 %collective-permute-start.53 = (f32[320,640]{1,0:T(8,128)}, f32[320,640]{1,0:T(8,128)S(1)}, u32[]{:S(2)}, u32[]{:S(2)}) collective-permute-start(f32[320,640]{1,0:T(8,128)} %get-tuple-element.137), channel_id=1, source_target_pairs={{0,2},{1,5},{2,0},{3,7},{4,6},{5,1},{6,4},{7,3}} | collective-permute-start | bytes 2457608 | tf_op jit(solution)/shard_map/ppermute | solution.py:55
  622.3 49.8 %collective-permute-start.55 = (f32[320,640]{1,0:T(8,128)}, f32[320,640]{1,0:T(8,128)S(1)}, u32[]{:S(2)}, u32[]{:S(2)}) collective-permute-start(f32[320,640]{1,0:T(8,128)} %get-tuple-element.143), channel_id=1, source_target_pairs={{0,2},{1,5},{2,0},{3,7},{4,6},{5,1},{6,4},{7,3}} | collective-permute-start | bytes 2457608 | tf_op jit(solution)/shard_map/ppermute | solution.py:55
  657.9 13.1 %collective-permute-start.73 = (f32[2,2,1360]{2,1,0:T(2,128)S(1)}, f32[2,2,1360]{2,1,0:T(2,128)S(1)}, u32[]{:S(2)}, u32[]{:S(2)}) collective-permute-start(f32[2,2,1360]{2,1,0:T(2,128)S(1)} %pad_maximum_fusion.1), channel_id=1, source_target_pairs={{0,2},{1,5},{2,0},{3,7},{4,6},{5,1},{6,4},{7,3}} | collective-permute-start | bytes 65288 | tf_op jit(solution)/shard_map/ppermute | solution.py:55
  671.0 14.7 %collective-permute-start.58 = (bf16[480,1280]{1,0:T(8,128)(2,1)}, bf16[480,1280]{1,0:T(8,128)(2,1)S(1)}, u32[]{:S(2)}, u32[]{:S(2)}) collective-permute-start(bf16[480,1280]{1,0:T(8,128)(2,1)} %get-tuple-element.144.mine_ref), channel_id=1, source_target_pairs={{0,1},{1,0},{2,3},{3,2},{4,5},{5,4},{6,7},{7,6}} | collective-permute-start | bytes 3686408 | tf_op jit(solution)/shard_map/ppermute | solution.py:55
  680.1 15.8 %collective-permute-start.61 = (bf16[480,1280]{1,0:T(8,128)(2,1)}, bf16[480,1280]{1,0:T(8,128)(2,1)}, u32[]{:S(2)}, u32[]{:S(2)}) collective-permute-start(bf16[480,1280]{1,0:T(8,128)(2,1)} %get-tuple-element.147.mine_ref), channel_id=1, source_target_pairs={{0,1},{1,0},{2,3},{3,2},{4,5},{5,4},{6,7},{7,6}} | collective-permute-start | bytes 3686408 | tf_op jit(solution)/shard_map/ppermute | solution.py:55
  684.5 24.6 %collective-permute-start.49 = (f32[640,640]{1,0:T(8,128)}, f32[640,640]{1,0:T(8,128)}, u32[]{:S(2)}, u32[]{:S(2)}) collective-permute-start(f32[640,640]{1,0:T(8,128)} %get-tuple-element.125), channel_id=1, source_target_pairs={{0,2},{1,5},{2,0},{3,7},{4,6},{5,1},{6,4},{7,3}} | collective-permute-start | bytes 4915208 | tf_op jit(solution)/shard_map/ppermute | solution.py:55
  685.7 53.6 %collective-permute-start.51 = (f32[640,640]{1,0:T(8,128)}, f32[640,640]{1,0:T(8,128)}, u32[]{:S(2)}, u32[]{:S(2)}) collective-permute-start(f32[640,640]{1,0:T(8,128)} %get-tuple-element.131), channel_id=1, source_target_pairs={{0,2},{1,5},{2,0},{3,7},{4,6},{5,1},{6,4},{7,3}} | collective-permute-start | bytes 4915208 | tf_op jit(solution)/shard_map/ppermute | solution.py:55
  695.9 97.7 %collective-permute-start.64 = (f32[1280,640]{1,0:T(8,128)}, f32[1280,640]{1,0:T(8,128)S(1)}, u32[]{:S(2)}, u32[]{:S(2)}) collective-permute-start(f32[1280,640]{1,0:T(8,128)} %get-tuple-element.151), channel_id=1, source_target_pairs={{0,2},{1,5},{2,0},{3,7},{4,6},{5,1},{6,4},{7,3}} | collective-permute-start | bytes 9830408 | tf_op jit(solution)/shard_map/ppermute | solution.py:55
  704.2 142.0 %collective-permute-start.66 = (f32[1280,640]{1,0:T(8,128)}, f32[1280,640]{1,0:T(8,128)S(1)}, u32[]{:S(2)}, u32[]{:S(2)}) collective-permute-start(f32[1280,640]{1,0:T(8,128)} %get-tuple-element.153), channel_id=1, source_target_pairs={{0,2},{1,5},{2,0},{3,7},{4,6},{5,1},{6,4},{7,3}} | collective-permute-start | bytes 9830408 | tf_op jit(solution)/shard_map/ppermute | solution.py:55
  706.7 34.9 %collective-permute-start.69 = (f32[320,640]{1,0:T(8,128)S(1)}, f32[320,640]{1,0:T(8,128)S(1)}, u32[]{:S(2)}, u32[]{:S(2)}) collective-permute-start(f32[320,640]{1,0:T(8,128)S(1)} %slice_add_fusion.10), channel_id=1, source_target_pairs={{0,4},{1,3},{2,6},{3,1},{4,0},{5,7},{6,2},{7,5}} | collective-permute-start | bytes 2457608 | tf_op jit(solution)/shard_map/ppermute | solution.py:55
  709.0 36.3 %collective-permute-start.71 = (f32[320,640]{1,0:T(8,128)S(1)}, f32[320,640]{1,0:T(8,128)S(1)}, u32[]{:S(2)}, u32[]{:S(2)}) collective-permute-start(f32[320,640]{1,0:T(8,128)S(1)} %slice_add_fusion.8), channel_id=1, source_target_pairs={{0,4},{1,3},{2,6},{3,1},{4,0},{5,7},{6,2},{7,5}} | collective-permute-start | bytes 2457608 | tf_op jit(solution)/shard_map/ppermute | solution.py:55
  739.3 23.7 %collective-permute-start.50 = (f32[320,640]{1,0:T(8,128)S(1)}, f32[320,640]{1,0:T(8,128)S(1)}, u32[]{:S(2)}, u32[]{:S(2)}) collective-permute-start(f32[320,640]{1,0:T(8,128)S(1)} %slice_add_fusion.14), channel_id=1, source_target_pairs={{0,4},{1,3},{2,6},{3,1},{4,0},{5,7},{6,2},{7,5}} | collective-permute-start | bytes 2457608 | tf_op jit(solution)/shard_map/ppermute | solution.py:55
  741.6 150.3 %collective-permute-start.59 = (f32[1024,640]{1,0:T(8,128)}, f32[1024,640]{1,0:T(8,128)S(1)}, u32[]{:S(2)}, u32[]{:S(2)}) collective-permute-start(f32[1024,640]{1,0:T(8,128)} %get-tuple-element.146), channel_id=1, source_target_pairs={{0,2},{1,5},{2,0},{3,7},{4,6},{5,1},{6,4},{7,3}} | collective-permute-start | bytes 7864328 | tf_op jit(solution)/shard_map/ppermute | solution.py:55
  745.4 35.1 %collective-permute-start.52 = (f32[320,640]{1,0:T(8,128)S(1)}, f32[320,640]{1,0:T(8,128)S(1)}, u32[]{:S(2)}, u32[]{:S(2)}) collective-permute-start(f32[320,640]{1,0:T(8,128)S(1)} %slice_add_fusion.12), channel_id=1, source_target_pairs={{0,4},{1,3},{2,6},{3,1},{4,0},{5,7},{6,2},{7,5}} | collective-permute-start | bytes 2457608 | tf_op jit(solution)/shard_map/ppermute | solution.py:55
  762.9 171.1 %collective-permute-start.62 = (f32[1024,640]{1,0:T(8,128)S(1)}, f32[1024,640]{1,0:T(8,128)S(1)}, u32[]{:S(2)}, u32[]{:S(2)}) collective-permute-start(f32[1024,640]{1,0:T(8,128)S(1)} %copy-done.42), channel_id=1, source_target_pairs={{0,2},{1,5},{2,0},{3,7},{4,6},{5,1},{6,4},{7,3}} | collective-permute-start | bytes 7864328 | tf_op jit(solution)/shard_map/ppermute | solution.py:55
  793.8 141.5 %collective-permute-start.65 = (f32[640,640]{1,0:T(8,128)S(1)}, f32[640,640]{1,0:T(8,128)S(1)}, u32[]{:S(2)}, u32[]{:S(2)}) collective-permute-start(f32[640,640]{1,0:T(8,128)S(1)} %slice_add_fusion.2), channel_id=1, source_target_pairs={{0,4},{1,3},{2,6},{3,1},{4,0},{5,7},{6,2},{7,5}} | collective-permute-start | bytes 4915208 | tf_op jit(solution)/shard_map/ppermute | solution.py:55
  846.4 89.3 %collective-permute-start.67 = (f32[640,640]{1,0:T(8,128)S(1)}, f32[640,640]{1,0:T(8,128)S(1)}, u32[]{:S(2)}, u32[]{:S(2)}) collective-permute-start(f32[640,640]{1,0:T(8,128)S(1)} %slice_add_fusion), channel_id=1, source_target_pairs={{0,4},{1,3},{2,6},{3,1},{4,0},{5,7},{6,2},{7,5}} | collective-permute-start | bytes 4915208 | tf_op jit(solution)/shard_map/ppermute | solution.py:55
  892.3 48.4 %collective-permute-start.60 = (f32[512,640]{1,0:T(8,128)S(1)}, f32[512,640]{1,0:T(8,128)S(1)}, u32[]{:S(2)}, u32[]{:S(2)}) collective-permute-start(f32[512,640]{1,0:T(8,128)S(1)} %slice_add_fusion.6), channel_id=1, source_target_pairs={{0,4},{1,3},{2,6},{3,1},{4,0},{5,7},{6,2},{7,5}} | collective-permute-start | bytes 3932168 | tf_op jit(solution)/shard_map/ppermute | solution.py:55
  934.2 17.6 %collective-permute-start.63 = (f32[512,640]{1,0:T(8,128)S(1)}, f32[512,640]{1,0:T(8,128)S(1)}, u32[]{:S(2)}, u32[]{:S(2)}) collective-permute-start(f32[512,640]{1,0:T(8,128)S(1)} %slice_add_fusion.4), channel_id=1, source_target_pairs={{0,4},{1,3},{2,6},{3,1},{4,0},{5,7},{6,2},{7,5}} | collective-permute-start | bytes 3932168 | tf_op jit(solution)/shard_map/ppermute | solution.py:55
  (64 other events, 955.6 us)

commit v3 on v2

--- a/solution.py
+++ b/solution.py
@@ -20,6 +20,7 @@
 
 F32 = jnp.float32
 BF16 = jnp.bfloat16
+ANY = pl.BlockSpec(memory_space=pl.ANY)
 
 
 def gather_perms(n_dev):
@@ -49,6 +50,30 @@
         out_shape=jax.ShapeDtypeStruct((rows, width), BF16),
         cost_estimate=pl.CostEstimate(flops=rows * width, bytes_accessed=rows * width * 4, transcendentals=0),
         name='pack')(*views, *extra)
+
+
+def vec_kernel(*refs):
+    pieces, (out, buf, sem) = refs[:8], refs[8:]
+    rows = out.shape[0]
+    copies = [pltpu.make_async_copy(piece.at[pl.ds(piece.shape[0] - rows, rows), :], buf.at[index], sem.at[index])
+              for index, piece in enumerate(pieces)]
+    for copy in copies:
+        copy.start()
+    total = None
+    for index, copy in enumerate(copies):
+        copy.wait()
+        total = buf[index].astype(F32) if total is None else total + buf[index].astype(F32)
+    out[...] = total
+
+
+def vec_sum(pieces, rows):
+    width = pieces[0].shape[1]
+    return pl.pallas_call(
+        vec_kernel, in_specs=[ANY] * 8, out_specs=pl.BlockSpec(memory_space=pltpu.VMEM),
+        out_shape=jax.ShapeDtypeStruct((rows, width), F32),
+        scratch_shapes=[pltpu.VMEM((8, rows, width), BF16), pltpu.SemaphoreType.DMA((8,))],
+        cost_estimate=pl.CostEstimate(flops=rows * width * 8, bytes_accessed=rows * width * 20, transcendentals=0),
+        name='vec_sum')(*pieces)
 
 
 def permute(array, perm):
@@ -413,9 +438,6 @@
     add_rows(vec_ref, step, [g_gain, g_shift, jnp.sum(grad, axis=0, keepdims=True)])
 
 
-ANY = pl.BlockSpec(memory_space=pl.ANY)
-
-
 def by_step(rows, columns):
     return pl.BlockSpec((rows, columns), lambda i: (i, 0))
 
@@ -524,26 +546,10 @@
         count * width * width * 8 + count * tokens * width * 10, 3e7)(grad, qkv, h, rows, *pieces)
 
 
-def scatter_sum(full, n_dev):
-    near, far, core_perm = gather_perms(n_dev)
-    me = lax.axis_index(AXIS)
-    core, chip = me % 2, me // 2
-    one, two = 1 + core, 2 - core
-    by_chip = full.reshape((n_dev // 2, 2) + full.shape[1:])
-    pick = lambda array, index: lax.dynamic_index_in_dim(array, index, 0, keepdims=False)
-    ours = lambda index: lax.dynamic_slice(by_chip, (index, core) + (0,) * (full.ndim - 1),
-                                           (1, 1) + full.shape[1:]).reshape(full.shape[1:])
-    got = permute(lax.dynamic_index_in_dim(by_chip, 1 - core, 1, keepdims=False), core_perm)
-    part = lambda index: ours(index) + pick(got, index)
-    x = jnp.bitwise_xor
-    second = permute(jnp.stack([part(x(chip, one)), part(x(x(chip, one), two))]), far)
-    third = permute(part(x(chip, two)) + second[1], near)
-    return part(chip) + second[0] + third
-
-
-def grad_kernel(tiles, group_rows, inputs, *refs):
-    ins, (far_ref, keep_ref, x_buf, turned, y_buf, tile, own, recv, x_sem, y_sem, send_sem, recv_sem) = refs[:inputs], refs[inputs:]
-    width = tile.shape[1]
+def grad_kernel(tiles, group_rows, inputs, with_context, *refs):
+    ins, refs = refs[:inputs], refs[inputs:]
+    far_ref, keep_ref, x_buf, turned, y_buf, tile, own, recv, x_sem, y_sem, send_sem, recv_sem = refs[:12]
+    width, summed = tile.shape[1], own.shape[1]
     me = lax.axis_index(AXIS)
     core, chip = lax.rem(me, 2), me // 2
     mate = me + 1 - 2 * core
@@ -571,6 +577,18 @@
     barrier = pltpu.get_barrier_semaphore()
     pl.semaphore_signal(barrier, inc=1, device_id=(mate,), device_id_type=pl.DeviceIdType.MESH)
     pl.semaphore_wait(barrier, 1)
+
+    if with_context:
+        kv_ref, ctx_refs = ins[-3], ins[-2:]
+        kv_mine, kv_other, ctx_mine, ctx_other, kv_sem, kv_send, kv_recv = refs[12:]
+        exchange = pltpu.make_async_remote_copy(
+            src_ref=kv_ref, dst_ref=kv_other, send_sem=kv_send, recv_sem=kv_recv, device_id=(mate,),
+            device_id_type=pl.DeviceIdType.MESH)
+        exchange.start()
+        kv_loads = [pltpu.make_async_copy(src, dst, kv_sem.at[index])
+                    for index, (src, dst) in enumerate(((kv_ref, kv_mine), (ctx_refs[0], ctx_mine), (ctx_refs[1], ctx_other)))]
+        for copy in kv_loads:
+            copy.start()
 
     def sends(q):
         *_, first_row, rows, chips = tiles[q]
@@ -611,6 +629,19 @@
     last = len(tiles) - 1
     for copy in sends(last):
         copy.start()
+    if with_context:
+        for copy in kv_loads:
+            copy.wait()
+        depth = ctx_mine.shape[0] // 4
+        at = lambda slot, block: slice((slot % 2) * group_rows + summed + block * depth, (slot % 2) * group_rows + summed + (block + 1) * depth)
+        for pair, (ctx, kv) in enumerate(((ctx_mine, kv_mine), (ctx_other, kv_other))):
+            if pair == 1:
+                exchange.wait()
+            for slot in range(4):
+                ref = keep_ref if slot < 2 else far_ref
+                for block in range(2):
+                    part = dot_nn(ctx[slot * depth:(slot + 1) * depth, :], kv[:, block * width:(block + 1) * width])
+                    ref[at(slot, block), :] = part if pair == 0 else ref[at(slot, block), :] + part
     for q in range(max(0, last - 2), last + 1):
         for copy in sends(q):
             copy.wait_send()
@@ -619,22 +650,85 @@
             copy.wait_recv()
     for slot in range(4):
         ref = keep_ref if slot < 2 else far_ref
-        ref[(slot % 2) * group_rows:(slot % 2 + 1) * group_rows, :] = own[slot] + recv[slot]
-
-
-def weight_grads(kind, arrays, tiles, group_rows):
+        ref[(slot % 2) * group_rows:(slot % 2) * group_rows + summed, :] = own[slot] + recv[slot]
+
+
+def weight_grads(kind, arrays, tiles, summed, context=None):
     count, width = arrays[0].shape[0], 640
     chips = max(len(t[-1]) for t in tiles)
+    extra, more, group_rows = [], [], summed
+    dma = pltpu.SemaphoreType.DMA
+    if context is not None:
+        more = list(context)
+        group_rows += context[1].shape[0] // 2
+        extra = [pltpu.VMEM(context[0].shape, BF16)] * 2 + [pltpu.VMEM(context[1].shape, BF16)] * 2 + [dma((3,)), dma, dma]
     out = jax.ShapeDtypeStruct((2 * group_rows, width), F32)
     return pl.pallas_call(
-        functools.partial(grad_kernel, tiles, group_rows, len(arrays)), in_specs=[ANY] * len(arrays),
+        functools.partial(grad_kernel, tiles, group_rows, len(arrays) + len(more), context is not None),
+        in_specs=[ANY] * (len(arrays) + len(more)),
         out_specs=[pl.BlockSpec(memory_space=pltpu.VMEM)] * 2, out_shape=[out, out],
         scratch_shapes=[pltpu.VMEM((2, count, width), BF16), pltpu.VMEM((width, count), BF16), pltpu.VMEM((2, count, width), BF16),
-                        pltpu.VMEM((3, width, width), F32), pltpu.VMEM((4, group_rows, width), F32),
-                        pltpu.VMEM((4, group_rows, width), F32), pltpu.SemaphoreType.DMA((2,)), pltpu.SemaphoreType.DMA((2,)),
-                        pltpu.SemaphoreType.DMA((3, chips)), pltpu.SemaphoreType.DMA((len(tiles), chips))],
-        cost_estimate=pl.CostEstimate(flops=2 * count * width * width * len(tiles), bytes_accessed=int(2e7), transcendentals=0),
-        compiler_params=pltpu.CompilerParams(collective_id=kind, has_side_effects=True, vmem_limit_bytes=VMEM_LIMIT))(*arrays)
+                        pltpu.VMEM((3, width, width), F32), pltpu.VMEM((4, summed, width), F32),
+                        pltpu.VMEM((4, summed, width), F32), dma((2,)), dma((2,)), dma((3, chips)), dma((len(tiles), chips))]
+        + extra,
+        cost_estimate=pl.CostEstimate(flops=2 * count * width * width * (len(tiles) + 2 * (context is not None)),
+                                      bytes_accessed=int(2e7), transcendentals=0),
+        compiler_params=pltpu.CompilerParams(collective_id=kind, has_side_effects=True, vmem_limit_bytes=VMEM_LIMIT))(*arrays, *more)
+
+
+def context_kernel(context_ref, ctx_ref, mine_ref, other_ref):
+    batch, valid, _ = context_ref.shape
+    padded = ctx_ref.shape[0] // batch
+    me = lax.axis_index(AXIS)
+    core, chip = lax.rem(me, 2), me // 2
+    ctx_ref[...] = jnp.zeros_like(ctx_ref)
+    for sample in range(batch):
+        ctx_ref[sample * padded:sample * padded + valid, :] = context_ref[sample]
+    each = mine_ref.shape[0] // 4
+    x = jnp.bitwise_xor
+    for of_core, ref in ((core, mine_ref), (1 - core, other_ref)):
+        for slot, other in enumerate((chip, x(chip, 2 - of_core), x(chip, 1 + of_core), x(chip, 3))):
+            column = pl.multiple_of((2 * other + of_core) * each, each)
+            ref[slot * each:(slot + 1) * each, :] = ctx_ref[:, pl.ds(column, each)].T
+
+
+def prepare_context(context, n_dev):
+    batch, valid, ctx_width = context.shape
+    rows = batch * ((valid + 15) // 16 * 16)
+    vmem = pl.BlockSpec(memory_space=pltpu.VMEM)
+    turned = shape(ctx_width // 2, rows, BF16)
+    ctx, mine, other = pl.pallas_call(
+        context_kernel, in_specs=[vmem], out_specs=[vmem] * 3, out_shape=[shape(rows, ctx_width, BF16), turned, turned],
+        cost_estimate=pl.CostEstimate(flops=rows * ctx_width * 8, bytes_accessed=int(8e6), transcendentals=0),
+        name='context')(context)
+    return ctx, mine, permute(other, gather_perms(n_dev)[2])
+
+
+def vec_pack_kernel(*refs):
+    ins, out = refs[:-1], refs[-1]
+    width = out.shape[1]
+    out[...] = jnp.zeros_like(out)
+    for layer in range(len(ins) // 4):
+        first, second, third, bias = ins[4 * layer:4 * layer + 4]
+        rows = [(first, 0), (first, 1), (second, 0), (second, 1), (third, 0), (third, 1), (first, 2), (second, 2), (third, 2)]
+        for index, (ref, row) in enumerate(rows):
+            out[17 * layer + index:17 * layer + index + 1, :] = ref[row:row + 1, :]
+        for index in range(8):
+            row = 17 * layer + 9 + index
+            out[row:row + 1, :] = bias[0:1, index * width:(index + 1) * width]
+
+
+def vec_total(parts, rows, n_dev):
+    vmem = pl.BlockSpec(memory_space=pltpu.VMEM)
+    width = parts[0].shape[1]
+    total = pl.pallas_call(
+        vec_pack_kernel, in_specs=[vmem] * len(parts), out_specs=vmem, out_shape=shape(rows, width, F32),
+        cost_estimate=pl.CostEstimate(flops=rows * width, bytes_accessed=rows * width * 8, transcendentals=0),
+        name='vec_pack')(*parts)
+    near, far, core = gather_perms(n_dev)
+    for perm in (core, far, near):
+        total = total + permute(total, perm)
+    return total
 
 
 def ff_grad_kernel(offset, with_down, grad_ref, save_a, save_g, norm_ref, h_ref, rows_ref, *refs):
@@ -672,8 +766,8 @@
     start_load(pieces[8:], offset, w_ff2, w2_sem)
 
     def parts(index):
-        chunk, step = divmod(index, steps)
-        at = (pl.ds(step * each, each), pl.ds(chunk * width, width))
+        chunk, step = index // steps, index % steps
+        at = (pl.ds(pl.multiple_of(step * each, each), each), pl.ds(pl.multiple_of(chunk * width, width), width))
         return [pltpu.make_async_copy(ref.at[at], buf.at[index % 2], part_sem.at[which, index % 2])
                 for which, (ref, buf) in enumerate(((save_a, part_a), (save_g, part_g)))]
 
@@ -696,67 +790,61 @@
     pl.semaphore_wait(barrier, 1)
 
     def load_z(chunk):
-        return pltpu.make_async_copy(gated_ref.at[:, pl.ds(chunk * width, width)], z_buf, z_sem)
+        return pltpu.make_async_copy(gated_ref.at[:, pl.ds(pl.multiple_of(chunk * width, width), width)], z_buf, z_sem)
 
     if with_down:
         load_z(0).start()
 
-    tiles = []
-    for chunk in range(chunks):
-        tiles += [(1, chunk), (1, chunks + chunk)] + ([(2, chunk)] if with_down else [])
-    ring = tile.shape[0]
-
-    def sends(q):
-        which, block = tiles[q]
+    kinds = (0, 1, 2) if with_down else (0, 1)
+
+    def sends(kind, chunk):
         copies = []
-        for index, other in enumerate(range(4) if which == 1 else (block,)):
-            rows = depth if which == 1 else deep
+        for index in range(4 if kind < 2 else 1):
+            rows = depth if kind < 2 else deep
             start = pl.multiple_of((2 * index + 1 - core) * rows, 16)
-            slot = slot_of(other, True)
-            dst = (recv1.at[block, pl.ds(pl.multiple_of(slot * rows, 16), rows), :] if which == 1 else recv2.at[block])
+            if kind < 2:
+                block = kind * chunks + chunk
+                slot = slot_of(index, True)
+                dst = recv1.at[block, pl.ds(pl.multiple_of(slot * rows, 16), rows), :]
+            else:
+                dst = recv2.at[chunk]
             copies.append(pltpu.make_async_remote_copy(
-                src_ref=tile.at[q % ring, pl.ds(start, rows), :], dst_ref=dst, send_sem=send_sem.at[q % ring, index],
-                recv_sem=recv_sem1.at[block, index] if which == 1 else recv_sem2.at[block],
+                src_ref=tile.at[kind, pl.ds(start, rows), :], dst_ref=dst, send_sem=send_sem.at[kind, index],
+                recv_sem=recv_sem1.at[block, index] if kind < 2 else recv_sem2.at[chunk],
                 device_id=(mate,), device_id_type=pl.DeviceIdType.MESH))
         return copies
 
-    def writes(q, branch=None):
-        which, block = tiles[q]
-        if which == 1:
-            return [pltpu.make_async_copy(
-                obuf.at[q % 2, pl.ds(slot * depth, depth), :],
-                (keep1 if slot < 2 else far1).at[pl.ds((slot % 2) * 8 * depth + block * depth, depth), :],
-                out_sem.at[q % 2]) for slot in range(4)]
-        slot = slot_of(block, False)
-        ref = keep2 if branch == 0 else far2
-        return [pltpu.make_async_copy(obuf.at[q % 2], ref.at[pl.ds(pl.multiple_of(lax.rem(slot, 2) * deep, 16), deep), :],
-                                      out_sem.at[q % 2])]
-
-    def wait_writes(q):
-        pltpu.make_async_copy(obuf.at[q % 2], obuf.at[q % 2], out_sem.at[q % 2]).wait()
-
-    def finish(q):
-        which, block = tiles[q]
-        for copy in sends(q):
+    def wait_write(kind):
+        pltpu.make_async_copy(obuf.at[kind], obuf.at[kind], out_sem.at[kind]).wait()
+
+    def finish(kind, chunk, first):
+        for copy in sends(kind, chunk):
             copy.wait_recv()
-        if q >= 2:
-            wait_writes(q - 2)
-        if which == 1:
+
+        @pl.when(jnp.logical_not(first))
+        def _():
+            wait_write(kind)
+
+        if kind < 2:
+            block = kind * chunks + chunk
             for slot in range(4):
                 start = pl.multiple_of((2 * chip_in(slot) + core) * depth, 16)
                 rows = slice(slot * depth, (slot + 1) * depth)
-                obuf[q % 2, rows, :] = tile[q % ring, pl.ds(start, depth), :] + recv1[block, rows, :]
-            for copy in writes(q):
-                copy.start()
+                obuf[kind, rows, :] = tile[kind, pl.ds(start, depth), :] + recv1[block, rows, :]
+            for slot in range(4):
+                ref = keep1 if slot < 2 else far1
+                row = pl.multiple_of((slot % 2) * 8 * depth + block * depth, 16)
+                pltpu.make_async_copy(obuf.at[kind, pl.ds(slot * depth, depth), :], ref.at[pl.ds(row, depth), :],
+                                      out_sem.at[kind]).start()
         else:
-            obuf[q % 2] = tile[q % ring, pl.ds(pl.multiple_of(core * deep, 16), deep), :] + recv2[block]
-            slot = slot_of(block, False)
-            for branch in range(2):
+            obuf[kind] = tile[kind, pl.ds(pl.multiple_of(core * deep, 16), deep), :] + recv2[chunk]
+            slot = slot_of(chunk, False)
+            row = pl.multiple_of(lax.rem(slot, 2) * deep, 16)
+            for branch, ref in enumerate((keep2, far2)):
                 @pl.when(slot // 2 == branch)
                 def _():
-                    for copy in writes(q, branch):
-                        copy.start()
-        for copy in sends(q):
+                    pltpu.make_async_copy(obuf.at[kind], ref.at[pl.ds(row, deep), :], out_sem.at[kind]).start()
+        for copy in sends(kind, chunk):
             copy.wait_send()
 
     load_grad.wait()
@@ -768,52 +856,64 @@
     vec_ref[...] = jnp.zeros_like(vec_ref)
     wait_load(w_ff2, w2_sem)
 
-    q = 0
-    for chunk in range(chunks):
+    def one_chunk(chunk, carry):
         for block in (chunk, chunks + chunk):
-            ref = w_ff1.at[:, pl.ds(block * width, width)]
+            ref = w_ff1.at[:, pl.ds(0, width)]
             pltpu.make_async_copy(ref, ref, w1_sem.at[block]).wait()
-        for step in range(steps):
+        hidden = pl.multiple_of(chunk * width, width)
+
+        def one_step(step, carry):
             index = chunk * steps + step
-            rows = slice(step * each, (step + 1) * each)
-            d_gated = dot_nt(grad_bf[rows, :], w_ff2[chunk * width:(chunk + 1) * width, :]).astype(BF16).astype(F32)
+            even = lax.rem(index, 2)
+            rows = pl.ds(pl.multiple_of(step * each, each), each)
+            d_gated = dot_nt(grad_bf[rows, :], w_ff2[pl.ds(hidden, width), :])
             for copy in parts(index):
                 copy.wait()
             total = acc[rows, :]
             for base, saved, kept in ((0, part_a, d_a), (half, part_g, d_g)):
-                d_part = d_gated * saved[index % 2]
-                columns = slice(base + chunk * width, base + (chunk + 1) * width)
+                columns = pl.ds(pl.multiple_of(base + hidden, 2 * HEAD), width)
+                d_part = d_gated * saved[even]
                 bias_ref[0:1, columns] += jnp.sum(d_part, axis=0, keepdims=True)
                 d_part = d_part.astype(BF16)
                 kept[rows, :] = d_part
                 total = total + dot_nt(d_part, w_ff1[:, columns])
             acc[rows, :] = total
-            if index + 2 < chunks * steps:
+
+            @pl.when(index + 2 < chunks * steps)
+            def _():
                 for copy in parts(index + 2):
                     copy.start()
-        for kept in (d_a, d_g):
-            tile[q % ring] = dot_nn(turned[...], kept[...])
-            if q >= 1:
-                for copy in sends(q - 1):
+
+            return carry
+
+        lax.fori_loop(0, steps, one_step, 0)
+        before = jnp.maximum(chunk - 1, 0)
+        for kind in kinds:
+            @pl.when(chunk > 0)
+            def _():
+                finish(kind, before, chunk == 1)
+
+            if kind < 2:
+                tile[kind] = dot_nn(turned[...], (d_a, d_g)[kind][...])
+            else:
+                load_z(chunk).wait()
+                z_turned[...] = z_buf[...].T
+
+                @pl.when(chunk + 1 < chunks)
+                def _():
+                    load_z(chunk + 1).start()
+
+                tile[kind] = dot_nn(z_turned[...], grad_bf[...])
+            if kind > 0:
+                for copy in sends(kind - 1, chunk):
                     copy.start()
-            if q >= 3:
-                finish(q - 3)
-            q += 1
-        if with_down:
-            load_z(chunk).wait()
-            z_turned[...] = z_buf[...].T
-            if chunk + 1 < chunks:
-                load_z(chunk + 1).start()
-            tile[q % ring] = dot_nn(z_turned[...], grad_bf[...])
-            for copy in sends(q - 1):
-                copy.start()
-            if q >= 3:
-                finish(q - 3)
-            q += 1
+        for copy in sends(kinds[-1], chunk):
+            copy.start()
+        return carry
+
+    lax.fori_loop(0, chunks, one_chunk, 0)
     load_h(0).start()
     load_h(1).start()
-    for copy in sends(q - 1):
-        copy.start()
     for step in range(steps):
         rows = slice(step * each, (step + 1) * each)
         load_h(step).wait()
@@ -825,10 +925,10 @@
         pltpu.make_async_copy(acc.at[pl.ds(step * each, each), :], out_ref.at[pl.ds(step * each, each), :], in_sem.at[0]).start()
         for at, row in enumerate((g_gain, g_shift, jnp.sum(mine, axis=0, keepdims=True))):
             vec_ref[at:at + 1, :] += row
-    for late in range(max(0, q - 3), q):
-        finish(late)
-    for late in range(max(0, q - 2), q):
-        wait_writes(late)
+    for kind in kinds:
+        finish(kind, chunks - 1, False)
+    for kind in kinds:
+        wait_write(kind)
     pltpu.make_async_copy(acc, out_ref, in_sem.at[0]).wait()
 
 
@@ -842,8 +942,8 @@
     scratch = [pltpu.VMEM((count, width), grad.dtype), pltpu.VMEM((count, width), BF16), pltpu.VMEM((width, count), BF16),
                pltpu.VMEM((count, width), F32), pltpu.VMEM((2, STEP, width), F32), pltpu.VMEM((2, STEP, width), F32),
                pltpu.VMEM((count, width), BF16), pltpu.VMEM((count, width), BF16), pltpu.VMEM((width, 2 * half), BF16),
-               pltpu.VMEM((half, width), BF16), pltpu.VMEM((4, width, width), F32), pltpu.VMEM((8, width // 2, width), F32),
-               pltpu.VMEM((2, width // 2, width), F32), dma((2,)), dma((2, 2)), dma((8,)), dma, dma((2,)), dma((4, 4)), dma((8, 4))]
+               pltpu.VMEM((half, width), BF16), pltpu.VMEM((2 + down, width, width), F32), pltpu.VMEM((8, width // 2, width), F32),
+               pltpu.VMEM((2 + down, width // 2, width), F32), dma((2,)), dma((2, 2)), dma((8,)), dma, dma((3,)), dma((3, 4)), dma((8, 4))]
     if down:
         scratch += [pltpu.VMEM((count, width), BF16), pltpu.VMEM((width, count), BF16), pltpu.VMEM((4, half // 8, width), F32),
                     dma, dma((4,))]
@@ -855,45 +955,6 @@
         scratch_shapes=scratch,
         cost_estimate=pl.CostEstimate(flops=count * width * half * (14 if down else 10), bytes_accessed=int(6e7), transcendentals=0),
         compiler_params=pltpu.CompilerParams(collective_id=kind, has_side_effects=True, vmem_limit_bytes=VMEM_MOST))(grad, save_a, save_g, norm, h, rows, *([gated] if down else []), *pieces)
-
-
-def context_grad_kernel(ctx_ref, mine_ref, other_ref, far_ref, keep_ref, d_kv):
-    rows, width = mine_ref.shape[0], far_ref.shape[1]
-    d_kv[0:rows, :] = mine_ref[...]
-    d_kv[rows:2 * rows, :] = other_ref[...]
-    depth = ctx_ref.shape[0] // 4
-    for slot in range(4):
-        ref = keep_ref if slot < 2 else far_ref
-        for block in range(2):
-            start = ((slot % 2) * 2 + block) * depth
-            ref[start:start + depth, :] = dot_nn(ctx_ref[slot * depth:(slot + 1) * depth, :], d_kv[:, block * width:(block + 1) * width])
-
-
-def context_grad(turned, mine, other):
-    width = mine.shape[1] // 2
-    out = jax.ShapeDtypeStruct((turned.shape[0], width), F32)
-    vmem = pl.BlockSpec(memory_space=pltpu.VMEM)
-    return pl.pallas_call(
-        context_grad_kernel, in_specs=[vmem] * 3, out_specs=[vmem] * 2, out_shape=[out, out],
-        scratch_shapes=[pltpu.VMEM((2 * mine.shape[0], 2 * width), BF16)],
-        cost_estimate=pl.CostEstimate(flops=2 * turned.size * 2 * width, bytes_accessed=int(2e7), transcendentals=0),
-        compiler_params=pltpu.CompilerParams(vmem_limit_bytes=VMEM_LIMIT), name='context_grad')(turned, mine, other)
-
-
-def context_columns(ctx, n_dev):
-    _, _, core_perm = gather_perms(n_dev)
-    me = lax.axis_index(AXIS)
-    core, chip = me % 2, me // 2
-    each = ctx.shape[1] // n_dev
-    x = jnp.bitwise_xor
-
-    def columns(of_core):
-        one, two = 1 + of_core, 2 - of_core
-        chips = [chip, x(chip, two), x(chip, one), x(chip, 3)]
-        return jnp.concatenate([lax.dynamic_slice(ctx, (0, (2 * c + of_core) * each), (ctx.shape[0], each)) for c in chips], 1)
-
-    other = permute(columns(1 - core), core_perm)
-    return jnp.concatenate([columns(core), other], 0).T
 
 
 def finish_scatter(far, keep, n_dev):
@@ -941,18 +1002,12 @@
         ff_groups = [groups[3 * layer + 2] * 2 if layer < blocks - 1 else groups[-2] + groups[-1] for layer in range(blocks)]
         ff_offsets = [8 * depth if layer < blocks - 1 else 0 for layer in range(blocks)]
 
-        group_rows = groups[0][0].shape[0]
-        vecs = jnp.zeros((vec_rows, width), F32)
-        for piece in groups[0]:
-            vecs = vecs + piece[group_rows - vec_rows:].astype(F32)
+        vecs = vec_sum(groups[0], vec_rows)
         vecs = vecs[:blocks * vec_each].reshape(blocks, vec_each, width)
         rows_all = jnp.pad(vecs[:, :9], ((0, 0), (0, 7), (0, 0)))
         bias_all = vecs[:, 9:].reshape(blocks, 1, 8 * width)
 
-        padded = (valid + 15) // 16 * 16
-        ctx = jnp.pad(context, ((0, 0), (0, padded - valid), (0, 0))).reshape(batch * padded, ctx_width)
-
-        turned_ctx = context_columns(ctx, n_dev)
+        ctx, ctx_mine, ctx_other = prepare_context(context, n_dev)
 
         h = tokens_x.reshape(count, width)
         saved = []
@@ -973,7 +1028,6 @@
         results, vec_grads = [None] * blocks, [None] * blocks
         every = tuple(range(n_dev // 2))
         by_column = lambda x, y, columns, first: [(x, 0, y, c * width, first + c * depth, depth, every) for c in range(columns)]
-        _, _, core_perm = gather_perms(n_dev)
         for layer in reversed(range(blocks)):
             turn = blocks - 1 - layer
             rows, group = rows_all[layer], groups[3 * layer:3 * layer + 2]
@@ -991,20 +1045,19 @@
             if turn > 0:
                 r_ff2 = reduce(pairs[2:])
             grad_bf, d_query, d_kv, grad, vec2 = cross_backward(grad, query, kv, h1, rows, group[1], tokens, valid)
-            d_kv_other = permute(d_kv, core_perm)
             r_cross = reduce(weight_grads(3, (norm2, d_query, mix2, grad_bf),
-                                             by_column(0, 1, 1, 0) + by_column(2, 3, 1, depth), 2 * depth))
-            r_kv = reduce(context_grad(turned_ctx, d_kv, d_kv_other))
+                                             by_column(0, 1, 1, 0) + by_column(2, 3, 1, depth), 2 * depth, (d_kv, ctx_mine, ctx_other)))
             grad_bf, d_qkv, grad, vec1 = self_backward(grad, qkv, h0, rows, group[0], tokens, BF16 if layer == 0 else F32)
             r_self = reduce(weight_grads(4, (norm1, d_qkv, mix1, grad_bf),
                                             by_column(0, 1, 3, 0) + by_column(2, 3, 1, 3 * depth), 4 * depth))
             side = lambda array, blocks_of: jnp.concatenate(jnp.split(array, blocks_of, 0), 1)
-            results[layer] = [side(r_self[:3 * depth], 3), r_self[3 * depth:], r_cross[:depth], side(r_kv, 2), r_cross[depth:],
+            results[layer] = [side(r_self[:3 * depth], 3), r_self[3 * depth:], r_cross[:depth], side(r_cross[2 * depth:], 2), r_cross[depth:2 * depth],
                               side(r_ff1, 8), r_ff2]
-            vec_grads[layer] = jnp.concatenate([vec1[0], vec1[1], vec2[0], vec2[1], vec3[0], vec3[1],
-                                                vec1[2], vec2[2], vec3[2], vec_b1[0]])
-        vec_full = jnp.stack([jnp.pad(g, (0, vec_len * n_dev - g.shape[0])).reshape(n_dev, vec_len) for g in vec_grads], 1)
-        vec_out = scatter_sum(vec_full, n_dev)
+            vec_grads[layer] = [vec1, vec2, vec3, vec_b1]
+        vec_out = vec_total([part for parts in vec_grads for part in parts], vec_rows, n_dev)
+        vec_out = vec_out[:blocks * vec_each].reshape(blocks, vec_each * width)
+        vec_out = jnp.pad(vec_out, ((0, 0), (0, vec_len * n_dev - vec_each * width)))
+        vec_out = lax.dynamic_slice(vec_out, (0, me * vec_len), (blocks, vec_len))
         outs = []
         for index in range(7):
             stacked = jnp.stack([results[layer][index] for layer in range(blocks)]) / total

time: 966 us -> 975 us (level)
  waiting for transfers between devices: 293 us -> 335 us
  local copies, waits for them, and re-layouts: 53 us -> 33.5 us
    ppermute x75 -> x69, waiting for transfers between devices: 293 us -> 335 us  [permute(): return lax.ppermute(array, AXIS, perm)]
    slice x14 -> x1, local copies, waits for them, and re-layouts: 12.2 us -> 0.9 us  [inner(): vecs = vecs[:blocks * vec_each].reshape(blocks, vec_each, width)]
    unnamed x155 -> x105, local copies, waits for them, and re-layouts: 32.7 us -> 26.9 us
    ppermute x75 -> x69, starting transfers between devices: 62 us -> 60 us  [permute(): return lax.ppermute(array, AXIS, perm)]
  transfers between devices with their start and end apart: 75 -> 69, of which waited for: 23 -> 19; matrix products, arithmetic and copies ran while one was open for 6% -> 4% of each run, Pallas kernels for 27% -> 26%
where the time goes in v3:
time: 975 us; the launch traced here: 966 us
  Pallas kernels  521 us (53%)
  waiting for transfers between devices  335 us (34%)
  starting transfers between devices  60 us (6%)
  local copies, waits for them, and re-layouts  33.5 us (3%)
  other arithmetic  15.7 us (2%)
    ppermute x69, waiting for transfers between devices, permute(): return lax.ppermute(array, AXIS, perm)  335 us
    pallas_call x2, Pallas kernels, ff_grads(): pl.pallas_call(functools.partial(ff_grad_kernel, offset, down), in_specs=...  127 us
    pallas_call x2, Pallas kernels, self_backward(): call(functools.partial(self_backward_kernel, STEP // tokens, tokens), cou...  84.5 us
    pallas_call x5, Pallas kernels, weight_grads(): pl.pallas_call(functools.partial(grad_kernel, tiles, group_rows, len(arra...  79.3 us
    ppermute x69, starting transfers between devices, permute(): return lax.ppermute(array, AXIS, perm)  60 us
    pallas_call x2, Pallas kernels, cross_backward(): call(functools.partial(cross_backward_kernel, STEP // tokens, tokens, val...  55.9 us
    pallas_call x2, Pallas kernels, self_forward(): call(functools.partial(self_forward_kernel, STEP // tokens, tokens), coun...  41.1 us
    pallas_call x2, Pallas kernels, cross_forward(): call(functools.partial(cross_forward_kernel, STEP // tokens, tokens, vali...  39 us
  transfers between devices with their start and end apart: 69, of which 19 were waited for; matrix products, arithmetic and copies ran while one was open for 4% of the time, Pallas kernels for 26%

profile of v3, /device:TPU:0, one launch (start us, length us, event | category | flops | bytes accessed | tf_op | source)
XLA Modules:
  0.0 966.5 jit_solution(7876681575332318409)
XLA Ops:
  0.7 1.6 copy.51
  2.3 2.0 copy.50
  4.3 1.8 pack.10.refs_0_
  6.9 2.5 collective-permute-start.22
  9.4 1.5 collective-permute-start.21
  12.0 1.9 pack.7.refs_0_
  17.0 1.8 pack.13.refs_0_.refs_8_
  22.1 1.5 collective-permute-start
  23.6 12.8 %collective-permute-done.43.refs_2_.refs_10_ = bf16[320,640]{1,0:T(8,128)(2,1)} collective-permute-done((bf16[320,640]{1,0:T(8,128)(2,1)}, bf16[320,640]{1,0:T(8,128)(2,1)}, u32[]{:S(2)}, u32[]{:S(2)}) %collective-permute-start.43) | collective-permute-done | bytes 409632 | tf_op jit(solution)/shard_map/ppermute | solution.py:80
  36.4 2.1 pack.12.refs_0_
  38.6 2.5 collective-permute-start.36
  41.0 1.5 collective-permute-start.35
  44.6 2.2 pack.8.refs_0_
  47.8 1.8 collective-permute-start.23
  49.5 24.5 %collective-permute-done.23.refs_3_ = bf16[320,640]{1,0:T(8,128)(2,1)} collective-permute-done((bf16[320,640]{1,0:T(8,128)(2,1)}, bf16[320,640]{1,0:T(8,128)(2,1)}, u32[]{:S(2)}, u32[]{:S(2)}) %collective-permute-start.23) | collective-permute-done | bytes 409632 | tf_op jit(solution)/shard_map/ppermute | solution.py:80
  74.1 1.6 collective-permute-start.7
  75.6 2.1 pack.11.refs_0_
  77.8 1.8 collective-permute-start.29
  80.5 2.5 pack.9.refs_0_.refs_8_.refs_1_.refs_9_
  84.1 9.0 collective-permute-done.7.refs_1_
  93.0 4.0 context.1
  100.1 1.8 collective-permute-start.2
  101.8 6.7 collective-permute-done.28.refs_1_
  108.6 2.3 collective-permute-start.9
  110.8 3.1 collective-permute-done.2.refs_3_
  114.0 1.8 collective-permute-start.15
  115.8 19.1 %collective-permute-done.14.refs_1_.refs_9_.refs_2_.refs_10_ = bf16[960,640]{1,0:T(8,128)(2,1)} collective-permute-done((bf16[960,640]{1,0:T(8,128)(2,1)}, bf16[960,640]{1,0:T(8,128)(2,1)}, u32[]{:S(2)}, u32[]{:S(2)}) %collective-permute-start.14) | collective-permute-done | bytes 1228832 | tf_op jit(solution)/shard_map/ppermute | solution.py:80
  134.9 2.3 collective-permute-start.16
  139.8 1.8 vec_sum.1
  146.8 11.5 %collective-permute-done.16.refs_3_.refs_11_.refs_4_.refs_12_ = bf16[960,640]{1,0:T(8,128)(2,1)} collective-permute-done((bf16[960,640]{1,0:T(8,128)(2,1)}, bf16[960,640]{1,0:T(8,128)(2,1)}, u32[]{:S(2)}, u32[]{:S(2)}) %collective-permute-start.16) | collective-permute-done | bytes 1228832 | tf_op jit(solution)/shard_map/ppermute | solution.py:80
  159.8 2.0 collective-permute-start.30
  161.8 20.2 %shard_map.186 = (bf16[1536,640]{1,0:T(8,128)(2,1)}, bf16[1536,1920]{1,0:T(8,128)(2,1)}, bf16[1536,640]{1,0:T(8,128)(2,1)}, f32[1536,640]{1,0:T(8,128)}) custom-call(bf16[1536,640]{1,0:T(8,128)(2,1)} %bitcast.117, f32[16,640]{1,0:T(8,128)} %get-tuple-element.183.rows_ref, bf16[368,640]{1,0:T(8,128)(2,1)} %pack.7.refs_0_, bf16[368,640]{1,0:T(8,128)(2,1)} %copy-done.23, ...), custom_call_target="tpu_custom_call" | custom-call | flops 6039797760 | bytes 20000000 | tf_op jit(solution)/shard_map/pallas_call | solution.py:462
  182.1 19.6 %shard_map.187 = (bf16[1536,640]{1,0:T(8,128)(2,1)}, bf16[1536,640]{1,0:T(8,128)(2,1)}, bf16[480,1280]{1,0:T(8,128)(2,1)}, bf16[1536,640]{1,0:T(8,128)(2,1)}, f32[1536,640]{1,0:T(8,128)}) custom-call(f32[1536,640]{1,0:T(8,128)} %get-tuple-element.89.h_ref, f32[16,640]{1,0:T(8,128)} %get-tuple-element.183.rows_ref, ...), custom_call_target="tpu_custom_call" | custom-call | flops 5536481280 | bytes 20000000 | tf_op jit(solution)/shard_map/pallas_call | solution.py:474
  203.7 31.7 %shard_map.188 = (bf16[1536,640]{1,0:T(8,128)(2,1)}, bf16[1536,2560]{1,0:T(8,128)(2,1)}, f32[1536,2560]{1,0:T(8,128)}, f32[1536,2560]{1,0:T(8,128)}, f32[1536,640]{1,0:T(8,128)}) custom-call(f32[1536,640]{1,0:T(8,128)} %get-tuple-element.94.h_ref, f32[16,640]{1,0:T(8,128)} %get-tuple-element.183.rows_ref, f32[1,5120]{1,0:T(1,128)} %bitcast.114, ...), custom_call_target="tpu_custom_call" | custom-call | flops 15099494400 | bytes 60000000 | tf_op jit(solution)/shard_map/pallas_call | solution.py:488
  236.5 20.9 %shard_map.189 = (bf16[1536,640]{1,0:T(8,128)(2,1)}, bf16[1536,1920]{1,0:T(8,128)(2,1)}, bf16[1536,640]{1,0:T(8,128)(2,1)}, f32[1536,640]{1,0:T(8,128)}) custom-call(f32[1536,640]{1,0:T(8,128)} %get-tuple-element.97.h_ref, f32[16,640]{1,0:T(8,128)} %get-tuple-element.182.rows_ref, bf16[320,640]{1,0:T(8,128)(2,1)} %pack.10.refs_0_, ...), custom_call_target="tpu_custom_call" | custom-call | flops 6039797760 | bytes 20000000 | tf_op jit(solution)/shard_map/pallas_call | solution.py:462
  258.4 19.4 %shard_map.190 = (bf16[1536,640]{1,0:T(8,128)(2,1)}, bf16[1536,640]{1,0:T(8,128)(2,1)}, bf16[480,1280]{1,0:T(8,128)(2,1)}, bf16[1536,640]{1,0:T(8,128)(2,1)}, f32[1536,640]{1,0:T(8,128)}) custom-call(f32[1536,640]{1,0:T(8,128)} %get-tuple-element.98.h_ref, f32[16,640]{1,0:T(8,128)} %get-tuple-element.182.rows_ref, ...), custom_call_target="tpu_custom_call" | custom-call | flops 5536481280 | bytes 20000000 | tf_op jit(solution)/shard_map/pallas_call | solution.py:474
  278.9 28.4 %shard_map.191 = (bf16[1536,640]{1,0:T(8,128)(2,1)}, bf16[1536,2560]{1,0:T(8,128)(2,1)}, f32[1536,2560]{1,0:T(8,128)}, f32[1536,2560]{1,0:T(8,128)}) custom-call(f32[1536,640]{1,0:T(8,128)} %get-tuple-element.99.h_ref, f32[16,640]{1,0:T(8,128)} %get-tuple-element.182.rows_ref, f32[1,5120]{1,0:T(1,128)} %bitcast.113, bf16[640,640]{1,0:T(8,128)(2,1)} %pack.12.refs_0_, ...), custom_call_target="tpu_custom_call" | custom-call | flops 10066329600 | bytes 50000000 | tf_op jit(solution)/shard_map/pallas_call | solution.py:501
  307.3 17.1 %shard_map.203 = (f32[640,640]{1,0:T(8,128)}, f32[640,640]{1,0:T(8,128)}) custom-call(bf16[1536,2560]{1,0:T(8,128)(2,1)} %get-tuple-element.100.gated_ref.refs_0_, bf16[1536,640]{1,0:T(8,128)(2,1)} %bitcast.115), custom_call_target="tpu_custom_call" | custom-call | flops 5033164800 | bytes 20000000 | tf_op jit(solution)/shard_map/pallas_call | solution.py:666
  326.1 59.2 %shard_map.193 = (f32[1536,640]{1,0:T(8,128)}, f32[8,640]{1,0:T(8,128)}, f32[8,5120]{1,0:T(8,128)}, f32[1280,640]{1,0:T(8,128)}, f32[1280,640]{1,0:T(8,128)}) custom-call(bf16[1536,640]{1,0:T(8,128)(2,1)} %bitcast.116, f32[1536,2560]{1,0:T(8,128)} %get-tuple-element.101.save_a, f32[1536,2560]{1,0:T(8,128)} %get-tuple-element.102.save_g, ...), custom_call_target="tpu_custom_call" | custom-call | flops 25165824000 | bytes 60000000 | tf_op jit(solution)/shard_map/pallas_call | solution.py:950
  385.4 27.9 %shard_map.194 = (bf16[1536,640]{1,0:T(8,128)(2,1)}, bf16[1536,640]{1,0:T(8,128)(2,1)}, bf16[480,1280]{1,0:T(8,128)(2,1)}, f32[1536,640]{1,0:T(8,128)}, f32[8,640]{1,0:T(8,128)}) custom-call(f32[1536,640]{1,0:T(8,128)} %get-tuple-element.104.grad_ref, bf16[1536,640]{1,0:T(8,128)(2,1)} %get-tuple-element.105.query_ref, ...), custom_call_target="tpu_custom_call" | custom-call | flops 3774873600 | bytes 20000000 | tf_op jit(solution)/shard_map/pallas_call | solution.py:525
  413.2 42.4 %shard_map.195 = (bf16[1536,640]{1,0:T(8,128)(2,1)}, bf16[1536,1920]{1,0:T(8,128)(2,1)}, f32[1536,640]{1,0:T(8,128)}, f32[8,640]{1,0:T(8,128)}) custom-call(f32[1536,640]{1,0:T(8,128)} %get-tuple-element.107.grad_ref, bf16[1536,1920]{1,0:T(8,128)(2,1)} %get-tuple-element.108.qkv_ref, f32[1536,640]{1,0:T(8,128)} %get-tuple-element.97.h_ref, ...), custom_call_target="tpu_custom_call" | custom-call | flops 7549747200 | bytes 30000000 | tf_op jit(solution)/shard_map/pallas_call | solution.py:539
  455.6 67.3 %shard_map.196 = (f32[1536,640]{1,0:T(8,128)}, f32[8,640]{1,0:T(8,128)}, f32[8,5120]{1,0:T(8,128)}, f32[1280,640]{1,0:T(8,128)}, f32[1280,640]{1,0:T(8,128)}, /*index=5*/f32[640,640]{1,0:T(8,128)}, f32[640,640]{1,0:T(8,128)}) custom-call(f32[1536,640]{1,0:T(8,128)} %get-tuple-element.109.grad_ref, f32[1536,2560]{1,0:T(8,128)} %get-tuple-element.110.save_a, ...), custom_call_target="tpu_custom_call" | custom-call | flops 35232153600 | bytes 60000000 | tf_op jit(solution)/shard_map/pallas_call | solution.py:950
  522.9 28.0 %shard_map.197 = (bf16[1536,640]{1,0:T(8,128)(2,1)}, bf16[1536,640]{1,0:T(8,128)(2,1)}, bf16[480,1280]{1,0:T(8,128)(2,1)}, f32[1536,640]{1,0:T(8,128)}, f32[8,640]{1,0:T(8,128)}) custom-call(f32[1536,640]{1,0:T(8,128)} %get-tuple-element.114.grad_ref, bf16[1536,640]{1,0:T(8,128)(2,1)} %get-tuple-element.115.query_ref, ...), custom_call_target="tpu_custom_call" | custom-call | flops 3774873600 | bytes 20000000 | tf_op jit(solution)/shard_map/pallas_call | solution.py:525
  551.0 42.1 %shard_map.198 = (bf16[1536,640]{1,0:T(8,128)(2,1)}, bf16[1536,1920]{1,0:T(8,128)(2,1)}, bf16[1536,640]{1,0:T(8,128)(2,1)}, f32[8,640]{1,0:T(8,128)}) custom-call(f32[1536,640]{1,0:T(8,128)} %get-tuple-element.117.grad_ref, bf16[1536,1920]{1,0:T(8,128)(2,1)} %get-tuple-element.118.qkv_ref, bf16[1536,640]{1,0:T(8,128)(2,1)} %bitcast.118, ...), custom_call_target="tpu_custom_call" | custom-call | flops 7549747200 | bytes 30000000 | tf_op jit(solution)/shard_map/pallas_call | solution.py:539
  593.0 1.8 vec_pack.1
  595.6 17.0 %shard_map.199 = (f32[640,640]{1,0:T(8,128)}, f32[640,640]{1,0:T(8,128)}) custom-call(bf16[1536,640]{1,0:T(8,128)(2,1)} %get-tuple-element.120.refs_0_, bf16[1536,1920]{1,0:T(8,128)(2,1)} %get-tuple-element.121.refs_1_, bf16[1536,640]{1,0:T(8,128)(2,1)} %get-tuple-element.122.refs_2_, bf16[1536,640]{1,0:T(8,128)(2,1)} %get-tuple-element.123.refs_3_), custom_call_target="tpu_custom_call" | custom-call | flops 5033164800 | bytes 20000000 | tf_op jit(solution)/shard_map/pallas_call | solution.py:666
  614.6 17.1 %shard_map.200 = (f32[640,640]{1,0:T(8,128)}, f32[640,640]{1,0:T(8,128)}) custom-call(bf16[1536,640]{1,0:T(8,128)(2,1)} %get-tuple-element.126.refs_0_, bf16[1536,1920]{1,0:T(8,128)(2,1)} %get-tuple-element.127.refs_1_, bf16[1536,640]{1,0:T(8,128)(2,1)} %get-tuple-element.128.refs_2_, bf16[1536,640]{1,0:T(8,128)(2,1)} %get-tuple-element.129.refs_3_), custom_call_target="tpu_custom_call" | custom-call | flops 5033164800 | bytes 20000000 | tf_op jit(solution)/shard_map/pallas_call | solution.py:666
  633.8 14.0 %shard_map.201 = (f32[1344,640]{1,0:T(8,128)}, f32[1344,640]{1,0:T(8,128)}) custom-call(bf16[1536,640]{1,0:T(8,128)(2,1)} %get-tuple-element.132.refs_0_, bf16[1536,640]{1,0:T(8,128)(2,1)} %get-tuple-element.133.refs_1_, bf16[1536,640]{1,0:T(8,128)(2,1)} %get-tuple-element.134.refs_2_, bf16[1536,640]{1,0:T(8,128)(2,1)} %get-tuple-element.135.refs_3_, ...), custom_call_target="tpu_custom_call" | custom-call | flops 5033164800 | bytes 20000000 | tf_op jit(solution)/shard_map/pallas_call | solution.py:666
  649.0 14.1 %shard_map.202 = (f32[1344,640]{1,0:T(8,128)}, f32[1344,640]{1,0:T(8,128)}) custom-call(bf16[1536,640]{1,0:T(8,128)(2,1)} %get-tuple-element.141.refs_0_, bf16[1536,640]{1,0:T(8,128)(2,1)} %get-tuple-element.142.refs_1_, bf16[1536,640]{1,0:T(8,128)(2,1)} %get-tuple-element.143.refs_2_, bf16[1536,640]{1,0:T(8,128)(2,1)} %get-tuple-element.144.refs_3_, ...), custom_call_target="tpu_custom_call" | custom-call | flops 5033164800 | bytes 20000000 | tf_op jit(solution)/shard_map/pallas_call | solution.py:666
  663.1 24.9 %collective-permute-done.67 = f32[48,640]{1,0:T(8,128)S(1)} collective-permute-done((f32[48,640]{1,0:T(8,128)S(1)}, f32[48,640]{1,0:T(8,128)S(1)}, u32[]{:S(2)}, u32[]{:S(2)}) %collective-permute-start.67) | collective-permute-done | bytes 122912 | tf_op jit(solution)/shard_map/ppermute | solution.py:80
  688.9 12.2 %shard_map.192 = bf16[1536,640]{1,0:T(8,128)(2,1)} custom-call(f32[1536,640]{1,0:T(8,128)} %get-tuple-element.99.h_ref, f32[16,640]{1,0:T(8,128)} %get-tuple-element.182.rows_ref, bf16[1536,2560]{1,0:T(8,128)(2,1)} %get-tuple-element.100.gated_ref.refs_0_, bf16[320,640]{1,0:T(8,128)(2,1)} %pack.13.refs_0_.refs_8_, ...), custom_call_target="tpu_custom_call" | custom-call | flops 5033164800 | bytes 20000000 | tf_op jit(solution)/shard_map/pallas_call | solution.py:513
  712.5 14.1 %collective-permute-done.50 = f32[320,640]{1,0:T(8,128)S(1)} collective-permute-done((f32[320,640]{1,0:T(8,128)S(1)}, f32[320,640]{1,0:T(8,128)S(1)}, u32[]{:S(2)}, u32[]{:S(2)}) %collective-permute-start.50) | collective-permute-done | bytes 819232 | tf_op jit(solution)/shard_map/ppermute | solution.py:80
  729.1 15.1 %collective-permute-done.52 = f32[320,640]{1,0:T(8,128)S(1)} collective-permute-done((f32[320,640]{1,0:T(8,128)S(1)}, f32[320,640]{1,0:T(8,128)S(1)}, u32[]{:S(2)}, u32[]{:S(2)}) %collective-permute-start.52) | collective-permute-done | bytes 819232 | tf_op jit(solution)/shard_map/ppermute | solution.py:80
  746.7 18.5 %collective-permute-done.63 = f32[320,640]{1,0:T(8,128)S(1)} collective-permute-done((f32[320,640]{1,0:T(8,128)S(1)}, f32[320,640]{1,0:T(8,128)S(1)}, u32[]{:S(2)}, u32[]{:S(2)}) %collective-permute-start.63) | collective-permute-done | bytes 819232 | tf_op jit(solution)/shard_map/ppermute | solution.py:80
  770.8 1.7 copy.33
  772.4 13.9 %collective-permute-done.65 = f32[320,640]{1,0:T(8,128)S(1)} collective-permute-done((f32[320,640]{1,0:T(8,128)S(1)}, f32[320,640]{1,0:T(8,128)S(1)}, u32[]{:S(2)}, u32[]{:S(2)}) %collective-permute-start.65) | collective-permute-done | bytes 819232 | tf_op jit(solution)/shard_map/ppermute | solution.py:80
  787.9 2.4 copy.39
  790.3 37.5 %collective-permute-done.60 = f32[1280,640]{1,0:T(8,128)S(1)} collective-permute-done((f32[1280,640]{1,0:T(8,128)}, f32[1280,640]{1,0:T(8,128)S(1)}, u32[]{:S(2)}, u32[]{:S(2)}) %collective-permute-start.60) | collective-permute-done | bytes 3276832 | tf_op jit(solution)/shard_map/ppermute | solution.py:80
  829.1 53.2 %collective-permute-done.54 = f32[1344,640]{1,0:T(8,128)S(1)} collective-permute-done((f32[1344,640]{1,0:T(8,128)}, f32[1344,640]{1,0:T(8,128)S(1)}, u32[]{:S(2)}, u32[]{:S(2)}) %collective-permute-start.54) | collective-permute-done | bytes 3440672 | tf_op jit(solution)/shard_map/ppermute | solution.py:80
  883.5 54.0 %collective-permute-done.56 = f32[1344,640]{1,0:T(8,128)S(1)} collective-permute-done((f32[1344,640]{1,0:T(8,128)}, f32[1344,640]{1,0:T(8,128)S(1)}, u32[]{:S(2)}, u32[]{:S(2)}) %collective-permute-start.56) | collective-permute-done | bytes 3440672 | tf_op jit(solution)/shard_map/ppermute | solution.py:80
  939.3 1.7 fusion.2
  941.5 4.2 copy.38
  946.1 13.7 %collective-permute-done.57 = f32[672,640]{1,0:T(8,128)S(1)} collective-permute-done((f32[672,640]{1,0:T(8,128)S(1)}, f32[672,640]{1,0:T(8,128)S(1)}, u32[]{:S(2)}, u32[]{:S(2)}) %collective-permute-start.57) | collective-permute-done | bytes 1720352 | tf_op jit(solution)/shard_map/ppermute | solution.py:80
  960.6 3.5 copy.36
  (258 shorter events, 70.5 us)
Async XLA Ops:
  6.1 12.8 %collective-permute-start.24 = (bf16[320,640]{1,0:T(8,128)(2,1)}, bf16[320,640]{1,0:T(8,128)(2,1)}, u32[]{:S(2)}, u32[]{:S(2)}) collective-permute-start(bf16[320,640]{1,0:T(8,128)(2,1)} %pack.10.refs_0_), channel_id=1, source_target_pairs={{0,1},{1,0},{2,3},{3,2},{4,5},{5,4},{6,7},{7,6}} | collective-permute-start | bytes 1228808 | tf_op jit(solution)/shard_map/ppermute | solution.py:80
  6.9 13.4 %collective-permute-start.22 = (bf16[320,640]{1,0:T(8,128)(2,1)}, bf16[320,640]{1,0:T(8,128)(2,1)}, u32[]{:S(2)}, u32[]{:S(2)}) collective-permute-start(bf16[320,640]{1,0:T(8,128)(2,1)} %pack.10.refs_0_), channel_id=1, source_target_pairs={{0,2},{1,5},{2,0},{3,7},{4,6},{5,1},{6,4},{7,3}} | collective-permute-start | bytes 1228808 | tf_op jit(solution)/shard_map/ppermute | solution.py:80
  9.4 12.7 %collective-permute-start.21 = (bf16[320,640]{1,0:T(8,128)(2,1)}, bf16[320,640]{1,0:T(8,128)(2,1)}, u32[]{:S(2)}, u32[]{:S(2)}) collective-permute-start(bf16[320,640]{1,0:T(8,128)(2,1)} %pack.10.refs_0_), channel_id=1, source_target_pairs={{0,4},{1,3},{2,6},{3,1},{4,0},{5,7},{6,2},{7,5}} | collective-permute-start | bytes 1228808 | tf_op jit(solution)/shard_map/ppermute | solution.py:80
  13.8 27.2 %collective-permute-start.3 = (bf16[368,640]{1,0:T(8,128)(2,1)}, bf16[368,640]{1,0:T(8,128)(2,1)S(1)}, u32[]{:S(2)}, u32[]{:S(2)}) collective-permute-start(bf16[368,640]{1,0:T(8,128)(2,1)} %pack.7.refs_0_), channel_id=1, source_target_pairs={{0,1},{1,0},{2,3},{3,2},{4,5},{5,4},{6,7},{7,6}} | collective-permute-start | bytes 1413128 | tf_op jit(solution)/shard_map/ppermute | solution.py:80
  14.0 28.6 %collective-permute-start.1 = (bf16[368,640]{1,0:T(8,128)(2,1)}, bf16[368,640]{1,0:T(8,128)(2,1)}, u32[]{:S(2)}, u32[]{:S(2)}) collective-permute-start(bf16[368,640]{1,0:T(8,128)(2,1)} %pack.7.refs_0_), channel_id=1, source_target_pairs={{0,2},{1,5},{2,0},{3,7},{4,6},{5,1},{6,4},{7,3}} | collective-permute-start | bytes 1413128 | tf_op jit(solution)/shard_map/ppermute | solution.py:80
  18.9 17.6 %collective-permute-start.43 = (bf16[320,640]{1,0:T(8,128)(2,1)}, bf16[320,640]{1,0:T(8,128)(2,1)}, u32[]{:S(2)}, u32[]{:S(2)}) collective-permute-start(bf16[320,640]{1,0:T(8,128)(2,1)} %pack.13.refs_0_.refs_8_), channel_id=1, source_target_pairs={{0,2},{1,5},{2,0},{3,7},{4,6},{5,1},{6,4},{7,3}} | collective-permute-start | bytes 1228808 | tf_op jit(solution)/shard_map/ppermute | solution.py:80
  20.3 18.3 %collective-permute-start.42 = (bf16[320,640]{1,0:T(8,128)(2,1)}, bf16[320,640]{1,0:T(8,128)(2,1)}, u32[]{:S(2)}, u32[]{:S(2)}) collective-permute-start(bf16[320,640]{1,0:T(8,128)(2,1)} %pack.13.refs_0_.refs_8_), channel_id=1, source_target_pairs={{0,4},{1,3},{2,6},{3,1},{4,0},{5,7},{6,2},{7,5}} | collective-permute-start | bytes 1228808 | tf_op jit(solution)/shard_map/ppermute | solution.py:80
  22.1 24.7 %collective-permute-start = (bf16[368,640]{1,0:T(8,128)(2,1)S(1)}, bf16[368,640]{1,0:T(8,128)(2,1)S(1)}, u32[]{:S(2)}, u32[]{:S(2)}) collective-permute-start(bf16[368,640]{1,0:T(8,128)(2,1)S(1)} %copy-done.4), channel_id=1, source_target_pairs={{0,4},{1,3},{2,6},{3,1},{4,0},{5,7},{6,2},{7,5}} | collective-permute-start | bytes 1413128 | tf_op jit(solution)/shard_map/ppermute | solution.py:80
  38.6 39.2 %collective-permute-start.36 = (bf16[640,640]{1,0:T(8,128)(2,1)}, bf16[640,640]{1,0:T(8,128)(2,1)}, u32[]{:S(2)}, u32[]{:S(2)}) collective-permute-start(bf16[640,640]{1,0:T(8,128)(2,1)} %pack.12.refs_0_), channel_id=1, source_target_pairs={{0,2},{1,5},{2,0},{3,7},{4,6},{5,1},{6,4},{7,3}} | collective-permute-start | bytes 2457608 | tf_op jit(solution)/shard_map/ppermute | solution.py:80
  41.0 36.7 %collective-permute-start.35 = (bf16[640,640]{1,0:T(8,128)(2,1)}, bf16[640,640]{1,0:T(8,128)(2,1)}, u32[]{:S(2)}, u32[]{:S(2)}) collective-permute-start(bf16[640,640]{1,0:T(8,128)(2,1)} %pack.12.refs_0_), channel_id=1, source_target_pairs={{0,4},{1,3},{2,6},{3,1},{4,0},{5,7},{6,2},{7,5}} | collective-permute-start | bytes 2457608 | tf_op jit(solution)/shard_map/ppermute | solution.py:80
  46.7 32.8 %collective-permute-start.10 = (bf16[672,640]{1,0:T(8,128)(2,1)}, bf16[672,640]{1,0:T(8,128)(2,1)S(1)}, u32[]{:S(2)}, u32[]{:S(2)}) collective-permute-start(bf16[672,640]{1,0:T(8,128)(2,1)} %pack.8.refs_0_), channel_id=1, source_target_pairs={{0,1},{1,0},{2,3},{3,2},{4,5},{5,4},{6,7},{7,6}} | collective-permute-start | bytes 2580488 | tf_op jit(solution)/shard_map/ppermute | solution.py:80
  47.5 35.4 %collective-permute-start.8 = (bf16[672,640]{1,0:T(8,128)(2,1)}, bf16[672,640]{1,0:T(8,128)(2,1)S(1)}, u32[]{:S(2)}, u32[]{:S(2)}) collective-permute-start(bf16[672,640]{1,0:T(8,128)(2,1)} %pack.8.refs_0_), channel_id=1, source_target_pairs={{0,2},{1,5},{2,0},{3,7},{4,6},{5,1},{6,4},{7,3}} | collective-permute-start | bytes 2580488 | tf_op jit(solution)/shard_map/ppermute | solution.py:80
  47.8 26.3 %collective-permute-start.23 = (bf16[320,640]{1,0:T(8,128)(2,1)}, bf16[320,640]{1,0:T(8,128)(2,1)}, u32[]{:S(2)}, u32[]{:S(2)}) collective-permute-start(bf16[320,640]{1,0:T(8,128)(2,1)} %collective-permute-done.21.refs_1_), channel_id=1, source_target_pairs={{0,2},{1,5},{2,0},{3,7},{4,6},{5,1},{6,4},{7,3}} | collective-permute-start | bytes 1228808 | tf_op jit(solution)/shard_map/ppermute | solution.py:80
  74.1 19.0 %collective-permute-start.7 = (bf16[672,640]{1,0:T(8,128)(2,1)}, bf16[672,640]{1,0:T(8,128)(2,1)S(1)}, u32[]{:S(2)}, u32[]{:S(2)}) collective-permute-start(bf16[672,640]{1,0:T(8,128)(2,1)} %pack.8.refs_0_), channel_id=1, source_target_pairs={{0,4},{1,3},{2,6},{3,1},{4,0},{5,7},{6,2},{7,5}} | collective-permute-start | bytes 2580488 | tf_op jit(solution)/shard_map/ppermute | solution.py:80
  77.7 20.8 %collective-permute-start.31 = (bf16[672,640]{1,0:T(8,128)(2,1)}, bf16[672,640]{1,0:T(8,128)(2,1)}, u32[]{:S(2)}, u32[]{:S(2)}) collective-permute-start(bf16[672,640]{1,0:T(8,128)(2,1)} %pack.11.refs_0_), channel_id=1, source_target_pairs={{0,1},{1,0},{2,3},{3,2},{4,5},{5,4},{6,7},{7,6}} | collective-permute-start | bytes 2580488 | tf_op jit(solution)/shard_map/ppermute | solution.py:80
  77.8 22.3 %collective-permute-start.29 = (bf16[672,640]{1,0:T(8,128)(2,1)}, bf16[672,640]{1,0:T(8,128)(2,1)}, u32[]{:S(2)}, u32[]{:S(2)}) collective-permute-start(bf16[672,640]{1,0:T(8,128)(2,1)} %pack.11.refs_0_), channel_id=1, source_target_pairs={{0,2},{1,5},{2,0},{3,7},{4,6},{5,1},{6,4},{7,3}} | collective-permute-start | bytes 2580488 | tf_op jit(solution)/shard_map/ppermute | solution.py:80
  79.5 29.0 %collective-permute-start.28 = (bf16[672,640]{1,0:T(8,128)(2,1)}, bf16[672,640]{1,0:T(8,128)(2,1)}, u32[]{:S(2)}, u32[]{:S(2)}) collective-permute-start(bf16[672,640]{1,0:T(8,128)(2,1)} %pack.11.refs_0_), channel_id=1, source_target_pairs={{0,4},{1,3},{2,6},{3,1},{4,0},{5,7},{6,2},{7,5}} | collective-permute-start | bytes 2580488 | tf_op jit(solution)/shard_map/ppermute | solution.py:80
  82.9 51.9 %collective-permute-start.14 = (bf16[960,640]{1,0:T(8,128)(2,1)}, bf16[960,640]{1,0:T(8,128)(2,1)}, u32[]{:S(2)}, u32[]{:S(2)}) collective-permute-start(bf16[960,640]{1,0:T(8,128)(2,1)} %pack.9.refs_0_.refs_8_.refs_1_.refs_9_), channel_id=1, source_target_pairs={{0,4},{1,3},{2,6},{3,1},{4,0},{5,7},{6,2},{7,5}} | collective-permute-start | bytes 3686408 | tf_op jit(solution)/shard_map/ppermute | solution.py:80
  93.0 15.5 %collective-permute-start.5 = (bf16[368,640]{1,0:T(8,128)(2,1)}, bf16[368,640]{1,0:T(8,128)(2,1)}, u32[]{:S(2)}, u32[]{:S(2)}) collective-permute-start(bf16[368,640]{1,0:T(8,128)(2,1)} %collective-permute-done.1.refs_2_), channel_id=1, source_target_pairs={{0,1},{1,0},{2,3},{3,2},{4,5},{5,4},{6,7},{7,6}} | collective-permute-start | bytes 1413128 | tf_op jit(solution)/shard_map/ppermute | solution.py:80
  98.5 38.6 %collective-permute-start.53 = (bf16[1024,480]{0,1:T(8,128)(2,1)S(1)}, bf16[1024,480]{0,1:T(8,128)(2,1)S(1)}, u32[]{:S(2)}, u32[]{:S(2)}) collective-permute-start(bf16[1024,480]{0,1:T(8,128)(2,1)S(1)} %copy.21), channel_id=1, source_target_pairs={{0,1},{1,0},{2,3},{3,2},{4,5},{5,4},{6,7},{7,6}} | collective-permute-start | bytes 2949128 | tf_op jit(solution)/shard_map/ppermute | solution.py:80
  100.1 13.9 %collective-permute-start.2 = (bf16[368,640]{1,0:T(8,128)(2,1)}, bf16[368,640]{1,0:T(8,128)(2,1)S(1)}, u32[]{:S(2)}, u32[]{:S(2)}) collective-permute-start(bf16[368,640]{1,0:T(8,128)(2,1)} %copy-done.23), channel_id=1, source_target_pairs={{0,2},{1,5},{2,0},{3,7},{4,6},{5,1},{6,4},{7,3}} | collective-permute-start | bytes 1413128 | tf_op jit(solution)/shard_map/ppermute | solution.py:80
  108.6 29.4 %collective-permute-start.9 = (bf16[672,640]{1,0:T(8,128)(2,1)}, bf16[672,640]{1,0:T(8,128)(2,1)}, u32[]{:S(2)}, u32[]{:S(2)}) collective-permute-start(bf16[672,640]{1,0:T(8,128)(2,1)} %copy-done.14), channel_id=1, source_target_pairs={{0,2},{1,5},{2,0},{3,7},{4,6},{5,1},{6,4},{7,3}} | collective-permute-start | bytes 2580488 | tf_op jit(solution)/shard_map/ppermute | solution.py:80
  113.9 23.2 %collective-permute-start.6 = (bf16[368,640]{1,0:T(8,128)(2,1)S(1)}, bf16[368,640]{1,0:T(8,128)(2,1)S(1)}, u32[]{:S(2)}, u32[]{:S(2)}) collective-permute-start(bf16[368,640]{1,0:T(8,128)(2,1)S(1)} %collective-permute-done.2.refs_3_), channel_id=1, source_target_pairs={{0,1},{1,0},{2,3},{3,2},{4,5},{5,4},{6,7},{7,6}} | collective-permute-start | bytes 1413128 | tf_op jit(solution)/shard_map/ppermute | solution.py:80
  114.0 31.2 %collective-permute-start.15 = (bf16[960,640]{1,0:T(8,128)(2,1)S(1)}, bf16[960,640]{1,0:T(8,128)(2,1)}, u32[]{:S(2)}, u32[]{:S(2)}) collective-permute-start(bf16[960,640]{1,0:T(8,128)(2,1)S(1)} %copy-done.11), channel_id=1, source_target_pairs={{0,2},{1,5},{2,0},{3,7},{4,6},{5,1},{6,4},{7,3}} | collective-permute-start | bytes 3686408 | tf_op jit(solution)/shard_map/ppermute | solution.py:80
  134.9 23.4 %collective-permute-start.16 = (bf16[960,640]{1,0:T(8,128)(2,1)}, bf16[960,640]{1,0:T(8,128)(2,1)}, u32[]{:S(2)}, u32[]{:S(2)}) collective-permute-start(bf16[960,640]{1,0:T(8,128)(2,1)} %collective-permute-done.14.refs_1_.refs_9_.refs_2_.refs_10_), channel_id=1, source_target_pairs={{0,2},{1,5},{2,0},{3,7},{4,6},{5,1},{6,4},{7,3}} | collective-permute-start | bytes 3686408 | tf_op jit(solution)/shard_map/ppermute | solution.py:80
  138.0 21.8 %collective-permute-start.13 = (bf16[672,640]{1,0:T(8,128)(2,1)}, bf16[672,640]{1,0:T(8,128)(2,1)}, u32[]{:S(2)}, u32[]{:S(2)}) collective-permute-start(bf16[672,640]{1,0:T(8,128)(2,1)} %collective-permute-done.9.refs_3_), channel_id=1, source_target_pairs={{0,1},{1,0},{2,3},{3,2},{4,5},{5,4},{6,7},{7,6}} | collective-permute-start | bytes 2580488 | tf_op jit(solution)/shard_map/ppermute | solution.py:80
  145.1 56.5 %collective-permute-start.17 = (bf16[960,640]{1,0:T(8,128)(2,1)S(1)}, bf16[960,640]{1,0:T(8,128)(2,1)}, u32[]{:S(2)}, u32[]{:S(2)}) collective-permute-start(bf16[960,640]{1,0:T(8,128)(2,1)S(1)} %copy-done.11), channel_id=1, source_target_pairs={{0,1},{1,0},{2,3},{3,2},{4,5},{5,4},{6,7},{7,6}} | collective-permute-start | bytes 3686408 | tf_op jit(solution)/shard_map/ppermute | solution.py:80
  146.3 56.9 %collective-permute-start.18 = (bf16[960,640]{1,0:T(8,128)(2,1)}, bf16[960,640]{1,0:T(8,128)(2,1)}, u32[]{:S(2)}, u32[]{:S(2)}) collective-permute-start(bf16[960,640]{1,0:T(8,128)(2,1)} %collective-permute-done.14.refs_1_.refs_9_.refs_2_.refs_10_), channel_id=1, source_target_pairs={{0,1},{1,0},{2,3},{3,2},{4,5},{5,4},{6,7},{7,6}} | collective-permute-start | bytes 3686408 | tf_op jit(solution)/shard_map/ppermute | solution.py:80
  146.3 56.3 %collective-permute-start.19 = (bf16[960,640]{1,0:T(8,128)(2,1)}, bf16[960,640]{1,0:T(8,128)(2,1)}, u32[]{:S(2)}, u32[]{:S(2)}) collective-permute-start(bf16[960,640]{1,0:T(8,128)(2,1)} %collective-permute-done.15.refs_2_.refs_10_.refs_3_.refs_11_), channel_id=1, source_target_pairs={{0,1},{1,0},{2,3},{3,2},{4,5},{5,4},{6,7},{7,6}} | collective-permute-start | bytes 3686408 | tf_op jit(solution)/shard_map/ppermute | solution.py:80
  158.3 44.9 %collective-permute-start.20 = (bf16[960,640]{1,0:T(8,128)(2,1)}, bf16[960,640]{1,0:T(8,128)(2,1)}, u32[]{:S(2)}, u32[]{:S(2)}) collective-permute-start(bf16[960,640]{1,0:T(8,128)(2,1)} %collective-permute-done.16.refs_3_.refs_11_.refs_4_.refs_12_), channel_id=1, source_target_pairs={{0,1},{1,0},{2,3},{3,2},{4,5},{5,4},{6,7},{7,6}} | collective-permute-start | bytes 3686408 | tf_op jit(solution)/shard_map/ppermute | solution.py:80
  159.8 41.9 %collective-permute-start.30 = (bf16[672,640]{1,0:T(8,128)(2,1)}, bf16[672,640]{1,0:T(8,128)(2,1)S(1)}, u32[]{:S(2)}, u32[]{:S(2)}) collective-permute-start(bf16[672,640]{1,0:T(8,128)(2,1)} %collective-permute-done.28.refs_1_), channel_id=1, source_target_pairs={{0,2},{1,5},{2,0},{3,7},{4,6},{5,1},{6,4},{7,3}} | collective-permute-start | bytes 2580488 | tf_op jit(solution)/shard_map/ppermute | solution.py:80
  201.6 33.7 %collective-permute-start.27 = (bf16[320,640]{1,0:T(8,128)(2,1)}, bf16[320,640]{1,0:T(8,128)(2,1)S(1)}, u32[]{:S(2)}, u32[]{:S(2)}) collective-permute-start(bf16[320,640]{1,0:T(8,128)(2,1)} %collective-permute-done.23.refs_3_), channel_id=1, source_target_pairs={{0,1},{1,0},{2,3},{3,2},{4,5},{5,4},{6,7},{7,6}} | collective-permute-start | bytes 1228808 | tf_op jit(solution)/shard_map/ppermute | solution.py:80
  201.7 33.8 %collective-permute-start.37 = (bf16[640,640]{1,0:T(8,128)(2,1)}, bf16[640,640]{1,0:T(8,128)(2,1)}, u32[]{:S(2)}, u32[]{:S(2)}) collective-permute-start(bf16[640,640]{1,0:T(8,128)(2,1)} %collective-permute-done.35.refs_1_), channel_id=1, source_target_pairs={{0,2},{1,5},{2,0},{3,7},{4,6},{5,1},{6,4},{7,3}} | collective-permute-start | bytes 2457608 | tf_op jit(solution)/shard_map/ppermute | solution.py:80
  202.7 33.3 %collective-permute-start.32 = (bf16[672,640]{1,0:T(8,128)(2,1)}, bf16[672,640]{1,0:T(8,128)(2,1)S(1)}, u32[]{:S(2)}, u32[]{:S(2)}) collective-permute-start(bf16[672,640]{1,0:T(8,128)(2,1)} %collective-permute-done.28.refs_1_), channel_id=1, source_target_pairs={{0,1},{1,0},{2,3},{3,2},{4,5},{5,4},{6,7},{7,6}} | collective-permute-start | bytes 2580488 | tf_op jit(solution)/shard_map/ppermute | solution.py:80
  203.2 32.7 %collective-permute-start.33 = (bf16[672,640]{1,0:T(8,128)(2,1)}, bf16[672,640]{1,0:T(8,128)(2,1)S(1)}, u32[]{:S(2)}, u32[]{:S(2)}) collective-permute-start(bf16[672,640]{1,0:T(8,128)(2,1)} %collective-permute-done.29.refs_2_), channel_id=1, source_target_pairs={{0,1},{1,0},{2,3},{3,2},{4,5},{5,4},{6,7},{7,6}} | collective-permute-start | bytes 2580488 | tf_op jit(solution)/shard_map/ppermute | solution.py:80
  203.2 54.2 %collective-permute-start.34 = (bf16[672,640]{1,0:T(8,128)(2,1)S(1)}, bf16[672,640]{1,0:T(8,128)(2,1)S(1)}, u32[]{:S(2)}, u32[]{:S(2)}) collective-permute-start(bf16[672,640]{1,0:T(8,128)(2,1)S(1)} %collective-permute-done.30.refs_3_), channel_id=1, source_target_pairs={{0,1},{1,0},{2,3},{3,2},{4,5},{5,4},{6,7},{7,6}} | collective-permute-start | bytes 2580488 | tf_op jit(solution)/shard_map/ppermute | solution.py:80
  235.4 42.5 %collective-permute-start.38 = (bf16[640,640]{1,0:T(8,128)(2,1)}, bf16[640,640]{1,0:T(8,128)(2,1)}, u32[]{:S(2)}, u32[]{:S(2)}) collective-permute-start(bf16[640,640]{1,0:T(8,128)(2,1)} %pack.12.refs_0_), channel_id=1, source_target_pairs={{0,1},{1,0},{2,3},{3,2},{4,5},{5,4},{6,7},{7,6}} | collective-permute-start | bytes 2457608 | tf_op jit(solution)/shard_map/ppermute | solution.py:80
  235.5 43.0 %collective-permute-start.39 = (bf16[640,640]{1,0:T(8,128)(2,1)}, bf16[640,640]{1,0:T(8,128)(2,1)}, u32[]{:S(2)}, u32[]{:S(2)}) collective-permute-start(bf16[640,640]{1,0:T(8,128)(2,1)} %collective-permute-done.35.refs_1_), channel_id=1, source_target_pairs={{0,1},{1,0},{2,3},{3,2},{4,5},{5,4},{6,7},{7,6}} | collective-permute-start | bytes 2457608 | tf_op jit(solution)/shard_map/ppermute | solution.py:80
  235.9 42.4 %collective-permute-start.40 = (bf16[640,640]{1,0:T(8,128)(2,1)}, bf16[640,640]{1,0:T(8,128)(2,1)}, u32[]{:S(2)}, u32[]{:S(2)}) collective-permute-start(bf16[640,640]{1,0:T(8,128)(2,1)} %collective-permute-done.36.refs_2_), channel_id=1, source_target_pairs={{0,1},{1,0},{2,3},{3,2},{4,5},{5,4},{6,7},{7,6}} | collective-permute-start | bytes 2457608 | tf_op jit(solution)/shard_map/ppermute | solution.py:80
  236.0 42.9 %collective-permute-start.41 = (bf16[640,640]{1,0:T(8,128)(2,1)}, bf16[640,640]{1,0:T(8,128)(2,1)}, u32[]{:S(2)}, u32[]{:S(2)}) collective-permute-start(bf16[640,640]{1,0:T(8,128)(2,1)} %collective-permute-done.37.refs_3_), channel_id=1, source_target_pairs={{0,1},{1,0},{2,3},{3,2},{4,5},{5,4},{6,7},{7,6}} | collective-permute-start | bytes 2457608 | tf_op jit(solution)/shard_map/ppermute | solution.py:80
  257.4 20.3 %collective-permute-start.44 = (bf16[320,640]{1,0:T(8,128)(2,1)}, bf16[320,640]{1,0:T(8,128)(2,1)S(1)}, u32[]{:S(2)}, u32[]{:S(2)}) collective-permute-start(bf16[320,640]{1,0:T(8,128)(2,1)} %collective-permute-done.42.refs_1_.refs_9_), channel_id=1, source_target_pairs={{0,2},{1,5},{2,0},{3,7},{4,6},{5,1},{6,4},{7,3}} | collective-permute-start | bytes 1228808 | tf_op jit(solution)/shard_map/ppermute | solution.py:80
  277.8 46.6 %collective-permute-start.45 = (bf16[320,640]{1,0:T(8,128)(2,1)S(1)}, bf16[320,640]{1,0:T(8,128)(2,1)S(1)}, u32[]{:S(2)}, u32[]{:S(2)}) collective-permute-start(bf16[320,640]{1,0:T(8,128)(2,1)S(1)} %copy-done.27), channel_id=1, source_target_pairs={{0,1},{1,0},{2,3},{3,2},{4,5},{5,4},{6,7},{7,6}} | collective-permute-start | bytes 1228808 | tf_op jit(solution)/shard_map/ppermute | solution.py:80
  277.9 46.6 %collective-permute-start.46 = (bf16[320,640]{1,0:T(8,128)(2,1)}, bf16[320,640]{1,0:T(8,128)(2,1)S(1)}, u32[]{:S(2)}, u32[]{:S(2)}) collective-permute-start(bf16[320,640]{1,0:T(8,128)(2,1)} %collective-permute-done.42.refs_1_.refs_9_), channel_id=1, source_target_pairs={{0,1},{1,0},{2,3},{3,2},{4,5},{5,4},{6,7},{7,6}} | collective-permute-start | bytes 1228808 | tf_op jit(solution)/shard_map/ppermute | solution.py:80
  278.3 46.1 %collective-permute-start.47 = (bf16[320,640]{1,0:T(8,128)(2,1)}, bf16[320,640]{1,0:T(8,128)(2,1)S(1)}, u32[]{:S(2)}, u32[]{:S(2)}) collective-permute-start(bf16[320,640]{1,0:T(8,128)(2,1)} %collective-permute-done.43.refs_2_.refs_10_), channel_id=1, source_target_pairs={{0,1},{1,0},{2,3},{3,2},{4,5},{5,4},{6,7},{7,6}} | collective-permute-start | bytes 1228808 | tf_op jit(solution)/shard_map/ppermute | solution.py:80
  278.4 46.1 %collective-permute-start.48 = (bf16[320,640]{1,0:T(8,128)(2,1)S(1)}, bf16[320,640]{1,0:T(8,128)(2,1)S(1)}, u32[]{:S(2)}, u32[]{:S(2)}) collective-permute-start(bf16[320,640]{1,0:T(8,128)(2,1)S(1)} %collective-permute-done.44.refs_3_.refs_11_), channel_id=1, source_target_pairs={{0,1},{1,0},{2,3},{3,2},{4,5},{5,4},{6,7},{7,6}} | collective-permute-start | bytes 1228808 | tf_op jit(solution)/shard_map/ppermute | solution.py:80
  594.8 53.0 %collective-permute-start.66 = (f32[48,640]{1,0:T(8,128)}, f32[48,640]{1,0:T(8,128)S(1)}, u32[]{:S(2)}, u32[]{:S(2)}) collective-permute-start(f32[48,640]{1,0:T(8,128)} %vec_pack.1), channel_id=1, source_target_pairs={{0,1},{1,0},{2,3},{3,2},{4,5},{5,4},{6,7},{7,6}} | collective-permute-start | bytes 368648 | tf_op jit(solution)/shard_map/ppermute | solution.py:80
  612.6 90.5 %collective-permute-start.49 = (f32[640,640]{1,0:T(8,128)}, f32[640,640]{1,0:T(8,128)}, u32[]{:S(2)}, u32[]{:S(2)}) collective-permute-start(f32[640,640]{1,0:T(8,128)} %get-tuple-element.125), channel_id=1, source_target_pairs={{0,2},{1,5},{2,0},{3,7},{4,6},{5,1},{6,4},{7,3}} | collective-permute-start | bytes 4915208 | tf_op jit(solution)/shard_map/ppermute | solution.py:80
  613.7 94.1 %collective-permute-start.62 = (f32[640,640]{1,0:T(8,128)}, f32[640,640]{1,0:T(8,128)}, u32[]{:S(2)}, u32[]{:S(2)}) collective-permute-start(f32[640,640]{1,0:T(8,128)} %get-tuple-element.153), channel_id=1, source_target_pairs={{0,2},{1,5},{2,0},{3,7},{4,6},{5,1},{6,4},{7,3}} | collective-permute-start | bytes 4915208 | tf_op jit(solution)/shard_map/ppermute | solution.py:80
  631.8 73.7 %collective-permute-start.51 = (f32[640,640]{1,0:T(8,128)}, f32[640,640]{1,0:T(8,128)}, u32[]{:S(2)}, u32[]{:S(2)}) collective-permute-start(f32[640,640]{1,0:T(8,128)} %get-tuple-element.131), channel_id=1, source_target_pairs={{0,2},{1,5},{2,0},{3,7},{4,6},{5,1},{6,4},{7,3}} | collective-permute-start | bytes 4915208 | tf_op jit(solution)/shard_map/ppermute | solution.py:80
  632.9 77.2 %collective-permute-start.64 = (f32[640,640]{1,0:T(8,128)}, f32[640,640]{1,0:T(8,128)}, u32[]{:S(2)}, u32[]{:S(2)}) collective-permute-start(f32[640,640]{1,0:T(8,128)} %get-tuple-element.155), channel_id=1, source_target_pairs={{0,2},{1,5},{2,0},{3,7},{4,6},{5,1},{6,4},{7,3}} | collective-permute-start | bytes 4915208 | tf_op jit(solution)/shard_map/ppermute | solution.py:80
  647.9 40.1 %collective-permute-start.67 = (f32[48,640]{1,0:T(8,128)S(1)}, f32[48,640]{1,0:T(8,128)S(1)}, u32[]{:S(2)}, u32[]{:S(2)}) collective-permute-start(f32[48,640]{1,0:T(8,128)S(1)} %add.112), channel_id=1, source_target_pairs={{0,2},{1,5},{2,0},{3,7},{4,6},{5,1},{6,4},{7,3}} | collective-permute-start | bytes 368648 | tf_op jit(solution)/shard_map/ppermute | solution.py:80
  687.9 13.2 %collective-permute-start.68 = (f32[48,640]{1,0:T(8,128)S(1)}, f32[48,640]{1,0:T(8,128)S(1)}, u32[]{:S(2)}, u32[]{:S(2)}) collective-permute-start(f32[48,640]{1,0:T(8,128)S(1)} %add.113), channel_id=1, source_target_pairs={{0,4},{1,3},{2,6},{3,1},{4,0},{5,7},{6,2},{7,5}} | collective-permute-start | bytes 368648 | tf_op jit(solution)/shard_map/ppermute | solution.py:80
  701.1 66.8 %collective-permute-start.58 = (f32[1280,640]{1,0:T(8,128)}, f32[1280,640]{1,0:T(8,128)S(1)}, u32[]{:S(2)}, u32[]{:S(2)}) collective-permute-start(f32[1280,640]{1,0:T(8,128)} %get-tuple-element.149), channel_id=1, source_target_pairs={{0,2},{1,5},{2,0},{3,7},{4,6},{5,1},{6,4},{7,3}} | collective-permute-start | bytes 9830408 | tf_op jit(solution)/shard_map/ppermute | solution.py:80
  703.1 124.7 %collective-permute-start.60 = (f32[1280,640]{1,0:T(8,128)}, f32[1280,640]{1,0:T(8,128)S(1)}, u32[]{:S(2)}, u32[]{:S(2)}) collective-permute-start(f32[1280,640]{1,0:T(8,128)} %get-tuple-element.151), channel_id=1, source_target_pairs={{0,2},{1,5},{2,0},{3,7},{4,6},{5,1},{6,4},{7,3}} | collective-permute-start | bytes 9830408 | tf_op jit(solution)/shard_map/ppermute | solution.py:80
  705.5 21.1 %collective-permute-start.50 = (f32[320,640]{1,0:T(8,128)S(1)}, f32[320,640]{1,0:T(8,128)S(1)}, u32[]{:S(2)}, u32[]{:S(2)}) collective-permute-start(f32[320,640]{1,0:T(8,128)S(1)} %slice_add_fusion.14), channel_id=1, source_target_pairs={{0,4},{1,3},{2,6},{3,1},{4,0},{5,7},{6,2},{7,5}} | collective-permute-start | bytes 2457608 | tf_op jit(solution)/shard_map/ppermute | solution.py:80
  707.8 36.4 %collective-permute-start.52 = (f32[320,640]{1,0:T(8,128)S(1)}, f32[320,640]{1,0:T(8,128)S(1)}, u32[]{:S(2)}, u32[]{:S(2)}) collective-permute-start(f32[320,640]{1,0:T(8,128)S(1)} %slice_add_fusion.12), channel_id=1, source_target_pairs={{0,4},{1,3},{2,6},{3,1},{4,0},{5,7},{6,2},{7,5}} | collective-permute-start | bytes 2457608 | tf_op jit(solution)/shard_map/ppermute | solution.py:80
  710.1 172.2 %collective-permute-start.54 = (f32[1344,640]{1,0:T(8,128)}, f32[1344,640]{1,0:T(8,128)S(1)}, u32[]{:S(2)}, u32[]{:S(2)}) collective-permute-start(f32[1344,640]{1,0:T(8,128)} %get-tuple-element.140), channel_id=1, source_target_pairs={{0,2},{1,5},{2,0},{3,7},{4,6},{5,1},{6,4},{7,3}} | collective-permute-start | bytes 10321928 | tf_op jit(solution)/shard_map/ppermute | solution.py:80
  726.6 210.9 %collective-permute-start.56 = (f32[1344,640]{1,0:T(8,128)}, f32[1344,640]{1,0:T(8,128)S(1)}, u32[]{:S(2)}, u32[]{:S(2)}) collective-permute-start(f32[1344,640]{1,0:T(8,128)} %get-tuple-element.147), channel_id=1, source_target_pairs={{0,2},{1,5},{2,0},{3,7},{4,6},{5,1},{6,4},{7,3}} | collective-permute-start | bytes 10321928 | tf_op jit(solution)/shard_map/ppermute | solution.py:80
  744.2 21.1 %collective-permute-start.63 = (f32[320,640]{1,0:T(8,128)S(1)}, f32[320,640]{1,0:T(8,128)S(1)}, u32[]{:S(2)}, u32[]{:S(2)}) collective-permute-start(f32[320,640]{1,0:T(8,128)S(1)} %slice_add_fusion.10), channel_id=1, source_target_pairs={{0,4},{1,3},{2,6},{3,1},{4,0},{5,7},{6,2},{7,5}} | collective-permute-start | bytes 2457608 | tf_op jit(solution)/shard_map/ppermute | solution.py:80
  765.3 21.1 %collective-permute-start.65 = (f32[320,640]{1,0:T(8,128)S(1)}, f32[320,640]{1,0:T(8,128)S(1)}, u32[]{:S(2)}, u32[]{:S(2)}) collective-permute-start(f32[320,640]{1,0:T(8,128)S(1)} %slice_add_fusion.8), channel_id=1, source_target_pairs={{0,4},{1,3},{2,6},{3,1},{4,0},{5,7},{6,2},{7,5}} | collective-permute-start | bytes 2457608 | tf_op jit(solution)/shard_map/ppermute | solution.py:80
  768.8 170.0 %collective-permute-start.59 = (f32[640,640]{1,0:T(8,128)S(1)}, f32[640,640]{1,0:T(8,128)S(1)}, u32[]{:S(2)}, u32[]{:S(2)}) collective-permute-start(f32[640,640]{1,0:T(8,128)S(1)} %slice_add_fusion.6), channel_id=1, source_target_pairs={{0,4},{1,3},{2,6},{3,1},{4,0},{5,7},{6,2},{7,5}} | collective-permute-start | bytes 4915208 | tf_op jit(solution)/shard_map/ppermute | solution.py:80
  828.0 111.3 %collective-permute-start.61 = (f32[640,640]{1,0:T(8,128)S(1)}, f32[640,640]{1,0:T(8,128)}, u32[]{:S(2)}, u32[]{:S(2)}) collective-permute-start(f32[640,640]{1,0:T(8,128)S(1)} %slice_add_fusion.4), channel_id=1, source_target_pairs={{0,4},{1,3},{2,6},{3,1},{4,0},{5,7},{6,2},{7,5}} | collective-permute-start | bytes 4915208 | tf_op jit(solution)/shard_map/ppermute | solution.py:80
  882.4 63.3 %collective-permute-start.55 = (f32[672,640]{1,0:T(8,128)S(1)}, f32[672,640]{1,0:T(8,128)S(1)}, u32[]{:S(2)}, u32[]{:S(2)}) collective-permute-start(f32[672,640]{1,0:T(8,128)S(1)} %slice_add_fusion.2), channel_id=1, source_target_pairs={{0,4},{1,3},{2,6},{3,1},{4,0},{5,7},{6,2},{7,5}} | collective-permute-start | bytes 5160968 | tf_op jit(solution)/shard_map/ppermute | solution.py:80
  937.7 22.0 %collective-permute-start.57 = (f32[672,640]{1,0:T(8,128)S(1)}, f32[672,640]{1,0:T(8,128)S(1)}, u32[]{:S(2)}, u32[]{:S(2)}) collective-permute-start(f32[672,640]{1,0:T(8,128)S(1)} %slice_add_fusion), channel_id=1, source_target_pairs={{0,4},{1,3},{2,6},{3,1},{4,0},{5,7},{6,2},{7,5}} | collective-permute-start | bytes 5160968 | tf_op jit(solution)/shard_map/ppermute | solution.py:80
  (43 other events, 620.6 us)

commit v4 on v3

--- a/solution.py
+++ b/solution.py
@@ -11,12 +11,12 @@
 HEAD = 64
 AXIS = 'fsdp'
 CHUNK = 1280
+FF_ROWS = 256
 FF_STEP = 256
 STEP = 512
 VMEM_LIMIT = 60 * 1024 * 1024
 VMEM_MOST = 67043328
 FORWARD_UNROLL = 10
-BACKWARD_UNROLL = 5
 
 F32 = jnp.float32
 BF16 = jnp.bfloat16
@@ -120,6 +120,10 @@
     return lax.dot_general(a, b, (((1,), (1,)), ((), ())), preferred_element_type=F32)
 
 
+def dot_tn(a, b):
+    return lax.dot_general(a, b, (((0,), (0,)), ((), ())), preferred_element_type=F32)
+
+
 def norm_stats(x):
     average = jnp.mean(x, axis=-1, keepdims=True)
     centered = x - average
@@ -145,50 +149,100 @@
     return lax.broadcasted_iota(jnp.int32, (rows, 2 * HEAD), 1) < HEAD
 
 
-def pair_scores(query, key, low, head, valid):
-    q_head = jnp.where(low if head == 0 else jnp.logical_not(low), query, jnp.zeros_like(query))
-    scores = dot_nt(q_head, key) * HEAD ** -0.5
-    if valid is not None:
-        column = lax.broadcasted_iota(jnp.int32, scores.shape, 1)
-        scores = jnp.where(column < valid, scores, -1e30)
-    return q_head, softmax_rows(scores)
+def heads_of(pair):
+    low, zero = low_lanes(pair.shape[0]), jnp.zeros_like(pair)
+    return jnp.where(low, pair, zero), jnp.where(low, zero, pair)
 
 
 def pair_forward(query, key, value, valid=None):
-    low = low_lanes(query.shape[0])
     mixed = []
-    for head in range(2):
-        _, probs = pair_scores(query, key, low, head, valid)
-        mixed.append(dot_nn(probs.astype(BF16), value))
-    return jnp.where(low, mixed[0], mixed[1]).astype(BF16)
-
-
-def pair_probs(key, query, low, head, valid):
-    q_head = jnp.where(low if head == 0 else jnp.logical_not(low), query, jnp.zeros_like(query))
-    scores = dot_nt(key, q_head) * HEAD ** -0.5
+    for q_head in heads_of(query * HEAD ** -0.5):
+        scores = dot_nt(q_head, key)
+        if valid is not None:
+            column = lax.broadcasted_iota(jnp.int32, scores.shape, 1)
+            scores = jnp.where(column < valid, scores, -1e30)
+        mixed.append(dot_nn(softmax_rows(scores).astype(BF16), value))
+    return jnp.where(low_lanes(query.shape[0]), mixed[0], mixed[1]).astype(BF16)
+
+
+def backward_scores(query, key, value, d_out):
+    q_heads, d_heads = heads_of(query * HEAD ** -0.5), heads_of(d_out)
+    return q_heads, d_heads, [dot_nt(key, q) for q in q_heads], [dot_nt(value, d) for d in d_heads]
+
+
+def backward_probs(scores, d_probs, valid):
     if valid is not None:
         row = lax.broadcasted_iota(jnp.int32, scores.shape, 0)
         scores = jnp.where(row < valid, scores, -1e30)
-    top = jnp.max(scores, axis=0, keepdims=True)
-    raised = jnp.exp(scores - top)
-    return q_head, raised * (1.0 / jnp.sum(raised, axis=0, keepdims=True))
-
-
-def pair_backward(query, key, value, d_out, valid=None):
-    low = low_lanes(query.shape[0])
-    turned = key.T
-    d_query, d_key, d_value = [], None, None
-    for head in range(2):
-        q_head, probs = pair_probs(key, query, low, head, valid)
-        d_head = jnp.where(low if head == 0 else jnp.logical_not(low), d_out, jnp.zeros_like(d_out))
-        d_probs = dot_nt(value, d_head).astype(BF16).astype(F32)
-        inner = jnp.sum(d_probs * probs, axis=0, keepdims=True)
-        d_scores = ((probs * (d_probs - inner)) * HEAD ** -0.5).astype(BF16)
-        d_query.append(dot_nn(turned[head * HEAD:(head + 1) * HEAD, :], d_scores))
-        dk, dv = dot_nn(d_scores, q_head), dot_nn(probs.astype(BF16), d_head)
-        d_key = dk if d_key is None else d_key + dk
-        d_value = dv if d_value is None else d_value + dv
-    return jnp.concatenate(d_query, 0).T.astype(BF16), d_key.astype(BF16), d_value.astype(BF16)
+    raised = jnp.exp(scores - jnp.max(scores, axis=0, keepdims=True))
+    probs = raised * (1.0 / jnp.sum(raised, axis=0, keepdims=True))
+    inner = jnp.sum(d_probs * probs, axis=0, keepdims=True)
+    return probs.astype(BF16), (probs * (d_probs - inner)).astype(BF16)
+
+
+def pairs_backward(pairs, load, store, valid=None):
+    ahead = load(0)
+    ahead = ahead, backward_scores(*ahead)
+    for pair in range(pairs):
+        (query, key, value, d_out), (q_heads, d_heads, scores, d_probs) = ahead
+        if pair + 1 < pairs:
+            ahead = load(pair + 1)
+            ahead = ahead, backward_scores(*ahead)
+        turned = key.T
+        d_query, d_key, d_value = [], 0.0, 0.0
+        for head in range(2):
+            probs, d_scores = backward_probs(scores[head], d_probs[head], valid)
+            d_query.append(dot_nn(turned[head * HEAD:(head + 1) * HEAD, :], d_scores))
+            d_key = d_key + dot_nn(d_scores, q_heads[head])
+            d_value = d_value + dot_nn(probs, d_heads[head])
+        d_query = (jnp.concatenate(d_query, 0) * HEAD ** -0.5).T
+        store(pair, d_query.astype(BF16), d_key.astype(BF16), d_value.astype(BF16))
+
+
+def chip_places(me):
+    core, chip = lax.rem(me, 2), me // 2
+    chip_x, chip_y = lax.rem(chip, 2), chip // 2
+
+    def mate_slot(other):
+        d_x, d_y = lax.rem(chip_x + other % 2, 2), lax.rem(chip_y + other // 2, 2)
+        return d_x + 2 * d_y + core * (d_x - d_y)
+
+    def own_chip(slot):
+        one, two = slot // 2, slot % 2
+        d_x, d_y = one + core * (two - one), two + core * (one - two)
+        return 2 * lax.rem(chip_y + d_y, 2) + lax.rem(chip_x + d_x, 2)
+
+    return core, me + 1 - 2 * core, mate_slot, own_chip
+
+
+def greet(mate):
+    barrier = pltpu.get_barrier_semaphore()
+    pl.semaphore_signal(barrier, inc=1, device_id=(mate,), device_id_type=pl.DeviceIdType.MESH)
+    pl.semaphore_wait(barrier, 1)
+
+
+def tile_sends(q, rows, tile, recv, send_sem, recv_sem):
+    core, mate, mate_slot, _ = chip_places(lax.axis_index(AXIS))
+    copies = []
+    for other in range(4):
+        start = pl.multiple_of((2 * other + 1 - core) * rows, 16)
+        copies.append(pltpu.make_async_remote_copy(
+            src_ref=tile.at[q, pl.ds(start, rows), :], dst_ref=recv.at[mate_slot(other), pl.ds(q * rows, rows), :],
+            send_sem=send_sem.at[q, other], recv_sem=recv_sem.at[q, other],
+            device_id=(mate,), device_id_type=pl.DeviceIdType.MESH))
+    return copies
+
+
+def finish_tiles(tiles, rows, group_rows, tile, recv, send_sem, recv_sem, far_ref, keep_ref):
+    core, _, _, own_chip = chip_places(lax.axis_index(AXIS))
+    for q in range(tiles):
+        for copy in tile_sends(q, rows, tile, recv, send_sem, recv_sem):
+            copy.wait()
+        for slot in range(4):
+            ref = keep_ref if slot < 2 else far_ref
+            start = pl.multiple_of((2 * own_chip(slot) + core) * rows, 16)
+            at = (slot % 2) * group_rows + q * rows
+            ref[at:at + rows, :] = tile[q, pl.ds(start, rows), :] + recv[slot, q * rows:(q + 1) * rows, :]
 
 
 def add_rows(ref, step, rows):
@@ -354,89 +408,173 @@
     out_ref[...] = (h_ref[...] + rows_ref[8:9, :] + dot_nn(gated_ref[...], w_ff2[...])).astype(BF16)
 
 
-def cross_backward_kernel(samples, tokens, valid, grad_ref, query_ref, kv_ref, h_ref, rows_ref, *refs):
-    pieces, (grad_bf_ref, d_query_ref, d_kv_ref, out_ref, vec_ref, d_mix, w_query, w_out, sems) = refs[:8], refs[8:]
+def cross_backward_kernel(samples, tokens, valid, grad_ref, query_ref, kv_ref, h_ref, rows_ref, norm_ref, mix_ref, ctx_mine_ref,
+                          ctx_other_ref, *refs):
+    pieces, refs = refs[:8], refs[8:]
+    (out_ref, vec_ref, far_ref, keep_ref, d_mix, w_query, w_out, d_query, grad_bf, d_kv, kv_other, x_norm, x_mix, ctx_mine, ctx_other,
+     tile, recv, sems, load_sem, kv_send, kv_recv, send_sem, recv_sem) = refs
     width = h_ref.shape[1]
-    step = pl.program_id(0)
+    depth = width // 8
+    step, last = pl.program_id(0), pl.num_programs(0) - 1
     padded = kv_ref.shape[0] // samples
-
-    @pl.when(step == 0)
-    def _():
-        depth = width // 8
+    context_rows = kv_ref.shape[0] * (last + 1)
+    mate = chip_places(lax.axis_index(AXIS))[1]
+    loads = [pltpu.make_async_copy(src, dst, load_sem.at[index]) for index, (src, dst) in enumerate(
+        ((norm_ref, x_norm), (mix_ref, x_mix), (ctx_mine_ref, ctx_mine), (ctx_other_ref, ctx_other)))]
+    exchange = pltpu.make_async_remote_copy(
+        src_ref=d_kv.at[pl.ds(0, context_rows), :], dst_ref=kv_other.at[pl.ds(0, context_rows), :], send_sem=kv_send, recv_sem=kv_recv,
+        device_id=(mate,), device_id_type=pl.DeviceIdType.MESH)
+
+    @pl.when(step == 0)
+    def _():
         base = pieces[0].shape[0] - 2 * depth
         start_load(pieces, base, w_query, sems.at[0])
         start_load(pieces, base + depth, w_out, sems.at[1])
+        for copy in loads:
+            copy.start()
+        for ref in (d_kv, kv_other):
+            ref[context_rows:, :] = jnp.zeros((ref.shape[0] - context_rows, ref.shape[1]), BF16)
+        greet(mate)
 
     grad = grad_ref[...]
-    grad_bf = grad.astype(BF16)
-    grad_bf_ref[...] = grad_bf
+    mine = pl.ds(pl.multiple_of(step * grad.shape[0], grad.shape[0]), grad.shape[0])
+    grad_bf[mine, :] = grad.astype(BF16)
 
     @pl.when(step == 0)
     def _():
         wait_load(w_query, sems.at[0])
         wait_load(w_out, sems.at[1])
 
-    d_mix[...] = dot_nt(grad_bf, w_out[...]).astype(BF16)
+    d_mix[...] = dot_nt(grad.astype(BF16), w_out[...]).astype(BF16)
     pairs = width // (2 * HEAD)
 
-    def body(index, carry):
-        sample = index // pairs
-        row = pl.multiple_of(sample * tokens, tokens)
-        kv_row = pl.multiple_of(sample * padded, 16)
-        col = pl.multiple_of((index % pairs) * 2 * HEAD, 2 * HEAD)
-        at = (pl.ds(row, tokens), pl.ds(col, 2 * HEAD))
-        at_key = (pl.ds(kv_row, padded), pl.ds(col, 2 * HEAD))
-        at_value = (pl.ds(kv_row, padded), pl.ds(width + col, 2 * HEAD))
-        dq, dk, dv = pair_backward(query_ref[at], kv_ref[at_key], kv_ref[at_value], d_mix[at], valid)
-        d_query_ref[at] = dq
-        d_kv_ref[at_key] = dk
-        d_kv_ref[at_value] = dv
-        return carry
-
-    lax.fori_loop(0, samples * pairs, body, 0, unroll=BACKWARD_UNROLL)
-    d_norm = dot_nt(d_query_ref[...], w_query[...])
+    at = lambda which, pair: slice(which * width + pair * 2 * HEAD, which * width + (pair + 1) * 2 * HEAD)
+
+    def load(index):
+        sample, pair = index // pairs, index % pairs
+        row, here = slice(sample * tokens, (sample + 1) * tokens), slice(sample * padded, (sample + 1) * padded)
+        return query_ref[row, at(0, pair)], kv_ref[here, at(0, pair)], kv_ref[here, at(1, pair)], d_mix[row, at(0, pair)]
+
+    def store(index, d_q, d_key, d_value):
+        sample, pair = index // pairs, index % pairs
+        d_query[pl.ds(pl.multiple_of((step * samples + sample) * tokens, tokens), tokens), at(0, pair)] = d_q
+        there = pl.ds(pl.multiple_of((step * samples + sample) * padded, 16), padded)
+        d_kv[there, at(0, pair)] = d_key
+        d_kv[there, at(1, pair)] = d_value
+
+    pairs_backward(samples * pairs, load, store, valid)
+    rows, summed = depth, 2 * depth
+    group_rows = keep_ref.shape[0] // 2
+    deep = ctx_mine.shape[0] // 4
+
+    def context_part(ctx, kv, slot, block):
+        return dot_nn(ctx[slot * deep:(slot + 1) * deep, :], kv[:, block * width:(block + 1) * width])
+
+    def context_at(slot, block):
+        start = (slot % 2) * group_rows + summed + block * deep
+        return slice(start, start + deep)
+
+    @pl.when(step == last)
+    def _():
+        for copy in loads:
+            copy.wait()
+        tile[0] = dot_tn(x_norm[...], d_query[...])
+        exchange.start()
+        tile[1] = dot_tn(x_mix[...], grad_bf[...])
+        for copy in tile_sends(0, rows, tile, recv, send_sem, recv_sem):
+            copy.start()
+        for slot in range(4):
+            for block in range(2):
+                (keep_ref if slot < 2 else far_ref)[context_at(slot, block), :] = context_part(ctx_mine, d_kv, slot, block)
+        for copy in tile_sends(1, rows, tile, recv, send_sem, recv_sem):
+            copy.start()
+
+    d_norm = dot_nt(d_query[mine, :], w_query[...])
     d_res, g_gain, g_shift = norm_back(h_ref[...], rows_ref[2:3, :], d_norm)
     out_ref[...] = grad + d_res
     add_rows(vec_ref, step, [g_gain, g_shift, jnp.sum(grad, axis=0, keepdims=True)])
 
-
-def self_backward_kernel(samples, tokens, grad_ref, qkv_ref, h_ref, rows_ref, *refs):
-    pieces, (grad_bf_ref, d_qkv_ref, out_ref, vec_ref, d_mix, w_qkv, w_out, sems) = refs[:8], refs[8:]
+    @pl.when(step == last)
+    def _():
+        exchange.wait()
+        for slot in range(4):
+            for block in range(2):
+                (keep_ref if slot < 2 else far_ref)[context_at(slot, block), :] += context_part(ctx_other, kv_other, slot, block)
+        finish_tiles(2, rows, group_rows, tile, recv, send_sem, recv_sem, far_ref, keep_ref)
+
+
+def self_backward_kernel(samples, tokens, grad_ref, qkv_ref, h_ref, rows_ref, norm_ref, mix_ref, *refs):
+    pieces, refs = refs[:8], refs[8:]
+    (out_ref, vec_ref, far_ref, keep_ref, d_mix, w_qkv, w_out, d_qkv, grad_bf, x_norm, x_mix, tile, recv, sems, load_sem,
+     send_sem, recv_sem) = refs
     width = h_ref.shape[1]
-    step = pl.program_id(0)
+    depth = width // 8
+    step, last = pl.program_id(0), pl.num_programs(0) - 1
+    mate = chip_places(lax.axis_index(AXIS))[1]
+    loads = [pltpu.make_async_copy(src, dst, load_sem.at[index]) for index, (src, dst) in enumerate(((norm_ref, x_norm), (mix_ref, x_mix)))]
 
     @pl.when(step == 0)
     def _():
         start_load(pieces, 0, w_qkv, sems.at[0])
-        start_load(pieces, 3 * (width // 8), w_out, sems.at[1])
+        start_load(pieces, 3 * depth, w_out, sems.at[1])
+        for copy in loads:
+            copy.start()
+        greet(mate)
 
     grad = grad_ref[...]
-    grad_bf = grad.astype(BF16)
-    grad_bf_ref[...] = grad_bf
+    mine = pl.ds(pl.multiple_of(step * grad.shape[0], grad.shape[0]), grad.shape[0])
+    grad_bf[mine, :] = grad.astype(BF16)
 
     @pl.when(step == 0)
     def _():
         wait_load(w_qkv, sems.at[0])
         wait_load(w_out, sems.at[1])
 
-    d_mix[...] = dot_nt(grad_bf, w_out[...]).astype(BF16)
+    d_mix[...] = dot_nt(grad.astype(BF16), w_out[...]).astype(BF16)
     pairs = width // (2 * HEAD)
 
-    def body(index, carry):
-        row = pl.multiple_of((index // pairs) * tokens, tokens)
-        col = pl.multiple_of((index % pairs) * 2 * HEAD, 2 * HEAD)
-        at = lambda which: (pl.ds(row, tokens), pl.ds(which * width + col, 2 * HEAD))
-        d_parts = pair_backward(qkv_ref[at(0)], qkv_ref[at(1)], qkv_ref[at(2)], d_mix[at(0)])
-        for which in range(3):
-            d_qkv_ref[at(which)] = d_parts[which]
-        return carry
-
-    lax.fori_loop(0, samples * pairs, body, 0, unroll=BACKWARD_UNROLL)
-    d_norm = dot_nt(d_qkv_ref[...], w_qkv[...])
+    at = lambda which, pair: slice(which * width + pair * 2 * HEAD, which * width + (pair + 1) * 2 * HEAD)
+    rows_of = lambda sample: slice(sample * tokens, (sample + 1) * tokens)
+    all_rows_of = lambda sample: pl.ds(pl.multiple_of((step * samples + sample) * tokens, tokens), tokens)
+
+    def load(index):
+        row, pair = rows_of(index // pairs), index % pairs
+        return tuple(qkv_ref[row, at(which, pair)] for which in range(3)) + (d_mix[row, at(0, pair)],)
+
+    def store(index, *parts):
+        for which, part in enumerate(parts):
+            d_qkv[all_rows_of(index // pairs), at(which, index % pairs)] = part
+
+    pairs_backward(samples * pairs, load, store)
+
+    @pl.when(step == last)
+    def _():
+        for copy in loads:
+            copy.wait()
+        for q in range(4):
+            if q < 3:
+                tile[q] = dot_tn(x_norm[...], d_qkv[:, q * width:(q + 1) * width])
+            else:
+                tile[q] = dot_tn(x_mix[...], grad_bf[...])
+            if q > 0:
+                for copy in tile_sends(q - 1, depth, tile, recv, send_sem, recv_sem):
+                    copy.start()
+
+    d_norm = dot_nt(d_qkv[mine, :], w_qkv[...])
+
+    @pl.when(step == last)
+    def _():
+        for copy in tile_sends(3, depth, tile, recv, send_sem, recv_sem):
+            copy.start()
+
     d_res, g_gain, g_shift = norm_back(h_ref[...].astype(F32), rows_ref[0:1, :], d_norm)
     out_ref[...] = (grad + d_res).astype(out_ref.dtype)
     add_rows(vec_ref, step, [g_gain, g_shift, jnp.sum(grad, axis=0, keepdims=True)])
 
+    @pl.when(step == last)
+    def _():
+        finish_tiles(4, depth, 4 * depth, tile, recv, send_sem, recv_sem, far_ref, keep_ref)
+
 
 def by_step(rows, columns):
     return pl.BlockSpec((rows, columns), lambda i: (i, 0))
@@ -450,11 +588,12 @@
     return jax.ShapeDtypeStruct((rows, columns), dtype)
 
 
-def call(kernel, steps, in_specs, out_specs, out_shapes, scratch, flops, moved):
+def call(kernel, steps, in_specs, out_specs, out_shapes, scratch, flops, moved, kind=None):
     return pl.pallas_call(
         kernel, grid=(steps,), in_specs=in_specs, out_specs=out_specs, out_shape=out_shapes, scratch_shapes=scratch,
         cost_estimate=pl.CostEstimate(flops=int(flops), bytes_accessed=int(moved), transcendentals=0),
-        compiler_params=pltpu.CompilerParams(dimension_semantics=('arbitrary',), vmem_limit_bytes=VMEM_LIMIT))
+        compiler_params=pltpu.CompilerParams(dimension_semantics=('arbitrary',), vmem_limit_bytes=VMEM_LIMIT, collective_id=kind,
+                                             has_side_effects=kind is not None))
 
 
 def self_forward(h, rows, pieces, tokens):
@@ -518,38 +657,47 @@
         count * width * half * 2, 2e7)(h, rows, gated, *pieces)
 
 
-def cross_backward(grad, query, kv, h, rows, pieces, tokens, valid):
+def cross_backward(grad, query, kv, h, rows, norm, mix, ctx_mine, ctx_other, pieces, tokens, valid):
     count, width = h.shape
     ctx_rows = kv.shape[0]
     steps = count // STEP
+    group_rows = 2 * (width // 8) + ctx_mine.shape[0] // 2
+    dma = pltpu.SemaphoreType.DMA
+    big = pltpu.VMEM((count, width), BF16)
+    kv_buf, ctx_buf = pltpu.VMEM((ctx_mine.shape[1], 2 * width), BF16), pltpu.VMEM(ctx_mine.shape, BF16)
     return call(
         functools.partial(cross_backward_kernel, STEP // tokens, tokens, valid), steps,
         [by_step(STEP, width), by_step(STEP, width), by_step(ctx_rows // steps, 2 * width), by_step(STEP, width),
-         whole(*rows.shape)] + [ANY] * 8,
-        [by_step(STEP, width), by_step(STEP, width), by_step(ctx_rows // steps, 2 * width), by_step(STEP, width), whole(8, width)],
-        [shape(count, width, BF16), shape(count, width, BF16), shape(ctx_rows, 2 * width, BF16), shape(count, width, F32),
-         shape(8, width, F32)],
-        [pltpu.VMEM((STEP, width), BF16), pltpu.VMEM((width, width), BF16), pltpu.VMEM((width, width), BF16),
-         pltpu.SemaphoreType.DMA((2,))],
-        count * width * width * 4 + count * 128 * width * 10, 2e7)(grad, query, kv, h, rows, *pieces)
-
-
-def self_backward(grad, qkv, h, rows, pieces, tokens, out_dtype):
+         whole(*rows.shape)] + [ANY] * 12,
+        [by_step(STEP, width), whole(8, width), whole(2 * group_rows, width), whole(2 * group_rows, width)],
+        [shape(count, width, F32), shape(8, width, F32), shape(2 * group_rows, width, F32), shape(2 * group_rows, width, F32)],
+        [pltpu.VMEM((STEP, width), BF16), pltpu.VMEM((width, width), BF16), pltpu.VMEM((width, width), BF16), big, big, kv_buf, kv_buf,
+         big, big, ctx_buf, ctx_buf, pltpu.VMEM((2, width, width), F32), pltpu.VMEM((4, 2 * (width // 8), width), F32),
+         dma((2,)), dma((4,)), dma, dma, dma((2, 4)), dma((2, 4))],
+        count * width * width * 8 + count * 128 * width * 10 + ctx_mine.size * width * 8, 2e7, 3)(
+            grad, query, kv, h, rows, norm, mix, ctx_mine, ctx_other, *pieces)
+
+
+def self_backward(kind, grad, qkv, h, rows, norm, mix, pieces, tokens, out_dtype):
     count, width = h.shape
+    group_rows = width // 2
+    dma = pltpu.SemaphoreType.DMA
+    big = pltpu.VMEM((count, width), BF16)
     return call(
         functools.partial(self_backward_kernel, STEP // tokens, tokens), count // STEP,
-        [by_step(STEP, width), by_step(STEP, 3 * width), by_step(STEP, width), whole(*rows.shape)] + [ANY] * 8,
-        [by_step(STEP, width), by_step(STEP, 3 * width), by_step(STEP, width), whole(8, width)],
-        [shape(count, width, BF16), shape(count, 3 * width, BF16), shape(count, width, out_dtype), shape(8, width, F32)],
+        [by_step(STEP, width), by_step(STEP, 3 * width), by_step(STEP, width), whole(*rows.shape)] + [ANY] * 10,
+        [by_step(STEP, width), whole(8, width), whole(2 * group_rows, width), whole(2 * group_rows, width)],
+        [shape(count, width, out_dtype), shape(8, width, F32), shape(2 * group_rows, width, F32), shape(2 * group_rows, width, F32)],
         [pltpu.VMEM((STEP, width), BF16), pltpu.VMEM((width, 3 * width), BF16), pltpu.VMEM((width, width), BF16),
-         pltpu.SemaphoreType.DMA((2,))],
-        count * width * width * 8 + count * tokens * width * 10, 3e7)(grad, qkv, h, rows, *pieces)
-
-
-def grad_kernel(tiles, group_rows, inputs, with_context, *refs):
+         pltpu.VMEM((count, 3 * width), BF16), big, big, big, pltpu.VMEM((4, width, width), F32),
+         pltpu.VMEM((4, group_rows, width), F32), dma((2,)), dma((2,)), dma((4, 4)), dma((4, 4))],
+        count * width * width * 16 + count * tokens * width * 10, 3e7, kind)(grad, qkv, h, rows, norm, mix, *pieces)
+
+
+def grad_kernel(tiles, group_rows, inputs, *refs):
     ins, refs = refs[:inputs], refs[inputs:]
     far_ref, keep_ref, x_buf, turned, y_buf, tile, own, recv, x_sem, y_sem, send_sem, recv_sem = refs[:12]
-    width, summed = tile.shape[1], own.shape[1]
+    width = tile.shape[1]
     me = lax.axis_index(AXIS)
     core, chip = lax.rem(me, 2), me // 2
     mate = me + 1 - 2 * core
@@ -577,18 +725,6 @@
     barrier = pltpu.get_barrier_semaphore()
     pl.semaphore_signal(barrier, inc=1, device_id=(mate,), device_id_type=pl.DeviceIdType.MESH)
     pl.semaphore_wait(barrier, 1)
-
-    if with_context:
-        kv_ref, ctx_refs = ins[-3], ins[-2:]
-        kv_mine, kv_other, ctx_mine, ctx_other, kv_sem, kv_send, kv_recv = refs[12:]
-        exchange = pltpu.make_async_remote_copy(
-            src_ref=kv_ref, dst_ref=kv_other, send_sem=kv_send, recv_sem=kv_recv, device_id=(mate,),
-            device_id_type=pl.DeviceIdType.MESH)
-        exchange.start()
-        kv_loads = [pltpu.make_async_copy(src, dst, kv_sem.at[index])
-                    for index, (src, dst) in enumerate(((kv_ref, kv_mine), (ctx_refs[0], ctx_mine), (ctx_refs[1], ctx_other)))]
-        for copy in kv_loads:
-            copy.start()
 
     def sends(q):
         *_, first_row, rows, chips = tiles[q]
@@ -629,19 +765,6 @@
     last = len(tiles) - 1
     for copy in sends(last):
         copy.start()
-    if with_context:
-        for copy in kv_loads:
-            copy.wait()
-        depth = ctx_mine.shape[0] // 4
-        at = lambda slot, block: slice((slot % 2) * group_rows + summed + block * depth, (slot % 2) * group_rows + summed + (block + 1) * depth)
-        for pair, (ctx, kv) in enumerate(((ctx_mine, kv_mine), (ctx_other, kv_other))):
-            if pair == 1:
-                exchange.wait()
-            for slot in range(4):
-                ref = keep_ref if slot < 2 else far_ref
-                for block in range(2):
-                    part = dot_nn(ctx[slot * depth:(slot + 1) * depth, :], kv[:, block * width:(block + 1) * width])
-                    ref[at(slot, block), :] = part if pair == 0 else ref[at(slot, block), :] + part
     for q in range(max(0, last - 2), last + 1):
         for copy in sends(q):
             copy.wait_send()
@@ -650,30 +773,22 @@
             copy.wait_recv()
     for slot in range(4):
         ref = keep_ref if slot < 2 else far_ref
-        ref[(slot % 2) * group_rows:(slot % 2) * group_rows + summed, :] = own[slot] + recv[slot]
-
-
-def weight_grads(kind, arrays, tiles, summed, context=None):
+        ref[(slot % 2) * group_rows:(slot % 2 + 1) * group_rows, :] = own[slot] + recv[slot]
+
+
+def weight_grads(kind, arrays, tiles, group_rows):
     count, width = arrays[0].shape[0], 640
     chips = max(len(t[-1]) for t in tiles)
-    extra, more, group_rows = [], [], summed
     dma = pltpu.SemaphoreType.DMA
-    if context is not None:
-        more = list(context)
-        group_rows += context[1].shape[0] // 2
-        extra = [pltpu.VMEM(context[0].shape, BF16)] * 2 + [pltpu.VMEM(context[1].shape, BF16)] * 2 + [dma((3,)), dma, dma]
     out = jax.ShapeDtypeStruct((2 * group_rows, width), F32)
     return pl.pallas_call(
-        functools.partial(grad_kernel, tiles, group_rows, len(arrays) + len(more), context is not None),
-        in_specs=[ANY] * (len(arrays) + len(more)),
+        functools.partial(grad_kernel, tiles, group_rows, len(arrays)), in_specs=[ANY] * len(arrays),
         out_specs=[pl.BlockSpec(memory_space=pltpu.VMEM)] * 2, out_shape=[out, out],
         scratch_shapes=[pltpu.VMEM((2, count, width), BF16), pltpu.VMEM((width, count), BF16), pltpu.VMEM((2, count, width), BF16),
-                        pltpu.VMEM((3, width, width), F32), pltpu.VMEM((4, summed, width), F32),
-                        pltpu.VMEM((4, summed, width), F32), dma((2,)), dma((2,)), dma((3, chips)), dma((len(tiles), chips))]
-        + extra,
-        cost_estimate=pl.CostEstimate(flops=2 * count * width * width * (len(tiles) + 2 * (context is not None)),
-                                      bytes_accessed=int(2e7), transcendentals=0),
-        compiler_params=pltpu.CompilerParams(collective_id=kind, has_side_effects=True, vmem_limit_bytes=VMEM_LIMIT))(*arrays, *more)
+                        pltpu.VMEM((3, width, width), F32), pltpu.VMEM((4, group_rows, width), F32),
+                        pltpu.VMEM((4, group_rows, width), F32), dma((2,)), dma((2,)), dma((3, chips)), dma((len(tiles), chips))],
+        cost_estimate=pl.CostEstimate(flops=2 * count * width * width * len(tiles), bytes_accessed=int(2e7), transcendentals=0),
+        compiler_params=pltpu.CompilerParams(collective_id=kind, has_side_effects=True, vmem_limit_bytes=VMEM_LIMIT))(*arrays)
 
 
 def context_kernel(context_ref, ctx_ref, mine_ref, other_ref):
@@ -684,19 +799,21 @@
     ctx_ref[...] = jnp.zeros_like(ctx_ref)
     for sample in range(batch):
         ctx_ref[sample * padded:sample * padded + valid, :] = context_ref[sample]
-    each = mine_ref.shape[0] // 4
+    each, rows = mine_ref.shape[0] // 4, ctx_ref.shape[0]
+    mine_ref[...] = jnp.zeros_like(mine_ref)
+    other_ref[...] = jnp.zeros_like(other_ref)
     x = jnp.bitwise_xor
     for of_core, ref in ((core, mine_ref), (1 - core, other_ref)):
         for slot, other in enumerate((chip, x(chip, 2 - of_core), x(chip, 1 + of_core), x(chip, 3))):
             column = pl.multiple_of((2 * other + of_core) * each, each)
-            ref[slot * each:(slot + 1) * each, :] = ctx_ref[:, pl.ds(column, each)].T
+            ref[slot * each:(slot + 1) * each, 0:rows] = ctx_ref[:, pl.ds(column, each)].T
 
 
 def prepare_context(context, n_dev):
     batch, valid, ctx_width = context.shape
     rows = batch * ((valid + 15) // 16 * 16)
     vmem = pl.BlockSpec(memory_space=pltpu.VMEM)
-    turned = shape(ctx_width // 2, rows, BF16)
+    turned = shape(ctx_width // 2, (rows + 127) // 128 * 128, BF16)
     ctx, mine, other = pl.pallas_call(
         context_kernel, in_specs=[vmem], out_specs=[vmem] * 3, out_shape=[shape(rows, ctx_width, BF16), turned, turned],
         cost_estimate=pl.CostEstimate(flops=rows * ctx_width * 8, bytes_accessed=int(8e6), transcendentals=0),
@@ -731,230 +848,157 @@
     return total
 
 
-def ff_grad_kernel(offset, with_down, grad_ref, save_a, save_g, norm_ref, h_ref, rows_ref, *refs):
-    gated_ref, refs = (refs[0], refs[1:]) if with_down else (None, refs)
+def ff_grad_kernel(offset, grad_ref, save_a, save_g, norm_ref, h_ref, rows_ref, *refs):
     pieces, refs = refs[:16], refs[16:]
-    out_ref, vec_ref, bias_ref, far1, keep1 = refs[:5]
-    far2, keep2 = refs[5:7] if with_down else (None, None)
-    (grad, grad_bf, turned, acc, part_a, part_g, d_a, d_g, w_ff1, w_ff2, tile, recv1, obuf,
-     in_sem, part_sem, w1_sem, w2_sem, out_sem, send_sem, recv_sem1) = refs[7 if with_down else 5:][:20]
-    if with_down:
-        z_buf, z_turned, recv2, z_sem, recv_sem2 = refs[-5:]
+    (out_ref, vec_ref, bias_ref, far_ref, keep_ref, grad, grad_bf, turned, acc, part_a, part_g, d_both, w_ff1, w_ff2, tile, recv, obuf,
+     in_sem, part_sem, w1_sem, w2_sem, out_sem, send_sem, recv_sem) = refs
     count, width = grad.shape
     half = w_ff2.shape[0]
-    chunks, each = half // width, STEP
-    steps = count // each
-    depth, deep = width // 8, half // 8
+    chunks, depth = half // width, width // 8
     me = lax.axis_index(AXIS)
-    core, chip = lax.rem(me, 2), me // 2
-    mate = me + 1 - 2 * core
-    chip_x, chip_y = lax.rem(chip, 2), chip // 2
-
-    def slot_of(other, of_mate):
-        d_x, d_y = lax.rem(chip_x + other % 2, 2), lax.rem(chip_y + other // 2, 2)
-        return d_x + 2 * d_y + core * (d_x - d_y) if of_mate else 2 * d_x + d_y + core * (d_y - d_x)
-
-    def chip_in(slot):
-        one, two = slot // 2, slot % 2
-        d_x, d_y = one + core * (two - one), two + core * (one - two)
-        return 2 * lax.rem(chip_y + d_y, 2) + lax.rem(chip_x + d_x, 2)
+    core, mate, mate_slot, own_chip = chip_places(me)
 
     load_grad = pltpu.make_async_copy(grad_ref, grad, in_sem.at[0])
-    load_norm = pltpu.make_async_copy(norm_ref, d_a, in_sem.at[1])
+    load_norm = pltpu.make_async_copy(norm_ref, d_both.at[:, pl.ds(0, width)], in_sem.at[1])
     load_grad.start()
     load_norm.start()
     start_load(pieces[8:], offset, w_ff2, w2_sem)
 
-    def parts(index):
-        chunk, step = index // steps, index % steps
-        at = (pl.ds(pl.multiple_of(step * each, each), each), pl.ds(pl.multiple_of(chunk * width, width), width))
-        return [pltpu.make_async_copy(ref.at[at], buf.at[index % 2], part_sem.at[which, index % 2])
+    def parts(chunk):
+        at = (slice(None), pl.ds(pl.multiple_of(chunk * width, width), width))
+        return [pltpu.make_async_copy(ref.at[at], buf.at[lax.rem(chunk, 2)], part_sem.at[which, lax.rem(chunk, 2)])
                 for which, (ref, buf) in enumerate(((save_a, part_a), (save_g, part_g)))]
 
     def load_h(step):
-        return pltpu.make_async_copy(h_ref.at[pl.ds(step * each, each), :], part_a.at[step % 2], part_sem.at[0, step % 2])
+        return pltpu.make_async_copy(h_ref.at[pl.ds(step * STEP, STEP), :], part_a.at[0, pl.ds(step * STEP, STEP), :], part_sem.at[0, 0])
 
     for copy in parts(0):
         copy.start()
     devices = piece_devices(me)
-    for block in [b + k for b in range(chunks) for k in (0, chunks)]:
-        for piece, device in zip(pieces[:8], devices):
-            pltpu.make_async_copy(piece.at[pl.ds(block * depth, depth), :],
-                                  w_ff1.at[pl.ds(pl.multiple_of(device * depth, 16), depth), pl.ds(block * width, width)],
-                                  w1_sem.at[block]).start()
-    for copy in parts(1):
-        copy.start()
-
-    barrier = pltpu.get_barrier_semaphore()
-    pl.semaphore_signal(barrier, inc=1, device_id=(mate,), device_id_type=pl.DeviceIdType.MESH)
-    pl.semaphore_wait(barrier, 1)
-
-    def load_z(chunk):
-        return pltpu.make_async_copy(gated_ref.at[:, pl.ds(pl.multiple_of(chunk * width, width), width)], z_buf, z_sem)
-
-    if with_down:
-        load_z(0).start()
-
-    kinds = (0, 1, 2) if with_down else (0, 1)
-
-    def sends(kind, chunk):
+    for chunk in range(chunks):
+        for kind in range(2):
+            for piece, device in zip(pieces[:8], devices):
+                pltpu.make_async_copy(
+                    piece.at[pl.ds((kind * chunks + chunk) * depth, depth), :],
+                    w_ff1.at[pl.ds(pl.multiple_of(device * depth, 16), depth), pl.ds((2 * chunk + kind) * width, width)],
+                    w1_sem.at[chunk]).start()
+    greet(mate)
+
+    def sends(chunk):
         copies = []
-        for index in range(4 if kind < 2 else 1):
-            rows = depth if kind < 2 else deep
-            start = pl.multiple_of((2 * index + 1 - core) * rows, 16)
-            if kind < 2:
-                block = kind * chunks + chunk
-                slot = slot_of(index, True)
-                dst = recv1.at[block, pl.ds(pl.multiple_of(slot * rows, 16), rows), :]
-            else:
-                dst = recv2.at[chunk]
+        for other in range(4):
+            start = pl.multiple_of((2 * other + 1 - core) * depth, 16)
+            to = pl.multiple_of(mate_slot(other) * depth, 16)
             copies.append(pltpu.make_async_remote_copy(
-                src_ref=tile.at[kind, pl.ds(start, rows), :], dst_ref=dst, send_sem=send_sem.at[kind, index],
-                recv_sem=recv_sem1.at[block, index] if kind < 2 else recv_sem2.at[chunk],
-                device_id=(mate,), device_id_type=pl.DeviceIdType.MESH))
+                src_ref=tile.at[pl.ds(start, depth), :], dst_ref=recv.at[chunk, pl.ds(to, depth), :], send_sem=send_sem.at[other],
+                recv_sem=recv_sem.at[chunk, other], device_id=(mate,), device_id_type=pl.DeviceIdType.MESH))
         return copies
 
-    def wait_write(kind):
-        pltpu.make_async_copy(obuf.at[kind], obuf.at[kind], out_sem.at[kind]).wait()
-
-    def finish(kind, chunk, first):
-        for copy in sends(kind, chunk):
+    def wait_write():
+        pltpu.make_async_copy(obuf, obuf, out_sem).wait()
+
+    def finish(chunk, first):
+        for copy in sends(chunk):
             copy.wait_recv()
 
         @pl.when(jnp.logical_not(first))
         def _():
-            wait_write(kind)
-
-        if kind < 2:
-            block = kind * chunks + chunk
-            for slot in range(4):
-                start = pl.multiple_of((2 * chip_in(slot) + core) * depth, 16)
-                rows = slice(slot * depth, (slot + 1) * depth)
-                obuf[kind, rows, :] = tile[kind, pl.ds(start, depth), :] + recv1[block, rows, :]
-            for slot in range(4):
-                ref = keep1 if slot < 2 else far1
-                row = pl.multiple_of((slot % 2) * 8 * depth + block * depth, 16)
-                pltpu.make_async_copy(obuf.at[kind, pl.ds(slot * depth, depth), :], ref.at[pl.ds(row, depth), :],
-                                      out_sem.at[kind]).start()
-        else:
-            obuf[kind] = tile[kind, pl.ds(pl.multiple_of(core * deep, 16), deep), :] + recv2[chunk]
-            slot = slot_of(chunk, False)
-            row = pl.multiple_of(lax.rem(slot, 2) * deep, 16)
-            for branch, ref in enumerate((keep2, far2)):
-                @pl.when(slot // 2 == branch)
-                def _():
-                    pltpu.make_async_copy(obuf.at[kind], ref.at[pl.ds(row, deep), :], out_sem.at[kind]).start()
-        for copy in sends(kind, chunk):
+            wait_write()
+
+        for slot in range(4):
+            start = pl.multiple_of((2 * own_chip(slot) + core) * depth, 16)
+            rows = slice(slot * depth, (slot + 1) * depth)
+            obuf[rows, :] = tile[pl.ds(start, depth), :] + recv[chunk, rows, :]
+        for slot in range(4):
+            ref = keep_ref if slot < 2 else far_ref
+            for kind in range(2):
+                row = pl.multiple_of((slot % 2) * 8 * depth + (kind * chunks + chunk) * depth, 16)
+                pltpu.make_async_copy(obuf.at[pl.ds(slot * depth, depth), pl.ds(kind * width, width)], ref.at[pl.ds(row, depth), :],
+                                      out_sem).start()
+        for copy in sends(chunk):
             copy.wait_send()
 
     load_grad.wait()
     grad_bf[...] = grad[...].astype(BF16)
     load_norm.wait()
-    turned[...] = d_a[...].T
+    turned[...] = d_both[:, 0:width].T
     acc[...] = jnp.zeros_like(acc)
     bias_ref[...] = jnp.zeros_like(bias_ref)
     vec_ref[...] = jnp.zeros_like(vec_ref)
     wait_load(w_ff2, w2_sem)
 
     def one_chunk(chunk, carry):
-        for block in (chunk, chunks + chunk):
-            ref = w_ff1.at[:, pl.ds(0, width)]
-            pltpu.make_async_copy(ref, ref, w1_sem.at[block]).wait()
-        hidden = pl.multiple_of(chunk * width, width)
-
-        def one_step(step, carry):
-            index = chunk * steps + step
-            even = lax.rem(index, 2)
-            rows = pl.ds(pl.multiple_of(step * each, each), each)
-            d_gated = dot_nt(grad_bf[rows, :], w_ff2[pl.ds(hidden, width), :])
-            for copy in parts(index):
-                copy.wait()
-            total = acc[rows, :]
-            for base, saved, kept in ((0, part_a, d_a), (half, part_g, d_g)):
-                columns = pl.ds(pl.multiple_of(base + hidden, 2 * HEAD), width)
-                d_part = d_gated * saved[even]
-                bias_ref[0:1, columns] += jnp.sum(d_part, axis=0, keepdims=True)
-                d_part = d_part.astype(BF16)
-                kept[rows, :] = d_part
-                total = total + dot_nt(d_part, w_ff1[:, columns])
-            acc[rows, :] = total
-
-            @pl.when(index + 2 < chunks * steps)
-            def _():
-                for copy in parts(index + 2):
-                    copy.start()
-
-            return carry
-
-        lax.fori_loop(0, steps, one_step, 0)
-        before = jnp.maximum(chunk - 1, 0)
-        for kind in kinds:
-            @pl.when(chunk > 0)
-            def _():
-                finish(kind, before, chunk == 1)
-
-            if kind < 2:
-                tile[kind] = dot_nn(turned[...], (d_a, d_g)[kind][...])
-            else:
-                load_z(chunk).wait()
-                z_turned[...] = z_buf[...].T
-
-                @pl.when(chunk + 1 < chunks)
-                def _():
-                    load_z(chunk + 1).start()
-
-                tile[kind] = dot_nn(z_turned[...], grad_bf[...])
-            if kind > 0:
-                for copy in sends(kind - 1, chunk):
-                    copy.start()
-        for copy in sends(kinds[-1], chunk):
+        w_pair = w_ff1.at[:, pl.ds(pl.multiple_of(chunk * 2 * width, width), 2 * width)]
+        pltpu.make_async_copy(w_pair, w_pair, w1_sem.at[chunk]).wait()
+        for copy in parts(chunk):
+            copy.wait()
+
+        @pl.when(chunk + 1 < chunks)
+        def _():
+            for copy in parts(chunk + 1):
+                copy.start()
+
+        even = lax.rem(chunk, 2)
+        w_down = w_ff2.at[pl.ds(pl.multiple_of(chunk * width, width), width), :]
+        sums = [0.0, 0.0]
+        ahead = dot_nt(grad_bf[0:FF_ROWS, :], w_down[...])
+        for start in range(0, count, FF_ROWS):
+            rows = slice(start, start + FF_ROWS)
+            d_gated = ahead
+            if start + FF_ROWS < count:
+                ahead = dot_nt(grad_bf[start + FF_ROWS:start + 2 * FF_ROWS, :], w_down[...])
+            for kind, saved in enumerate((part_a, part_g)):
+                d_part = d_gated * saved[even, rows, :]
+                sums[kind] = sums[kind] + jnp.sum(d_part, axis=0, keepdims=True)
+                d_both[rows, kind * width:(kind + 1) * width] = d_part.astype(BF16)
+            acc[rows, :] += dot_nt(d_both[rows, :], w_pair[...])
+        for kind in range(2):
+            bias_ref[0:1, pl.ds(pl.multiple_of(kind * half + chunk * width, 2 * HEAD), width)] += sums[kind]
+
+        @pl.when(chunk > 0)
+        def _():
+            finish(jnp.maximum(chunk - 1, 0), chunk == 1)
+
+        tile[...] = dot_nn(turned[...], d_both[...])
+        for copy in sends(chunk):
             copy.start()
         return carry
 
     lax.fori_loop(0, chunks, one_chunk, 0)
-    load_h(0).start()
-    load_h(1).start()
+    steps = count // STEP
     for step in range(steps):
-        rows = slice(step * each, (step + 1) * each)
-        load_h(step).wait()
+        load_h(step).start()
+    pltpu.make_async_copy(part_a.at[0], part_a.at[0], part_sem.at[0, 0]).wait()
+    for step in range(steps):
+        rows = slice(step * STEP, (step + 1) * STEP)
         mine = grad[rows, :].astype(F32)
-        d_res, g_gain, g_shift = norm_back(part_a[step % 2], rows_ref[4:5, :], acc[rows, :])
-        if step + 2 < steps:
-            load_h(step + 2).start()
+        d_res, g_gain, g_shift = norm_back(part_a[0, rows, :], rows_ref[4:5, :], acc[rows, :])
         acc[rows, :] = mine + d_res
-        pltpu.make_async_copy(acc.at[pl.ds(step * each, each), :], out_ref.at[pl.ds(step * each, each), :], in_sem.at[0]).start()
+        pltpu.make_async_copy(acc.at[pl.ds(step * STEP, STEP), :], out_ref.at[pl.ds(step * STEP, STEP), :], in_sem.at[0]).start()
         for at, row in enumerate((g_gain, g_shift, jnp.sum(mine, axis=0, keepdims=True))):
             vec_ref[at:at + 1, :] += row
-    for kind in kinds:
-        finish(kind, chunks - 1, False)
-    for kind in kinds:
-        wait_write(kind)
+    finish(chunks - 1, False)
+    wait_write()
     pltpu.make_async_copy(acc, out_ref, in_sem.at[0]).wait()
 
 
-def ff_grads(kind, grad, save_a, save_g, norm, h, rows, gated, pieces, offset):
+def ff_grads(kind, grad, save_a, save_g, norm, h, rows, pieces, offset):
     count, width = h.shape
     half = save_a.shape[1]
-    down = gated is not None
     vmem = pl.BlockSpec(memory_space=pltpu.VMEM)
-    big, small = shape(2 * width, width, F32), shape(half // 4, width, F32)
+    big = shape(2 * width, width, F32)
     dma = pltpu.SemaphoreType.DMA
-    scratch = [pltpu.VMEM((count, width), grad.dtype), pltpu.VMEM((count, width), BF16), pltpu.VMEM((width, count), BF16),
-               pltpu.VMEM((count, width), F32), pltpu.VMEM((2, STEP, width), F32), pltpu.VMEM((2, STEP, width), F32),
-               pltpu.VMEM((count, width), BF16), pltpu.VMEM((count, width), BF16), pltpu.VMEM((width, 2 * half), BF16),
-               pltpu.VMEM((half, width), BF16), pltpu.VMEM((2 + down, width, width), F32), pltpu.VMEM((8, width // 2, width), F32),
-               pltpu.VMEM((2 + down, width // 2, width), F32), dma((2,)), dma((2, 2)), dma((8,)), dma, dma((3,)), dma((3, 4)), dma((8, 4))]
-    if down:
-        scratch += [pltpu.VMEM((count, width), BF16), pltpu.VMEM((width, count), BF16), pltpu.VMEM((4, half // 8, width), F32),
-                    dma, dma((4,))]
+    saved = pltpu.VMEM((2, count, width), F32)
     return pl.pallas_call(
-        functools.partial(ff_grad_kernel, offset, down),
-        in_specs=[ANY] * 5 + [vmem] + [ANY] * (16 + down),
-        out_specs=[ANY, vmem, vmem, ANY, ANY] + [ANY, ANY] * down,
-        out_shape=[shape(count, width, F32), shape(8, width, F32), shape(8, 2 * half, F32), big, big] + [small, small] * down,
-        scratch_shapes=scratch,
-        cost_estimate=pl.CostEstimate(flops=count * width * half * (14 if down else 10), bytes_accessed=int(6e7), transcendentals=0),
-        compiler_params=pltpu.CompilerParams(collective_id=kind, has_side_effects=True, vmem_limit_bytes=VMEM_MOST))(grad, save_a, save_g, norm, h, rows, *([gated] if down else []), *pieces)
+        functools.partial(ff_grad_kernel, offset), in_specs=[ANY] * 5 + [vmem] + [ANY] * 16, out_specs=[ANY, vmem, vmem, ANY, ANY],
+        out_shape=[shape(count, width, F32), shape(8, width, F32), shape(8, 2 * half, F32), big, big],
+        scratch_shapes=[pltpu.VMEM((count, width), grad.dtype), pltpu.VMEM((count, width), BF16), pltpu.VMEM((width, count), BF16),
+                        pltpu.VMEM((count, width), F32), saved, saved, pltpu.VMEM((count, 2 * width), BF16),
+                        pltpu.VMEM((width, 2 * half), BF16), pltpu.VMEM((half, width), BF16), pltpu.VMEM((width, 2 * width), F32),
+                        pltpu.VMEM((4, width // 2, 2 * width), F32), pltpu.VMEM((width // 2, 2 * width), F32),
+                        dma((2,)), dma((2, 2)), dma((4,)), dma, dma, dma((4,)), dma((4, 4))],
+        cost_estimate=pl.CostEstimate(flops=count * width * half * 10, bytes_accessed=int(6e7), transcendentals=0),
+        compiler_params=pltpu.CompilerParams(collective_id=kind, has_side_effects=True, vmem_limit_bytes=VMEM_MOST))(grad, save_a, save_g, norm, h, rows, *pieces)
 
 
 def finish_scatter(far, keep, n_dev):
@@ -1026,8 +1070,6 @@
 
         grad = cot_out.reshape(count, width)
         results, vec_grads = [None] * blocks, [None] * blocks
-        every = tuple(range(n_dev // 2))
-        by_column = lambda x, y, columns, first: [(x, 0, y, c * width, first + c * depth, depth, every) for c in range(columns)]
         for layer in reversed(range(blocks)):
             turn = blocks - 1 - layer
             rows, group = rows_all[layer], groups[3 * layer:3 * layer + 2]
@@ -1036,20 +1078,17 @@
             def reduce(pair):
                 return finish_scatter(pair[0], pair[1], n_dev)
 
-            if turn == 0:
-                r_ff2 = reduce(weight_grads(1, (gated, grad.astype(BF16)),
-                                               [(0, c * width, 1, 0, 0, half // n_dev, (c,)) for c in range(half // width)], half // n_dev))
-            grad, vec3, vec_b1, *pairs = ff_grads(5 + min(turn, 1), grad, save_a, save_g, norm3, h2, rows,
-                                                  gated if turn > 0 else None, ff_groups[layer], ff_offsets[layer])
-            r_ff1 = reduce(pairs[:2])
-            if turn > 0:
-                r_ff2 = reduce(pairs[2:])
-            grad_bf, d_query, d_kv, grad, vec2 = cross_backward(grad, query, kv, h1, rows, group[1], tokens, valid)
-            r_cross = reduce(weight_grads(3, (norm2, d_query, mix2, grad_bf),
-                                             by_column(0, 1, 1, 0) + by_column(2, 3, 1, depth), 2 * depth, (d_kv, ctx_mine, ctx_other)))
-            grad_bf, d_qkv, grad, vec1 = self_backward(grad, qkv, h0, rows, group[0], tokens, BF16 if layer == 0 else F32)
-            r_self = reduce(weight_grads(4, (norm1, d_qkv, mix1, grad_bf),
-                                            by_column(0, 1, 3, 0) + by_column(2, 3, 1, 3 * depth), 4 * depth))
+            r_ff2 = reduce(weight_grads(1, (gated, grad.astype(BF16)),
+                                           [(0, c * width, 1, 0, 0, half // n_dev, (c,)) for c in range(half // width)], half // n_dev))
+            grad, vec3, vec_b1, *pair = ff_grads(5 + turn, grad, save_a, save_g, norm3, h2, rows, ff_groups[layer],
+                                                 ff_offsets[layer])
+            r_ff1 = reduce(pair)
+            grad, vec2, *pair = cross_backward(grad, query, kv, h1, rows, norm2, mix2, ctx_mine, ctx_other, group[1],
+                                               tokens, valid)
+            r_cross = reduce(pair)
+            grad, vec1, *pair = self_backward(8 + turn, grad, qkv, h0, rows, norm1, mix1, group[0], tokens,
+                                              BF16 if layer == 0 else F32)
+            r_self = reduce(pair)
             side = lambda array, blocks_of: jnp.concatenate(jnp.split(array, blocks_of, 0), 1)
             results[layer] = [side(r_self[:3 * depth], 3), r_self[3 * depth:], r_cross[:depth], side(r_cross[2 * depth:], 2), r_cross[depth:2 * depth],
                               side(r_ff1, 8), r_ff2]

time: 975 us -> 898 us (0.921)
  Pallas kernels: 521 us -> 445 us
    pallas_call x5 -> x2, Pallas kernels: 79.3 us -> 34.2 us  [weight_grads(): pl.pallas_call(functools.partial(grad_kernel, tiles, group_rows, len(arra...]
    pallas_call x2, Pallas kernels: 127 us -> 96.7 us  [ff_grads(): pl.pallas_call(functools.partial(ff_grad_kernel, offset), in_specs=[ANY]...]
    unnamed x105 -> x112, local copies, waits for them, and re-layouts: 26.9 us -> 27.6 us
  transfers between devices with their start and end apart: 69 -> 69, of which waited for: 19 -> 19; matrix products, arithmetic and copies ran while one was open for 4% -> 4% of each run, Pallas kernels for 26% -> 28%
where the time goes in v4:
time: 898 us; the launch traced here: 890 us
  Pallas kernels  445 us (50%)
  waiting for transfers between devices  337 us (38%)
  starting transfers between devices  56.3 us (6%)
  local copies, waits for them, and re-layouts  32.3 us (4%)
  other arithmetic  17.1 us (2%)
    ppermute x69, waiting for transfers between devices, permute(): return lax.ppermute(array, AXIS, perm)  337 us
    pallas_call x2, Pallas kernels, ff_grads(): pl.pallas_call(functools.partial(ff_grad_kernel, offset), in_specs=[ANY]...  96.7 us
    pallas_call x2, Pallas kernels, self_backward(): call(functools.partial(self_backward_kernel, STEP // tokens, tokens), cou...  82.8 us
    pallas_call x2, Pallas kernels, cross_backward(): call(functools.partial(cross_backward_kernel, STEP // tokens, tokens, val...  56.8 us
    ppermute x69, starting transfers between devices, permute(): return lax.ppermute(array, AXIS, perm)  56.3 us
    pallas_call x2, Pallas kernels, self_forward(): call(functools.partial(self_forward_kernel, STEP // tokens, tokens), coun...  41 us
    pallas_call x2, Pallas kernels, cross_forward(): call(functools.partial(cross_forward_kernel, STEP // tokens, tokens, vali...  39.1 us
    pallas_call x2, Pallas kernels, weight_grads(): pl.pallas_call(functools.partial(grad_kernel, tiles, group_rows, len(arra...  34.2 us
  transfers between devices with their start and end apart: 69, of which 19 were waited for; matrix products, arithmetic and copies ran while one was open for 4% of the time, Pallas kernels for 28%

profile of v4, /device:TPU:0, one launch (start us, length us, event | category | flops | bytes accessed | tf_op | source)
XLA Modules:
  0.0 889.9 jit_solution(16352511575328336751)
XLA Ops:
  0.7 1.6 copy.48
  2.3 2.0 copy.47
  4.3 1.8 pack.10.refs_0_
  6.9 2.5 collective-permute-start.22
  9.4 1.5 collective-permute-start.21
  12.0 1.9 pack.7.refs_0_
  17.0 1.8 pack.13.refs_0_.refs_8_
  22.1 1.5 collective-permute-start
  23.6 12.8 %collective-permute-done.43.refs_2_.refs_10_ = bf16[320,640]{1,0:T(8,128)(2,1)} collective-permute-done((bf16[320,640]{1,0:T(8,128)(2,1)}, bf16[320,640]{1,0:T(8,128)(2,1)}, u32[]{:S(2)}, u32[]{:S(2)}) %collective-permute-start.43) | collective-permute-done | bytes 409632 | tf_op jit(solution)/shard_map/ppermute | solution.py:80
  36.9 2.1 pack.12.refs_0_
  39.1 2.5 collective-permute-start.36
  41.5 1.5 collective-permute-start.35
  43.1 1.7 copy_bitcast_fusion.4
  46.0 2.1 pack.8.refs_0_
  48.2 2.0 collective-permute-start.8
  50.2 15.1 %collective-permute-done.23.refs_3_ = bf16[320,640]{1,0:T(8,128)(2,1)} collective-permute-done((bf16[320,640]{1,0:T(8,128)(2,1)}, bf16[320,640]{1,0:T(8,128)(2,1)}, u32[]{:S(2)}, u32[]{:S(2)}) %collective-permute-start.23) | collective-permute-done | bytes 409632 | tf_op jit(solution)/shard_map/ppermute | solution.py:80
  66.4 2.1 pack.11.refs_0_
  68.6 2.5 pack.9.refs_0_.refs_8_
  72.3 1.7 collective-permute-start.29
  74.0 7.4 collective-permute-done.8.refs_2_
  82.1 5.6 collective-permute-done.7.refs_1_
  87.7 2.0 collective-permute-start.2
  89.7 10.0 %collective-permute-done.29.refs_2_ = bf16[672,640]{1,0:T(8,128)(2,1)S(1)} collective-permute-done((bf16[672,640]{1,0:T(8,128)(2,1)S(1)}, bf16[672,640]{1,0:T(8,128)(2,1)S(1)}, u32[]{:S(2)}, u32[]{:S(2)}) %collective-permute-start.29) | collective-permute-done | bytes 860192 | tf_op jit(solution)/shard_map/ppermute | solution.py:80
  99.8 2.3 collective-permute-start.9
  102.1 26.3 %collective-permute-done.28.refs_1_ = bf16[672,640]{1,0:T(8,128)(2,1)S(1)} collective-permute-done((bf16[672,640]{1,0:T(8,128)(2,1)S(1)}, bf16[672,640]{1,0:T(8,128)(2,1)S(1)}, u32[]{:S(2)}, u32[]{:S(2)}) %collective-permute-start.28) | collective-permute-done | bytes 860192 | tf_op jit(solution)/shard_map/ppermute | solution.py:80
  130.3 2.0 collective-permute-start.15
  133.9 3.8 context.1
  137.7 1.9 vec_sum.1
  141.8 5.5 collective-permute-done.15.refs_2_.refs_10_
  147.9 12.6 %collective-permute-done.16.refs_3_.refs_11_ = bf16[960,640]{1,0:T(8,128)(2,1)} collective-permute-done((bf16[960,640]{1,0:T(8,128)(2,1)}, bf16[960,640]{1,0:T(8,128)(2,1)}, u32[]{:S(2)}, u32[]{:S(2)}) %collective-permute-start.16) | collective-permute-done | bytes 1228832 | tf_op jit(solution)/shard_map/ppermute | solution.py:80
  161.2 2.0 collective-permute-start.30
  163.2 20.1 %shard_map.186 = (bf16[1536,640]{1,0:T(8,128)(2,1)}, bf16[1536,1920]{1,0:T(8,128)(2,1)}, bf16[1536,640]{1,0:T(8,128)(2,1)}, f32[1536,640]{1,0:T(8,128)}) custom-call(bf16[1536,640]{1,0:T(8,128)(2,1)} %bitcast.116, f32[16,640]{1,0:T(8,128)} %get-tuple-element.163.rows_ref, bf16[368,640]{1,0:T(8,128)(2,1)} %pack.7.refs_0_, bf16[368,640]{1,0:T(8,128)(2,1)} %copy-done.20, ...), custom_call_target="tpu_custom_call" | custom-call | flops 6039797760 | bytes 20000000 | tf_op jit(solution)/shard_map/pallas_call | solution.py:601
  183.3 19.6 %shard_map.187 = (bf16[1536,640]{1,0:T(8,128)(2,1)}, bf16[1536,640]{1,0:T(8,128)(2,1)}, bf16[480,1280]{1,0:T(8,128)(2,1)}, bf16[1536,640]{1,0:T(8,128)(2,1)}, f32[1536,640]{1,0:T(8,128)}) custom-call(f32[1536,640]{1,0:T(8,128)} %get-tuple-element.79.h_ref, f32[16,640]{1,0:T(8,128)} %get-tuple-element.163.rows_ref, ...), custom_call_target="tpu_custom_call" | custom-call | flops 5536481280 | bytes 20000000 | tf_op jit(solution)/shard_map/pallas_call | solution.py:613
  204.7 31.7 %shard_map.188 = (bf16[1536,640]{1,0:T(8,128)(2,1)}, bf16[1536,2560]{1,0:T(8,128)(2,1)}, f32[1536,2560]{1,0:T(8,128)}, f32[1536,2560]{1,0:T(8,128)}, f32[1536,640]{1,0:T(8,128)}) custom-call(f32[1536,640]{1,0:T(8,128)} %get-tuple-element.84.h_ref, f32[16,640]{1,0:T(8,128)} %get-tuple-element.163.rows_ref, f32[1,5120]{1,0:T(1,128)} %bitcast.115, ...), custom_call_target="tpu_custom_call" | custom-call | flops 15099494400 | bytes 60000000 | tf_op jit(solution)/shard_map/pallas_call | solution.py:627
  237.4 20.9 %shard_map.189 = (bf16[1536,640]{1,0:T(8,128)(2,1)}, bf16[1536,1920]{1,0:T(8,128)(2,1)}, bf16[1536,640]{1,0:T(8,128)(2,1)}, f32[1536,640]{1,0:T(8,128)}) custom-call(f32[1536,640]{1,0:T(8,128)} %get-tuple-element.87.h_ref, f32[16,640]{1,0:T(8,128)} %get-tuple-element.162.rows_ref, bf16[320,640]{1,0:T(8,128)(2,1)} %pack.10.refs_0_, ...), custom_call_target="tpu_custom_call" | custom-call | flops 6039797760 | bytes 20000000 | tf_op jit(solution)/shard_map/pallas_call | solution.py:601
  259.4 19.5 %shard_map.190 = (bf16[1536,640]{1,0:T(8,128)(2,1)}, bf16[1536,640]{1,0:T(8,128)(2,1)}, bf16[480,1280]{1,0:T(8,128)(2,1)}, bf16[1536,640]{1,0:T(8,128)(2,1)}, f32[1536,640]{1,0:T(8,128)}) custom-call(f32[1536,640]{1,0:T(8,128)} %get-tuple-element.88.h_ref, f32[16,640]{1,0:T(8,128)} %get-tuple-element.162.rows_ref, ...), custom_call_target="tpu_custom_call" | custom-call | flops 5536481280 | bytes 20000000 | tf_op jit(solution)/shard_map/pallas_call | solution.py:613
  280.5 28.3 %shard_map.191 = (bf16[1536,640]{1,0:T(8,128)(2,1)}, bf16[1536,2560]{1,0:T(8,128)(2,1)}, f32[1536,2560]{1,0:T(8,128)}, f32[1536,2560]{1,0:T(8,128)}) custom-call(f32[1536,640]{1,0:T(8,128)} %get-tuple-element.89.h_ref, f32[16,640]{1,0:T(8,128)} %get-tuple-element.162.rows_ref, f32[1,5120]{1,0:T(1,128)} %bitcast.114, bf16[640,640]{1,0:T(8,128)(2,1)} %pack.12.refs_0_, ...), custom_call_target="tpu_custom_call" | custom-call | flops 10066329600 | bytes 50000000 | tf_op jit(solution)/shard_map/pallas_call | solution.py:640
  309.9 48.1 %shard_map.193 = (f32[1536,640]{1,0:T(8,128)}, f32[8,640]{1,0:T(8,128)}, f32[8,5120]{1,0:T(8,128)}, f32[1280,640]{1,0:T(8,128)}, f32[1280,640]{1,0:T(8,128)}) custom-call(bf16[1536,640]{1,0:T(8,128)(2,1)} %bitcast.118, f32[1536,2560]{1,0:T(8,128)} %get-tuple-element.91.save_a, f32[1536,2560]{1,0:T(8,128)} %get-tuple-element.92.save_g, ...), custom_call_target="tpu_custom_call" | custom-call | flops 25165824000 | bytes 60000000 | tf_op jit(solution)/shard_map/pallas_call | solution.py:992
  358.0 28.4 %shard_map.194 = (f32[1536,640]{1,0:T(8,128)}, f32[8,640]{1,0:T(8,128)}, f32[1344,640]{1,0:T(8,128)}, f32[1344,640]{1,0:T(8,128)}) custom-call(f32[1536,640]{1,0:T(8,128)} %get-tuple-element.94.grad_ref, bf16[1536,640]{1,0:T(8,128)(2,1)} %get-tuple-element.95.query_ref, bf16[480,1280]{1,0:T(8,128)(2,1)} %get-tuple-element.96.kv_ref, ...), custom_call_target="tpu_custom_call" | custom-call | flops 8975810560 | bytes 20000000 | tf_op jit(solution)/shard_map/pallas_call | solution.py:668
  386.5 41.8 %shard_map.195 = (f32[1536,640]{1,0:T(8,128)}, f32[8,640]{1,0:T(8,128)}, f32[640,640]{1,0:T(8,128)}, f32[640,640]{1,0:T(8,128)}) custom-call(f32[1536,640]{1,0:T(8,128)} %get-tuple-element.101.grad_ref, bf16[1536,1920]{1,0:T(8,128)(2,1)} %get-tuple-element.102.qkv_ref, f32[1536,640]{1,0:T(8,128)} %get-tuple-element.87.h_ref, ...), custom_call_target="tpu_custom_call" | custom-call | flops 12582912000 | bytes 30000000 | tf_op jit(solution)/shard_map/pallas_call | solution.py:686
  428.3 48.6 %shard_map.196 = (f32[1536,640]{1,0:T(8,128)}, f32[8,640]{1,0:T(8,128)}, f32[8,5120]{1,0:T(8,128)}, f32[1280,640]{1,0:T(8,128)}, f32[1280,640]{1,0:T(8,128)}) custom-call(f32[1536,640]{1,0:T(8,128)} %get-tuple-element.105.grad_ref, f32[1536,2560]{1,0:T(8,128)} %get-tuple-element.106.save_a, f32[1536,2560]{1,0:T(8,128)} %get-tuple-element.107.save_g, ...), custom_call_target="tpu_custom_call" | custom-call | flops 25165824000 | bytes 60000000 | tf_op jit(solution)/shard_map/pallas_call | solution.py:992
  476.9 28.4 %shard_map.197 = (f32[1536,640]{1,0:T(8,128)}, f32[8,640]{1,0:T(8,128)}, f32[1344,640]{1,0:T(8,128)}, f32[1344,640]{1,0:T(8,128)}) custom-call(f32[1536,640]{1,0:T(8,128)} %get-tuple-element.109.grad_ref, bf16[1536,640]{1,0:T(8,128)(2,1)} %get-tuple-element.110.query_ref, bf16[480,1280]{1,0:T(8,128)(2,1)} %get-tuple-element.111.kv_ref, ...), custom_call_target="tpu_custom_call" | custom-call | flops 8975810560 | bytes 20000000 | tf_op jit(solution)/shard_map/pallas_call | solution.py:668
  505.4 41.0 %shard_map.198 = (bf16[1536,640]{1,0:T(8,128)(2,1)}, f32[8,640]{1,0:T(8,128)}, f32[640,640]{1,0:T(8,128)}, f32[640,640]{1,0:T(8,128)}) custom-call(f32[1536,640]{1,0:T(8,128)} %get-tuple-element.114.grad_ref, bf16[1536,1920]{1,0:T(8,128)(2,1)} %get-tuple-element.115.qkv_ref, bf16[1536,640]{1,0:T(8,128)(2,1)} %bitcast.117, ...), custom_call_target="tpu_custom_call" | custom-call | flops 12582912000 | bytes 30000000 | tf_op jit(solution)/shard_map/pallas_call | solution.py:686
  546.4 1.8 vec_pack.1
  549.3 17.2 %shard_map.200 = (f32[640,640]{1,0:T(8,128)}, f32[640,640]{1,0:T(8,128)}) custom-call(bf16[1536,2560]{1,0:T(8,128)(2,1)} %get-tuple-element.90.gated_ref.refs_0_, bf16[1536,640]{1,0:T(8,128)(2,1)} %bitcast.119), custom_call_target="tpu_custom_call" | custom-call | flops 5033164800 | bytes 20000000 | tf_op jit(solution)/shard_map/pallas_call | solution.py:784
  566.5 1.5 convert_element_type.7.refs_1_
  571.3 17.1 %shard_map.199 = (f32[640,640]{1,0:T(8,128)}, f32[640,640]{1,0:T(8,128)}) custom-call(bf16[1536,2560]{1,0:T(8,128)(2,1)} %get-tuple-element.131.refs_0_, bf16[1536,640]{1,0:T(8,128)(2,1)} %convert_element_type.7.refs_1_), custom_call_target="tpu_custom_call" | custom-call | flops 5033164800 | bytes 20000000 | tf_op jit(solution)/shard_map/pallas_call | solution.py:784
  589.2 19.0 %collective-permute-done.67 = f32[48,640]{1,0:T(8,128)S(1)} collective-permute-done((f32[48,640]{1,0:T(8,128)S(1)}, f32[48,640]{1,0:T(8,128)S(1)}, u32[]{:S(2)}, u32[]{:S(2)}) %collective-permute-start.67) | collective-permute-done | bytes 122912 | tf_op jit(solution)/shard_map/ppermute | solution.py:80
  609.4 12.2 %shard_map.192 = bf16[1536,640]{1,0:T(8,128)(2,1)} custom-call(f32[1536,640]{1,0:T(8,128)} %get-tuple-element.89.h_ref, f32[16,640]{1,0:T(8,128)} %get-tuple-element.162.rows_ref, bf16[1536,2560]{1,0:T(8,128)(2,1)} %get-tuple-element.90.gated_ref.refs_0_, bf16[320,640]{1,0:T(8,128)(2,1)} %pack.13.refs_0_.refs_8_, ...), custom_call_target="tpu_custom_call" | custom-call | flops 5033164800 | bytes 20000000 | tf_op jit(solution)/shard_map/pallas_call | solution.py:652
  632.7 14.4 %collective-permute-done.53 = f32[320,640]{1,0:T(8,128)S(1)} collective-permute-done((f32[320,640]{1,0:T(8,128)S(1)}, f32[320,640]{1,0:T(8,128)S(1)}, u32[]{:S(2)}, u32[]{:S(2)}) %collective-permute-start.53) | collective-permute-done | bytes 819232 | tf_op jit(solution)/shard_map/ppermute | solution.py:80
  649.3 15.4 %collective-permute-done.51 = f32[320,640]{1,0:T(8,128)S(1)} collective-permute-done((f32[320,640]{1,0:T(8,128)S(1)}, f32[320,640]{1,0:T(8,128)S(1)}, u32[]{:S(2)}, u32[]{:S(2)}) %collective-permute-start.51) | collective-permute-done | bytes 819232 | tf_op jit(solution)/shard_map/ppermute | solution.py:80
  667.0 18.8 %collective-permute-done.65 = f32[320,640]{1,0:T(8,128)S(1)} collective-permute-done((f32[320,640]{1,0:T(8,128)S(1)}, f32[320,640]{1,0:T(8,128)S(1)}, u32[]{:S(2)}, u32[]{:S(2)}) %collective-permute-start.65) | collective-permute-done | bytes 819232 | tf_op jit(solution)/shard_map/ppermute | solution.py:80
  688.2 3.6 collective-permute-done.58
  691.9 1.5 collective-permute-start.59
  694.5 1.7 copy.30
  696.1 10.8 %collective-permute-done.63 = f32[320,640]{1,0:T(8,128)S(1)} collective-permute-done((f32[320,640]{1,0:T(8,128)S(1)}, f32[320,640]{1,0:T(8,128)S(1)}, u32[]{:S(2)}, u32[]{:S(2)}) %collective-permute-start.63) | collective-permute-done | bytes 819232 | tf_op jit(solution)/shard_map/ppermute | solution.py:80
  708.4 2.4 copy.36
  710.8 39.2 %collective-permute-done.60 = f32[1280,640]{1,0:T(8,128)S(1)} collective-permute-done((f32[1280,640]{1,0:T(8,128)}, f32[1280,640]{1,0:T(8,128)S(1)}, u32[]{:S(2)}, u32[]{:S(2)}) %collective-permute-start.60) | collective-permute-done | bytes 3276832 | tf_op jit(solution)/shard_map/ppermute | solution.py:80
  751.3 53.0 %collective-permute-done.54 = f32[1344,640]{1,0:T(8,128)S(1)} collective-permute-done((f32[1344,640]{1,0:T(8,128)}, f32[1344,640]{1,0:T(8,128)S(1)}, u32[]{:S(2)}, u32[]{:S(2)}) %collective-permute-start.54) | collective-permute-done | bytes 3440672 | tf_op jit(solution)/shard_map/ppermute | solution.py:80
  805.8 53.9 %collective-permute-done.56 = f32[1344,640]{1,0:T(8,128)S(1)} collective-permute-done((f32[1344,640]{1,0:T(8,128)}, f32[1344,640]{1,0:T(8,128)S(1)}, u32[]{:S(2)}, u32[]{:S(2)}) %collective-permute-start.56) | collective-permute-done | bytes 3440672 | tf_op jit(solution)/shard_map/ppermute | solution.py:80
  861.6 1.7 fusion.2
  863.7 4.2 copy.35
  868.3 13.5 %collective-permute-done.57 = f32[672,640]{1,0:T(8,128)S(1)} collective-permute-done((f32[672,640]{1,0:T(8,128)S(1)}, f32[672,640]{1,0:T(8,128)S(1)}, u32[]{:S(2)}, u32[]{:S(2)}) %collective-permute-start.57) | collective-permute-done | bytes 1720352 | tf_op jit(solution)/shard_map/ppermute | solution.py:80
  882.7 3.5 copy.33
  (261 shorter events, 62.8 us)
Async XLA Ops:
  6.1 12.7 %collective-permute-start.24 = (bf16[320,640]{1,0:T(8,128)(2,1)}, bf16[320,640]{1,0:T(8,128)(2,1)}, u32[]{:S(2)}, u32[]{:S(2)}) collective-permute-start(bf16[320,640]{1,0:T(8,128)(2,1)} %pack.10.refs_0_), channel_id=1, source_target_pairs={{0,1},{1,0},{2,3},{3,2},{4,5},{5,4},{6,7},{7,6}} | collective-permute-start | bytes 1228808 | tf_op jit(solution)/shard_map/ppermute | solution.py:80
  6.9 13.4 %collective-permute-start.22 = (bf16[320,640]{1,0:T(8,128)(2,1)}, bf16[320,640]{1,0:T(8,128)(2,1)}, u32[]{:S(2)}, u32[]{:S(2)}) collective-permute-start(bf16[320,640]{1,0:T(8,128)(2,1)} %pack.10.refs_0_), channel_id=1, source_target_pairs={{0,2},{1,5},{2,0},{3,7},{4,6},{5,1},{6,4},{7,3}} | collective-permute-start | bytes 1228808 | tf_op jit(solution)/shard_map/ppermute | solution.py:80
  13.9 25.2 %collective-permute-start.3 = (bf16[368,640]{1,0:T(8,128)(2,1)}, bf16[368,640]{1,0:T(8,128)(2,1)S(1)}, u32[]{:S(2)}, u32[]{:S(2)}) collective-permute-start(bf16[368,640]{1,0:T(8,128)(2,1)} %pack.7.refs_0_), channel_id=1, source_target_pairs={{0,1},{1,0},{2,3},{3,2},{4,5},{5,4},{6,7},{7,6}} | collective-permute-start | bytes 1413128 | tf_op jit(solution)/shard_map/ppermute | solution.py:80
  14.0 27.6 %collective-permute-start.1 = (bf16[368,640]{1,0:T(8,128)(2,1)}, bf16[368,640]{1,0:T(8,128)(2,1)S(1)}, u32[]{:S(2)}, u32[]{:S(2)}) collective-permute-start(bf16[368,640]{1,0:T(8,128)(2,1)} %pack.7.refs_0_), channel_id=1, source_target_pairs={{0,2},{1,5},{2,0},{3,7},{4,6},{5,1},{6,4},{7,3}} | collective-permute-start | bytes 1413128 | tf_op jit(solution)/shard_map/ppermute | solution.py:80
  18.8 17.6 %collective-permute-start.43 = (bf16[320,640]{1,0:T(8,128)(2,1)}, bf16[320,640]{1,0:T(8,128)(2,1)}, u32[]{:S(2)}, u32[]{:S(2)}) collective-permute-start(bf16[320,640]{1,0:T(8,128)(2,1)} %pack.13.refs_0_.refs_8_), channel_id=1, source_target_pairs={{0,2},{1,5},{2,0},{3,7},{4,6},{5,1},{6,4},{7,3}} | collective-permute-start | bytes 1228808 | tf_op jit(solution)/shard_map/ppermute | solution.py:80
  20.3 16.1 %collective-permute-start.42 = (bf16[320,640]{1,0:T(8,128)(2,1)}, bf16[320,640]{1,0:T(8,128)(2,1)}, u32[]{:S(2)}, u32[]{:S(2)}) collective-permute-start(bf16[320,640]{1,0:T(8,128)(2,1)} %pack.13.refs_0_.refs_8_), channel_id=1, source_target_pairs={{0,4},{1,3},{2,6},{3,1},{4,0},{5,7},{6,2},{7,5}} | collective-permute-start | bytes 1228808 | tf_op jit(solution)/shard_map/ppermute | solution.py:80
  22.1 26.1 %collective-permute-start = (bf16[368,640]{1,0:T(8,128)(2,1)S(1)}, bf16[368,640]{1,0:T(8,128)(2,1)S(1)}, u32[]{:S(2)}, u32[]{:S(2)}) collective-permute-start(bf16[368,640]{1,0:T(8,128)(2,1)S(1)} %copy-done.6), channel_id=1, source_target_pairs={{0,4},{1,3},{2,6},{3,1},{4,0},{5,7},{6,2},{7,5}} | collective-permute-start | bytes 1413128 | tf_op jit(solution)/shard_map/ppermute | solution.py:80
  39.1 29.5 %collective-permute-start.36 = (bf16[640,640]{1,0:T(8,128)(2,1)}, bf16[640,640]{1,0:T(8,128)(2,1)}, u32[]{:S(2)}, u32[]{:S(2)}) collective-permute-start(bf16[640,640]{1,0:T(8,128)(2,1)} %pack.12.refs_0_), channel_id=1, source_target_pairs={{0,2},{1,5},{2,0},{3,7},{4,6},{5,1},{6,4},{7,3}} | collective-permute-start | bytes 2457608 | tf_op jit(solution)/shard_map/ppermute | solution.py:80
  41.5 29.5 %collective-permute-start.35 = (bf16[640,640]{1,0:T(8,128)(2,1)}, bf16[640,640]{1,0:T(8,128)(2,1)}, u32[]{:S(2)}, u32[]{:S(2)}) collective-permute-start(bf16[640,640]{1,0:T(8,128)(2,1)} %pack.12.refs_0_), channel_id=1, source_target_pairs={{0,4},{1,3},{2,6},{3,1},{4,0},{5,7},{6,2},{7,5}} | collective-permute-start | bytes 2457608 | tf_op jit(solution)/shard_map/ppermute | solution.py:80
  48.1 24.1 %collective-permute-start.10 = (bf16[672,640]{1,0:T(8,128)(2,1)}, bf16[672,640]{1,0:T(8,128)(2,1)S(1)}, u32[]{:S(2)}, u32[]{:S(2)}) collective-permute-start(bf16[672,640]{1,0:T(8,128)(2,1)} %pack.8.refs_0_), channel_id=1, source_target_pairs={{0,1},{1,0},{2,3},{3,2},{4,5},{5,4},{6,7},{7,6}} | collective-permute-start | bytes 2580488 | tf_op jit(solution)/shard_map/ppermute | solution.py:80
  48.1 17.2 %collective-permute-start.23 = (bf16[320,640]{1,0:T(8,128)(2,1)}, bf16[320,640]{1,0:T(8,128)(2,1)}, u32[]{:S(2)}, u32[]{:S(2)}) collective-permute-start(bf16[320,640]{1,0:T(8,128)(2,1)} %collective-permute-done.21.refs_1_), channel_id=1, source_target_pairs={{0,2},{1,5},{2,0},{3,7},{4,6},{5,1},{6,4},{7,3}} | collective-permute-start | bytes 1228808 | tf_op jit(solution)/shard_map/ppermute | solution.py:80
  48.2 33.2 %collective-permute-start.8 = (bf16[672,640]{1,0:T(8,128)(2,1)}, bf16[672,640]{1,0:T(8,128)(2,1)}, u32[]{:S(2)}, u32[]{:S(2)}) collective-permute-start(bf16[672,640]{1,0:T(8,128)(2,1)} %pack.8.refs_0_), channel_id=1, source_target_pairs={{0,2},{1,5},{2,0},{3,7},{4,6},{5,1},{6,4},{7,3}} | collective-permute-start | bytes 2580488 | tf_op jit(solution)/shard_map/ppermute | solution.py:80
  65.3 22.3 %collective-permute-start.7 = (bf16[672,640]{1,0:T(8,128)(2,1)}, bf16[672,640]{1,0:T(8,128)(2,1)}, u32[]{:S(2)}, u32[]{:S(2)}) collective-permute-start(bf16[672,640]{1,0:T(8,128)(2,1)} %pack.8.refs_0_), channel_id=1, source_target_pairs={{0,4},{1,3},{2,6},{3,1},{4,0},{5,7},{6,2},{7,5}} | collective-permute-start | bytes 2580488 | tf_op jit(solution)/shard_map/ppermute | solution.py:80
  68.6 21.1 %collective-permute-start.31 = (bf16[672,640]{1,0:T(8,128)(2,1)}, bf16[672,640]{1,0:T(8,128)(2,1)}, u32[]{:S(2)}, u32[]{:S(2)}) collective-permute-start(bf16[672,640]{1,0:T(8,128)(2,1)} %pack.11.refs_0_), channel_id=1, source_target_pairs={{0,1},{1,0},{2,3},{3,2},{4,5},{5,4},{6,7},{7,6}} | collective-permute-start | bytes 2580488 | tf_op jit(solution)/shard_map/ppermute | solution.py:80
  71.0 61.3 %collective-permute-start.14 = (bf16[960,640]{1,0:T(8,128)(2,1)}, bf16[960,640]{1,0:T(8,128)(2,1)}, u32[]{:S(2)}, u32[]{:S(2)}) collective-permute-start(bf16[960,640]{1,0:T(8,128)(2,1)} %pack.9.refs_0_.refs_8_), channel_id=1, source_target_pairs={{0,4},{1,3},{2,6},{3,1},{4,0},{5,7},{6,2},{7,5}} | collective-permute-start | bytes 3686408 | tf_op jit(solution)/shard_map/ppermute | solution.py:80
  72.3 27.5 %collective-permute-start.29 = (bf16[672,640]{1,0:T(8,128)(2,1)S(1)}, bf16[672,640]{1,0:T(8,128)(2,1)S(1)}, u32[]{:S(2)}, u32[]{:S(2)}) collective-permute-start(bf16[672,640]{1,0:T(8,128)(2,1)S(1)} %copy-done.14), channel_id=1, source_target_pairs={{0,2},{1,5},{2,0},{3,7},{4,6},{5,1},{6,4},{7,3}} | collective-permute-start | bytes 2580488 | tf_op jit(solution)/shard_map/ppermute | solution.py:80
  81.4 47.0 %collective-permute-start.28 = (bf16[672,640]{1,0:T(8,128)(2,1)S(1)}, bf16[672,640]{1,0:T(8,128)(2,1)S(1)}, u32[]{:S(2)}, u32[]{:S(2)}) collective-permute-start(bf16[672,640]{1,0:T(8,128)(2,1)S(1)} %copy-done.14), channel_id=1, source_target_pairs={{0,4},{1,3},{2,6},{3,1},{4,0},{5,7},{6,2},{7,5}} | collective-permute-start | bytes 2580488 | tf_op jit(solution)/shard_map/ppermute | solution.py:80
  87.7 41.7 %collective-permute-start.2 = (bf16[368,640]{1,0:T(8,128)(2,1)S(1)}, bf16[368,640]{1,0:T(8,128)(2,1)S(1)}, u32[]{:S(2)}, u32[]{:S(2)}) collective-permute-start(bf16[368,640]{1,0:T(8,128)(2,1)S(1)} %collective-permute-done.refs_1_), channel_id=1, source_target_pairs={{0,2},{1,5},{2,0},{3,7},{4,6},{5,1},{6,4},{7,3}} | collective-permute-start | bytes 1413128 | tf_op jit(solution)/shard_map/ppermute | solution.py:80
  89.7 40.6 %collective-permute-start.5 = (bf16[368,640]{1,0:T(8,128)(2,1)S(1)}, bf16[368,640]{1,0:T(8,128)(2,1)S(1)}, u32[]{:S(2)}, u32[]{:S(2)}) collective-permute-start(bf16[368,640]{1,0:T(8,128)(2,1)S(1)} %collective-permute-done.1.refs_2_), channel_id=1, source_target_pairs={{0,1},{1,0},{2,3},{3,2},{4,5},{5,4},{6,7},{7,6}} | collective-permute-start | bytes 1413128 | tf_op jit(solution)/shard_map/ppermute | solution.py:80
  99.8 34.1 %collective-permute-start.9 = (bf16[672,640]{1,0:T(8,128)(2,1)}, bf16[672,640]{1,0:T(8,128)(2,1)}, u32[]{:S(2)}, u32[]{:S(2)}) collective-permute-start(bf16[672,640]{1,0:T(8,128)(2,1)} %collective-permute-done.7.refs_1_), channel_id=1, source_target_pairs={{0,2},{1,5},{2,0},{3,7},{4,6},{5,1},{6,4},{7,3}} | collective-permute-start | bytes 2580488 | tf_op jit(solution)/shard_map/ppermute | solution.py:80
  130.3 17.0 %collective-permute-start.15 = (bf16[960,640]{1,0:T(8,128)(2,1)}, bf16[960,640]{1,0:T(8,128)(2,1)}, u32[]{:S(2)}, u32[]{:S(2)}) collective-permute-start(bf16[960,640]{1,0:T(8,128)(2,1)} %pack.9.refs_0_.refs_8_), channel_id=1, source_target_pairs={{0,2},{1,5},{2,0},{3,7},{4,6},{5,1},{6,4},{7,3}} | collective-permute-start | bytes 3686408 | tf_op jit(solution)/shard_map/ppermute | solution.py:80
  132.3 28.2 %collective-permute-start.16 = (bf16[960,640]{1,0:T(8,128)(2,1)}, bf16[960,640]{1,0:T(8,128)(2,1)}, u32[]{:S(2)}, u32[]{:S(2)}) collective-permute-start(bf16[960,640]{1,0:T(8,128)(2,1)} %collective-permute-done.14.refs_1_.refs_9_), channel_id=1, source_target_pairs={{0,2},{1,5},{2,0},{3,7},{4,6},{5,1},{6,4},{7,3}} | collective-permute-start | bytes 3686408 | tf_op jit(solution)/shard_map/ppermute | solution.py:80
  132.4 15.0 %collective-permute-start.12 = (bf16[672,640]{1,0:T(8,128)(2,1)}, bf16[672,640]{1,0:T(8,128)(2,1)}, u32[]{:S(2)}, u32[]{:S(2)}) collective-permute-start(bf16[672,640]{1,0:T(8,128)(2,1)} %collective-permute-done.8.refs_2_), channel_id=1, source_target_pairs={{0,1},{1,0},{2,3},{3,2},{4,5},{5,4},{6,7},{7,6}} | collective-permute-start | bytes 2580488 | tf_op jit(solution)/shard_map/ppermute | solution.py:80
  133.1 14.7 %collective-permute-start.11 = (bf16[672,640]{1,0:T(8,128)(2,1)}, bf16[672,640]{1,0:T(8,128)(2,1)}, u32[]{:S(2)}, u32[]{:S(2)}) collective-permute-start(bf16[672,640]{1,0:T(8,128)(2,1)} %collective-permute-done.7.refs_1_), channel_id=1, source_target_pairs={{0,1},{1,0},{2,3},{3,2},{4,5},{5,4},{6,7},{7,6}} | collective-permute-start | bytes 2580488 | tf_op jit(solution)/shard_map/ppermute | solution.py:80
  133.9 27.2 %collective-permute-start.13 = (bf16[672,640]{1,0:T(8,128)(2,1)}, bf16[672,640]{1,0:T(8,128)(2,1)}, u32[]{:S(2)}, u32[]{:S(2)}) collective-permute-start(bf16[672,640]{1,0:T(8,128)(2,1)} %collective-permute-done.9.refs_3_), channel_id=1, source_target_pairs={{0,1},{1,0},{2,3},{3,2},{4,5},{5,4},{6,7},{7,6}} | collective-permute-start | bytes 2580488 | tf_op jit(solution)/shard_map/ppermute | solution.py:80
  147.3 55.6 %collective-permute-start.17 = (bf16[960,640]{1,0:T(8,128)(2,1)S(1)}, bf16[960,640]{1,0:T(8,128)(2,1)S(1)}, u32[]{:S(2)}, u32[]{:S(2)}) collective-permute-start(bf16[960,640]{1,0:T(8,128)(2,1)S(1)} %copy-done.13), channel_id=1, source_target_pairs={{0,1},{1,0},{2,3},{3,2},{4,5},{5,4},{6,7},{7,6}} | collective-permute-start | bytes 3686408 | tf_op jit(solution)/shard_map/ppermute | solution.py:80
  147.4 56.8 %collective-permute-start.18 = (bf16[960,640]{1,0:T(8,128)(2,1)}, bf16[960,640]{1,0:T(8,128)(2,1)}, u32[]{:S(2)}, u32[]{:S(2)}) collective-permute-start(bf16[960,640]{1,0:T(8,128)(2,1)} %collective-permute-done.14.refs_1_.refs_9_), channel_id=1, source_target_pairs={{0,1},{1,0},{2,3},{3,2},{4,5},{5,4},{6,7},{7,6}} | collective-permute-start | bytes 3686408 | tf_op jit(solution)/shard_map/ppermute | solution.py:80
  147.9 56.2 %collective-permute-start.19 = (bf16[960,640]{1,0:T(8,128)(2,1)}, bf16[960,640]{1,0:T(8,128)(2,1)}, u32[]{:S(2)}, u32[]{:S(2)}) collective-permute-start(bf16[960,640]{1,0:T(8,128)(2,1)} %collective-permute-done.15.refs_2_.refs_10_), channel_id=1, source_target_pairs={{0,1},{1,0},{2,3},{3,2},{4,5},{5,4},{6,7},{7,6}} | collective-permute-start | bytes 3686408 | tf_op jit(solution)/shard_map/ppermute | solution.py:80
  160.5 44.1 %collective-permute-start.20 = (bf16[960,640]{1,0:T(8,128)(2,1)}, bf16[960,640]{1,0:T(8,128)(2,1)}, u32[]{:S(2)}, u32[]{:S(2)}) collective-permute-start(bf16[960,640]{1,0:T(8,128)(2,1)} %collective-permute-done.16.refs_3_.refs_11_), channel_id=1, source_target_pairs={{0,1},{1,0},{2,3},{3,2},{4,5},{5,4},{6,7},{7,6}} | collective-permute-start | bytes 3686408 | tf_op jit(solution)/shard_map/ppermute | solution.py:80
  161.2 41.9 %collective-permute-start.30 = (bf16[672,640]{1,0:T(8,128)(2,1)}, bf16[672,640]{1,0:T(8,128)(2,1)}, u32[]{:S(2)}, u32[]{:S(2)}) collective-permute-start(bf16[672,640]{1,0:T(8,128)(2,1)} %copy-done.33), channel_id=1, source_target_pairs={{0,2},{1,5},{2,0},{3,7},{4,6},{5,1},{6,4},{7,3}} | collective-permute-start | bytes 2580488 | tf_op jit(solution)/shard_map/ppermute | solution.py:80
  203.0 33.4 %collective-permute-start.27 = (bf16[320,640]{1,0:T(8,128)(2,1)}, bf16[320,640]{1,0:T(8,128)(2,1)}, u32[]{:S(2)}, u32[]{:S(2)}) collective-permute-start(bf16[320,640]{1,0:T(8,128)(2,1)} %collective-permute-done.23.refs_3_), channel_id=1, source_target_pairs={{0,1},{1,0},{2,3},{3,2},{4,5},{5,4},{6,7},{7,6}} | collective-permute-start | bytes 1228808 | tf_op jit(solution)/shard_map/ppermute | solution.py:80
  203.1 33.8 %collective-permute-start.37 = (bf16[640,640]{1,0:T(8,128)(2,1)}, bf16[640,640]{1,0:T(8,128)(2,1)}, u32[]{:S(2)}, u32[]{:S(2)}) collective-permute-start(bf16[640,640]{1,0:T(8,128)(2,1)} %collective-permute-done.35.refs_1_), channel_id=1, source_target_pairs={{0,2},{1,5},{2,0},{3,7},{4,6},{5,1},{6,4},{7,3}} | collective-permute-start | bytes 2457608 | tf_op jit(solution)/shard_map/ppermute | solution.py:80
  204.1 33.3 %collective-permute-start.32 = (bf16[672,640]{1,0:T(8,128)(2,1)}, bf16[672,640]{1,0:T(8,128)(2,1)S(1)}, u32[]{:S(2)}, u32[]{:S(2)}) collective-permute-start(bf16[672,640]{1,0:T(8,128)(2,1)} %copy-done.33), channel_id=1, source_target_pairs={{0,1},{1,0},{2,3},{3,2},{4,5},{5,4},{6,7},{7,6}} | collective-permute-start | bytes 2580488 | tf_op jit(solution)/shard_map/ppermute | solution.py:80
  204.1 32.8 %collective-permute-start.33 = (bf16[672,640]{1,0:T(8,128)(2,1)S(1)}, bf16[672,640]{1,0:T(8,128)(2,1)}, u32[]{:S(2)}, u32[]{:S(2)}) collective-permute-start(bf16[672,640]{1,0:T(8,128)(2,1)S(1)} %copy-done.32), channel_id=1, source_target_pairs={{0,1},{1,0},{2,3},{3,2},{4,5},{5,4},{6,7},{7,6}} | collective-permute-start | bytes 2580488 | tf_op jit(solution)/shard_map/ppermute | solution.py:80
  204.6 53.7 %collective-permute-start.34 = (bf16[672,640]{1,0:T(8,128)(2,1)}, bf16[672,640]{1,0:T(8,128)(2,1)}, u32[]{:S(2)}, u32[]{:S(2)}) collective-permute-start(bf16[672,640]{1,0:T(8,128)(2,1)} %collective-permute-done.30.refs_3_), channel_id=1, source_target_pairs={{0,1},{1,0},{2,3},{3,2},{4,5},{5,4},{6,7},{7,6}} | collective-permute-start | bytes 2580488 | tf_op jit(solution)/shard_map/ppermute | solution.py:80
  236.4 42.9 %collective-permute-start.38 = (bf16[640,640]{1,0:T(8,128)(2,1)S(1)}, bf16[640,640]{1,0:T(8,128)(2,1)S(1)}, u32[]{:S(2)}, u32[]{:S(2)}) collective-permute-start(bf16[640,640]{1,0:T(8,128)(2,1)S(1)} %copy-done.16), channel_id=1, source_target_pairs={{0,1},{1,0},{2,3},{3,2},{4,5},{5,4},{6,7},{7,6}} | collective-permute-start | bytes 2457608 | tf_op jit(solution)/shard_map/ppermute | solution.py:80
  236.9 42.9 %collective-permute-start.39 = (bf16[640,640]{1,0:T(8,128)(2,1)}, bf16[640,640]{1,0:T(8,128)(2,1)}, u32[]{:S(2)}, u32[]{:S(2)}) collective-permute-start(bf16[640,640]{1,0:T(8,128)(2,1)} %collective-permute-done.35.refs_1_), channel_id=1, source_target_pairs={{0,1},{1,0},{2,3},{3,2},{4,5},{5,4},{6,7},{7,6}} | collective-permute-start | bytes 2457608 | tf_op jit(solution)/shard_map/ppermute | solution.py:80
  236.9 42.5 %collective-permute-start.40 = (bf16[640,640]{1,0:T(8,128)(2,1)}, bf16[640,640]{1,0:T(8,128)(2,1)S(1)}, u32[]{:S(2)}, u32[]{:S(2)}) collective-permute-start(bf16[640,640]{1,0:T(8,128)(2,1)} %collective-permute-done.36.refs_2_), channel_id=1, source_target_pairs={{0,1},{1,0},{2,3},{3,2},{4,5},{5,4},{6,7},{7,6}} | collective-permute-start | bytes 2457608 | tf_op jit(solution)/shard_map/ppermute | solution.py:80
  237.4 42.5 %collective-permute-start.41 = (bf16[640,640]{1,0:T(8,128)(2,1)}, bf16[640,640]{1,0:T(8,128)(2,1)}, u32[]{:S(2)}, u32[]{:S(2)}) collective-permute-start(bf16[640,640]{1,0:T(8,128)(2,1)} %collective-permute-done.37.refs_3_), channel_id=1, source_target_pairs={{0,1},{1,0},{2,3},{3,2},{4,5},{5,4},{6,7},{7,6}} | collective-permute-start | bytes 2457608 | tf_op jit(solution)/shard_map/ppermute | solution.py:80
  258.3 20.5 %collective-permute-start.44 = (bf16[320,640]{1,0:T(8,128)(2,1)}, bf16[320,640]{1,0:T(8,128)(2,1)S(1)}, u32[]{:S(2)}, u32[]{:S(2)}) collective-permute-start(bf16[320,640]{1,0:T(8,128)(2,1)} %collective-permute-done.42.refs_1_.refs_9_), channel_id=1, source_target_pairs={{0,2},{1,5},{2,0},{3,7},{4,6},{5,1},{6,4},{7,3}} | collective-permute-start | bytes 1228808 | tf_op jit(solution)/shard_map/ppermute | solution.py:80
  278.9 30.0 %collective-permute-start.45 = (bf16[320,640]{1,0:T(8,128)(2,1)S(1)}, bf16[320,640]{1,0:T(8,128)(2,1)S(1)}, u32[]{:S(2)}, u32[]{:S(2)}) collective-permute-start(bf16[320,640]{1,0:T(8,128)(2,1)S(1)} %copy-done.25), channel_id=1, source_target_pairs={{0,1},{1,0},{2,3},{3,2},{4,5},{5,4},{6,7},{7,6}} | collective-permute-start | bytes 1228808 | tf_op jit(solution)/shard_map/ppermute | solution.py:80
  279.3 78.8 %collective-permute-start.49 = (bf16[1024,512]{1,0:T(8,128)(2,1)}, bf16[1024,512]{1,0:T(8,128)(2,1)}, u32[]{:S(2)}, u32[]{:S(2)}) collective-permute-start(bf16[1024,512]{1,0:T(8,128)(2,1)} %get-tuple-element.100), channel_id=1, source_target_pairs={{0,1},{1,0},{2,3},{3,2},{4,5},{5,4},{6,7},{7,6}} | collective-permute-start | bytes 3145736 | tf_op jit(solution)/shard_map/ppermute | solution.py:80
  279.4 29.5 %collective-permute-start.46 = (bf16[320,640]{1,0:T(8,128)(2,1)}, bf16[320,640]{1,0:T(8,128)(2,1)S(1)}, u32[]{:S(2)}, u32[]{:S(2)}) collective-permute-start(bf16[320,640]{1,0:T(8,128)(2,1)} %collective-permute-done.42.refs_1_.refs_9_), channel_id=1, source_target_pairs={{0,1},{1,0},{2,3},{3,2},{4,5},{5,4},{6,7},{7,6}} | collective-permute-start | bytes 1228808 | tf_op jit(solution)/shard_map/ppermute | solution.py:80
  279.8 29.1 %collective-permute-start.47 = (bf16[320,640]{1,0:T(8,128)(2,1)}, bf16[320,640]{1,0:T(8,128)(2,1)S(1)}, u32[]{:S(2)}, u32[]{:S(2)}) collective-permute-start(bf16[320,640]{1,0:T(8,128)(2,1)} %collective-permute-done.43.refs_2_.refs_10_), channel_id=1, source_target_pairs={{0,1},{1,0},{2,3},{3,2},{4,5},{5,4},{6,7},{7,6}} | collective-permute-start | bytes 1228808 | tf_op jit(solution)/shard_map/ppermute | solution.py:80
  279.9 29.0 %collective-permute-start.48 = (bf16[320,640]{1,0:T(8,128)(2,1)S(1)}, bf16[320,640]{1,0:T(8,128)(2,1)}, u32[]{:S(2)}, u32[]{:S(2)}) collective-permute-start(bf16[320,640]{1,0:T(8,128)(2,1)S(1)} %collective-permute-done.44.refs_3_.refs_11_), channel_id=1, source_target_pairs={{0,1},{1,0},{2,3},{3,2},{4,5},{5,4},{6,7},{7,6}} | collective-permute-start | bytes 1228808 | tf_op jit(solution)/shard_map/ppermute | solution.py:80
  548.2 21.8 %collective-permute-start.66 = (f32[48,640]{1,0:T(8,128)}, f32[48,640]{1,0:T(8,128)S(1)}, u32[]{:S(2)}, u32[]{:S(2)}) collective-permute-start(f32[48,640]{1,0:T(8,128)} %vec_pack.1), channel_id=1, source_target_pairs={{0,1},{1,0},{2,3},{3,2},{4,5},{5,4},{6,7},{7,6}} | collective-permute-start | bytes 368648 | tf_op jit(solution)/shard_map/ppermute | solution.py:80
  548.4 74.9 %collective-permute-start.52 = (f32[640,640]{1,0:T(8,128)}, f32[640,640]{1,0:T(8,128)}, u32[]{:S(2)}, u32[]{:S(2)}) collective-permute-start(f32[640,640]{1,0:T(8,128)} %get-tuple-element.122), channel_id=1, source_target_pairs={{0,2},{1,5},{2,0},{3,7},{4,6},{5,1},{6,4},{7,3}} | collective-permute-start | bytes 4915208 | tf_op jit(solution)/shard_map/ppermute | solution.py:80
  568.0 58.0 %collective-permute-start.50 = (f32[640,640]{1,0:T(8,128)}, f32[640,640]{1,0:T(8,128)}, u32[]{:S(2)}, u32[]{:S(2)}) collective-permute-start(f32[640,640]{1,0:T(8,128)} %get-tuple-element.120), channel_id=1, source_target_pairs={{0,2},{1,5},{2,0},{3,7},{4,6},{5,1},{6,4},{7,3}} | collective-permute-start | bytes 4915208 | tf_op jit(solution)/shard_map/ppermute | solution.py:80
  569.2 58.9 %collective-permute-start.64 = (f32[640,640]{1,0:T(8,128)}, f32[640,640]{1,0:T(8,128)}, u32[]{:S(2)}, u32[]{:S(2)}) collective-permute-start(f32[640,640]{1,0:T(8,128)} %get-tuple-element.135), channel_id=1, source_target_pairs={{0,2},{1,5},{2,0},{3,7},{4,6},{5,1},{6,4},{7,3}} | collective-permute-start | bytes 4915208 | tf_op jit(solution)/shard_map/ppermute | solution.py:80
  570.0 38.1 %collective-permute-start.67 = (f32[48,640]{1,0:T(8,128)S(1)}, f32[48,640]{1,0:T(8,128)S(1)}, u32[]{:S(2)}, u32[]{:S(2)}) collective-permute-start(f32[48,640]{1,0:T(8,128)S(1)} %add.112), channel_id=1, source_target_pairs={{0,2},{1,5},{2,0},{3,7},{4,6},{5,1},{6,4},{7,3}} | collective-permute-start | bytes 368648 | tf_op jit(solution)/shard_map/ppermute | solution.py:80
  588.4 42.2 %collective-permute-start.62 = (f32[640,640]{1,0:T(8,128)}, f32[640,640]{1,0:T(8,128)}, u32[]{:S(2)}, u32[]{:S(2)}) collective-permute-start(f32[640,640]{1,0:T(8,128)} %get-tuple-element.133), channel_id=1, source_target_pairs={{0,2},{1,5},{2,0},{3,7},{4,6},{5,1},{6,4},{7,3}} | collective-permute-start | bytes 4915208 | tf_op jit(solution)/shard_map/ppermute | solution.py:80
  608.2 13.4 %collective-permute-start.68 = (f32[48,640]{1,0:T(8,128)S(1)}, f32[48,640]{1,0:T(8,128)S(1)}, u32[]{:S(2)}, u32[]{:S(2)}) collective-permute-start(f32[48,640]{1,0:T(8,128)S(1)} %add.113), channel_id=1, source_target_pairs={{0,4},{1,3},{2,6},{3,1},{4,0},{5,7},{6,2},{7,5}} | collective-permute-start | bytes 368648 | tf_op jit(solution)/shard_map/ppermute | solution.py:80
  621.6 70.1 %collective-permute-start.58 = (f32[1280,640]{1,0:T(8,128)}, f32[1280,640]{1,0:T(8,128)S(1)}, u32[]{:S(2)}, u32[]{:S(2)}) collective-permute-start(f32[1280,640]{1,0:T(8,128)} %get-tuple-element.128), channel_id=1, source_target_pairs={{0,2},{1,5},{2,0},{3,7},{4,6},{5,1},{6,4},{7,3}} | collective-permute-start | bytes 9830408 | tf_op jit(solution)/shard_map/ppermute | solution.py:80
  623.3 126.6 %collective-permute-start.60 = (f32[1280,640]{1,0:T(8,128)}, f32[1280,640]{1,0:T(8,128)S(1)}, u32[]{:S(2)}, u32[]{:S(2)}) collective-permute-start(f32[1280,640]{1,0:T(8,128)} %get-tuple-element.130), channel_id=1, source_target_pairs={{0,2},{1,5},{2,0},{3,7},{4,6},{5,1},{6,4},{7,3}} | collective-permute-start | bytes 9830408 | tf_op jit(solution)/shard_map/ppermute | solution.py:80
  626.0 21.1 %collective-permute-start.53 = (f32[320,640]{1,0:T(8,128)S(1)}, f32[320,640]{1,0:T(8,128)S(1)}, u32[]{:S(2)}, u32[]{:S(2)}) collective-permute-start(f32[320,640]{1,0:T(8,128)S(1)} %slice_add_fusion.12), channel_id=1, source_target_pairs={{0,4},{1,3},{2,6},{3,1},{4,0},{5,7},{6,2},{7,5}} | collective-permute-start | bytes 2457608 | tf_op jit(solution)/shard_map/ppermute | solution.py:80
  628.1 36.6 %collective-permute-start.51 = (f32[320,640]{1,0:T(8,128)S(1)}, f32[320,640]{1,0:T(8,128)S(1)}, u32[]{:S(2)}, u32[]{:S(2)}) collective-permute-start(f32[320,640]{1,0:T(8,128)S(1)} %slice_add_fusion.14), channel_id=1, source_target_pairs={{0,4},{1,3},{2,6},{3,1},{4,0},{5,7},{6,2},{7,5}} | collective-permute-start | bytes 2457608 | tf_op jit(solution)/shard_map/ppermute | solution.py:80
  630.6 173.8 %collective-permute-start.54 = (f32[1344,640]{1,0:T(8,128)}, f32[1344,640]{1,0:T(8,128)S(1)}, u32[]{:S(2)}, u32[]{:S(2)}) collective-permute-start(f32[1344,640]{1,0:T(8,128)} %get-tuple-element.124), channel_id=1, source_target_pairs={{0,2},{1,5},{2,0},{3,7},{4,6},{5,1},{6,4},{7,3}} | collective-permute-start | bytes 10321928 | tf_op jit(solution)/shard_map/ppermute | solution.py:80
  647.1 212.6 %collective-permute-start.56 = (f32[1344,640]{1,0:T(8,128)}, f32[1344,640]{1,0:T(8,128)S(1)}, u32[]{:S(2)}, u32[]{:S(2)}) collective-permute-start(f32[1344,640]{1,0:T(8,128)} %get-tuple-element.126), channel_id=1, source_target_pairs={{0,2},{1,5},{2,0},{3,7},{4,6},{5,1},{6,4},{7,3}} | collective-permute-start | bytes 10321928 | tf_op jit(solution)/shard_map/ppermute | solution.py:80
  664.6 21.1 %collective-permute-start.65 = (f32[320,640]{1,0:T(8,128)S(1)}, f32[320,640]{1,0:T(8,128)S(1)}, u32[]{:S(2)}, u32[]{:S(2)}) collective-permute-start(f32[320,640]{1,0:T(8,128)S(1)} %slice_add_fusion.8), channel_id=1, source_target_pairs={{0,4},{1,3},{2,6},{3,1},{4,0},{5,7},{6,2},{7,5}} | collective-permute-start | bytes 2457608 | tf_op jit(solution)/shard_map/ppermute | solution.py:80
  685.8 21.1 %collective-permute-start.63 = (f32[320,640]{1,0:T(8,128)S(1)}, f32[320,640]{1,0:T(8,128)S(1)}, u32[]{:S(2)}, u32[]{:S(2)}) collective-permute-start(f32[320,640]{1,0:T(8,128)S(1)} %slice_add_fusion.10), channel_id=1, source_target_pairs={{0,4},{1,3},{2,6},{3,1},{4,0},{5,7},{6,2},{7,5}} | collective-permute-start | bytes 2457608 | tf_op jit(solution)/shard_map/ppermute | solution.py:80
  691.9 169.1 %collective-permute-start.59 = (f32[640,640]{1,0:T(8,128)S(1)}, f32[640,640]{1,0:T(8,128)S(1)}, u32[]{:S(2)}, u32[]{:S(2)}) collective-permute-start(f32[640,640]{1,0:T(8,128)S(1)} %slice_add_fusion.6), channel_id=1, source_target_pairs={{0,4},{1,3},{2,6},{3,1},{4,0},{5,7},{6,2},{7,5}} | collective-permute-start | bytes 4915208 | tf_op jit(solution)/shard_map/ppermute | solution.py:80
  750.1 111.4 %collective-permute-start.61 = (f32[640,640]{1,0:T(8,128)S(1)}, f32[640,640]{1,0:T(8,128)}, u32[]{:S(2)}, u32[]{:S(2)}) collective-permute-start(f32[640,640]{1,0:T(8,128)S(1)} %slice_add_fusion.4), channel_id=1, source_target_pairs={{0,4},{1,3},{2,6},{3,1},{4,0},{5,7},{6,2},{7,5}} | collective-permute-start | bytes 4915208 | tf_op jit(solution)/shard_map/ppermute | solution.py:80
  804.6 63.4 %collective-permute-start.55 = (f32[672,640]{1,0:T(8,128)S(1)}, f32[672,640]{1,0:T(8,128)S(1)}, u32[]{:S(2)}, u32[]{:S(2)}) collective-permute-start(f32[672,640]{1,0:T(8,128)S(1)} %slice_add_fusion.2), channel_id=1, source_target_pairs={{0,4},{1,3},{2,6},{3,1},{4,0},{5,7},{6,2},{7,5}} | collective-permute-start | bytes 5160968 | tf_op jit(solution)/shard_map/ppermute | solution.py:80
  859.8 22.0 %collective-permute-start.57 = (f32[672,640]{1,0:T(8,128)S(1)}, f32[672,640]{1,0:T(8,128)S(1)}, u32[]{:S(2)}, u32[]{:S(2)}) collective-permute-start(f32[672,640]{1,0:T(8,128)S(1)} %slice_add_fusion), channel_id=1, source_target_pairs={{0,4},{1,3},{2,6},{3,1},{4,0},{5,7},{6,2},{7,5}} | collective-permute-start | bytes 5160968 | tf_op jit(solution)/shard_map/ppermute | solution.py:80
  (46 other events, 659.4 us)

commit v5 on v4

--- a/solution.py
+++ b/solution.py
@@ -254,16 +254,49 @@
         ref[pl.ds(index, 1), :] += row
 
 
+def self_loads(pieces, w_qkv, w_out, sems):
+    start_load(pieces, 0, w_qkv, sems.at[0])
+    start_load(pieces, 3 * (w_out.shape[0] // 8), w_out, sems.at[1])
+
+
+def cross_loads(pieces, offset, w_kv, w_query, w_out, sems):
+    deep, depth = w_kv.shape[0] // 8, w_out.shape[0] // 8
+    start_load(pieces, offset, w_kv, sems.at[0])
+    start_load(pieces, offset + 2 * deep, w_query, sems.at[1])
+    start_load(pieces, offset + 2 * deep + depth, w_out, sems.at[2])
+
+
 def self_forward_kernel(samples, tokens, h_ref, rows_ref, *refs):
-    pieces, (norm_ref, qkv_ref, mix_ref, out_ref, w_qkv, w_out, sems) = refs[:8], refs[8:]
+    @pl.when(pl.program_id(0) == 0)
+    def _():
+        self_loads(refs[:8], *refs[12:])
+
+    self_forward_step(samples, tokens, h_ref, rows_ref, *refs[8:])
+
+
+def cross_forward_kernel(samples, tokens, valid, h_ref, rows_ref, ctx_ref, *refs):
+    @pl.when(pl.program_id(0) == 0)
+    def _():
+        cross_loads(refs[:8], 0, *refs[13:])
+
+    cross_forward_step(samples, tokens, valid, h_ref, rows_ref, ctx_ref, *refs[8:])
+
+
+def attention_forward_kernel(samples, tokens, valid, h_ref, rows_ref, ctx_ref, *refs):
+    pieces, self_outs, cross_outs, self_scratch, cross_scratch = refs[:8], refs[8:12], refs[12:17], refs[17:20], refs[20:24]
+
+    @pl.when(pl.program_id(0) == 0)
+    def _():
+        self_loads(pieces, *self_scratch)
+        cross_loads(pieces, 4 * (h_ref.shape[1] // 8), *cross_scratch)
+
+    self_forward_step(samples, tokens, h_ref, rows_ref, *self_outs, *self_scratch)
+    cross_forward_step(samples, tokens, valid, self_outs[3], rows_ref, ctx_ref, *cross_outs, *cross_scratch)
+
+
+def self_forward_step(samples, tokens, h_ref, rows_ref, norm_ref, qkv_ref, mix_ref, out_ref, w_qkv, w_out, sems):
     width = h_ref.shape[1]
     step = pl.program_id(0)
-
-    @pl.when(step == 0)
-    def _():
-        start_load(pieces, 0, w_qkv, sems.at[0])
-        start_load(pieces, 3 * (width // 8), w_out, sems.at[1])
-
     x = h_ref[...].astype(F32)
     unit, _ = norm_stats(x)
     normed = (unit * rows_ref[0:1, :] + rows_ref[1:2, :]).astype(BF16)
@@ -288,19 +321,11 @@
     out_ref[...] = x + dot_nn(mix_ref[...], w_out[...]) + rows_ref[6:7, :]
 
 
-def cross_forward_kernel(samples, tokens, valid, h_ref, rows_ref, ctx_ref, *refs):
-    pieces, (norm_ref, query_ref, kv_ref, mix_ref, out_ref, w_kv, w_query, w_out, sems) = refs[:8], refs[8:]
+def cross_forward_step(samples, tokens, valid, h_ref, rows_ref, ctx_ref, norm_ref, query_ref, kv_ref, mix_ref, out_ref, w_kv, w_query,
+                       w_out, sems):
     width = h_ref.shape[1]
     step = pl.program_id(0)
     padded = ctx_ref.shape[0] // (samples * pl.num_programs(0))
-
-    @pl.when(step == 0)
-    def _():
-        deep, depth = w_kv.shape[0] // 8, width // 8
-        start_load(pieces, 0, w_kv, sems.at[0])
-        start_load(pieces, 2 * deep, w_query, sems.at[1])
-        start_load(pieces, 2 * deep + depth, w_out, sems.at[2])
-
     x = h_ref[...]
     unit, _ = norm_stats(x)
     normed = (unit * rows_ref[2:3, :] + rows_ref[3:4, :]).astype(BF16)
@@ -505,7 +530,7 @@
 
 def self_backward_kernel(samples, tokens, grad_ref, qkv_ref, h_ref, rows_ref, norm_ref, mix_ref, *refs):
     pieces, refs = refs[:8], refs[8:]
-    (out_ref, vec_ref, far_ref, keep_ref, d_mix, w_qkv, w_out, d_qkv, grad_bf, x_norm, x_mix, tile, recv, sems, load_sem,
+    (out_ref, rounded_ref, vec_ref, far_ref, keep_ref, d_mix, w_qkv, w_out, d_qkv, grad_bf, x_norm, x_mix, tile, recv, sems, load_sem,
      send_sem, recv_sem) = refs
     width = h_ref.shape[1]
     depth = width // 8
@@ -568,7 +593,8 @@
             copy.start()
 
     d_res, g_gain, g_shift = norm_back(h_ref[...].astype(F32), rows_ref[0:1, :], d_norm)
-    out_ref[...] = (grad + d_res).astype(out_ref.dtype)
+    out_ref[...] = grad + d_res
+    rounded_ref[...] = (grad + d_res).astype(BF16)
     add_rows(vec_ref, step, [g_gain, g_shift, jnp.sum(grad, axis=0, keepdims=True)])
 
     @pl.when(step == last)
@@ -621,6 +647,22 @@
         count * width * width * 4 + ctx_rows * ctx_width * width * 4 + count * 128 * width * 4, 2e7)(h, rows, ctx, *pieces)
 
 
+def attention_forward(h, rows, ctx, pieces, tokens, valid):
+    count, width = h.shape
+    ctx_rows, ctx_width = ctx.shape
+    one, kv = by_step(STEP, width), whole(ctx_rows, 2 * width)
+    thin, full = shape(count, width, BF16), shape(count, width, F32)
+    square = pltpu.VMEM((width, width), BF16)
+    return call(
+        functools.partial(attention_forward_kernel, STEP // tokens, tokens, valid), count // STEP,
+        [one, whole(*rows.shape), whole(ctx_rows, ctx_width)] + [ANY] * 8,
+        [one, by_step(STEP, 3 * width), one, one, one, one, kv, one, one],
+        [thin, shape(count, 3 * width, BF16), thin, full, thin, thin, shape(ctx_rows, 2 * width, BF16), thin, full],
+        [pltpu.VMEM((width, 3 * width), BF16), square, pltpu.SemaphoreType.DMA((2,)), pltpu.VMEM((ctx_width, 2 * width), BF16), square,
+         square, pltpu.SemaphoreType.DMA((3,))],
+        count * width * width * 12 + ctx_rows * ctx_width * width * 4 + count * tokens * width * 6, 4e7)(h, rows, ctx, *pieces)
+
+
 def ff_forward(h, rows, bias, pieces, offset):
     count, width = h.shape
     half = bias.shape[1] // 2
@@ -657,7 +699,7 @@
         count * width * half * 2, 2e7)(h, rows, gated, *pieces)
 
 
-def cross_backward(grad, query, kv, h, rows, norm, mix, ctx_mine, ctx_other, pieces, tokens, valid):
+def cross_backward(kind, grad, query, kv, h, rows, norm, mix, ctx_mine, ctx_other, pieces, tokens, valid):
     count, width = h.shape
     ctx_rows = kv.shape[0]
     steps = count // STEP
@@ -674,11 +716,11 @@
         [pltpu.VMEM((STEP, width), BF16), pltpu.VMEM((width, width), BF16), pltpu.VMEM((width, width), BF16), big, big, kv_buf, kv_buf,
          big, big, ctx_buf, ctx_buf, pltpu.VMEM((2, width, width), F32), pltpu.VMEM((4, 2 * (width // 8), width), F32),
          dma((2,)), dma((4,)), dma, dma, dma((2, 4)), dma((2, 4))],
-        count * width * width * 8 + count * 128 * width * 10 + ctx_mine.size * width * 8, 2e7, 3)(
+        count * width * width * 8 + count * 128 * width * 10 + ctx_mine.size * width * 8, 2e7, kind)(
             grad, query, kv, h, rows, norm, mix, ctx_mine, ctx_other, *pieces)
 
 
-def self_backward(kind, grad, qkv, h, rows, norm, mix, pieces, tokens, out_dtype):
+def self_backward(kind, grad, qkv, h, rows, norm, mix, pieces, tokens):
     count, width = h.shape
     group_rows = width // 2
     dma = pltpu.SemaphoreType.DMA
@@ -686,8 +728,8 @@
     return call(
         functools.partial(self_backward_kernel, STEP // tokens, tokens), count // STEP,
         [by_step(STEP, width), by_step(STEP, 3 * width), by_step(STEP, width), whole(*rows.shape)] + [ANY] * 10,
-        [by_step(STEP, width), whole(8, width), whole(2 * group_rows, width), whole(2 * group_rows, width)],
-        [shape(count, width, out_dtype), shape(8, width, F32), shape(2 * group_rows, width, F32), shape(2 * group_rows, width, F32)],
+        [by_step(STEP, width), by_step(STEP, width), whole(8, width), whole(2 * group_rows, width), whole(2 * group_rows, width)],
+        [shape(count, width, F32), shape(count, width, BF16), shape(8, width, F32), shape(2 * group_rows, width, F32), shape(2 * group_rows, width, F32)],
         [pltpu.VMEM((STEP, width), BF16), pltpu.VMEM((width, 3 * width), BF16), pltpu.VMEM((width, width), BF16),
          pltpu.VMEM((count, 3 * width), BF16), big, big, big, pltpu.VMEM((4, width, width), F32),
          pltpu.VMEM((4, group_rows, width), F32), dma((2,)), dma((2,)), dma((4, 4)), dma((4, 4))],
@@ -821,25 +863,28 @@
     return ctx, mine, permute(other, gather_perms(n_dev)[2])
 
 
-def vec_pack_kernel(*refs):
-    ins, out = refs[:-1], refs[-1]
+def vec_pack_kernel(biases, *refs):
+    ins, out = list(refs[:-1]), refs[-1]
     width = out.shape[1]
     out[...] = jnp.zeros_like(out)
-    for layer in range(len(ins) // 4):
-        first, second, third, bias = ins[4 * layer:4 * layer + 4]
+    for layer, parts in enumerate(biases):
+        first, second, third = ins[:3]
         rows = [(first, 0), (first, 1), (second, 0), (second, 1), (third, 0), (third, 1), (first, 2), (second, 2), (third, 2)]
         for index, (ref, row) in enumerate(rows):
             out[17 * layer + index:17 * layer + index + 1, :] = ref[row:row + 1, :]
-        for index in range(8):
-            row = 17 * layer + 9 + index
-            out[row:row + 1, :] = bias[0:1, index * width:(index + 1) * width]
-
-
-def vec_total(parts, rows, n_dev):
+        for (start, chunks), bias in zip(parts, ins[3:]):
+            for kind in range(2):
+                for chunk in range(chunks):
+                    row, column = 17 * layer + 9 + 4 * kind + start + chunk, (kind * chunks + chunk) * width
+                    out[row:row + 1, :] = bias[0:1, column:column + width]
+        ins = ins[3 + len(parts):]
+
+
+def vec_total(parts, biases, rows, n_dev):
     vmem = pl.BlockSpec(memory_space=pltpu.VMEM)
     width = parts[0].shape[1]
     total = pl.pallas_call(
-        vec_pack_kernel, in_specs=[vmem] * len(parts), out_specs=vmem, out_shape=shape(rows, width, F32),
+        functools.partial(vec_pack_kernel, biases), in_specs=[vmem] * len(parts), out_specs=vmem, out_shape=shape(rows, width, F32),
         cost_estimate=pl.CostEstimate(flops=rows * width, bytes_accessed=rows * width * 8, transcendentals=0),
         name='vec_pack')(*parts)
     near, far, core = gather_perms(n_dev)
@@ -848,24 +893,29 @@
     return total
 
 
-def ff_grad_kernel(offset, grad_ref, save_a, save_g, norm_ref, h_ref, rows_ref, *refs):
+def ff_grad_kernel(offset, first, resumed, final, grad_ref, save_a, save_g, norm_ref, h_ref, rows_ref, *refs):
+    before_ref, refs = (refs[0], refs[1:]) if resumed else (None, refs)
     pieces, refs = refs[:16], refs[16:]
-    (out_ref, vec_ref, bias_ref, far_ref, keep_ref, grad, grad_bf, turned, acc, part_a, part_g, d_both, w_ff1, w_ff2, tile, recv, obuf,
+    out_ref, refs = refs[0], refs[1:]
+    vec_ref, refs = (refs[0], refs[1:]) if final else (None, refs)
+    (bias_ref, far_ref, keep_ref, grad, grad_bf, turned, acc, part_a, part_g, d_both, w_ff1, w_ff2, tile, recv, obuf,
      in_sem, part_sem, w1_sem, w2_sem, out_sem, send_sem, recv_sem) = refs
     count, width = grad.shape
-    half = w_ff2.shape[0]
-    chunks, depth = half // width, width // 8
+    every, chunks, depth = w_ff2.shape[0] // width, recv.shape[0], width // 8
     me = lax.axis_index(AXIS)
     core, mate, mate_slot, own_chip = chip_places(me)
 
     load_grad = pltpu.make_async_copy(grad_ref, grad, in_sem.at[0])
     load_norm = pltpu.make_async_copy(norm_ref, d_both.at[:, pl.ds(0, width)], in_sem.at[1])
+    load_before = pltpu.make_async_copy(before_ref, acc, in_sem.at[2]) if resumed else None
     load_grad.start()
     load_norm.start()
+    if resumed:
+        load_before.start()
     start_load(pieces[8:], offset, w_ff2, w2_sem)
 
     def parts(chunk):
-        at = (slice(None), pl.ds(pl.multiple_of(chunk * width, width), width))
+        at = (slice(None), pl.ds(pl.multiple_of((first + chunk) * width, width), width))
         return [pltpu.make_async_copy(ref.at[at], buf.at[lax.rem(chunk, 2)], part_sem.at[which, lax.rem(chunk, 2)])
                 for which, (ref, buf) in enumerate(((save_a, part_a), (save_g, part_g)))]
 
@@ -879,7 +929,7 @@
         for kind in range(2):
             for piece, device in zip(pieces[:8], devices):
                 pltpu.make_async_copy(
-                    piece.at[pl.ds((kind * chunks + chunk) * depth, depth), :],
+                    piece.at[pl.ds((kind * every + first + chunk) * depth, depth), :],
                     w_ff1.at[pl.ds(pl.multiple_of(device * depth, 16), depth), pl.ds((2 * chunk + kind) * width, width)],
                     w1_sem.at[chunk]).start()
     greet(mate)
@@ -912,7 +962,7 @@
         for slot in range(4):
             ref = keep_ref if slot < 2 else far_ref
             for kind in range(2):
-                row = pl.multiple_of((slot % 2) * 8 * depth + (kind * chunks + chunk) * depth, 16)
+                row = pl.multiple_of((slot % 2) * 2 * chunks * depth + (kind * chunks + chunk) * depth, 16)
                 pltpu.make_async_copy(obuf.at[pl.ds(slot * depth, depth), pl.ds(kind * width, width)], ref.at[pl.ds(row, depth), :],
                                       out_sem).start()
         for copy in sends(chunk):
@@ -922,9 +972,11 @@
     grad_bf[...] = grad[...].astype(BF16)
     load_norm.wait()
     turned[...] = d_both[:, 0:width].T
-    acc[...] = jnp.zeros_like(acc)
+    if resumed:
+        load_before.wait()
+    else:
+        acc[...] = jnp.zeros_like(acc)
     bias_ref[...] = jnp.zeros_like(bias_ref)
-    vec_ref[...] = jnp.zeros_like(vec_ref)
     wait_load(w_ff2, w2_sem)
 
     def one_chunk(chunk, carry):
@@ -939,7 +991,7 @@
                 copy.start()
 
         even = lax.rem(chunk, 2)
-        w_down = w_ff2.at[pl.ds(pl.multiple_of(chunk * width, width), width), :]
+        w_down = w_ff2.at[pl.ds(pl.multiple_of((first + chunk) * width, width), width), :]
         sums = [0.0, 0.0]
         ahead = dot_nt(grad_bf[0:FF_ROWS, :], w_down[...])
         for start in range(0, count, FF_ROWS):
@@ -953,7 +1005,7 @@
                 d_both[rows, kind * width:(kind + 1) * width] = d_part.astype(BF16)
             acc[rows, :] += dot_nt(d_both[rows, :], w_pair[...])
         for kind in range(2):
-            bias_ref[0:1, pl.ds(pl.multiple_of(kind * half + chunk * width, 2 * HEAD), width)] += sums[kind]
+            bias_ref[0:1, pl.ds(pl.multiple_of((kind * chunks + chunk) * width, 2 * HEAD), width)] += sums[kind]
 
         @pl.when(chunk > 0)
         def _():
@@ -965,48 +1017,94 @@
         return carry
 
     lax.fori_loop(0, chunks, one_chunk, 0)
-    steps = count // STEP
-    for step in range(steps):
-        load_h(step).start()
-    pltpu.make_async_copy(part_a.at[0], part_a.at[0], part_sem.at[0, 0]).wait()
-    for step in range(steps):
-        rows = slice(step * STEP, (step + 1) * STEP)
-        mine = grad[rows, :].astype(F32)
-        d_res, g_gain, g_shift = norm_back(part_a[0, rows, :], rows_ref[4:5, :], acc[rows, :])
-        acc[rows, :] = mine + d_res
-        pltpu.make_async_copy(acc.at[pl.ds(step * STEP, STEP), :], out_ref.at[pl.ds(step * STEP, STEP), :], in_sem.at[0]).start()
-        for at, row in enumerate((g_gain, g_shift, jnp.sum(mine, axis=0, keepdims=True))):
-            vec_ref[at:at + 1, :] += row
-    finish(chunks - 1, False)
+    if final:
+        steps = count // STEP
+        vec_ref[...] = jnp.zeros_like(vec_ref)
+        for step in range(steps):
+            load_h(step).start()
+        pltpu.make_async_copy(part_a.at[0], part_a.at[0], part_sem.at[0, 0]).wait()
+        for step in range(steps):
+            rows = slice(step * STEP, (step + 1) * STEP)
+            mine = grad[rows, :].astype(F32)
+            d_res, g_gain, g_shift = norm_back(part_a[0, rows, :], rows_ref[4:5, :], acc[rows, :])
+            acc[rows, :] = mine + d_res
+            pltpu.make_async_copy(acc.at[pl.ds(step * STEP, STEP), :], out_ref.at[pl.ds(step * STEP, STEP), :], in_sem.at[0]).start()
+            for at, row in enumerate((g_gain, g_shift, jnp.sum(mine, axis=0, keepdims=True))):
+                vec_ref[at:at + 1, :] += row
+    else:
+        pltpu.make_async_copy(acc, out_ref, in_sem.at[0]).start()
+    finish(chunks - 1, chunks == 1)
     wait_write()
     pltpu.make_async_copy(acc, out_ref, in_sem.at[0]).wait()
 
 
-def ff_grads(kind, grad, save_a, save_g, norm, h, rows, pieces, offset):
+def ff_grads(kind, grad, save_a, save_g, norm, h, rows, pieces, offset, first, chunks, before):
     count, width = h.shape
     half = save_a.shape[1]
+    final = first + chunks == half // width
     vmem = pl.BlockSpec(memory_space=pltpu.VMEM)
-    big = shape(2 * width, width, F32)
+    big = shape(4 * chunks * (width // 8), width, F32)
     dma = pltpu.SemaphoreType.DMA
     saved = pltpu.VMEM((2, count, width), F32)
+    resumed = before is not None
     return pl.pallas_call(
-        functools.partial(ff_grad_kernel, offset), in_specs=[ANY] * 5 + [vmem] + [ANY] * 16, out_specs=[ANY, vmem, vmem, ANY, ANY],
-        out_shape=[shape(count, width, F32), shape(8, width, F32), shape(8, 2 * half, F32), big, big],
+        functools.partial(ff_grad_kernel, offset, first, resumed, final), in_specs=[ANY] * 5 + [vmem] + [ANY] * (16 + resumed),
+        out_specs=[ANY] + [vmem] * final + [vmem, ANY, ANY],
+        out_shape=[shape(count, width, F32)] + [shape(8, width, F32)] * final + [shape(8, 2 * chunks * width, F32), big, big],
         scratch_shapes=[pltpu.VMEM((count, width), grad.dtype), pltpu.VMEM((count, width), BF16), pltpu.VMEM((width, count), BF16),
                         pltpu.VMEM((count, width), F32), saved, saved, pltpu.VMEM((count, 2 * width), BF16),
-                        pltpu.VMEM((width, 2 * half), BF16), pltpu.VMEM((half, width), BF16), pltpu.VMEM((width, 2 * width), F32),
-                        pltpu.VMEM((4, width // 2, 2 * width), F32), pltpu.VMEM((width // 2, 2 * width), F32),
-                        dma((2,)), dma((2, 2)), dma((4,)), dma, dma, dma((4,)), dma((4, 4))],
-        cost_estimate=pl.CostEstimate(flops=count * width * half * 10, bytes_accessed=int(6e7), transcendentals=0),
-        compiler_params=pltpu.CompilerParams(collective_id=kind, has_side_effects=True, vmem_limit_bytes=VMEM_MOST))(grad, save_a, save_g, norm, h, rows, *pieces)
-
-
-def finish_scatter(far, keep, n_dev):
+                        pltpu.VMEM((width, 2 * chunks * width), BF16), pltpu.VMEM((half, width), BF16),
+                        pltpu.VMEM((width, 2 * width), F32), pltpu.VMEM((chunks, width // 2, 2 * width), F32),
+                        pltpu.VMEM((width // 2, 2 * width), F32),
+                        dma((3,)), dma((2, 2)), dma((chunks,)), dma, dma, dma((4,)), dma((chunks, 4))],
+        cost_estimate=pl.CostEstimate(flops=count * width * width * chunks * 10, bytes_accessed=int(6e7), transcendentals=0),
+        compiler_params=pltpu.CompilerParams(collective_id=kind, has_side_effects=True, vmem_limit_bytes=VMEM_MOST))(grad, save_a, save_g, norm, h, rows, *([before] if resumed else []), *pieces)
+
+
+def scatter(far, keep, n_dev):
     near_perm, far_perm, _ = gather_perms(n_dev)
     rows = keep.shape[0] // 2
     second = permute(far, far_perm)
     third = permute(keep[rows:] + second[rows:], near_perm)
-    return keep[:rows] + second[:rows] + third
+    return keep, second, third
+
+
+def total_kernel(plans, counts, depths, scale, *refs):
+    ins, outs = refs[:3 * sum(counts)], refs[3 * sum(counts):]
+    width, lanes, layers = ins[0].shape[1], outs[0].shape[1], len(plans)
+    for layer, plan in enumerate(plans):
+        base = 3 * sum(counts[:layer])
+        for out, blocks, depth in zip(outs, plan, depths):
+            stride = layers * len(blocks) * width // lanes
+            for index, (part, row) in enumerate(blocks):
+                keep, second, third = (ref[row:row + depth, :] for ref in ins[base + 3 * part:base + 3 * part + 3])
+                block = ((keep + second) + third) * scale
+                for column in range(0, width, lanes):
+                    start = layers * ((index * width + column) // lanes) + layer
+                    out[pl.ds(start, depth, stride), :] = block[:, column:column + lanes]
+
+
+def totals(layers, plans, depths, scale):
+    width, lanes = layers[0][0][0].shape[1], 128
+    arrays, specs = [], []
+    for parts in layers:
+        for terms in parts:
+            rows = terms[2].shape[0]
+            arrays += list(terms)
+            specs += [whole(rows, width)] * 3
+    sizes = [depth * len(blocks) * width for depth, blocks in zip(depths, plans[0])]
+    shapes = [shape(len(layers) * size // lanes, lanes, F32) for size in sizes]
+    sums = pl.pallas_call(
+        functools.partial(total_kernel, plans, [len(parts) for parts in layers], depths, scale), grid=(1,), in_specs=specs,
+        out_specs=[whole(*out.shape) for out in shapes], out_shape=shapes,
+        cost_estimate=pl.CostEstimate(flops=sum(a.size for a in arrays), bytes_accessed=4 * sum(a.size for a in arrays),
+                                      transcendentals=0),
+        compiler_params=pltpu.CompilerParams(vmem_limit_bytes=VMEM_LIMIT), name='totals')(*arrays)
+    result = []
+    for total, size in zip(sums, sizes):
+        total = lax.optimization_barrier(total.reshape(size // lanes, len(layers), lanes))
+        result.append(jnp.swapaxes(total, 0, 1).reshape(len(layers), size))
+    return result
 
 
 def solution(mesh):
@@ -1037,8 +1135,10 @@
 
         members = []
         for layer in range(blocks):
-            members += [(layer, [qkv_s, out_s]), (layer, [kv2_s, q2_s, out2_s])]
-            members += [(layer, [ff1_s, ff2_s])] if layer < blocks - 1 else [(layer, [ff1_s]), (layer, [ff2_s])]
+            if layer < blocks - 1:
+                members += [(layer, [qkv_s, out_s]), (layer, [kv2_s, q2_s, out2_s]), (layer, [ff1_s, ff2_s])]
+            else:
+                members += [(layer, [qkv_s, out_s, kv2_s, q2_s, out2_s]), (layer, [ff1_s]), (layer, [ff2_s])]
         groups = []
         for index, (layer, parts) in enumerate(members):
             block = pack(parts, layer, [vec_block] if index == 0 else [], width)
@@ -1054,56 +1154,70 @@
         ctx, ctx_mine, ctx_other = prepare_context(context, n_dev)
 
         h = tokens_x.reshape(count, width)
-        saved = []
+        saved, attention_groups = [], []
         for layer in range(blocks):
             rows, bias = rows_all[layer], bias_all[layer]
-            group = groups[3 * layer:3 * layer + 2]
-            norm1, qkv, mix1, h1 = self_forward(h, rows, group[0], tokens)
-            norm2, query, kv, mix2, h2 = cross_forward(h1, rows, ctx, group[1], tokens, valid)
+            group = groups[3 * layer:3 * layer + 2] if layer < blocks - 1 else [groups[3 * layer]] * 2
+            attention_groups.append(group)
             if layer < blocks - 1:
+                norm1, qkv, mix1, h1 = self_forward(h, rows, group[0], tokens)
+                norm2, query, kv, mix2, h2 = cross_forward(h1, rows, ctx, group[1], tokens, valid)
                 norm3, gated, save_a, save_g, h3 = ff_forward(h2, rows, bias, ff_groups[layer], ff_offsets[layer])
             else:
+                norm1, qkv, mix1, h1, norm2, query, kv, mix2, h2 = attention_forward(h, rows, ctx, group[0], tokens, valid)
                 norm3, gated, save_a, save_g = ff_up_forward(h2, rows, bias, groups[-2])
                 out_tokens = ff_down_forward(h2, rows, gated, groups[-1])
             saved.append((h, norm1, qkv, mix1, h1, norm2, query, kv, mix2, h2, norm3, gated, save_a, save_g))
             h = h3 if layer < blocks - 1 else None
 
-        grad = cot_out.reshape(count, width)
+        grad = rounded = cot_out.reshape(count, width)
         results, vec_grads = [None] * blocks, [None] * blocks
         for layer in reversed(range(blocks)):
             turn = blocks - 1 - layer
-            rows, group = rows_all[layer], groups[3 * layer:3 * layer + 2]
+            rows, group = rows_all[layer], attention_groups[layer]
             h0, norm1, qkv, mix1, h1, norm2, query, kv, mix2, h2, norm3, gated, save_a, save_g = saved[layer]
 
             def reduce(pair):
-                return finish_scatter(pair[0], pair[1], n_dev)
-
-            r_ff2 = reduce(weight_grads(1, (gated, grad.astype(BF16)),
+                return scatter(pair[0], pair[1], n_dev)
+
+            r_ff2 = reduce(weight_grads(1, (gated, rounded),
                                            [(0, c * width, 1, 0, 0, half // n_dev, (c,)) for c in range(half // width)], half // n_dev))
-            grad, vec3, vec_b1, *pair = ff_grads(5 + turn, grad, save_a, save_g, norm3, h2, rows, ff_groups[layer],
-                                                 ff_offsets[layer])
-            r_ff1 = reduce(pair)
-            grad, vec2, *pair = cross_backward(grad, query, kv, h1, rows, norm2, mix2, ctx_mine, ctx_other, group[1],
+            sizes = (4,) if turn == 0 else (2, 2)
+            d_norm, r_ff1, bias_grads, first_chunk = None, [], [], 0
+            for index, chunks in enumerate(sizes):
+                *out, vec_b1, far, keep = ff_grads(5 + turn + index, grad, save_a, save_g, norm3, h2, rows,
+                                                   ff_groups[layer], ff_offsets[layer], first_chunk, chunks, d_norm)
+                d_norm = out[0]
+                bias_grads.append(((first_chunk, chunks), vec_b1))
+                r_ff1.append(reduce((far, keep)))
+                first_chunk += chunks
+            grad, vec3 = out
+            grad, vec2, *pair = cross_backward(3 + turn, grad, query, kv, h1, rows, norm2, mix2, ctx_mine, ctx_other, group[1],
                                                tokens, valid)
             r_cross = reduce(pair)
-            grad, vec1, *pair = self_backward(8 + turn, grad, qkv, h0, rows, norm1, mix1, group[0], tokens,
-                                              BF16 if layer == 0 else F32)
+            grad, rounded, vec1, *pair = self_backward(8 + turn, grad, qkv, h0, rows, norm1, mix1, group[0], tokens)
             r_self = reduce(pair)
-            side = lambda array, blocks_of: jnp.concatenate(jnp.split(array, blocks_of, 0), 1)
-            results[layer] = [side(r_self[:3 * depth], 3), r_self[3 * depth:], r_cross[:depth], side(r_cross[2 * depth:], 2), r_cross[depth:2 * depth],
-                              side(r_ff1, 8), r_ff2]
-            vec_grads[layer] = [vec1, vec2, vec3, vec_b1]
-        vec_out = vec_total([part for parts in vec_grads for part in parts], vec_rows, n_dev)
+            results[layer] = [r_self], [r_cross], r_ff1, [r_ff2], sizes
+            vec_grads[layer] = ([vec1, vec2, vec3] + [array for _, array in bias_grads], tuple(where for where, _ in bias_grads))
+        vec_out = vec_total([part for parts, _ in vec_grads for part in parts], tuple(where for _, where in vec_grads), vec_rows, n_dev)
         vec_out = vec_out[:blocks * vec_each].reshape(blocks, vec_each * width)
         vec_out = jnp.pad(vec_out, ((0, 0), (0, vec_len * n_dev - vec_each * width)))
         vec_out = lax.dynamic_slice(vec_out, (0, me * vec_len), (blocks, vec_len))
-        outs = []
-        for index in range(7):
-            stacked = jnp.stack([results[layer][index] for layer in range(blocks)]) / total
-            stacked = lax.optimization_barrier(stacked)
-            outs.append(stacked.reshape(blocks, -1))
+        ff1_plans = []
+        for layer in range(blocks):
+            size = results[layer][4][0]
+            ff1_plans.append([[(chunk // size, (kind * size + chunk % size) * depth) for kind in range(2) for chunk in range(4)]])
+        deep = ctx_width // n_dev
+        plans = ([[[(0, 0), (0, depth), (0, 2 * depth)], [(0, 3 * depth)]]] * blocks,
+                 [[[(0, 0)], [(0, depth)], [(0, 2 * depth), (0, 2 * depth + deep)]]] * blocks, ff1_plans, [[[(0, 0)]]] * blocks)
+        depths = ((depth, depth), (depth, depth, deep), (depth,), (half // n_dev,))
+        summed = []
+        for index in range(4):
+            summed += totals([results[layer][index] for layer in range(blocks)], plans[index], depths[index], 1.0 / total)
+        g_qkv, g_out, g_q2, g_out2, g_kv2, g_ff1, g_ff2 = summed
+        outs = [g_qkv, g_out, g_q2, g_kv2, g_out2, g_ff1, g_ff2]
         outs.append(vec_out / total)
-        return tuple([out_tokens.reshape(tokens_x.shape), grad.reshape(tokens_x.shape)] + outs)
+        return tuple([out_tokens.reshape(tokens_x.shape), rounded.reshape(tokens_x.shape)] + outs)
 
     param_spec = P(None, AXIS)
     in_specs = (P(AXIS), P(AXIS), P(AXIS)) + (param_spec,) * 8

time: 898 us -> 858 us (0.955)
  waiting for transfers between devices: 337 us -> 289 us
  Pallas kernels: 445 us -> 476 us
  local copies, waits for them, and re-layouts: 32.3 us -> 18.6 us
    pallas_call x3 -> x9, Pallas kernels: 98.5 us -> 170 us  [the longest x3 109 us: ff_grads(): pl.pallas_call(functools.partial(ff_grad_kernel, offset, first, resumed,...]
    ppermute x69 -> x64, waiting for transfers between devices: 337 us -> 289 us  [permute(): return lax.ppermute(array, AXIS, perm)]
    pallas_call x2 -> x1, Pallas kernels: 41 us -> 20.2 us  [self_forward(): call(functools.partial(self_forward_kernel, STEP // tokens, tokens), coun...]
    pallas_call x2 -> x1, Pallas kernels: 39.1 us -> 19.9 us  [cross_forward(): call(functools.partial(cross_forward_kernel, STEP // tokens, tokens, vali...]
    unnamed x112 -> x95, local copies, waits for them, and re-layouts: 27.6 us -> 15.1 us
    ppermute x69 -> x64, starting transfers between devices: 56.3 us -> 52.3 us  [permute(): return lax.ppermute(array, AXIS, perm)]
  transfers between devices with their start and end apart: 69 -> 64, of which waited for: 19 -> 14; matrix products, arithmetic and copies ran while one was open for 4% -> 2% of each run, Pallas kernels for 28% -> 45%
where the time goes in v5:
time: 858 us; the launch traced here: 850 us
  Pallas kernels  476 us (55%)
  waiting for transfers between devices  289 us (34%)
  starting transfers between devices  52.3 us (6%)
  local copies, waits for them, and re-layouts  18.6 us (2%)
  other arithmetic  12.8 us (1%)
    ppermute x64, waiting for transfers between devices, permute(): return lax.ppermute(array, AXIS, perm)  289 us
    pallas_call x3, Pallas kernels, ff_grads(): pl.pallas_call(functools.partial(ff_grad_kernel, offset, first, resumed,...  109 us
    pallas_call x2, Pallas kernels, self_backward(): call(functools.partial(self_backward_kernel, STEP // tokens, tokens), cou...  84.2 us
    pallas_call x2, Pallas kernels, cross_backward(): call(functools.partial(cross_backward_kernel, STEP // tokens, tokens, val...  56.8 us
    ppermute x64, starting transfers between devices, permute(): return lax.ppermute(array, AXIS, perm)  52.3 us
    pallas_call x1, Pallas kernels, attention_forward(): call(functools.partial(attention_forward_kernel, STEP // tokens, tokens,...  37.6 us
    pallas_call x2, Pallas kernels, weight_grads(): pl.pallas_call(functools.partial(grad_kernel, tiles, group_rows, len(arra...  34.7 us
    pallas_call x1, Pallas kernels, ff_forward(): call(functools.partial(ff_forward_kernel, offset), count // FF_STEP, [by_...  31.7 us
  transfers between devices with their start and end apart: 64, of which 14 were waited for; matrix products, arithmetic and copies ran while one was open for 2% of the time, Pallas kernels for 45%

profile of v5, /device:TPU:0, one launch (start us, length us, event | category | flops | bytes accessed | tf_op | source)
XLA Modules:
  0.0 850.3 jit_solution(12986513128868252102)
XLA Ops:
  0.7 2.2 copy.53
  2.9 1.5 copy.51
  4.4 1.8 pack.11.refs_0_.refs_8_
  6.2 3.3 collective-permute-start.36
  9.5 1.5 collective-permute-start.35
  13.7 1.9 pack.6.refs_0_
  16.4 2.1 pack.10.refs_0_
  19.8 2.3 collective-permute-start.29
  22.1 1.6 collective-permute-start.28
  24.5 2.1 pack.7.refs_0_
  26.7 3.0 collective-permute-done.1.refs_2_
  29.7 2.4 collective-permute-start.8
  32.1 1.6 collective-permute-start.7
  33.7 2.4 pack.8.refs_0_.refs_8_.refs_1_.refs_9_
  36.1 11.1 %collective-permute-done.29.refs_2_ = bf16[640,640]{1,0:T(8,128)(2,1)S(1)} collective-permute-done((bf16[640,640]{1,0:T(8,128)(2,1)S(1)}, bf16[640,640]{1,0:T(8,128)(2,1)S(1)}, u32[]{:S(2)}, u32[]{:S(2)}) %collective-permute-start.29) | collective-permute-done | bytes 819232 | tf_op jit(solution)/shard_map/ppermute | solution.py:80
  48.1 2.0 collective-permute-start.14
  50.1 15.6 %collective-permute-done.8.refs_2_ = bf16[672,640]{1,0:T(8,128)(2,1)} collective-permute-done((bf16[672,640]{1,0:T(8,128)(2,1)}, bf16[672,640]{1,0:T(8,128)(2,1)}, u32[]{:S(2)}, u32[]{:S(2)}) %collective-permute-start.8) | collective-permute-done | bytes 860192 | tf_op jit(solution)/shard_map/ppermute | solution.py:80
  65.7 2.5 collective-permute-start.15
  68.2 2.1 collective-permute-start.9
  70.4 27.3 %collective-permute-done.2.refs_3_ = bf16[368,640]{1,0:T(8,128)(2,1)} collective-permute-done((bf16[368,640]{1,0:T(8,128)(2,1)}, bf16[368,640]{1,0:T(8,128)(2,1)}, u32[]{:S(2)}, u32[]{:S(2)}) %collective-permute-start.2) | collective-permute-done | bytes 471072 | tf_op jit(solution)/shard_map/ppermute | solution.py:80
  97.6 2.4 pack.9.refs_0_
  101.1 1.6 collective-permute-start.16
  103.2 6.7 collective-permute-done.9.refs_3_
  109.9 3.7 context.1
  113.7 1.8 vec_sum.1
  117.7 13.4 %collective-permute-done.21.refs_1_ = bf16[992,640]{1,0:T(8,128)(2,1)} collective-permute-done((bf16[992,640]{1,0:T(8,128)(2,1)}, bf16[992,640]{1,0:T(8,128)(2,1)}, u32[]{:S(2)}, u32[]{:S(2)}) %collective-permute-start.21) | collective-permute-done | bytes 1269792 | tf_op jit(solution)/shard_map/ppermute | solution.py:80
  131.2 2.0 collective-permute-start.22
  133.7 1.9 collective-permute-start.23
  136.3 20.2 %shard_map.186 = (bf16[1536,640]{1,0:T(8,128)(2,1)}, bf16[1536,1920]{1,0:T(8,128)(2,1)}, bf16[1536,640]{1,0:T(8,128)(2,1)}, f32[1536,640]{1,0:T(8,128)}) custom-call(bf16[1536,640]{1,0:T(8,128)(2,1)} %bitcast.91, f32[16,640]{1,0:T(8,128)} %get-tuple-element.167.rows_ref, bf16[368,640]{1,0:T(8,128)(2,1)} %pack.6.refs_0_, ...), custom_call_target="tpu_custom_call" | custom-call | flops 6039797760 | bytes 20000000 | tf_op jit(solution)/shard_map/pallas_call | solution.py:627
  156.5 19.9 %shard_map.187 = (bf16[1536,640]{1,0:T(8,128)(2,1)}, bf16[1536,640]{1,0:T(8,128)(2,1)}, bf16[480,1280]{1,0:T(8,128)(2,1)}, bf16[1536,640]{1,0:T(8,128)(2,1)}, f32[1536,640]{1,0:T(8,128)}) custom-call(f32[1536,640]{1,0:T(8,128)} %get-tuple-element.89.h_ref, f32[16,640]{1,0:T(8,128)} %get-tuple-element.167.rows_ref, ...), custom_call_target="tpu_custom_call" | custom-call | flops 5536481280 | bytes 20000000 | tf_op jit(solution)/shard_map/pallas_call | solution.py:639
  178.1 31.7 %shard_map.188 = (bf16[1536,640]{1,0:T(8,128)(2,1)}, bf16[1536,2560]{1,0:T(8,128)(2,1)}, f32[1536,2560]{1,0:T(8,128)}, f32[1536,2560]{1,0:T(8,128)}, f32[1536,640]{1,0:T(8,128)}) custom-call(f32[1536,640]{1,0:T(8,128)} %get-tuple-element.94.h_ref, f32[16,640]{1,0:T(8,128)} %get-tuple-element.167.rows_ref, f32[1,5120]{1,0:T(1,128)} %bitcast.89, ...), custom_call_target="tpu_custom_call" | custom-call | flops 15099494400 | bytes 60000000 | tf_op jit(solution)/shard_map/pallas_call | solution.py:669
  210.1 1.7 collective-permute-start.37
  212.9 37.6 %shard_map.189 = (bf16[1536,640]{1,0:T(8,128)(2,1)}, bf16[1536,1920]{1,0:T(8,128)(2,1)}, bf16[1536,640]{1,0:T(8,128)(2,1)}, f32[1536,640]{1,0:T(8,128)}, bf16[15...) custom-call(f32[1536,640]{1,0:T(8,128)} %get-tuple-element.97.h_ref,, ...), custom_call_target="tpu_custom_call" | custom-call | flops 11576279040 | bytes 40000000 | tf_op jit(solution)/shard_map/pallas_call | solution.py:656
  252.1 28.5 %shard_map.190 = (bf16[1536,640]{1,0:T(8,128)(2,1)}, bf16[1536,2560]{1,0:T(8,128)(2,1)}, f32[1536,2560]{1,0:T(8,128)}, f32[1536,2560]{1,0:T(8,128)}) custom-call(f32[1536,640]{1,0:T(8,128)} %get-tuple-element.98.h_ref, f32[16,640]{1,0:T(8,128)} %get-tuple-element.166.rows_ref, f32[1,5120]{1,0:T(1,128)} %bitcast.88, bf16[640,640]{1,0:T(8,128)(2,1)} %pack.10.refs_0_, ...), custom_call_target="tpu_custom_call" | custom-call | flops 10066329600 | bytes 50000000 | tf_op jit(solution)/shard_map/pallas_call | solution.py:682
  282.2 48.4 %shard_map.192 = (f32[1536,640]{1,0:T(8,128)}, f32[8,640]{1,0:T(8,128)}, f32[8,5120]{1,0:T(8,128)}, f32[1280,640]{1,0:T(8,128)}, f32[1280,640]{1,0:T(8,128)}) custom-call(bf16[1536,640]{1,0:T(8,128)(2,1)} %bitcast.93, f32[1536,2560]{1,0:T(8,128)} %get-tuple-element.100.save_a, f32[1536,2560]{1,0:T(8,128)} %get-tuple-element.101.save_g, ...), custom_call_target="tpu_custom_call" | custom-call | flops 25165824000 | bytes 60000000 | tf_op jit(solution)/shard_map/pallas_call | solution.py:1050
  330.7 28.2 %shard_map.193 = (f32[1536,640]{1,0:T(8,128)}, f32[8,640]{1,0:T(8,128)}, f32[1344,640]{1,0:T(8,128)}, f32[1344,640]{1,0:T(8,128)}) custom-call(f32[1536,640]{1,0:T(8,128)} %get-tuple-element.103.grad_ref, bf16[1536,640]{1,0:T(8,128)(2,1)} %get-tuple-element.104.query_ref, bf16[480,1280]{1,0:T(8,128)(2,1)} %get-tuple-element.105.kv_ref, ...), custom_call_target="tpu_custom_call" | custom-call | flops 8975810560 | bytes 20000000 | tf_op jit(solution)/shard_map/pallas_call | solution.py:710
  358.9 41.2 %shard_map.194 = (f32[1536,640]{1,0:T(8,128)}, bf16[1536,640]{1,0:T(8,128)(2,1)}, f32[8,640]{1,0:T(8,128)}, f32[640,640]{1,0:T(8,128)}, f32[640,640]{1,0:T(8,128)}) custom-call(f32[1536,640]{1,0:T(8,128)} %get-tuple-element.111.grad_ref, bf16[1536,1920]{1,0:T(8,128)(2,1)} %get-tuple-element.112.qkv_ref, f32[1536,640]{1,0:T(8,128)} %get-tuple-element.97.h_ref, ...), custom_call_target="tpu_custom_call" | custom-call | flops 12582912000 | bytes 30000000 | tf_op jit(solution)/shard_map/pallas_call | solution.py:728
  400.1 17.5 %shard_map.199 = (f32[640,640]{1,0:T(8,128)}, f32[640,640]{1,0:T(8,128)}) custom-call(bf16[1536,2560]{1,0:T(8,128)(2,1)} %get-tuple-element.149.refs_0_, bf16[1536,640]{1,0:T(8,128)(2,1)} %get-tuple-element.150.refs_1_), custom_call_target="tpu_custom_call" | custom-call | flops 5033164800 | bytes 20000000 | tf_op jit(solution)/shard_map/pallas_call | solution.py:826
  418.1 1.5 collective-permute-start.45
  420.2 28.4 %shard_map.195 = (f32[1536,640]{1,0:T(8,128)}, f32[8,2560]{1,0:T(8,128)}, f32[640,640]{1,0:T(8,128)}, f32[640,640]{1,0:T(8,128)}) custom-call(f32[1536,640]{1,0:T(8,128)} %get-tuple-element.115.grad_ref, f32[1536,2560]{1,0:T(8,128)} %get-tuple-element.116.save_a, f32[1536,2560]{1,0:T(8,128)} %get-tuple-element.117.save_g, ...), custom_call_target="tpu_custom_call" | custom-call | flops 12582912000 | bytes 60000000 | tf_op jit(solution)/shard_map/pallas_call | solution.py:1050
  448.5 32.2 %shard_map.196 = (f32[1536,640]{1,0:T(8,128)}, f32[8,640]{1,0:T(8,128)}, f32[8,2560]{1,0:T(8,128)}, f32[640,640]{1,0:T(8,128)}, f32[640,640]{1,0:T(8,128)}) custom-call(f32[1536,640]{1,0:T(8,128)} %get-tuple-element.115.grad_ref, f32[1536,2560]{1,0:T(8,128)} %get-tuple-element.116.save_a, f32[1536,2560]{1,0:T(8,128)} %get-tuple-element.117.save_g, ...), custom_call_target="tpu_custom_call" | custom-call | flops 12582912000 | bytes 60000000 | tf_op jit(solution)/shard_map/pallas_call | solution.py:1050
  480.8 28.6 %shard_map.197 = (f32[1536,640]{1,0:T(8,128)}, f32[8,640]{1,0:T(8,128)}, f32[1344,640]{1,0:T(8,128)}, f32[1344,640]{1,0:T(8,128)}) custom-call(f32[1536,640]{1,0:T(8,128)} %get-tuple-element.120.grad_ref, bf16[1536,640]{1,0:T(8,128)(2,1)} %get-tuple-element.121.query_ref, bf16[480,1280]{1,0:T(8,128)(2,1)} %get-tuple-element.122.kv_ref, ...), custom_call_target="tpu_custom_call" | custom-call | flops 8975810560 | bytes 20000000 | tf_op jit(solution)/shard_map/pallas_call | solution.py:710
  509.3 43.0 %shard_map.198 = (f32[1536,640]{1,0:T(8,128)}, bf16[1536,640]{1,0:T(8,128)(2,1)}, f32[8,640]{1,0:T(8,128)}, f32[640,640]{1,0:T(8,128)}, f32[640,640]{1,0:T(8,128)}) custom-call(f32[1536,640]{1,0:T(8,128)} %get-tuple-element.125.grad_ref, bf16[1536,1920]{1,0:T(8,128)(2,1)} %get-tuple-element.126.qkv_ref, bf16[1536,640]{1,0:T(8,128)(2,1)} %bitcast.92, ...), custom_call_target="tpu_custom_call" | custom-call | flops 12582912000 | bytes 30000000 | tf_op jit(solution)/shard_map/pallas_call | solution.py:728
  552.4 1.8 vec_pack.1
  554.4 1.5 collective-permute-start.47
  558.2 38.2 %collective-permute-done.62 = f32[48,640]{1,0:T(8,128)S(1)} collective-permute-done((f32[48,640]{1,0:T(8,128)S(1)}, f32[48,640]{1,0:T(8,128)S(1)}, u32[]{:S(2)}, u32[]{:S(2)}) %collective-permute-start.62) | collective-permute-done | bytes 122912 | tf_op jit(solution)/shard_map/ppermute | solution.py:80
  596.4 1.4 collective-permute-start.63
  597.8 17.2 %shard_map.200 = (f32[640,640]{1,0:T(8,128)}, f32[640,640]{1,0:T(8,128)}) custom-call(bf16[1536,2560]{1,0:T(8,128)(2,1)} %get-tuple-element.99.gated_ref.refs_0_, bf16[1536,640]{1,0:T(8,128)(2,1)} %bitcast.94), custom_call_target="tpu_custom_call" | custom-call | flops 5033164800 | bytes 20000000 | tf_op jit(solution)/shard_map/pallas_call | solution.py:826
  617.8 18.6 %collective-permute-done.59.refs_4_ = f32[640,640]{1,0:T(8,128)S(1)} collective-permute-done((f32[640,640]{1,0:T(8,128)}, f32[640,640]{1,0:T(8,128)S(1)}, u32[]{:S(2)}, u32[]{:S(2)}) %collective-permute-start.59) | collective-permute-done | bytes 1638432 | tf_op jit(solution)/shard_map/ppermute | solution.py:80
  637.0 16.9 %collective-permute-done.43.refs_1_ = f32[640,640]{1,0:T(8,128)S(1)} collective-permute-done((f32[640,640]{1,0:T(8,128)S(1)}, f32[640,640]{1,0:T(8,128)S(1)}, u32[]{:S(2)}, u32[]{:S(2)}) %collective-permute-start.43) | collective-permute-done | bytes 1638432 | tf_op jit(solution)/shard_map/ppermute | solution.py:80
  657.6 1.4 collective-permute-start.58
  659.8 3.0 slice_add_fusion
  662.9 1.8 slice_add_fusion.1
  664.7 59.4 %collective-permute-done.53.refs_4_ = f32[640,640]{1,0:T(8,128)S(1)} collective-permute-done((f32[640,640]{1,0:T(8,128)}, f32[640,640]{1,0:T(8,128)S(1)}, u32[]{:S(2)}, u32[]{:S(2)}) %collective-permute-start.53) | collective-permute-done | bytes 1638432 | tf_op jit(solution)/shard_map/ppermute | solution.py:80
  724.8 25.7 %collective-permute-done.51.refs_1_ = f32[640,640]{1,0:T(8,128)S(1)} collective-permute-done((f32[640,640]{1,0:T(8,128)}, f32[640,640]{1,0:T(8,128)S(1)}, u32[]{:S(2)}, u32[]{:S(2)}) %collective-permute-start.51) | collective-permute-done | bytes 1638432 | tf_op jit(solution)/shard_map/ppermute | solution.py:80
  751.1 1.4 collective-permute-start.50
  759.9 2.9 collective-permute-done.44.refs_2_
  764.4 12.2 %shard_map.191 = bf16[1536,640]{1,0:T(8,128)(2,1)} custom-call(f32[1536,640]{1,0:T(8,128)} %get-tuple-element.98.h_ref, f32[16,640]{1,0:T(8,128)} %get-tuple-element.166.rows_ref, bf16[1536,2560]{1,0:T(8,128)(2,1)} %get-tuple-element.99.gated_ref.refs_0_, bf16[320,640]{1,0:T(8,128)(2,1)} %pack.11.refs_0_.refs_8_, ...), custom_call_target="tpu_custom_call" | custom-call | flops 5033164800 | bytes 20000000 | tf_op jit(solution)/shard_map/pallas_call | solution.py:694
  777.4 3.8 totals.7
  781.2 3.8 totals.4
  785.0 41.1 %collective-permute-done.54.refs_5_ = f32[320,640]{1,0:T(8,128)} collective-permute-done((f32[320,640]{1,0:T(8,128)}, f32[320,640]{1,0:T(8,128)}, u32[]{:S(2)}, u32[]{:S(2)}) %collective-permute-start.54) | collective-permute-done | bytes 819232 | tf_op jit(solution)/shard_map/ppermute | solution.py:80
  826.1 8.8 %collective-permute-done.52.refs_2_ = f32[320,640]{1,0:T(8,128)} collective-permute-done((f32[320,640]{1,0:T(8,128)}, f32[320,640]{1,0:T(8,128)}, u32[]{:S(2)}, u32[]{:S(2)}) %collective-permute-start.52) | collective-permute-done | bytes 819232 | tf_op jit(solution)/shard_map/ppermute | solution.py:80
  834.9 7.5 totals.6
  842.4 6.4 totals.5
  (210 shorter events, 41.4 us)
Async XLA Ops:
  6.2 13.4 %collective-permute-start.36 = (bf16[320,640]{1,0:T(8,128)(2,1)}, bf16[320,640]{1,0:T(8,128)(2,1)}, u32[]{:S(2)}, u32[]{:S(2)}) collective-permute-start(bf16[320,640]{1,0:T(8,128)(2,1)} %pack.11.refs_0_.refs_8_), channel_id=1, source_target_pairs={{0,2},{1,5},{2,0},{3,7},{4,6},{5,1},{6,4},{7,3}} | collective-permute-start | bytes 1228808 | tf_op jit(solution)/shard_map/ppermute | solution.py:80
  9.5 12.6 %collective-permute-start.35 = (bf16[320,640]{1,0:T(8,128)(2,1)}, bf16[320,640]{1,0:T(8,128)(2,1)}, u32[]{:S(2)}, u32[]{:S(2)}) collective-permute-start(bf16[320,640]{1,0:T(8,128)(2,1)} %pack.11.refs_0_.refs_8_), channel_id=1, source_target_pairs={{0,4},{1,3},{2,6},{3,1},{4,0},{5,7},{6,2},{7,5}} | collective-permute-start | bytes 1228808 | tf_op jit(solution)/shard_map/ppermute | solution.py:80
  15.7 11.0 %collective-permute-start.3 = (bf16[368,640]{1,0:T(8,128)(2,1)}, bf16[368,640]{1,0:T(8,128)(2,1)S(1)}, u32[]{:S(2)}, u32[]{:S(2)}) collective-permute-start(bf16[368,640]{1,0:T(8,128)(2,1)} %pack.6.refs_0_), channel_id=1, source_target_pairs={{0,1},{1,0},{2,3},{3,2},{4,5},{5,4},{6,7},{7,6}} | collective-permute-start | bytes 1413128 | tf_op jit(solution)/shard_map/ppermute | solution.py:80
  15.7 14.0 %collective-permute-start.1 = (bf16[368,640]{1,0:T(8,128)(2,1)}, bf16[368,640]{1,0:T(8,128)(2,1)S(1)}, u32[]{:S(2)}, u32[]{:S(2)}) collective-permute-start(bf16[368,640]{1,0:T(8,128)(2,1)} %pack.6.refs_0_), channel_id=1, source_target_pairs={{0,2},{1,5},{2,0},{3,7},{4,6},{5,1},{6,4},{7,3}} | collective-permute-start | bytes 1413128 | tf_op jit(solution)/shard_map/ppermute | solution.py:80
  16.4 15.7 %collective-permute-start = (bf16[368,640]{1,0:T(8,128)(2,1)}, bf16[368,640]{1,0:T(8,128)(2,1)}, u32[]{:S(2)}, u32[]{:S(2)}) collective-permute-start(bf16[368,640]{1,0:T(8,128)(2,1)} %pack.6.refs_0_), channel_id=1, source_target_pairs={{0,4},{1,3},{2,6},{3,1},{4,0},{5,7},{6,2},{7,5}} | collective-permute-start | bytes 1413128 | tf_op jit(solution)/shard_map/ppermute | solution.py:80
  19.8 27.3 %collective-permute-start.29 = (bf16[640,640]{1,0:T(8,128)(2,1)S(1)}, bf16[640,640]{1,0:T(8,128)(2,1)S(1)}, u32[]{:S(2)}, u32[]{:S(2)}) collective-permute-start(bf16[640,640]{1,0:T(8,128)(2,1)S(1)} %copy-done.22), channel_id=1, source_target_pairs={{0,2},{1,5},{2,0},{3,7},{4,6},{5,1},{6,4},{7,3}} | collective-permute-start | bytes 2457608 | tf_op jit(solution)/shard_map/ppermute | solution.py:80
  22.1 26.0 %collective-permute-start.28 = (bf16[640,640]{1,0:T(8,128)(2,1)S(1)}, bf16[640,640]{1,0:T(8,128)(2,1)}, u32[]{:S(2)}, u32[]{:S(2)}) collective-permute-start(bf16[640,640]{1,0:T(8,128)(2,1)S(1)} %copy-done.22), channel_id=1, source_target_pairs={{0,4},{1,3},{2,6},{3,1},{4,0},{5,7},{6,2},{7,5}} | collective-permute-start | bytes 2457608 | tf_op jit(solution)/shard_map/ppermute | solution.py:80
  26.7 23.4 %collective-permute-start.10 = (bf16[672,640]{1,0:T(8,128)(2,1)}, bf16[672,640]{1,0:T(8,128)(2,1)}, u32[]{:S(2)}, u32[]{:S(2)}) collective-permute-start(bf16[672,640]{1,0:T(8,128)(2,1)} %pack.7.refs_0_), channel_id=1, source_target_pairs={{0,1},{1,0},{2,3},{3,2},{4,5},{5,4},{6,7},{7,6}} | collective-permute-start | bytes 2580488 | tf_op jit(solution)/shard_map/ppermute | solution.py:80
  29.7 36.0 %collective-permute-start.8 = (bf16[672,640]{1,0:T(8,128)(2,1)}, bf16[672,640]{1,0:T(8,128)(2,1)}, u32[]{:S(2)}, u32[]{:S(2)}) collective-permute-start(bf16[672,640]{1,0:T(8,128)(2,1)} %pack.7.refs_0_), channel_id=1, source_target_pairs={{0,2},{1,5},{2,0},{3,7},{4,6},{5,1},{6,4},{7,3}} | collective-permute-start | bytes 2580488 | tf_op jit(solution)/shard_map/ppermute | solution.py:80
  32.1 33.6 %collective-permute-start.7 = (bf16[672,640]{1,0:T(8,128)(2,1)}, bf16[672,640]{1,0:T(8,128)(2,1)}, u32[]{:S(2)}, u32[]{:S(2)}) collective-permute-start(bf16[672,640]{1,0:T(8,128)(2,1)} %pack.7.refs_0_), channel_id=1, source_target_pairs={{0,4},{1,3},{2,6},{3,1},{4,0},{5,7},{6,2},{7,5}} | collective-permute-start | bytes 2580488 | tf_op jit(solution)/shard_map/ppermute | solution.py:80
  47.2 52.9 %collective-permute-start.17 = (bf16[960,640]{1,0:T(8,128)(2,1)}, bf16[960,640]{1,0:T(8,128)(2,1)S(1)}, u32[]{:S(2)}, u32[]{:S(2)}) collective-permute-start(bf16[960,640]{1,0:T(8,128)(2,1)} %pack.8.refs_0_.refs_8_.refs_1_.refs_9_), channel_id=1, source_target_pairs={{0,1},{1,0},{2,3},{3,2},{4,5},{5,4},{6,7},{7,6}} | collective-permute-start | bytes 3686408 | tf_op jit(solution)/shard_map/ppermute | solution.py:80
  48.1 53.0 %collective-permute-start.14 = (bf16[960,640]{1,0:T(8,128)(2,1)}, bf16[960,640]{1,0:T(8,128)(2,1)S(1)}, u32[]{:S(2)}, u32[]{:S(2)}) collective-permute-start(bf16[960,640]{1,0:T(8,128)(2,1)} %pack.8.refs_0_.refs_8_.refs_1_.refs_9_), channel_id=1, source_target_pairs={{0,4},{1,3},{2,6},{3,1},{4,0},{5,7},{6,2},{7,5}} | collective-permute-start | bytes 3686408 | tf_op jit(solution)/shard_map/ppermute | solution.py:80
  50.1 18.1 %collective-permute-start.5 = (bf16[368,640]{1,0:T(8,128)(2,1)}, bf16[368,640]{1,0:T(8,128)(2,1)}, u32[]{:S(2)}, u32[]{:S(2)}) collective-permute-start(bf16[368,640]{1,0:T(8,128)(2,1)} %copy-done.27), channel_id=1, source_target_pairs={{0,1},{1,0},{2,3},{3,2},{4,5},{5,4},{6,7},{7,6}} | collective-permute-start | bytes 1413128 | tf_op jit(solution)/shard_map/ppermute | solution.py:80
  65.7 2.5 collective-permute-start.4
  65.7 37.0 %collective-permute-start.15 = (bf16[960,640]{1,0:T(8,128)(2,1)}, bf16[960,640]{1,0:T(8,128)(2,1)}, u32[]{:S(2)}, u32[]{:S(2)}) collective-permute-start(bf16[960,640]{1,0:T(8,128)(2,1)} %pack.8.refs_0_.refs_8_.refs_1_.refs_9_), channel_id=1, source_target_pairs={{0,2},{1,5},{2,0},{3,7},{4,6},{5,1},{6,4},{7,3}} | collective-permute-start | bytes 3686408 | tf_op jit(solution)/shard_map/ppermute | solution.py:80
  68.2 29.5 %collective-permute-start.2 = (bf16[368,640]{1,0:T(8,128)(2,1)}, bf16[368,640]{1,0:T(8,128)(2,1)}, u32[]{:S(2)}, u32[]{:S(2)}) collective-permute-start(bf16[368,640]{1,0:T(8,128)(2,1)} %collective-permute-done.refs_1_), channel_id=1, source_target_pairs={{0,2},{1,5},{2,0},{3,7},{4,6},{5,1},{6,4},{7,3}} | collective-permute-start | bytes 1413128 | tf_op jit(solution)/shard_map/ppermute | solution.py:80
  68.2 41.7 %collective-permute-start.9 = (bf16[672,640]{1,0:T(8,128)(2,1)}, bf16[672,640]{1,0:T(8,128)(2,1)}, u32[]{:S(2)}, u32[]{:S(2)}) collective-permute-start(bf16[672,640]{1,0:T(8,128)(2,1)} %collective-permute-done.7.refs_1_), channel_id=1, source_target_pairs={{0,2},{1,5},{2,0},{3,7},{4,6},{5,1},{6,4},{7,3}} | collective-permute-start | bytes 2580488 | tf_op jit(solution)/shard_map/ppermute | solution.py:80
  97.6 5.1 collective-permute-start.6
  100.1 31.1 %collective-permute-start.21 = (bf16[992,640]{1,0:T(8,128)(2,1)}, bf16[992,640]{1,0:T(8,128)(2,1)}, u32[]{:S(2)}, u32[]{:S(2)}) collective-permute-start(bf16[992,640]{1,0:T(8,128)(2,1)} %pack.9.refs_0_), channel_id=1, source_target_pairs={{0,4},{1,3},{2,6},{3,1},{4,0},{5,7},{6,2},{7,5}} | collective-permute-start | bytes 3809288 | tf_op jit(solution)/shard_map/ppermute | solution.py:80
  101.1 32.6 %collective-permute-start.16 = (bf16[960,640]{1,0:T(8,128)(2,1)S(1)}, bf16[960,640]{1,0:T(8,128)(2,1)}, u32[]{:S(2)}, u32[]{:S(2)}) collective-permute-start(bf16[960,640]{1,0:T(8,128)(2,1)S(1)} %collective-permute-done.14.refs_1_.refs_9_.refs_2_.refs_10_), channel_id=1, source_target_pairs={{0,2},{1,5},{2,0},{3,7},{4,6},{5,1},{6,4},{7,3}} | collective-permute-start | bytes 3686408 | tf_op jit(solution)/shard_map/ppermute | solution.py:80
  102.7 30.5 %collective-permute-start.12 = (bf16[672,640]{1,0:T(8,128)(2,1)}, bf16[672,640]{1,0:T(8,128)(2,1)}, u32[]{:S(2)}, u32[]{:S(2)}) collective-permute-start(bf16[672,640]{1,0:T(8,128)(2,1)} %collective-permute-done.8.refs_2_), channel_id=1, source_target_pairs={{0,1},{1,0},{2,3},{3,2},{4,5},{5,4},{6,7},{7,6}} | collective-permute-start | bytes 2580488 | tf_op jit(solution)/shard_map/ppermute | solution.py:80
  102.7 30.5 %collective-permute-start.11 = (bf16[672,640]{1,0:T(8,128)(2,1)}, bf16[672,640]{1,0:T(8,128)(2,1)}, u32[]{:S(2)}, u32[]{:S(2)}) collective-permute-start(bf16[672,640]{1,0:T(8,128)(2,1)} %collective-permute-done.7.refs_1_), channel_id=1, source_target_pairs={{0,1},{1,0},{2,3},{3,2},{4,5},{5,4},{6,7},{7,6}} | collective-permute-start | bytes 2580488 | tf_op jit(solution)/shard_map/ppermute | solution.py:80
  109.9 25.7 %collective-permute-start.13 = (bf16[672,640]{1,0:T(8,128)(2,1)}, bf16[672,640]{1,0:T(8,128)(2,1)}, u32[]{:S(2)}, u32[]{:S(2)}) collective-permute-start(bf16[672,640]{1,0:T(8,128)(2,1)} %collective-permute-done.9.refs_3_), channel_id=1, source_target_pairs={{0,1},{1,0},{2,3},{3,2},{4,5},{5,4},{6,7},{7,6}} | collective-permute-start | bytes 2580488 | tf_op jit(solution)/shard_map/ppermute | solution.py:80
  131.2 45.2 %collective-permute-start.22 = (bf16[992,640]{1,0:T(8,128)(2,1)}, bf16[992,640]{1,0:T(8,128)(2,1)}, u32[]{:S(2)}, u32[]{:S(2)}) collective-permute-start(bf16[992,640]{1,0:T(8,128)(2,1)} %pack.9.refs_0_), channel_id=1, source_target_pairs={{0,2},{1,5},{2,0},{3,7},{4,6},{5,1},{6,4},{7,3}} | collective-permute-start | bytes 3809288 | tf_op jit(solution)/shard_map/ppermute | solution.py:80
  133.2 43.8 %collective-permute-start.18 = (bf16[960,640]{1,0:T(8,128)(2,1)S(1)}, bf16[960,640]{1,0:T(8,128)(2,1)S(1)}, u32[]{:S(2)}, u32[]{:S(2)}) collective-permute-start(bf16[960,640]{1,0:T(8,128)(2,1)S(1)} %collective-permute-done.14.refs_1_.refs_9_.refs_2_.refs_10_), channel_id=1, source_target_pairs={{0,1},{1,0},{2,3},{3,2},{4,5},{5,4},{6,7},{7,6}} | collective-permute-start | bytes 3686408 | tf_op jit(solution)/shard_map/ppermute | solution.py:80
  133.2 43.7 %collective-permute-start.19 = (bf16[960,640]{1,0:T(8,128)(2,1)}, bf16[960,640]{1,0:T(8,128)(2,1)}, u32[]{:S(2)}, u32[]{:S(2)}) collective-permute-start(bf16[960,640]{1,0:T(8,128)(2,1)} %collective-permute-done.15.refs_2_.refs_10_.refs_3_.refs_11_), channel_id=1, source_target_pairs={{0,1},{1,0},{2,3},{3,2},{4,5},{5,4},{6,7},{7,6}} | collective-permute-start | bytes 3686408 | tf_op jit(solution)/shard_map/ppermute | solution.py:80
  133.7 43.6 %collective-permute-start.23 = (bf16[992,640]{1,0:T(8,128)(2,1)}, bf16[992,640]{1,0:T(8,128)(2,1)}, u32[]{:S(2)}, u32[]{:S(2)}) collective-permute-start(bf16[992,640]{1,0:T(8,128)(2,1)} %collective-permute-done.21.refs_1_), channel_id=1, source_target_pairs={{0,2},{1,5},{2,0},{3,7},{4,6},{5,1},{6,4},{7,3}} | collective-permute-start | bytes 3809288 | tf_op jit(solution)/shard_map/ppermute | solution.py:80
  135.7 41.9 %collective-permute-start.20 = (bf16[960,640]{1,0:T(8,128)(2,1)}, bf16[960,640]{1,0:T(8,128)(2,1)}, u32[]{:S(2)}, u32[]{:S(2)}) collective-permute-start(bf16[960,640]{1,0:T(8,128)(2,1)} %collective-permute-done.16.refs_3_.refs_11_.refs_4_.refs_12_), channel_id=1, source_target_pairs={{0,1},{1,0},{2,3},{3,2},{4,5},{5,4},{6,7},{7,6}} | collective-permute-start | bytes 3686408 | tf_op jit(solution)/shard_map/ppermute | solution.py:80
  176.4 33.4 %collective-permute-start.24 = (bf16[992,640]{1,0:T(8,128)(2,1)}, bf16[992,640]{1,0:T(8,128)(2,1)}, u32[]{:S(2)}, u32[]{:S(2)}) collective-permute-start(bf16[992,640]{1,0:T(8,128)(2,1)} %pack.9.refs_0_), channel_id=1, source_target_pairs={{0,1},{1,0},{2,3},{3,2},{4,5},{5,4},{6,7},{7,6}} | collective-permute-start | bytes 3809288 | tf_op jit(solution)/shard_map/ppermute | solution.py:80
  176.9 33.2 %collective-permute-start.30 = (bf16[640,640]{1,0:T(8,128)(2,1)}, bf16[640,640]{1,0:T(8,128)(2,1)}, u32[]{:S(2)}, u32[]{:S(2)}) collective-permute-start(bf16[640,640]{1,0:T(8,128)(2,1)} %collective-permute-done.28.refs_1_), channel_id=1, source_target_pairs={{0,2},{1,5},{2,0},{3,7},{4,6},{5,1},{6,4},{7,3}} | collective-permute-start | bytes 2457608 | tf_op jit(solution)/shard_map/ppermute | solution.py:80
  177.0 34.8 %collective-permute-start.25 = (bf16[992,640]{1,0:T(8,128)(2,1)}, bf16[992,640]{1,0:T(8,128)(2,1)S(1)}, u32[]{:S(2)}, u32[]{:S(2)}) collective-permute-start(bf16[992,640]{1,0:T(8,128)(2,1)} %collective-permute-done.21.refs_1_), channel_id=1, source_target_pairs={{0,1},{1,0},{2,3},{3,2},{4,5},{5,4},{6,7},{7,6}} | collective-permute-start | bytes 3809288 | tf_op jit(solution)/shard_map/ppermute | solution.py:80
  177.3 34.5 %collective-permute-start.26 = (bf16[992,640]{1,0:T(8,128)(2,1)}, bf16[992,640]{1,0:T(8,128)(2,1)}, u32[]{:S(2)}, u32[]{:S(2)}) collective-permute-start(bf16[992,640]{1,0:T(8,128)(2,1)} %collective-permute-done.22.refs_2_), channel_id=1, source_target_pairs={{0,1},{1,0},{2,3},{3,2},{4,5},{5,4},{6,7},{7,6}} | collective-permute-start | bytes 3809288 | tf_op jit(solution)/shard_map/ppermute | solution.py:80
  177.6 34.8 %collective-permute-start.27 = (bf16[992,640]{1,0:T(8,128)(2,1)}, bf16[992,640]{1,0:T(8,128)(2,1)}, u32[]{:S(2)}, u32[]{:S(2)}) collective-permute-start(bf16[992,640]{1,0:T(8,128)(2,1)} %collective-permute-done.23.refs_3_), channel_id=1, source_target_pairs={{0,1},{1,0},{2,3},{3,2},{4,5},{5,4},{6,7},{7,6}} | collective-permute-start | bytes 3809288 | tf_op jit(solution)/shard_map/ppermute | solution.py:80
  209.8 41.2 %collective-permute-start.31 = (bf16[640,640]{1,0:T(8,128)(2,1)S(1)}, bf16[640,640]{1,0:T(8,128)(2,1)S(1)}, u32[]{:S(2)}, u32[]{:S(2)}) collective-permute-start(bf16[640,640]{1,0:T(8,128)(2,1)S(1)} %copy-done.22), channel_id=1, source_target_pairs={{0,1},{1,0},{2,3},{3,2},{4,5},{5,4},{6,7},{7,6}} | collective-permute-start | bytes 2457608 | tf_op jit(solution)/shard_map/ppermute | solution.py:80
  210.1 40.4 %collective-permute-start.37 = (bf16[320,640]{1,0:T(8,128)(2,1)}, bf16[320,640]{1,0:T(8,128)(2,1)S(1)}, u32[]{:S(2)}, u32[]{:S(2)}) collective-permute-start(bf16[320,640]{1,0:T(8,128)(2,1)} %collective-permute-done.35.refs_1_.refs_9_), channel_id=1, source_target_pairs={{0,2},{1,5},{2,0},{3,7},{4,6},{5,1},{6,4},{7,3}} | collective-permute-start | bytes 1228808 | tf_op jit(solution)/shard_map/ppermute | solution.py:80
  211.8 39.8 %collective-permute-start.32 = (bf16[640,640]{1,0:T(8,128)(2,1)}, bf16[640,640]{1,0:T(8,128)(2,1)}, u32[]{:S(2)}, u32[]{:S(2)}) collective-permute-start(bf16[640,640]{1,0:T(8,128)(2,1)} %collective-permute-done.28.refs_1_), channel_id=1, source_target_pairs={{0,1},{1,0},{2,3},{3,2},{4,5},{5,4},{6,7},{7,6}} | collective-permute-start | bytes 2457608 | tf_op jit(solution)/shard_map/ppermute | solution.py:80
  211.8 39.3 %collective-permute-start.33 = (bf16[640,640]{1,0:T(8,128)(2,1)}, bf16[640,640]{1,0:T(8,128)(2,1)}, u32[]{:S(2)}, u32[]{:S(2)}) collective-permute-start(bf16[640,640]{1,0:T(8,128)(2,1)} %copy-done.36), channel_id=1, source_target_pairs={{0,1},{1,0},{2,3},{3,2},{4,5},{5,4},{6,7},{7,6}} | collective-permute-start | bytes 2457608 | tf_op jit(solution)/shard_map/ppermute | solution.py:80
  212.3 39.3 %collective-permute-start.34 = (bf16[640,640]{1,0:T(8,128)(2,1)}, bf16[640,640]{1,0:T(8,128)(2,1)}, u32[]{:S(2)}, u32[]{:S(2)}) collective-permute-start(bf16[640,640]{1,0:T(8,128)(2,1)} %collective-permute-done.30.refs_3_), channel_id=1, source_target_pairs={{0,1},{1,0},{2,3},{3,2},{4,5},{5,4},{6,7},{7,6}} | collective-permute-start | bytes 2457608 | tf_op jit(solution)/shard_map/ppermute | solution.py:80
  250.5 30.0 %collective-permute-start.38 = (bf16[320,640]{1,0:T(8,128)(2,1)S(1)}, bf16[320,640]{1,0:T(8,128)(2,1)S(1)}, u32[]{:S(2)}, u32[]{:S(2)}) collective-permute-start(bf16[320,640]{1,0:T(8,128)(2,1)S(1)} %copy-done.28), channel_id=1, source_target_pairs={{0,1},{1,0},{2,3},{3,2},{4,5},{5,4},{6,7},{7,6}} | collective-permute-start | bytes 1228808 | tf_op jit(solution)/shard_map/ppermute | solution.py:80
  251.1 79.6 %collective-permute-start.42 = (bf16[1024,512]{1,0:T(8,128)(2,1)}, bf16[1024,512]{1,0:T(8,128)(2,1)}, u32[]{:S(2)}, u32[]{:S(2)}) collective-permute-start(bf16[1024,512]{1,0:T(8,128)(2,1)} %get-tuple-element.110), channel_id=1, source_target_pairs={{0,1},{1,0},{2,3},{3,2},{4,5},{5,4},{6,7},{7,6}} | collective-permute-start | bytes 3145736 | tf_op jit(solution)/shard_map/ppermute | solution.py:80
  251.1 29.5 %collective-permute-start.39 = (bf16[320,640]{1,0:T(8,128)(2,1)}, bf16[320,640]{1,0:T(8,128)(2,1)S(1)}, u32[]{:S(2)}, u32[]{:S(2)}) collective-permute-start(bf16[320,640]{1,0:T(8,128)(2,1)} %collective-permute-done.35.refs_1_.refs_9_), channel_id=1, source_target_pairs={{0,1},{1,0},{2,3},{3,2},{4,5},{5,4},{6,7},{7,6}} | collective-permute-start | bytes 1228808 | tf_op jit(solution)/shard_map/ppermute | solution.py:80
  251.6 29.0 %collective-permute-start.40 = (bf16[320,640]{1,0:T(8,128)(2,1)}, bf16[320,640]{1,0:T(8,128)(2,1)S(1)}, u32[]{:S(2)}, u32[]{:S(2)}) collective-permute-start(bf16[320,640]{1,0:T(8,128)(2,1)} %collective-permute-done.36.refs_2_.refs_10_), channel_id=1, source_target_pairs={{0,1},{1,0},{2,3},{3,2},{4,5},{5,4},{6,7},{7,6}} | collective-permute-start | bytes 1228808 | tf_op jit(solution)/shard_map/ppermute | solution.py:80
  251.6 29.0 %collective-permute-start.41 = (bf16[320,640]{1,0:T(8,128)(2,1)S(1)}, bf16[320,640]{1,0:T(8,128)(2,1)S(1)}, u32[]{:S(2)}, u32[]{:S(2)}) collective-permute-start(bf16[320,640]{1,0:T(8,128)(2,1)S(1)} %collective-permute-done.37.refs_3_.refs_11_), channel_id=1, source_target_pairs={{0,1},{1,0},{2,3},{3,2},{4,5},{5,4},{6,7},{7,6}} | collective-permute-start | bytes 1228808 | tf_op jit(solution)/shard_map/ppermute | solution.py:80
  417.6 198.2 %collective-permute-start.57 = (f32[640,640]{1,0:T(8,128)}, f32[640,640]{1,0:T(8,128)}, u32[]{:S(2)}, u32[]{:S(2)}) collective-permute-start(f32[640,640]{1,0:T(8,128)} %get-tuple-element.152), channel_id=1, source_target_pairs={{0,2},{1,5},{2,0},{3,7},{4,6},{5,1},{6,4},{7,3}} | collective-permute-start | bytes 4915208 | tf_op jit(solution)/shard_map/ppermute | solution.py:80
  418.1 198.9 %collective-permute-start.45 = (f32[640,640]{1,0:T(8,128)}, f32[640,640]{1,0:T(8,128)}, u32[]{:S(2)}, u32[]{:S(2)}) collective-permute-start(f32[640,640]{1,0:T(8,128)} %get-tuple-element.133), channel_id=1, source_target_pairs={{0,2},{1,5},{2,0},{3,7},{4,6},{5,1},{6,4},{7,3}} | collective-permute-start | bytes 4915208 | tf_op jit(solution)/shard_map/ppermute | solution.py:80
  419.6 238.0 %collective-permute-start.49 = (f32[1344,640]{1,0:T(8,128)}, f32[1344,640]{1,0:T(8,128)}, u32[]{:S(2)}, u32[]{:S(2)}) collective-permute-start(f32[1344,640]{1,0:T(8,128)} %get-tuple-element.139), channel_id=1, source_target_pairs={{0,2},{1,5},{2,0},{3,7},{4,6},{5,1},{6,4},{7,3}} | collective-permute-start | bytes 10321928 | tf_op jit(solution)/shard_map/ppermute | solution.py:80
  554.2 1.7 collective-permute-start.61
  554.4 104.8 %collective-permute-start.47 = (f32[1344,640]{1,0:T(8,128)}, f32[1344,640]{1,0:T(8,128)}, u32[]{:S(2)}, u32[]{:S(2)}) collective-permute-start(f32[1344,640]{1,0:T(8,128)} %get-tuple-element.137), channel_id=1, source_target_pairs={{0,2},{1,5},{2,0},{3,7},{4,6},{5,1},{6,4},{7,3}} | collective-permute-start | bytes 10321928 | tf_op jit(solution)/shard_map/ppermute | solution.py:80
  556.8 39.6 %collective-permute-start.62 = (f32[48,640]{1,0:T(8,128)S(1)}, f32[48,640]{1,0:T(8,128)S(1)}, u32[]{:S(2)}, u32[]{:S(2)}) collective-permute-start(f32[48,640]{1,0:T(8,128)S(1)} %add.52), channel_id=1, source_target_pairs={{0,2},{1,5},{2,0},{3,7},{4,6},{5,1},{6,4},{7,3}} | collective-permute-start | bytes 368648 | tf_op jit(solution)/shard_map/ppermute | solution.py:80
  596.4 18.6 %collective-permute-start.63 = (f32[48,640]{1,0:T(8,128)S(1)}, f32[48,640]{1,0:T(8,128)S(1)}, u32[]{:S(2)}, u32[]{:S(2)}) collective-permute-start(f32[48,640]{1,0:T(8,128)S(1)} %add.53), channel_id=1, source_target_pairs={{0,4},{1,3},{2,6},{3,1},{4,0},{5,7},{6,2},{7,5}} | collective-permute-start | bytes 368648 | tf_op jit(solution)/shard_map/ppermute | solution.py:80
  615.0 21.4 %collective-permute-start.59 = (f32[640,640]{1,0:T(8,128)}, f32[640,640]{1,0:T(8,128)S(1)}, u32[]{:S(2)}, u32[]{:S(2)}) collective-permute-start(f32[640,640]{1,0:T(8,128)} %get-tuple-element.154), channel_id=1, source_target_pairs={{0,2},{1,5},{2,0},{3,7},{4,6},{5,1},{6,4},{7,3}} | collective-permute-start | bytes 4915208 | tf_op jit(solution)/shard_map/ppermute | solution.py:80
  615.7 38.2 %collective-permute-start.43 = (f32[640,640]{1,0:T(8,128)S(1)}, f32[640,640]{1,0:T(8,128)S(1)}, u32[]{:S(2)}, u32[]{:S(2)}) collective-permute-start(f32[640,640]{1,0:T(8,128)S(1)} %copy-done.34), channel_id=1, source_target_pairs={{0,2},{1,5},{2,0},{3,7},{4,6},{5,1},{6,4},{7,3}} | collective-permute-start | bytes 4915208 | tf_op jit(solution)/shard_map/ppermute | solution.py:80
  617.1 135.4 %collective-permute-start.55 = (f32[1280,640]{1,0:T(8,128)}, f32[1280,640]{1,0:T(8,128)S(1)}, u32[]{:S(2)}, u32[]{:S(2)}) collective-permute-start(f32[1280,640]{1,0:T(8,128)} %get-tuple-element.148), channel_id=1, source_target_pairs={{0,2},{1,5},{2,0},{3,7},{4,6},{5,1},{6,4},{7,3}} | collective-permute-start | bytes 9830408 | tf_op jit(solution)/shard_map/ppermute | solution.py:80
  636.4 87.8 %collective-permute-start.53 = (f32[640,640]{1,0:T(8,128)}, f32[640,640]{1,0:T(8,128)S(1)}, u32[]{:S(2)}, u32[]{:S(2)}) collective-permute-start(f32[640,640]{1,0:T(8,128)} %get-tuple-element.146), channel_id=1, source_target_pairs={{0,2},{1,5},{2,0},{3,7},{4,6},{5,1},{6,4},{7,3}} | collective-permute-start | bytes 4915208 | tf_op jit(solution)/shard_map/ppermute | solution.py:80
  653.9 96.6 %collective-permute-start.51 = (f32[640,640]{1,0:T(8,128)}, f32[640,640]{1,0:T(8,128)S(1)}, u32[]{:S(2)}, u32[]{:S(2)}) collective-permute-start(f32[640,640]{1,0:T(8,128)} %get-tuple-element.144), channel_id=1, source_target_pairs={{0,2},{1,5},{2,0},{3,7},{4,6},{5,1},{6,4},{7,3}} | collective-permute-start | bytes 4915208 | tf_op jit(solution)/shard_map/ppermute | solution.py:80
  657.6 93.5 %collective-permute-start.58 = (f32[320,640]{1,0:T(8,128)S(1)}, f32[320,640]{1,0:T(8,128)S(1)}, u32[]{:S(2)}, u32[]{:S(2)}) collective-permute-start(f32[320,640]{1,0:T(8,128)S(1)} %slice_add_fusion.4), channel_id=1, source_target_pairs={{0,4},{1,3},{2,6},{3,1},{4,0},{5,7},{6,2},{7,5}} | collective-permute-start | bytes 2457608 | tf_op jit(solution)/shard_map/ppermute | solution.py:80
  659.2 95.7 %collective-permute-start.46 = (f32[320,640]{1,0:T(8,128)S(1)}, f32[320,640]{1,0:T(8,128)S(1)}, u32[]{:S(2)}, u32[]{:S(2)}) collective-permute-start(f32[320,640]{1,0:T(8,128)S(1)} %slice_add_fusion.7), channel_id=1, source_target_pairs={{0,4},{1,3},{2,6},{3,1},{4,0},{5,7},{6,2},{7,5}} | collective-permute-start | bytes 2457608 | tf_op jit(solution)/shard_map/ppermute | solution.py:80
  724.1 33.8 %collective-permute-start.60 = (f32[320,640]{1,0:T(8,128)S(1)}, f32[320,640]{1,0:T(8,128)S(1)}, u32[]{:S(2)}, u32[]{:S(2)}) collective-permute-start(f32[320,640]{1,0:T(8,128)S(1)} %slice_add_fusion.3), channel_id=1, source_target_pairs={{0,4},{1,3},{2,6},{3,1},{4,0},{5,7},{6,2},{7,5}} | collective-permute-start | bytes 2457608 | tf_op jit(solution)/shard_map/ppermute | solution.py:80
  750.5 12.3 %collective-permute-start.44 = (f32[320,640]{1,0:T(8,128)S(1)}, f32[320,640]{1,0:T(8,128)S(1)}, u32[]{:S(2)}, u32[]{:S(2)}) collective-permute-start(f32[320,640]{1,0:T(8,128)S(1)} %slice_add_fusion.8), channel_id=1, source_target_pairs={{0,4},{1,3},{2,6},{3,1},{4,0},{5,7},{6,2},{7,5}} | collective-permute-start | bytes 2457608 | tf_op jit(solution)/shard_map/ppermute | solution.py:80
  751.1 91.3 %collective-permute-start.50 = (f32[672,640]{1,0:T(8,128)}, f32[672,640]{1,0:T(8,128)}, u32[]{:S(2)}, u32[]{:S(2)}) collective-permute-start(f32[672,640]{1,0:T(8,128)} %slice_add_fusion), channel_id=1, source_target_pairs={{0,4},{1,3},{2,6},{3,1},{4,0},{5,7},{6,2},{7,5}} | collective-permute-start | bytes 5160968 | tf_op jit(solution)/shard_map/ppermute | solution.py:80
  752.5 89.9 %collective-permute-start.48 = (f32[672,640]{1,0:T(8,128)S(1)}, f32[672,640]{1,0:T(8,128)}, u32[]{:S(2)}, u32[]{:S(2)}) collective-permute-start(f32[672,640]{1,0:T(8,128)S(1)} %slice_add_fusion.1), channel_id=1, source_target_pairs={{0,4},{1,3},{2,6},{3,1},{4,0},{5,7},{6,2},{7,5}} | collective-permute-start | bytes 5160968 | tf_op jit(solution)/shard_map/ppermute | solution.py:80
  754.9 80.0 %collective-permute-start.56 = (f32[640,640]{1,0:T(8,128)}, f32[640,640]{1,0:T(8,128)}, u32[]{:S(2)}, u32[]{:S(2)}) collective-permute-start(f32[640,640]{1,0:T(8,128)} %slice_add_fusion.2), channel_id=1, source_target_pairs={{0,4},{1,3},{2,6},{3,1},{4,0},{5,7},{6,2},{7,5}} | collective-permute-start | bytes 4915208 | tf_op jit(solution)/shard_map/ppermute | solution.py:80
  758.9 67.2 %collective-permute-start.54 = (f32[320,640]{1,0:T(8,128)}, f32[320,640]{1,0:T(8,128)}, u32[]{:S(2)}, u32[]{:S(2)}) collective-permute-start(f32[320,640]{1,0:T(8,128)} %slice_add_fusion.5), channel_id=1, source_target_pairs={{0,4},{1,3},{2,6},{3,1},{4,0},{5,7},{6,2},{7,5}} | collective-permute-start | bytes 2457608 | tf_op jit(solution)/shard_map/ppermute | solution.py:80
  763.8 71.1 %collective-permute-start.52 = (f32[320,640]{1,0:T(8,128)}, f32[320,640]{1,0:T(8,128)}, u32[]{:S(2)}, u32[]{:S(2)}) collective-permute-start(f32[320,640]{1,0:T(8,128)} %slice_add_fusion.6), channel_id=1, source_target_pairs={{0,4},{1,3},{2,6},{3,1},{4,0},{5,7},{6,2},{7,5}} | collective-permute-start | bytes 2457608 | tf_op jit(solution)/shard_map/ppermute | solution.py:80
  (43 other events, 512.7 us)

commit v6 on v5

--- a/solution.py
+++ b/solution.py
@@ -10,7 +10,7 @@
 
 HEAD = 64
 AXIS = 'fsdp'
-CHUNK = 1280
+CHUNK = 256
 FF_ROWS = 256
 FF_STEP = 256
 STEP = 512
@@ -245,6 +245,26 @@
             ref[at:at + rows, :] = tile[q, pl.ds(start, rows), :] + recv[slot, q * rows:(q + 1) * rows, :]
 
 
+def down_send(chip, tile, recv, send_sem, recv_sem):
+    core, mate, _, _ = chip_places(lax.axis_index(AXIS))
+    rows = recv.shape[1]
+    return pltpu.make_async_remote_copy(
+        src_ref=tile.at[chip, pl.ds(pl.multiple_of((1 - core) * rows, rows), rows), :], dst_ref=recv.at[chip],
+        send_sem=send_sem.at[chip], recv_sem=recv_sem.at[chip], device_id=(mate,), device_id_type=pl.DeviceIdType.MESH)
+
+
+def down_finish(tile, recv, send_sem, recv_sem, far_ref, keep_ref):
+    core, _, _, own_chip = chip_places(lax.axis_index(AXIS))
+    rows = recv.shape[1]
+    for chip in range(4):
+        down_send(chip, tile, recv, send_sem, recv_sem).wait()
+    for slot in range(4):
+        chip = own_chip(slot)
+        ref = keep_ref if slot < 2 else far_ref
+        at = (slot % 2) * rows
+        ref[at:at + rows, :] = tile[chip, pl.ds(pl.multiple_of(core * rows, rows), rows), :] + recv[chip]
+
+
 def add_rows(ref, step, rows):
     @pl.when(step == 0)
     def _():
@@ -361,17 +381,26 @@
     start_load(pieces[8:], offset, w_ff2, sems.at[1])
 
 
-def ff_up(normed, bias_ref, w_ff1, half, start, gated_ref, save_a, save_g):
-    u_a = dot_nn(normed, w_ff1[:, start:start + CHUNK]) + bias_ref[:, start:start + CHUNK]
-    u_g = dot_nn(normed, w_ff1[:, half + start:half + start + CHUNK]) + bias_ref[:, half + start:half + start + CHUNK]
-    cumulative = 0.5 * (1.0 + lax.erf(u_g * math.sqrt(0.5)))
-    gate = u_g * cumulative
-    slope = cumulative + u_g * (jnp.exp(-0.5 * u_g * u_g) * (1.0 / math.sqrt(2.0 * math.pi)))
-    gated = (u_a * gate).astype(BF16)
-    gated_ref[:, start:start + CHUNK] = gated
-    save_a[:, start:start + CHUNK] = gate
-    save_g[:, start:start + CHUNK] = u_a * slope
-    return gated
+def ff_hidden(normed, bias_ref, w_ff1, start):
+    return dot_nn(normed, w_ff1[:, start:start + CHUNK]) + bias_ref[:, start:start + CHUNK]
+
+
+def ff_up(normed, bias_ref, w_ff1, half, gated_ref, save_a, save_g, each=None):
+    starts = list(range(0, half, CHUNK))
+    ahead = (ff_hidden(normed, bias_ref, w_ff1, 0), ff_hidden(normed, bias_ref, w_ff1, half))
+    for start in starts:
+        u_a, u_g = ahead
+        if start + CHUNK < half:
+            ahead = tuple(ff_hidden(normed, bias_ref, w_ff1, base + start + CHUNK) for base in (0, half))
+        cumulative = 0.5 * (1.0 + lax.erf(u_g * math.sqrt(0.5)))
+        gate = u_g * cumulative
+        slope = cumulative + u_g * (jnp.exp(-0.5 * u_g * u_g) * (1.0 / math.sqrt(2.0 * math.pi)))
+        gated = (u_a * gate).astype(BF16)
+        gated_ref[:, start:start + CHUNK] = gated
+        save_a[:, start:start + CHUNK] = gate
+        save_g[:, start:start + CHUNK] = u_a * slope
+        if each is not None:
+            each(start, gated)
 
 
 def ff_forward_kernel(offset, h_ref, rows_ref, bias_ref, *refs):
@@ -393,21 +422,26 @@
         wait_load(w_ff1, sems.at[0])
         wait_load(w_ff2, sems.at[1])
 
-    total = x + rows_ref[8:9, :]
-    for start in range(0, half, CHUNK):
-        gated = ff_up(normed, bias_ref, w_ff1, half, start, gated_ref, save_a, save_g)
-        total = total + dot_nn(gated, w_ff2[start:start + CHUNK, :])
-    out_ref[...] = total
-
-
-def ff_up_kernel(h_ref, rows_ref, bias_ref, *refs):
-    pieces, (norm_ref, gated_ref, save_a, save_g, w_ff1, sems) = refs[:8], refs[8:]
-    half = w_ff1.shape[1] // 2
-    step = pl.program_id(0)
+    out_ref[...] = x + rows_ref[8:9, :]
+
+    def down(start, gated):
+        out_ref[...] += dot_nn(gated, w_ff2[start:start + CHUNK, :])
+
+    ff_up(normed, bias_ref, w_ff1, half, gated_ref, save_a, save_g, down)
+
+
+def ff_up_kernel(h_ref, rows_ref, bias_ref, cot_ref, *refs):
+    pieces, refs = refs[:8], refs[8:]
+    (norm_ref, gated_ref, save_a, save_g, far_ref, keep_ref, w_ff1, every, grad, tile, recv, sems, grad_sem, send_sem, recv_sem) = refs
+    half, width = w_ff1.shape[1] // 2, grad.shape[1]
+    step, last = pl.program_id(0), pl.num_programs(0) - 1
+    load_grad = pltpu.make_async_copy(cot_ref, grad, grad_sem)
 
     @pl.when(step == 0)
     def _():
         start_load(pieces, 0, w_ff1, sems.at[0])
+        load_grad.start()
+        greet(chip_places(lax.axis_index(AXIS))[1])
 
     unit, _ = norm_stats(h_ref[...])
     normed = (unit * rows_ref[4:5, :] + rows_ref[5:6, :]).astype(BF16)
@@ -417,8 +451,20 @@
     def _():
         wait_load(w_ff1, sems.at[0])
 
-    for start in range(0, half, CHUNK):
-        ff_up(normed, bias_ref, w_ff1, half, start, gated_ref, save_a, save_g)
+    mine = pl.ds(pl.multiple_of(step * normed.shape[0], normed.shape[0]), normed.shape[0])
+
+    def keep_gated(start, gated):
+        every[mine, start:start + CHUNK] = gated
+
+    ff_up(normed, bias_ref, w_ff1, half, gated_ref, save_a, save_g, keep_gated)
+
+    @pl.when(step == last)
+    def _():
+        load_grad.wait()
+        for chip in range(4):
+            tile[chip] = dot_tn(every[:, chip * width:(chip + 1) * width], grad[...])
+            down_send(chip, tile, recv, send_sem, recv_sem).start()
+        down_finish(tile, recv, send_sem, recv_sem, far_ref, keep_ref)
 
 
 def ff_down_kernel(h_ref, rows_ref, gated_ref, *refs):
@@ -584,14 +630,10 @@
             if q > 0:
                 for copy in tile_sends(q - 1, depth, tile, recv, send_sem, recv_sem):
                     copy.start()
-
-    d_norm = dot_nt(d_qkv[mine, :], w_qkv[...])
-
-    @pl.when(step == last)
-    def _():
         for copy in tile_sends(3, depth, tile, recv, send_sem, recv_sem):
             copy.start()
 
+    d_norm = dot_nt(d_qkv[mine, :], w_qkv[...])
     d_res, g_gain, g_shift = norm_back(h_ref[...].astype(F32), rows_ref[0:1, :], d_norm)
     out_ref[...] = grad + d_res
     rounded_ref[...] = (grad + d_res).astype(BF16)
@@ -676,16 +718,20 @@
         count * width * half * 6, 6e7)(h, rows, bias, *pieces)
 
 
-def ff_up_forward(h, rows, bias, pieces):
+def ff_up_forward(kind, h, rows, bias, cot, pieces):
     count, width = h.shape
     half = bias.shape[1] // 2
+    dma = pltpu.SemaphoreType.DMA
     return call(
         ff_up_kernel, count // FF_STEP,
-        [by_step(FF_STEP, width), whole(*rows.shape), whole(1, 2 * half)] + [ANY] * 8,
-        [by_step(FF_STEP, width), by_step(FF_STEP, half), by_step(FF_STEP, half), by_step(FF_STEP, half)],
-        [shape(count, width, BF16), shape(count, half, BF16), shape(count, half, F32), shape(count, half, F32)],
-        [pltpu.VMEM((width, 2 * half), BF16), pltpu.SemaphoreType.DMA((1,))],
-        count * width * half * 4, 5e7)(h, rows, bias, *pieces)
+        [by_step(FF_STEP, width), whole(*rows.shape), whole(1, 2 * half)] + [ANY] * 9,
+        [by_step(FF_STEP, width), by_step(FF_STEP, half), by_step(FF_STEP, half), by_step(FF_STEP, half), whole(width, width),
+         whole(width, width)],
+        [shape(count, width, BF16), shape(count, half, BF16), shape(count, half, F32), shape(count, half, F32), shape(width, width, F32),
+         shape(width, width, F32)],
+        [pltpu.VMEM((width, 2 * half), BF16), pltpu.VMEM((count, half), BF16), pltpu.VMEM((count, width), BF16),
+         pltpu.VMEM((4, width, width), F32), pltpu.VMEM((4, width // 2, width), F32), dma((1,)), dma, dma((4,)), dma((4,))],
+        count * width * half * 6, 5e7, kind)(h, rows, bias, cot, *pieces)
 
 
 def ff_down_forward(h, rows, gated, pieces):
@@ -893,45 +939,59 @@
     return total
 
 
-def ff_grad_kernel(offset, first, resumed, final, grad_ref, save_a, save_g, norm_ref, h_ref, rows_ref, *refs):
+def ff_grad_kernel(offset, first, resumed, final, rounded_ref, grad_ref, save_a, save_g, norm_ref, h_ref, rows_ref, *refs):
     before_ref, refs = (refs[0], refs[1:]) if resumed else (None, refs)
     pieces, refs = refs[:16], refs[16:]
     out_ref, refs = refs[0], refs[1:]
     vec_ref, refs = (refs[0], refs[1:]) if final else (None, refs)
-    (bias_ref, far_ref, keep_ref, grad, grad_bf, turned, acc, part_a, part_g, d_both, w_ff1, w_ff2, tile, recv, obuf,
+    (bias_ref, far_ref, keep_ref, grad, grad_bf, norm_buf, turned, acc, part_a, part_g, d_both, w_ff1, w_ff2, tile, recv, obuf,
      in_sem, part_sem, w1_sem, w2_sem, out_sem, send_sem, recv_sem) = refs
     count, width = grad.shape
     every, chunks, depth = w_ff2.shape[0] // width, recv.shape[0], width // 8
     me = lax.axis_index(AXIS)
     core, mate, mate_slot, own_chip = chip_places(me)
 
+    load_rounded = pltpu.make_async_copy(rounded_ref, grad_bf, in_sem.at[3])
     load_grad = pltpu.make_async_copy(grad_ref, grad, in_sem.at[0])
-    load_norm = pltpu.make_async_copy(norm_ref, d_both.at[:, pl.ds(0, width)], in_sem.at[1])
+    load_norm = pltpu.make_async_copy(norm_ref, norm_buf, in_sem.at[1])
     load_before = pltpu.make_async_copy(before_ref, acc, in_sem.at[2]) if resumed else None
-    load_grad.start()
-    load_norm.start()
-    if resumed:
-        load_before.start()
+    load_rounded.start()
     start_load(pieces[8:], offset, w_ff2, w2_sem)
 
-    def parts(chunk):
-        at = (slice(None), pl.ds(pl.multiple_of((first + chunk) * width, width), width))
-        return [pltpu.make_async_copy(ref.at[at], buf.at[lax.rem(chunk, 2)], part_sem.at[which, lax.rem(chunk, 2)])
+    blocks = count // STEP
+
+    def parts(chunk, block):
+        rows = pl.ds(block * STEP, STEP)
+        at = (rows, pl.ds(pl.multiple_of((first + chunk) * width, width), width))
+        return [pltpu.make_async_copy(ref.at[at], buf.at[lax.rem(chunk, 2), rows, :], part_sem.at[which, lax.rem(chunk, 2), block])
                 for which, (ref, buf) in enumerate(((save_a, part_a), (save_g, part_g)))]
 
     def load_h(step):
-        return pltpu.make_async_copy(h_ref.at[pl.ds(step * STEP, STEP), :], part_a.at[0, pl.ds(step * STEP, STEP), :], part_sem.at[0, 0])
-
-    for copy in parts(0):
+        return pltpu.make_async_copy(h_ref.at[pl.ds(step * STEP, STEP), :], part_a.at[0, pl.ds(step * STEP, STEP), :], part_sem.at[0, 0, step])
+
+    for copy in parts(0, 0):
         copy.start()
     devices = piece_devices(me)
-    for chunk in range(chunks):
+
+    def load_w1(chunk):
         for kind in range(2):
             for piece, device in zip(pieces[:8], devices):
                 pltpu.make_async_copy(
                     piece.at[pl.ds((kind * every + first + chunk) * depth, depth), :],
                     w_ff1.at[pl.ds(pl.multiple_of(device * depth, 16), depth), pl.ds((2 * chunk + kind) * width, width)],
                     w1_sem.at[chunk]).start()
+
+    load_w1(0)
+    for block in range(1, blocks):
+        for copy in parts(0, block):
+            copy.start()
+    load_norm.start()
+    if resumed:
+        load_before.start()
+    for chunk in range(1, chunks):
+        load_w1(chunk)
+    if final:
+        load_grad.start()
     greet(mate)
 
     def sends(chunk):
@@ -968,10 +1028,9 @@
         for copy in sends(chunk):
             copy.wait_send()
 
-    load_grad.wait()
-    grad_bf[...] = grad[...].astype(BF16)
+    load_rounded.wait()
     load_norm.wait()
-    turned[...] = d_both[:, 0:width].T
+    turned[...] = norm_buf[...].T
     if resumed:
         load_before.wait()
     else:
@@ -982,14 +1041,16 @@
     def one_chunk(chunk, carry):
         w_pair = w_ff1.at[:, pl.ds(pl.multiple_of(chunk * 2 * width, width), 2 * width)]
         pltpu.make_async_copy(w_pair, w_pair, w1_sem.at[chunk]).wait()
-        for copy in parts(chunk):
-            copy.wait()
 
         @pl.when(chunk + 1 < chunks)
         def _():
-            for copy in parts(chunk + 1):
-                copy.start()
-
+            for block in range(blocks):
+                for copy in parts(chunk + 1, block):
+                    copy.start()
+
+        for block in range(blocks):
+            for copy in parts(chunk, block):
+                copy.wait()
         even = lax.rem(chunk, 2)
         w_down = w_ff2.at[pl.ds(pl.multiple_of((first + chunk) * width, width), width), :]
         sums = [0.0, 0.0]
@@ -1022,9 +1083,10 @@
         vec_ref[...] = jnp.zeros_like(vec_ref)
         for step in range(steps):
             load_h(step).start()
-        pltpu.make_async_copy(part_a.at[0], part_a.at[0], part_sem.at[0, 0]).wait()
+        load_grad.wait()
         for step in range(steps):
             rows = slice(step * STEP, (step + 1) * STEP)
+            load_h(step).wait()
             mine = grad[rows, :].astype(F32)
             d_res, g_gain, g_shift = norm_back(part_a[0, rows, :], rows_ref[4:5, :], acc[rows, :])
             acc[rows, :] = mine + d_res
@@ -1038,7 +1100,7 @@
     pltpu.make_async_copy(acc, out_ref, in_sem.at[0]).wait()
 
 
-def ff_grads(kind, grad, save_a, save_g, norm, h, rows, pieces, offset, first, chunks, before):
+def ff_grads(kind, rounded, grad, save_a, save_g, norm, h, rows, pieces, offset, first, chunks, before):
     count, width = h.shape
     half = save_a.shape[1]
     final = first + chunks == half // width
@@ -1048,17 +1110,18 @@
     saved = pltpu.VMEM((2, count, width), F32)
     resumed = before is not None
     return pl.pallas_call(
-        functools.partial(ff_grad_kernel, offset, first, resumed, final), in_specs=[ANY] * 5 + [vmem] + [ANY] * (16 + resumed),
+        functools.partial(ff_grad_kernel, offset, first, resumed, final), in_specs=[ANY] * 6 + [vmem] + [ANY] * (16 + resumed),
         out_specs=[ANY] + [vmem] * final + [vmem, ANY, ANY],
         out_shape=[shape(count, width, F32)] + [shape(8, width, F32)] * final + [shape(8, 2 * chunks * width, F32), big, big],
-        scratch_shapes=[pltpu.VMEM((count, width), grad.dtype), pltpu.VMEM((count, width), BF16), pltpu.VMEM((width, count), BF16),
+        scratch_shapes=[pltpu.VMEM((count, width), grad.dtype), pltpu.VMEM((count, width), BF16), pltpu.VMEM((count, width), BF16),
+                        pltpu.VMEM((width, count), BF16),
                         pltpu.VMEM((count, width), F32), saved, saved, pltpu.VMEM((count, 2 * width), BF16),
                         pltpu.VMEM((width, 2 * chunks * width), BF16), pltpu.VMEM((half, width), BF16),
                         pltpu.VMEM((width, 2 * width), F32), pltpu.VMEM((chunks, width // 2, 2 * width), F32),
                         pltpu.VMEM((width // 2, 2 * width), F32),
-                        dma((3,)), dma((2, 2)), dma((chunks,)), dma, dma, dma((4,)), dma((chunks, 4))],
+                        dma((4,)), dma((2, 2, count // STEP)), dma((chunks,)), dma, dma, dma((4,)), dma((chunks, 4))],
         cost_estimate=pl.CostEstimate(flops=count * width * width * chunks * 10, bytes_accessed=int(6e7), transcendentals=0),
-        compiler_params=pltpu.CompilerParams(collective_id=kind, has_side_effects=True, vmem_limit_bytes=VMEM_MOST))(grad, save_a, save_g, norm, h, rows, *([before] if resumed else []), *pieces)
+        compiler_params=pltpu.CompilerParams(collective_id=kind, has_side_effects=True, vmem_limit_bytes=VMEM_MOST))(rounded, grad, save_a, save_g, norm, h, rows, *([before] if resumed else []), *pieces)
 
 
 def scatter(far, keep, n_dev):
@@ -1154,6 +1217,7 @@
         ctx, ctx_mine, ctx_other = prepare_context(context, n_dev)
 
         h = tokens_x.reshape(count, width)
+        cot = cot_out.reshape(count, width)
         saved, attention_groups = [], []
         for layer in range(blocks):
             rows, bias = rows_all[layer], bias_all[layer]
@@ -1165,12 +1229,12 @@
                 norm3, gated, save_a, save_g, h3 = ff_forward(h2, rows, bias, ff_groups[layer], ff_offsets[layer])
             else:
                 norm1, qkv, mix1, h1, norm2, query, kv, mix2, h2 = attention_forward(h, rows, ctx, group[0], tokens, valid)
-                norm3, gated, save_a, save_g = ff_up_forward(h2, rows, bias, groups[-2])
+                norm3, gated, save_a, save_g, *down_pair = ff_up_forward(2, h2, rows, bias, cot, groups[-2])
                 out_tokens = ff_down_forward(h2, rows, gated, groups[-1])
             saved.append((h, norm1, qkv, mix1, h1, norm2, query, kv, mix2, h2, norm3, gated, save_a, save_g))
             h = h3 if layer < blocks - 1 else None
 
-        grad = rounded = cot_out.reshape(count, width)
+        grad = rounded = cot
         results, vec_grads = [None] * blocks, [None] * blocks
         for layer in reversed(range(blocks)):
             turn = blocks - 1 - layer
@@ -1180,12 +1244,14 @@
             def reduce(pair):
                 return scatter(pair[0], pair[1], n_dev)
 
-            r_ff2 = reduce(weight_grads(1, (gated, rounded),
-                                           [(0, c * width, 1, 0, 0, half // n_dev, (c,)) for c in range(half // width)], half // n_dev))
+            if turn > 0:
+                down_pair = weight_grads(1, (gated, rounded),
+                                               [(0, c * width, 1, 0, 0, half // n_dev, (c,)) for c in range(half // width)], half // n_dev)
+            r_ff2 = reduce(down_pair)
             sizes = (4,) if turn == 0 else (2, 2)
             d_norm, r_ff1, bias_grads, first_chunk = None, [], [], 0
             for index, chunks in enumerate(sizes):
-                *out, vec_b1, far, keep = ff_grads(5 + turn + index, grad, save_a, save_g, norm3, h2, rows,
+                *out, vec_b1, far, keep = ff_grads(10 + 2 * turn + index, rounded, grad, save_a, save_g, norm3, h2, rows,
                                                    ff_groups[layer], ff_offsets[layer], first_chunk, chunks, d_norm)
                 d_norm = out[0]
                 bias_grads.append(((first_chunk, chunks), vec_b1))

time: 858 us -> 815 us (0.950)
  waiting for transfers between devices: 289 us -> 261 us
  Pallas kernels: 476 us -> 464 us
    ppermute x64, waiting for transfers between devices: 289 us -> 261 us  [permute(): return lax.ppermute(array, AXIS, perm)]
    pallas_call x2 -> x1, Pallas kernels: 34.7 us -> 17.3 us  [weight_grads(): pl.pallas_call(functools.partial(grad_kernel, tiles, group_rows, len(arra...]
    pallas_call x1, Pallas kernels: 28.5 us -> 38.9 us  [ff_up_forward(): call(ff_up_kernel, count // FF_STEP, [by_step(FF_STEP, width), whole(*row...]
  transfers between devices with their start and end apart: 64 -> 64, of which waited for: 14 -> 16; matrix products, arithmetic and copies ran while one was open for 2% -> 2% of each run, Pallas kernels for 45% -> 48%
where the time goes in v6:
time: 815 us; the launch traced here: 808 us
  Pallas kernels  464 us (57%)
  waiting for transfers between devices  261 us (32%)
  starting transfers between devices  50.8 us (6%)
  local copies, waits for them, and re-layouts  17.9 us (2%)
  other arithmetic  12.7 us (2%)
    ppermute x64, waiting for transfers between devices, permute(): return lax.ppermute(array, AXIS, perm)  261 us
    pallas_call x3, Pallas kernels, ff_grads(): pl.pallas_call(functools.partial(ff_grad_kernel, offset, first, resumed,...  108 us
    pallas_call x2, Pallas kernels, self_backward(): call(functools.partial(self_backward_kernel, STEP // tokens, tokens), cou...  80.6 us
    pallas_call x2, Pallas kernels, cross_backward(): call(functools.partial(cross_backward_kernel, STEP // tokens, tokens, val...  57.1 us
    ppermute x64, starting transfers between devices, permute(): return lax.ppermute(array, AXIS, perm)  50.8 us
    pallas_call x1, Pallas kernels, ff_up_forward(): call(ff_up_kernel, count // FF_STEP, [by_step(FF_STEP, width), whole(*row...  38.9 us
    pallas_call x1, Pallas kernels, attention_forward(): call(functools.partial(attention_forward_kernel, STEP // tokens, tokens,...  37.9 us
    pallas_call x1, Pallas kernels, ff_forward(): call(functools.partial(ff_forward_kernel, offset), count // FF_STEP, [by_...  30.1 us
  transfers between devices with their start and end apart: 64, of which 16 were waited for; matrix products, arithmetic and copies ran while one was open for 2% of the time, Pallas kernels for 48%

profile of v6, /device:TPU:0, one launch (start us, length us, event | category | flops | bytes accessed | tf_op | source)
XLA Modules:
  0.0 807.9 jit_solution(1394929450642688180)
XLA Ops:
  0.7 2.2 copy.53
  2.9 1.5 copy.51
  4.4 1.8 pack.11.refs_0_.refs_8_
  6.2 3.3 collective-permute-start.36
  9.5 1.5 collective-permute-start.35
  13.7 1.9 pack.6.refs_0_
  16.4 2.1 pack.10.refs_0_
  19.8 2.3 collective-permute-start.29
  22.1 1.6 collective-permute-start.28
  24.5 2.2 pack.7.refs_0_
  26.7 3.0 collective-permute-done.1.refs_2_
  29.7 2.4 collective-permute-start.8
  32.1 1.6 collective-permute-start.7
  33.7 2.4 pack.8.refs_0_.refs_8_.refs_1_.refs_9_
  36.1 11.1 %collective-permute-done.29.refs_2_ = bf16[640,640]{1,0:T(8,128)(2,1)S(1)} collective-permute-done((bf16[640,640]{1,0:T(8,128)(2,1)S(1)}, bf16[640,640]{1,0:T(8,128)(2,1)S(1)}, u32[]{:S(2)}, u32[]{:S(2)}) %collective-permute-start.29) | collective-permute-done | bytes 819232 | tf_op jit(solution)/shard_map/ppermute | solution.py:80
  48.1 2.0 collective-permute-start.14
  50.1 15.6 %collective-permute-done.8.refs_2_ = bf16[672,640]{1,0:T(8,128)(2,1)} collective-permute-done((bf16[672,640]{1,0:T(8,128)(2,1)}, bf16[672,640]{1,0:T(8,128)(2,1)}, u32[]{:S(2)}, u32[]{:S(2)}) %collective-permute-start.8) | collective-permute-done | bytes 860192 | tf_op jit(solution)/shard_map/ppermute | solution.py:80
  65.7 2.5 collective-permute-start.15
  68.2 2.1 collective-permute-start.9
  70.4 27.3 %collective-permute-done.2.refs_3_ = bf16[368,640]{1,0:T(8,128)(2,1)} collective-permute-done((bf16[368,640]{1,0:T(8,128)(2,1)}, bf16[368,640]{1,0:T(8,128)(2,1)}, u32[]{:S(2)}, u32[]{:S(2)}) %collective-permute-start.2) | collective-permute-done | bytes 471072 | tf_op jit(solution)/shard_map/ppermute | solution.py:80
  97.6 2.4 pack.9.refs_0_
  101.1 1.6 collective-permute-start.16
  103.2 6.7 collective-permute-done.9.refs_3_
  109.9 3.8 context.1
  113.7 1.8 vec_sum.1
  117.8 13.4 %collective-permute-done.21.refs_1_ = bf16[992,640]{1,0:T(8,128)(2,1)} collective-permute-done((bf16[992,640]{1,0:T(8,128)(2,1)}, bf16[992,640]{1,0:T(8,128)(2,1)}, u32[]{:S(2)}, u32[]{:S(2)}) %collective-permute-start.21) | collective-permute-done | bytes 1269792 | tf_op jit(solution)/shard_map/ppermute | solution.py:80
  131.2 2.0 collective-permute-start.22
  133.7 1.9 collective-permute-start.23
  136.3 20.2 %shard_map.186 = (bf16[1536,640]{1,0:T(8,128)(2,1)}, bf16[1536,1920]{1,0:T(8,128)(2,1)}, bf16[1536,640]{1,0:T(8,128)(2,1)}, f32[1536,640]{1,0:T(8,128)}) custom-call(bf16[1536,640]{1,0:T(8,128)(2,1)} %bitcast.94, f32[16,640]{1,0:T(8,128)} %get-tuple-element.167.rows_ref, bf16[368,640]{1,0:T(8,128)(2,1)} %pack.6.refs_0_, ...), custom_call_target="tpu_custom_call" | custom-call | flops 6039797760 | bytes 20000000 | tf_op jit(solution)/shard_map/pallas_call | solution.py:669
  156.5 19.7 %shard_map.187 = (bf16[1536,640]{1,0:T(8,128)(2,1)}, bf16[1536,640]{1,0:T(8,128)(2,1)}, bf16[480,1280]{1,0:T(8,128)(2,1)}, bf16[1536,640]{1,0:T(8,128)(2,1)}, f32[1536,640]{1,0:T(8,128)}) custom-call(f32[1536,640]{1,0:T(8,128)} %get-tuple-element.89.h_ref, f32[16,640]{1,0:T(8,128)} %get-tuple-element.167.rows_ref, ...), custom_call_target="tpu_custom_call" | custom-call | flops 5536481280 | bytes 20000000 | tf_op jit(solution)/shard_map/pallas_call | solution.py:681
  177.8 30.1 %shard_map.188 = (bf16[1536,640]{1,0:T(8,128)(2,1)}, bf16[1536,2560]{1,0:T(8,128)(2,1)}, f32[1536,2560]{1,0:T(8,128)}, f32[1536,2560]{1,0:T(8,128)}, f32[1536,640]{1,0:T(8,128)}) custom-call(f32[1536,640]{1,0:T(8,128)} %get-tuple-element.94.h_ref, f32[16,640]{1,0:T(8,128)} %get-tuple-element.167.rows_ref, f32[1,5120]{1,0:T(1,128)} %bitcast.89, ...), custom_call_target="tpu_custom_call" | custom-call | flops 15099494400 | bytes 60000000 | tf_op jit(solution)/shard_map/pallas_call | solution.py:711
  208.2 1.7 collective-permute-start.37
  211.0 37.9 %shard_map.189 = (bf16[1536,640]{1,0:T(8,128)(2,1)}, bf16[1536,1920]{1,0:T(8,128)(2,1)}, bf16[1536,640]{1,0:T(8,128)(2,1)}, f32[1536,640]{1,0:T(8,128)}, bf16[15...) custom-call(f32[1536,640]{1,0:T(8,128)} %get-tuple-element.97.h_ref,, ...), custom_call_target="tpu_custom_call" | custom-call | flops 11576279040 | bytes 40000000 | tf_op jit(solution)/shard_map/pallas_call | solution.py:698
  250.5 38.9 %shard_map.190 = (bf16[1536,640]{1,0:T(8,128)(2,1)}, bf16[1536,2560]{1,0:T(8,128)(2,1)}, f32[1536,2560]{1,0:T(8,128)}, f32[1536,2560]{1,0:T(8,128)}, f32[640,640]{1,0:T(8,128)}, /*index=5*/f32[640,640]{1,0:T(8,128)}) custom-call(f32[1536,640]{1,0:T(8,128)} %get-tuple-element.98.h_ref, f32[16,640]{1,0:T(8,128)} %get-tuple-element.166.rows_ref, ...), custom_call_target="tpu_custom_call" | custom-call | flops 15099494400 | bytes 50000000 | tf_op jit(solution)/shard_map/pallas_call | solution.py:725
  291.1 48.0 %shard_map.192 = (f32[1536,640]{1,0:T(8,128)}, f32[8,640]{1,0:T(8,128)}, f32[8,5120]{1,0:T(8,128)}, f32[1280,640]{1,0:T(8,128)}, f32[1280,640]{1,0:T(8,128)}) custom-call(bf16[1536,640]{1,0:T(8,128)(2,1)} %bitcast.92, bf16[1536,640]{1,0:T(8,128)(2,1)} %bitcast.93, f32[1536,2560]{1,0:T(8,128)} %get-tuple-element.100.save_a, ...), custom_call_target="tpu_custom_call" | custom-call | flops 25165824000 | bytes 60000000 | tf_op jit(solution)/shard_map/pallas_call | solution.py:1112
  339.1 28.6 %shard_map.193 = (f32[1536,640]{1,0:T(8,128)}, f32[8,640]{1,0:T(8,128)}, f32[1344,640]{1,0:T(8,128)}, f32[1344,640]{1,0:T(8,128)}) custom-call(f32[1536,640]{1,0:T(8,128)} %get-tuple-element.103.grad_ref, bf16[1536,640]{1,0:T(8,128)(2,1)} %get-tuple-element.104.query_ref, bf16[480,1280]{1,0:T(8,128)(2,1)} %get-tuple-element.105.kv_ref, ...), custom_call_target="tpu_custom_call" | custom-call | flops 8975810560 | bytes 20000000 | tf_op jit(solution)/shard_map/pallas_call | solution.py:756
  367.8 39.7 %shard_map.194 = (f32[1536,640]{1,0:T(8,128)}, bf16[1536,640]{1,0:T(8,128)(2,1)}, f32[8,640]{1,0:T(8,128)}, f32[640,640]{1,0:T(8,128)}, f32[640,640]{1,0:T(8,128)}) custom-call(f32[1536,640]{1,0:T(8,128)} %get-tuple-element.111.grad_ref, bf16[1536,1920]{1,0:T(8,128)(2,1)} %get-tuple-element.112.qkv_ref, f32[1536,640]{1,0:T(8,128)} %get-tuple-element.97.h_ref, ...), custom_call_target="tpu_custom_call" | custom-call | flops 12582912000 | bytes 30000000 | tf_op jit(solution)/shard_map/pallas_call | solution.py:774
  407.9 17.3 %shard_map.199 = (f32[640,640]{1,0:T(8,128)}, f32[640,640]{1,0:T(8,128)}) custom-call(bf16[1536,2560]{1,0:T(8,128)(2,1)} %get-tuple-element.150.refs_0_, bf16[1536,640]{1,0:T(8,128)(2,1)} %get-tuple-element.115.rounded_ref.refs_1_), custom_call_target="tpu_custom_call" | custom-call | flops 5033164800 | bytes 20000000 | tf_op jit(solution)/shard_map/pallas_call | solution.py:872
  425.2 1.4 collective-permute-start.57
  427.2 29.4 %shard_map.195 = (f32[1536,640]{1,0:T(8,128)}, f32[8,2560]{1,0:T(8,128)}, f32[640,640]{1,0:T(8,128)}, f32[640,640]{1,0:T(8,128)}) custom-call(bf16[1536,640]{1,0:T(8,128)(2,1)} %get-tuple-element.115.rounded_ref.refs_1_, f32[1536,640]{1,0:T(8,128)} %get-tuple-element.116.grad_ref, f32[1536,2560]{1,0:T(8,128)} %get-tuple-element.117.save_a, ...), custom_call_target="tpu_custom_call" | custom-call | flops 12582912000 | bytes 60000000 | tf_op jit(solution)/shard_map/pallas_call | solution.py:1112
  456.7 31.0 %shard_map.196 = (f32[1536,640]{1,0:T(8,128)}, f32[8,640]{1,0:T(8,128)}, f32[8,2560]{1,0:T(8,128)}, f32[640,640]{1,0:T(8,128)}, f32[640,640]{1,0:T(8,128)}) custom-call(bf16[1536,640]{1,0:T(8,128)(2,1)} %get-tuple-element.115.rounded_ref.refs_1_, f32[1536,640]{1,0:T(8,128)} %get-tuple-element.116.grad_ref, f32[1536,2560]{1,0:T(8,128)} %get-tuple-element.117.save_a, ...), custom_call_target="tpu_custom_call" | custom-call | flops 12582912000 | bytes 60000000 | tf_op jit(solution)/shard_map/pallas_call | solution.py:1112
  487.7 28.5 %shard_map.197 = (f32[1536,640]{1,0:T(8,128)}, f32[8,640]{1,0:T(8,128)}, f32[1344,640]{1,0:T(8,128)}, f32[1344,640]{1,0:T(8,128)}) custom-call(f32[1536,640]{1,0:T(8,128)} %get-tuple-element.121.grad_ref, bf16[1536,640]{1,0:T(8,128)(2,1)} %get-tuple-element.122.query_ref, bf16[480,1280]{1,0:T(8,128)(2,1)} %get-tuple-element.123.kv_ref, ...), custom_call_target="tpu_custom_call" | custom-call | flops 8975810560 | bytes 20000000 | tf_op jit(solution)/shard_map/pallas_call | solution.py:756
  516.2 1.6 collective-permute-start.47
  517.8 40.9 %shard_map.198 = (f32[1536,640]{1,0:T(8,128)}, bf16[1536,640]{1,0:T(8,128)(2,1)}, f32[8,640]{1,0:T(8,128)}, f32[640,640]{1,0:T(8,128)}, f32[640,640]{1,0:T(8,128)}) custom-call(f32[1536,640]{1,0:T(8,128)} %get-tuple-element.126.grad_ref, bf16[1536,1920]{1,0:T(8,128)(2,1)} %get-tuple-element.127.qkv_ref, bf16[1536,640]{1,0:T(8,128)(2,1)} %bitcast.95, ...), custom_call_target="tpu_custom_call" | custom-call | flops 12582912000 | bytes 30000000 | tf_op jit(solution)/shard_map/pallas_call | solution.py:774
  558.7 1.8 vec_pack.1
  563.7 4.2 collective-permute-done.62
  568.6 4.3 collective-permute-done.63
  575.5 18.4 %collective-permute-done.59.refs_4_ = f32[640,640]{1,0:T(8,128)S(1)} collective-permute-done((f32[640,640]{1,0:T(8,128)S(1)}, f32[640,640]{1,0:T(8,128)S(1)}, u32[]{:S(2)}, u32[]{:S(2)}) %collective-permute-start.59) | collective-permute-done | bytes 1638432 | tf_op jit(solution)/shard_map/ppermute | solution.py:80
  594.6 16.9 %collective-permute-done.43.refs_1_ = f32[640,640]{1,0:T(8,128)S(1)} collective-permute-done((f32[640,640]{1,0:T(8,128)}, f32[640,640]{1,0:T(8,128)S(1)}, u32[]{:S(2)}, u32[]{:S(2)}) %collective-permute-start.43) | collective-permute-done | bytes 1638432 | tf_op jit(solution)/shard_map/ppermute | solution.py:80
  613.4 1.4 slice_add_fusion.4
  615.2 1.4 collective-permute-start.46
  617.4 3.0 slice_add_fusion
  620.4 1.8 slice_add_fusion.1
  622.2 59.5 %collective-permute-done.53.refs_4_ = f32[640,640]{1,0:T(8,128)S(1)} collective-permute-done((f32[640,640]{1,0:T(8,128)}, f32[640,640]{1,0:T(8,128)S(1)}, u32[]{:S(2)}, u32[]{:S(2)}) %collective-permute-start.53) | collective-permute-done | bytes 1638432 | tf_op jit(solution)/shard_map/ppermute | solution.py:80
  682.4 25.7 %collective-permute-done.51.refs_1_ = f32[640,640]{1,0:T(8,128)S(1)} collective-permute-done((f32[640,640]{1,0:T(8,128)}, f32[640,640]{1,0:T(8,128)S(1)}, u32[]{:S(2)}, u32[]{:S(2)}) %collective-permute-start.51) | collective-permute-done | bytes 1638432 | tf_op jit(solution)/shard_map/ppermute | solution.py:80
  708.7 1.4 collective-permute-start.50
  717.5 3.0 collective-permute-done.44.refs_2_
  721.4 12.0 %shard_map.191 = bf16[1536,640]{1,0:T(8,128)(2,1)} custom-call(f32[1536,640]{1,0:T(8,128)} %get-tuple-element.98.h_ref, f32[16,640]{1,0:T(8,128)} %get-tuple-element.166.rows_ref, bf16[1536,2560]{1,0:T(8,128)(2,1)} %get-tuple-element.99.gated_ref, bf16[320,640]{1,0:T(8,128)(2,1)} %pack.11.refs_0_.refs_8_, ...), custom_call_target="tpu_custom_call" | custom-call | flops 5033164800 | bytes 20000000 | tf_op jit(solution)/shard_map/pallas_call | solution.py:740
  734.1 3.8 totals.7
  738.0 3.8 totals.4
  741.8 41.9 %collective-permute-done.54.refs_5_ = f32[320,640]{1,0:T(8,128)S(1)} collective-permute-done((f32[320,640]{1,0:T(8,128)}, f32[320,640]{1,0:T(8,128)S(1)}, u32[]{:S(2)}, u32[]{:S(2)}) %collective-permute-start.54) | collective-permute-done | bytes 819232 | tf_op jit(solution)/shard_map/ppermute | solution.py:80
  783.7 8.9 %collective-permute-done.52.refs_2_ = f32[320,640]{1,0:T(8,128)} collective-permute-done((f32[320,640]{1,0:T(8,128)}, f32[320,640]{1,0:T(8,128)}, u32[]{:S(2)}, u32[]{:S(2)}) %collective-permute-start.52) | collective-permute-done | bytes 819232 | tf_op jit(solution)/shard_map/ppermute | solution.py:80
  792.5 7.5 totals.6
  800.0 6.4 totals.5
  (211 shorter events, 40.3 us)
Async XLA Ops:
  6.2 13.4 %collective-permute-start.36 = (bf16[320,640]{1,0:T(8,128)(2,1)}, bf16[320,640]{1,0:T(8,128)(2,1)}, u32[]{:S(2)}, u32[]{:S(2)}) collective-permute-start(bf16[320,640]{1,0:T(8,128)(2,1)} %pack.11.refs_0_.refs_8_), channel_id=1, source_target_pairs={{0,2},{1,5},{2,0},{3,7},{4,6},{5,1},{6,4},{7,3}} | collective-permute-start | bytes 1228808 | tf_op jit(solution)/shard_map/ppermute | solution.py:80
  9.5 12.6 %collective-permute-start.35 = (bf16[320,640]{1,0:T(8,128)(2,1)}, bf16[320,640]{1,0:T(8,128)(2,1)}, u32[]{:S(2)}, u32[]{:S(2)}) collective-permute-start(bf16[320,640]{1,0:T(8,128)(2,1)} %pack.11.refs_0_.refs_8_), channel_id=1, source_target_pairs={{0,4},{1,3},{2,6},{3,1},{4,0},{5,7},{6,2},{7,5}} | collective-permute-start | bytes 1228808 | tf_op jit(solution)/shard_map/ppermute | solution.py:80
  15.7 11.0 %collective-permute-start.3 = (bf16[368,640]{1,0:T(8,128)(2,1)}, bf16[368,640]{1,0:T(8,128)(2,1)S(1)}, u32[]{:S(2)}, u32[]{:S(2)}) collective-permute-start(bf16[368,640]{1,0:T(8,128)(2,1)} %pack.6.refs_0_), channel_id=1, source_target_pairs={{0,1},{1,0},{2,3},{3,2},{4,5},{5,4},{6,7},{7,6}} | collective-permute-start | bytes 1413128 | tf_op jit(solution)/shard_map/ppermute | solution.py:80
  15.7 14.0 %collective-permute-start.1 = (bf16[368,640]{1,0:T(8,128)(2,1)}, bf16[368,640]{1,0:T(8,128)(2,1)S(1)}, u32[]{:S(2)}, u32[]{:S(2)}) collective-permute-start(bf16[368,640]{1,0:T(8,128)(2,1)} %pack.6.refs_0_), channel_id=1, source_target_pairs={{0,2},{1,5},{2,0},{3,7},{4,6},{5,1},{6,4},{7,3}} | collective-permute-start | bytes 1413128 | tf_op jit(solution)/shard_map/ppermute | solution.py:80
  16.4 15.7 %collective-permute-start = (bf16[368,640]{1,0:T(8,128)(2,1)}, bf16[368,640]{1,0:T(8,128)(2,1)}, u32[]{:S(2)}, u32[]{:S(2)}) collective-permute-start(bf16[368,640]{1,0:T(8,128)(2,1)} %pack.6.refs_0_), channel_id=1, source_target_pairs={{0,4},{1,3},{2,6},{3,1},{4,0},{5,7},{6,2},{7,5}} | collective-permute-start | bytes 1413128 | tf_op jit(solution)/shard_map/ppermute | solution.py:80
  19.8 27.3 %collective-permute-start.29 = (bf16[640,640]{1,0:T(8,128)(2,1)S(1)}, bf16[640,640]{1,0:T(8,128)(2,1)S(1)}, u32[]{:S(2)}, u32[]{:S(2)}) collective-permute-start(bf16[640,640]{1,0:T(8,128)(2,1)S(1)} %copy-done.22), channel_id=1, source_target_pairs={{0,2},{1,5},{2,0},{3,7},{4,6},{5,1},{6,4},{7,3}} | collective-permute-start | bytes 2457608 | tf_op jit(solution)/shard_map/ppermute | solution.py:80
  22.1 26.0 %collective-permute-start.28 = (bf16[640,640]{1,0:T(8,128)(2,1)S(1)}, bf16[640,640]{1,0:T(8,128)(2,1)}, u32[]{:S(2)}, u32[]{:S(2)}) collective-permute-start(bf16[640,640]{1,0:T(8,128)(2,1)S(1)} %copy-done.22), channel_id=1, source_target_pairs={{0,4},{1,3},{2,6},{3,1},{4,0},{5,7},{6,2},{7,5}} | collective-permute-start | bytes 2457608 | tf_op jit(solution)/shard_map/ppermute | solution.py:80
  26.7 23.4 %collective-permute-start.10 = (bf16[672,640]{1,0:T(8,128)(2,1)}, bf16[672,640]{1,0:T(8,128)(2,1)}, u32[]{:S(2)}, u32[]{:S(2)}) collective-permute-start(bf16[672,640]{1,0:T(8,128)(2,1)} %pack.7.refs_0_), channel_id=1, source_target_pairs={{0,1},{1,0},{2,3},{3,2},{4,5},{5,4},{6,7},{7,6}} | collective-permute-start | bytes 2580488 | tf_op jit(solution)/shard_map/ppermute | solution.py:80
  29.7 36.0 %collective-permute-start.8 = (bf16[672,640]{1,0:T(8,128)(2,1)}, bf16[672,640]{1,0:T(8,128)(2,1)}, u32[]{:S(2)}, u32[]{:S(2)}) collective-permute-start(bf16[672,640]{1,0:T(8,128)(2,1)} %pack.7.refs_0_), channel_id=1, source_target_pairs={{0,2},{1,5},{2,0},{3,7},{4,6},{5,1},{6,4},{7,3}} | collective-permute-start | bytes 2580488 | tf_op jit(solution)/shard_map/ppermute | solution.py:80
  32.1 33.6 %collective-permute-start.7 = (bf16[672,640]{1,0:T(8,128)(2,1)}, bf16[672,640]{1,0:T(8,128)(2,1)}, u32[]{:S(2)}, u32[]{:S(2)}) collective-permute-start(bf16[672,640]{1,0:T(8,128)(2,1)} %pack.7.refs_0_), channel_id=1, source_target_pairs={{0,4},{1,3},{2,6},{3,1},{4,0},{5,7},{6,2},{7,5}} | collective-permute-start | bytes 2580488 | tf_op jit(solution)/shard_map/ppermute | solution.py:80
  47.2 52.9 %collective-permute-start.17 = (bf16[960,640]{1,0:T(8,128)(2,1)}, bf16[960,640]{1,0:T(8,128)(2,1)S(1)}, u32[]{:S(2)}, u32[]{:S(2)}) collective-permute-start(bf16[960,640]{1,0:T(8,128)(2,1)} %pack.8.refs_0_.refs_8_.refs_1_.refs_9_), channel_id=1, source_target_pairs={{0,1},{1,0},{2,3},{3,2},{4,5},{5,4},{6,7},{7,6}} | collective-permute-start | bytes 3686408 | tf_op jit(solution)/shard_map/ppermute | solution.py:80
  48.1 53.0 %collective-permute-start.14 = (bf16[960,640]{1,0:T(8,128)(2,1)}, bf16[960,640]{1,0:T(8,128)(2,1)S(1)}, u32[]{:S(2)}, u32[]{:S(2)}) collective-permute-start(bf16[960,640]{1,0:T(8,128)(2,1)} %pack.8.refs_0_.refs_8_.refs_1_.refs_9_), channel_id=1, source_target_pairs={{0,4},{1,3},{2,6},{3,1},{4,0},{5,7},{6,2},{7,5}} | collective-permute-start | bytes 3686408 | tf_op jit(solution)/shard_map/ppermute | solution.py:80
  50.1 18.1 %collective-permute-start.5 = (bf16[368,640]{1,0:T(8,128)(2,1)}, bf16[368,640]{1,0:T(8,128)(2,1)}, u32[]{:S(2)}, u32[]{:S(2)}) collective-permute-start(bf16[368,640]{1,0:T(8,128)(2,1)} %copy-done.28), channel_id=1, source_target_pairs={{0,1},{1,0},{2,3},{3,2},{4,5},{5,4},{6,7},{7,6}} | collective-permute-start | bytes 1413128 | tf_op jit(solution)/shard_map/ppermute | solution.py:80
  65.7 2.5 collective-permute-start.4
  65.7 37.0 %collective-permute-start.15 = (bf16[960,640]{1,0:T(8,128)(2,1)}, bf16[960,640]{1,0:T(8,128)(2,1)}, u32[]{:S(2)}, u32[]{:S(2)}) collective-permute-start(bf16[960,640]{1,0:T(8,128)(2,1)} %pack.8.refs_0_.refs_8_.refs_1_.refs_9_), channel_id=1, source_target_pairs={{0,2},{1,5},{2,0},{3,7},{4,6},{5,1},{6,4},{7,3}} | collective-permute-start | bytes 3686408 | tf_op jit(solution)/shard_map/ppermute | solution.py:80
  68.2 29.5 %collective-permute-start.2 = (bf16[368,640]{1,0:T(8,128)(2,1)}, bf16[368,640]{1,0:T(8,128)(2,1)}, u32[]{:S(2)}, u32[]{:S(2)}) collective-permute-start(bf16[368,640]{1,0:T(8,128)(2,1)} %collective-permute-done.refs_1_), channel_id=1, source_target_pairs={{0,2},{1,5},{2,0},{3,7},{4,6},{5,1},{6,4},{7,3}} | collective-permute-start | bytes 1413128 | tf_op jit(solution)/shard_map/ppermute | solution.py:80
  68.2 41.7 %collective-permute-start.9 = (bf16[672,640]{1,0:T(8,128)(2,1)}, bf16[672,640]{1,0:T(8,128)(2,1)}, u32[]{:S(2)}, u32[]{:S(2)}) collective-permute-start(bf16[672,640]{1,0:T(8,128)(2,1)} %collective-permute-done.7.refs_1_), channel_id=1, source_target_pairs={{0,2},{1,5},{2,0},{3,7},{4,6},{5,1},{6,4},{7,3}} | collective-permute-start | bytes 2580488 | tf_op jit(solution)/shard_map/ppermute | solution.py:80
  97.6 5.1 collective-permute-start.6
  100.1 31.1 %collective-permute-start.21 = (bf16[992,640]{1,0:T(8,128)(2,1)}, bf16[992,640]{1,0:T(8,128)(2,1)}, u32[]{:S(2)}, u32[]{:S(2)}) collective-permute-start(bf16[992,640]{1,0:T(8,128)(2,1)} %pack.9.refs_0_), channel_id=1, source_target_pairs={{0,4},{1,3},{2,6},{3,1},{4,0},{5,7},{6,2},{7,5}} | collective-permute-start | bytes 3809288 | tf_op jit(solution)/shard_map/ppermute | solution.py:80
  101.1 32.6 %collective-permute-start.16 = (bf16[960,640]{1,0:T(8,128)(2,1)S(1)}, bf16[960,640]{1,0:T(8,128)(2,1)}, u32[]{:S(2)}, u32[]{:S(2)}) collective-permute-start(bf16[960,640]{1,0:T(8,128)(2,1)S(1)} %collective-permute-done.14.refs_1_.refs_9_.refs_2_.refs_10_), channel_id=1, source_target_pairs={{0,2},{1,5},{2,0},{3,7},{4,6},{5,1},{6,4},{7,3}} | collective-permute-start | bytes 3686408 | tf_op jit(solution)/shard_map/ppermute | solution.py:80
  102.7 30.5 %collective-permute-start.12 = (bf16[672,640]{1,0:T(8,128)(2,1)}, bf16[672,640]{1,0:T(8,128)(2,1)}, u32[]{:S(2)}, u32[]{:S(2)}) collective-permute-start(bf16[672,640]{1,0:T(8,128)(2,1)} %collective-permute-done.8.refs_2_), channel_id=1, source_target_pairs={{0,1},{1,0},{2,3},{3,2},{4,5},{5,4},{6,7},{7,6}} | collective-permute-start | bytes 2580488 | tf_op jit(solution)/shard_map/ppermute | solution.py:80
  102.7 30.5 %collective-permute-start.11 = (bf16[672,640]{1,0:T(8,128)(2,1)}, bf16[672,640]{1,0:T(8,128)(2,1)}, u32[]{:S(2)}, u32[]{:S(2)}) collective-permute-start(bf16[672,640]{1,0:T(8,128)(2,1)} %collective-permute-done.7.refs_1_), channel_id=1, source_target_pairs={{0,1},{1,0},{2,3},{3,2},{4,5},{5,4},{6,7},{7,6}} | collective-permute-start | bytes 2580488 | tf_op jit(solution)/shard_map/ppermute | solution.py:80
  109.9 25.7 %collective-permute-start.13 = (bf16[672,640]{1,0:T(8,128)(2,1)}, bf16[672,640]{1,0:T(8,128)(2,1)}, u32[]{:S(2)}, u32[]{:S(2)}) collective-permute-start(bf16[672,640]{1,0:T(8,128)(2,1)} %collective-permute-done.9.refs_3_), channel_id=1, source_target_pairs={{0,1},{1,0},{2,3},{3,2},{4,5},{5,4},{6,7},{7,6}} | collective-permute-start | bytes 2580488 | tf_op jit(solution)/shard_map/ppermute | solution.py:80
  131.2 45.0 %collective-permute-start.22 = (bf16[992,640]{1,0:T(8,128)(2,1)}, bf16[992,640]{1,0:T(8,128)(2,1)}, u32[]{:S(2)}, u32[]{:S(2)}) collective-permute-start(bf16[992,640]{1,0:T(8,128)(2,1)} %pack.9.refs_0_), channel_id=1, source_target_pairs={{0,2},{1,5},{2,0},{3,7},{4,6},{5,1},{6,4},{7,3}} | collective-permute-start | bytes 3809288 | tf_op jit(solution)/shard_map/ppermute | solution.py:80
  133.2 43.6 %collective-permute-start.18 = (bf16[960,640]{1,0:T(8,128)(2,1)S(1)}, bf16[960,640]{1,0:T(8,128)(2,1)S(1)}, u32[]{:S(2)}, u32[]{:S(2)}) collective-permute-start(bf16[960,640]{1,0:T(8,128)(2,1)S(1)} %collective-permute-done.14.refs_1_.refs_9_.refs_2_.refs_10_), channel_id=1, source_target_pairs={{0,1},{1,0},{2,3},{3,2},{4,5},{5,4},{6,7},{7,6}} | collective-permute-start | bytes 3686408 | tf_op jit(solution)/shard_map/ppermute | solution.py:80
  133.2 43.5 %collective-permute-start.19 = (bf16[960,640]{1,0:T(8,128)(2,1)}, bf16[960,640]{1,0:T(8,128)(2,1)}, u32[]{:S(2)}, u32[]{:S(2)}) collective-permute-start(bf16[960,640]{1,0:T(8,128)(2,1)} %collective-permute-done.15.refs_2_.refs_10_.refs_3_.refs_11_), channel_id=1, source_target_pairs={{0,1},{1,0},{2,3},{3,2},{4,5},{5,4},{6,7},{7,6}} | collective-permute-start | bytes 3686408 | tf_op jit(solution)/shard_map/ppermute | solution.py:80
  133.7 43.4 %collective-permute-start.23 = (bf16[992,640]{1,0:T(8,128)(2,1)}, bf16[992,640]{1,0:T(8,128)(2,1)}, u32[]{:S(2)}, u32[]{:S(2)}) collective-permute-start(bf16[992,640]{1,0:T(8,128)(2,1)} %collective-permute-done.21.refs_1_), channel_id=1, source_target_pairs={{0,2},{1,5},{2,0},{3,7},{4,6},{5,1},{6,4},{7,3}} | collective-permute-start | bytes 3809288 | tf_op jit(solution)/shard_map/ppermute | solution.py:80
  135.7 41.7 %collective-permute-start.20 = (bf16[960,640]{1,0:T(8,128)(2,1)}, bf16[960,640]{1,0:T(8,128)(2,1)}, u32[]{:S(2)}, u32[]{:S(2)}) collective-permute-start(bf16[960,640]{1,0:T(8,128)(2,1)} %collective-permute-done.16.refs_3_.refs_11_.refs_4_.refs_12_), channel_id=1, source_target_pairs={{0,1},{1,0},{2,3},{3,2},{4,5},{5,4},{6,7},{7,6}} | collective-permute-start | bytes 3686408 | tf_op jit(solution)/shard_map/ppermute | solution.py:80
  176.2 31.8 %collective-permute-start.24 = (bf16[992,640]{1,0:T(8,128)(2,1)}, bf16[992,640]{1,0:T(8,128)(2,1)}, u32[]{:S(2)}, u32[]{:S(2)}) collective-permute-start(bf16[992,640]{1,0:T(8,128)(2,1)} %pack.9.refs_0_), channel_id=1, source_target_pairs={{0,1},{1,0},{2,3},{3,2},{4,5},{5,4},{6,7},{7,6}} | collective-permute-start | bytes 3809288 | tf_op jit(solution)/shard_map/ppermute | solution.py:80
  176.7 31.5 %collective-permute-start.30 = (bf16[640,640]{1,0:T(8,128)(2,1)}, bf16[640,640]{1,0:T(8,128)(2,1)}, u32[]{:S(2)}, u32[]{:S(2)}) collective-permute-start(bf16[640,640]{1,0:T(8,128)(2,1)} %collective-permute-done.28.refs_1_), channel_id=1, source_target_pairs={{0,2},{1,5},{2,0},{3,7},{4,6},{5,1},{6,4},{7,3}} | collective-permute-start | bytes 2457608 | tf_op jit(solution)/shard_map/ppermute | solution.py:80
  176.8 33.1 %collective-permute-start.25 = (bf16[992,640]{1,0:T(8,128)(2,1)}, bf16[992,640]{1,0:T(8,128)(2,1)S(1)}, u32[]{:S(2)}, u32[]{:S(2)}) collective-permute-start(bf16[992,640]{1,0:T(8,128)(2,1)} %collective-permute-done.21.refs_1_), channel_id=1, source_target_pairs={{0,1},{1,0},{2,3},{3,2},{4,5},{5,4},{6,7},{7,6}} | collective-permute-start | bytes 3809288 | tf_op jit(solution)/shard_map/ppermute | solution.py:80
  177.1 32.8 %collective-permute-start.26 = (bf16[992,640]{1,0:T(8,128)(2,1)}, bf16[992,640]{1,0:T(8,128)(2,1)}, u32[]{:S(2)}, u32[]{:S(2)}) collective-permute-start(bf16[992,640]{1,0:T(8,128)(2,1)} %collective-permute-done.22.refs_2_), channel_id=1, source_target_pairs={{0,1},{1,0},{2,3},{3,2},{4,5},{5,4},{6,7},{7,6}} | collective-permute-start | bytes 3809288 | tf_op jit(solution)/shard_map/ppermute | solution.py:80
  177.3 33.1 %collective-permute-start.27 = (bf16[992,640]{1,0:T(8,128)(2,1)}, bf16[992,640]{1,0:T(8,128)(2,1)}, u32[]{:S(2)}, u32[]{:S(2)}) collective-permute-start(bf16[992,640]{1,0:T(8,128)(2,1)} %collective-permute-done.23.refs_3_), channel_id=1, source_target_pairs={{0,1},{1,0},{2,3},{3,2},{4,5},{5,4},{6,7},{7,6}} | collective-permute-start | bytes 3809288 | tf_op jit(solution)/shard_map/ppermute | solution.py:80
  207.9 41.5 %collective-permute-start.31 = (bf16[640,640]{1,0:T(8,128)(2,1)S(1)}, bf16[640,640]{1,0:T(8,128)(2,1)S(1)}, u32[]{:S(2)}, u32[]{:S(2)}) collective-permute-start(bf16[640,640]{1,0:T(8,128)(2,1)S(1)} %copy-done.22), channel_id=1, source_target_pairs={{0,1},{1,0},{2,3},{3,2},{4,5},{5,4},{6,7},{7,6}} | collective-permute-start | bytes 2457608 | tf_op jit(solution)/shard_map/ppermute | solution.py:80
  208.2 40.7 %collective-permute-start.37 = (bf16[320,640]{1,0:T(8,128)(2,1)}, bf16[320,640]{1,0:T(8,128)(2,1)S(1)}, u32[]{:S(2)}, u32[]{:S(2)}) collective-permute-start(bf16[320,640]{1,0:T(8,128)(2,1)} %collective-permute-done.35.refs_1_.refs_9_), channel_id=1, source_target_pairs={{0,2},{1,5},{2,0},{3,7},{4,6},{5,1},{6,4},{7,3}} | collective-permute-start | bytes 1228808 | tf_op jit(solution)/shard_map/ppermute | solution.py:80
  209.9 40.0 %collective-permute-start.32 = (bf16[640,640]{1,0:T(8,128)(2,1)}, bf16[640,640]{1,0:T(8,128)(2,1)}, u32[]{:S(2)}, u32[]{:S(2)}) collective-permute-start(bf16[640,640]{1,0:T(8,128)(2,1)} %collective-permute-done.28.refs_1_), channel_id=1, source_target_pairs={{0,1},{1,0},{2,3},{3,2},{4,5},{5,4},{6,7},{7,6}} | collective-permute-start | bytes 2457608 | tf_op jit(solution)/shard_map/ppermute | solution.py:80
  210.0 39.6 %collective-permute-start.33 = (bf16[640,640]{1,0:T(8,128)(2,1)}, bf16[640,640]{1,0:T(8,128)(2,1)}, u32[]{:S(2)}, u32[]{:S(2)}) collective-permute-start(bf16[640,640]{1,0:T(8,128)(2,1)} %copy-done.37), channel_id=1, source_target_pairs={{0,1},{1,0},{2,3},{3,2},{4,5},{5,4},{6,7},{7,6}} | collective-permute-start | bytes 2457608 | tf_op jit(solution)/shard_map/ppermute | solution.py:80
  210.5 39.6 %collective-permute-start.34 = (bf16[640,640]{1,0:T(8,128)(2,1)}, bf16[640,640]{1,0:T(8,128)(2,1)}, u32[]{:S(2)}, u32[]{:S(2)}) collective-permute-start(bf16[640,640]{1,0:T(8,128)(2,1)} %collective-permute-done.30.refs_3_), channel_id=1, source_target_pairs={{0,1},{1,0},{2,3},{3,2},{4,5},{5,4},{6,7},{7,6}} | collective-permute-start | bytes 2457608 | tf_op jit(solution)/shard_map/ppermute | solution.py:80
  248.9 40.5 %collective-permute-start.38 = (bf16[320,640]{1,0:T(8,128)(2,1)S(1)}, bf16[320,640]{1,0:T(8,128)(2,1)S(1)}, u32[]{:S(2)}, u32[]{:S(2)}) collective-permute-start(bf16[320,640]{1,0:T(8,128)(2,1)S(1)} %copy-done.29), channel_id=1, source_target_pairs={{0,1},{1,0},{2,3},{3,2},{4,5},{5,4},{6,7},{7,6}} | collective-permute-start | bytes 1228808 | tf_op jit(solution)/shard_map/ppermute | solution.py:80
  249.4 89.7 %collective-permute-start.42 = (bf16[1024,512]{1,0:T(8,128)(2,1)}, bf16[1024,512]{1,0:T(8,128)(2,1)}, u32[]{:S(2)}, u32[]{:S(2)}) collective-permute-start(bf16[1024,512]{1,0:T(8,128)(2,1)} %get-tuple-element.110), channel_id=1, source_target_pairs={{0,1},{1,0},{2,3},{3,2},{4,5},{5,4},{6,7},{7,6}} | collective-permute-start | bytes 3145736 | tf_op jit(solution)/shard_map/ppermute | solution.py:80
  249.5 40.0 %collective-permute-start.39 = (bf16[320,640]{1,0:T(8,128)(2,1)}, bf16[320,640]{1,0:T(8,128)(2,1)S(1)}, u32[]{:S(2)}, u32[]{:S(2)}) collective-permute-start(bf16[320,640]{1,0:T(8,128)(2,1)} %collective-permute-done.35.refs_1_.refs_9_), channel_id=1, source_target_pairs={{0,1},{1,0},{2,3},{3,2},{4,5},{5,4},{6,7},{7,6}} | collective-permute-start | bytes 1228808 | tf_op jit(solution)/shard_map/ppermute | solution.py:80
  250.0 39.5 %collective-permute-start.40 = (bf16[320,640]{1,0:T(8,128)(2,1)}, bf16[320,640]{1,0:T(8,128)(2,1)S(1)}, u32[]{:S(2)}, u32[]{:S(2)}) collective-permute-start(bf16[320,640]{1,0:T(8,128)(2,1)} %collective-permute-done.36.refs_2_.refs_10_), channel_id=1, source_target_pairs={{0,1},{1,0},{2,3},{3,2},{4,5},{5,4},{6,7},{7,6}} | collective-permute-start | bytes 1228808 | tf_op jit(solution)/shard_map/ppermute | solution.py:80
  250.0 39.5 %collective-permute-start.41 = (bf16[320,640]{1,0:T(8,128)(2,1)S(1)}, bf16[320,640]{1,0:T(8,128)(2,1)S(1)}, u32[]{:S(2)}, u32[]{:S(2)}) collective-permute-start(bf16[320,640]{1,0:T(8,128)(2,1)S(1)} %collective-permute-done.37.refs_3_.refs_11_), channel_id=1, source_target_pairs={{0,1},{1,0},{2,3},{3,2},{4,5},{5,4},{6,7},{7,6}} | collective-permute-start | bytes 1228808 | tf_op jit(solution)/shard_map/ppermute | solution.py:80
  407.5 166.0 %collective-permute-start.45 = (f32[640,640]{1,0:T(8,128)}, f32[640,640]{1,0:T(8,128)}, u32[]{:S(2)}, u32[]{:S(2)}) collective-permute-start(f32[640,640]{1,0:T(8,128)} %get-tuple-element.134), channel_id=1, source_target_pairs={{0,2},{1,5},{2,0},{3,7},{4,6},{5,1},{6,4},{7,3}} | collective-permute-start | bytes 4915208 | tf_op jit(solution)/shard_map/ppermute | solution.py:80
  425.2 149.7 %collective-permute-start.57 = (f32[640,640]{1,0:T(8,128)}, f32[640,640]{1,0:T(8,128)}, u32[]{:S(2)}, u32[]{:S(2)}) collective-permute-start(f32[640,640]{1,0:T(8,128)} %get-tuple-element.152), channel_id=1, source_target_pairs={{0,2},{1,5},{2,0},{3,7},{4,6},{5,1},{6,4},{7,3}} | collective-permute-start | bytes 4915208 | tf_op jit(solution)/shard_map/ppermute | solution.py:80
  426.6 188.5 %collective-permute-start.49 = (f32[1344,640]{1,0:T(8,128)}, f32[1344,640]{1,0:T(8,128)}, u32[]{:S(2)}, u32[]{:S(2)}) collective-permute-start(f32[1344,640]{1,0:T(8,128)} %get-tuple-element.140), channel_id=1, source_target_pairs={{0,2},{1,5},{2,0},{3,7},{4,6},{5,1},{6,4},{7,3}} | collective-permute-start | bytes 10321928 | tf_op jit(solution)/shard_map/ppermute | solution.py:80
  516.2 100.5 %collective-permute-start.47 = (f32[1344,640]{1,0:T(8,128)}, f32[1344,640]{1,0:T(8,128)}, u32[]{:S(2)}, u32[]{:S(2)}) collective-permute-start(f32[1344,640]{1,0:T(8,128)} %get-tuple-element.138), channel_id=1, source_target_pairs={{0,2},{1,5},{2,0},{3,7},{4,6},{5,1},{6,4},{7,3}} | collective-permute-start | bytes 10321928 | tf_op jit(solution)/shard_map/ppermute | solution.py:80
  560.5 1.5 collective-permute-start.61
  563.0 4.9 collective-permute-start.62
  567.9 4.9 collective-permute-start.63
  572.8 21.1 %collective-permute-start.59 = (f32[640,640]{1,0:T(8,128)S(1)}, f32[640,640]{1,0:T(8,128)S(1)}, u32[]{:S(2)}, u32[]{:S(2)}) collective-permute-start(f32[640,640]{1,0:T(8,128)S(1)} %copy-done.35), channel_id=1, source_target_pairs={{0,2},{1,5},{2,0},{3,7},{4,6},{5,1},{6,4},{7,3}} | collective-permute-start | bytes 4915208 | tf_op jit(solution)/shard_map/ppermute | solution.py:80
  573.5 38.0 %collective-permute-start.43 = (f32[640,640]{1,0:T(8,128)}, f32[640,640]{1,0:T(8,128)S(1)}, u32[]{:S(2)}, u32[]{:S(2)}) collective-permute-start(f32[640,640]{1,0:T(8,128)} %get-tuple-element.132), channel_id=1, source_target_pairs={{0,2},{1,5},{2,0},{3,7},{4,6},{5,1},{6,4},{7,3}} | collective-permute-start | bytes 4915208 | tf_op jit(solution)/shard_map/ppermute | solution.py:80
  574.9 135.3 %collective-permute-start.55 = (f32[1280,640]{1,0:T(8,128)}, f32[1280,640]{1,0:T(8,128)S(1)}, u32[]{:S(2)}, u32[]{:S(2)}) collective-permute-start(f32[1280,640]{1,0:T(8,128)} %get-tuple-element.149), channel_id=1, source_target_pairs={{0,2},{1,5},{2,0},{3,7},{4,6},{5,1},{6,4},{7,3}} | collective-permute-start | bytes 9830408 | tf_op jit(solution)/shard_map/ppermute | solution.py:80
  594.0 87.8 %collective-permute-start.53 = (f32[640,640]{1,0:T(8,128)}, f32[640,640]{1,0:T(8,128)S(1)}, u32[]{:S(2)}, u32[]{:S(2)}) collective-permute-start(f32[640,640]{1,0:T(8,128)} %get-tuple-element.147), channel_id=1, source_target_pairs={{0,2},{1,5},{2,0},{3,7},{4,6},{5,1},{6,4},{7,3}} | collective-permute-start | bytes 4915208 | tf_op jit(solution)/shard_map/ppermute | solution.py:80
  611.5 96.6 %collective-permute-start.51 = (f32[640,640]{1,0:T(8,128)}, f32[640,640]{1,0:T(8,128)S(1)}, u32[]{:S(2)}, u32[]{:S(2)}) collective-permute-start(f32[640,640]{1,0:T(8,128)} %get-tuple-element.145), channel_id=1, source_target_pairs={{0,2},{1,5},{2,0},{3,7},{4,6},{5,1},{6,4},{7,3}} | collective-permute-start | bytes 4915208 | tf_op jit(solution)/shard_map/ppermute | solution.py:80
  615.2 93.6 %collective-permute-start.46 = (f32[320,640]{1,0:T(8,128)S(1)}, f32[320,640]{1,0:T(8,128)S(1)}, u32[]{:S(2)}, u32[]{:S(2)}) collective-permute-start(f32[320,640]{1,0:T(8,128)S(1)} %slice_add_fusion.7), channel_id=1, source_target_pairs={{0,4},{1,3},{2,6},{3,1},{4,0},{5,7},{6,2},{7,5}} | collective-permute-start | bytes 2457608 | tf_op jit(solution)/shard_map/ppermute | solution.py:80
  616.7 95.8 %collective-permute-start.58 = (f32[320,640]{1,0:T(8,128)S(1)}, f32[320,640]{1,0:T(8,128)S(1)}, u32[]{:S(2)}, u32[]{:S(2)}) collective-permute-start(f32[320,640]{1,0:T(8,128)S(1)} %slice_add_fusion.4), channel_id=1, source_target_pairs={{0,4},{1,3},{2,6},{3,1},{4,0},{5,7},{6,2},{7,5}} | collective-permute-start | bytes 2457608 | tf_op jit(solution)/shard_map/ppermute | solution.py:80
  681.8 33.8 %collective-permute-start.60 = (f32[320,640]{1,0:T(8,128)S(1)}, f32[320,640]{1,0:T(8,128)S(1)}, u32[]{:S(2)}, u32[]{:S(2)}) collective-permute-start(f32[320,640]{1,0:T(8,128)S(1)} %slice_add_fusion.3), channel_id=1, source_target_pairs={{0,4},{1,3},{2,6},{3,1},{4,0},{5,7},{6,2},{7,5}} | collective-permute-start | bytes 2457608 | tf_op jit(solution)/shard_map/ppermute | solution.py:80
  708.1 12.3 %collective-permute-start.44 = (f32[320,640]{1,0:T(8,128)S(1)}, f32[320,640]{1,0:T(8,128)S(1)}, u32[]{:S(2)}, u32[]{:S(2)}) collective-permute-start(f32[320,640]{1,0:T(8,128)S(1)} %slice_add_fusion.8), channel_id=1, source_target_pairs={{0,4},{1,3},{2,6},{3,1},{4,0},{5,7},{6,2},{7,5}} | collective-permute-start | bytes 2457608 | tf_op jit(solution)/shard_map/ppermute | solution.py:80
  708.7 91.3 %collective-permute-start.50 = (f32[672,640]{1,0:T(8,128)}, f32[672,640]{1,0:T(8,128)}, u32[]{:S(2)}, u32[]{:S(2)}) collective-permute-start(f32[672,640]{1,0:T(8,128)} %slice_add_fusion), channel_id=1, source_target_pairs={{0,4},{1,3},{2,6},{3,1},{4,0},{5,7},{6,2},{7,5}} | collective-permute-start | bytes 5160968 | tf_op jit(solution)/shard_map/ppermute | solution.py:80
  710.2 89.9 %collective-permute-start.48 = (f32[672,640]{1,0:T(8,128)S(1)}, f32[672,640]{1,0:T(8,128)}, u32[]{:S(2)}, u32[]{:S(2)}) collective-permute-start(f32[672,640]{1,0:T(8,128)S(1)} %slice_add_fusion.1), channel_id=1, source_target_pairs={{0,4},{1,3},{2,6},{3,1},{4,0},{5,7},{6,2},{7,5}} | collective-permute-start | bytes 5160968 | tf_op jit(solution)/shard_map/ppermute | solution.py:80
  712.5 80.0 %collective-permute-start.56 = (f32[640,640]{1,0:T(8,128)}, f32[640,640]{1,0:T(8,128)}, u32[]{:S(2)}, u32[]{:S(2)}) collective-permute-start(f32[640,640]{1,0:T(8,128)} %slice_add_fusion.2), channel_id=1, source_target_pairs={{0,4},{1,3},{2,6},{3,1},{4,0},{5,7},{6,2},{7,5}} | collective-permute-start | bytes 4915208 | tf_op jit(solution)/shard_map/ppermute | solution.py:80
  716.5 67.2 %collective-permute-start.54 = (f32[320,640]{1,0:T(8,128)}, f32[320,640]{1,0:T(8,128)S(1)}, u32[]{:S(2)}, u32[]{:S(2)}) collective-permute-start(f32[320,640]{1,0:T(8,128)} %slice_add_fusion.5), channel_id=1, source_target_pairs={{0,4},{1,3},{2,6},{3,1},{4,0},{5,7},{6,2},{7,5}} | collective-permute-start | bytes 2457608 | tf_op jit(solution)/shard_map/ppermute | solution.py:80
  720.5 72.1 %collective-permute-start.52 = (f32[320,640]{1,0:T(8,128)}, f32[320,640]{1,0:T(8,128)}, u32[]{:S(2)}, u32[]{:S(2)}) collective-permute-start(f32[320,640]{1,0:T(8,128)} %slice_add_fusion.6), channel_id=1, source_target_pairs={{0,4},{1,3},{2,6},{3,1},{4,0},{5,7},{6,2},{7,5}} | collective-permute-start | bytes 2457608 | tf_op jit(solution)/shard_map/ppermute | solution.py:80
  (44 other events, 605.1 us)

commit v7 on v6

--- a/solution.py
+++ b/solution.py
@@ -160,7 +160,7 @@
         scores = dot_nt(q_head, key)
         if valid is not None:
             column = lax.broadcasted_iota(jnp.int32, scores.shape, 1)
-            scores = jnp.where(column < valid, scores, -1e30)
+            scores = jnp.where(column < valid, scores, -jnp.inf)
         mixed.append(dot_nn(softmax_rows(scores).astype(BF16), value))
     return jnp.where(low_lanes(query.shape[0]), mixed[0], mixed[1]).astype(BF16)
 
@@ -173,7 +173,7 @@
 def backward_probs(scores, d_probs, valid):
     if valid is not None:
         row = lax.broadcasted_iota(jnp.int32, scores.shape, 0)
-        scores = jnp.where(row < valid, scores, -1e30)
+        scores = jnp.where(row < valid, scores, -jnp.inf)
     raised = jnp.exp(scores - jnp.max(scores, axis=0, keepdims=True))
     probs = raised * (1.0 / jnp.sum(raised, axis=0, keepdims=True))
     inner = jnp.sum(d_probs * probs, axis=0, keepdims=True)
@@ -1248,7 +1248,7 @@
                 down_pair = weight_grads(1, (gated, rounded),
                                                [(0, c * width, 1, 0, 0, half // n_dev, (c,)) for c in range(half // width)], half // n_dev)
             r_ff2 = reduce(down_pair)
-            sizes = (4,) if turn == 0 else (2, 2)
+            sizes = (4,)
             d_norm, r_ff1, bias_grads, first_chunk = None, [], [], 0
             for index, chunks in enumerate(sizes):
                 *out, vec_b1, far, keep = ff_grads(10 + 2 * turn + index, rounded, grad, save_a, save_g, norm3, h2, rows,

time: 815 us -> 882 us (1.082)
  waiting for transfers between devices: 261 us -> 343 us
  Pallas kernels: 464 us -> 450 us
    ppermute x64 -> x62, waiting for transfers between devices: 261 us -> 343 us  [permute(): return lax.ppermute(array, AXIS, perm)]
    pallas_call x3 -> x2, Pallas kernels: 108 us -> 95.7 us  [ff_grads(): pl.pallas_call(functools.partial(ff_grad_kernel, offset, first, resumed,...]
    ppermute x64 -> x62, starting transfers between devices: 50.8 us -> 49.2 us  [permute(): return lax.ppermute(array, AXIS, perm)]
  transfers between devices with their start and end apart: 64 -> 62, of which waited for: 16 -> 13; matrix products, arithmetic and copies ran while one was open for 2% -> 3% of each run, Pallas kernels for 48% -> 29%
where the time goes in v7:
time: 882 us; the launch traced here: 875 us
  Pallas kernels  450 us (51%)
  waiting for transfers between devices  343 us (39%)
  starting transfers between devices  49.2 us (6%)
  local copies, waits for them, and re-layouts  15.9 us (2%)
  other arithmetic  14.8 us (2%)
    ppermute x62, waiting for transfers between devices, permute(): return lax.ppermute(array, AXIS, perm)  343 us
    pallas_call x2, Pallas kernels, ff_grads(): pl.pallas_call(functools.partial(ff_grad_kernel, offset, first, resumed,...  95.7 us
    pallas_call x2, Pallas kernels, self_backward(): call(functools.partial(self_backward_kernel, STEP // tokens, tokens), cou...  80.3 us
    pallas_call x2, Pallas kernels, cross_backward(): call(functools.partial(cross_backward_kernel, STEP // tokens, tokens, val...  56.8 us
    ppermute x62, starting transfers between devices, permute(): return lax.ppermute(array, AXIS, perm)  49.2 us
    pallas_call x1, Pallas kernels, ff_up_forward(): call(ff_up_kernel, count // FF_STEP, [by_step(FF_STEP, width), whole(*row...  39.2 us
    pallas_call x1, Pallas kernels, attention_forward(): call(functools.partial(attention_forward_kernel, STEP // tokens, tokens,...  37.5 us
    pallas_call x1, Pallas kernels, ff_forward(): call(functools.partial(ff_forward_kernel, offset), count // FF_STEP, [by_...  30.1 us
  transfers between devices with their start and end apart: 62, of which 13 were waited for; matrix products, arithmetic and copies ran while one was open for 3% of the time, Pallas kernels for 29%

profile of v7, /device:TPU:0, one launch (start us, length us, event | category | flops | bytes accessed | tf_op | source)
XLA Modules:
  0.0 874.8 jit_solution(536735331460323303)
XLA Ops:
  0.7 2.2 copy.53
  2.9 1.5 copy.51
  4.4 1.8 pack.11.refs_0_.refs_8_
  6.2 3.3 collective-permute-start.36
  9.5 1.5 collective-permute-start.35
  13.7 1.9 pack.6.refs_0_
  16.4 2.1 pack.10.refs_0_
  19.8 2.3 collective-permute-start.29
  22.1 1.6 collective-permute-start.28
  24.5 2.2 pack.7.refs_0_
  26.7 3.0 collective-permute-done.1.refs_2_
  29.7 2.4 collective-permute-start.8
  32.1 1.6 collective-permute-start.7
  33.7 2.4 pack.8.refs_0_.refs_8_
  36.1 11.1 %collective-permute-done.29.refs_2_ = bf16[640,640]{1,0:T(8,128)(2,1)} collective-permute-done((bf16[640,640]{1,0:T(8,128)(2,1)S(1)}, bf16[640,640]{1,0:T(8,128)(2,1)}, u32[]{:S(2)}, u32[]{:S(2)}) %collective-permute-start.29) | collective-permute-done | bytes 819232 | tf_op jit(solution)/shard_map/ppermute | solution.py:80
  47.9 2.2 collective-permute-start.14
  50.1 15.6 %collective-permute-done.8.refs_2_ = bf16[672,640]{1,0:T(8,128)(2,1)} collective-permute-done((bf16[672,640]{1,0:T(8,128)(2,1)}, bf16[672,640]{1,0:T(8,128)(2,1)}, u32[]{:S(2)}, u32[]{:S(2)}) %collective-permute-start.8) | collective-permute-done | bytes 860192 | tf_op jit(solution)/shard_map/ppermute | solution.py:80
  65.7 2.5 collective-permute-start.15
  68.2 2.1 collective-permute-start.9
  70.4 27.2 %collective-permute-done.2.refs_3_ = bf16[368,640]{1,0:T(8,128)(2,1)S(1)} collective-permute-done((bf16[368,640]{1,0:T(8,128)(2,1)}, bf16[368,640]{1,0:T(8,128)(2,1)S(1)}, u32[]{:S(2)}, u32[]{:S(2)}) %collective-permute-start.2) | collective-permute-done | bytes 471072 | tf_op jit(solution)/shard_map/ppermute | solution.py:80
  97.5 2.6 pack.9.refs_0_
  101.1 1.7 collective-permute-start.16
  103.3 6.7 collective-permute-done.9.refs_3_
  110.0 3.8 context.1
  113.8 1.9 vec_sum.1
  117.9 13.3 %collective-permute-done.21.refs_1_ = bf16[992,640]{1,0:T(8,128)(2,1)} collective-permute-done((bf16[992,640]{1,0:T(8,128)(2,1)}, bf16[992,640]{1,0:T(8,128)(2,1)}, u32[]{:S(2)}, u32[]{:S(2)}) %collective-permute-start.21) | collective-permute-done | bytes 1269792 | tf_op jit(solution)/shard_map/ppermute | solution.py:80
  131.3 2.0 collective-permute-start.22
  133.8 1.9 collective-permute-start.23
  136.3 20.2 %shard_map.186 = (bf16[1536,640]{1,0:T(8,128)(2,1)}, bf16[1536,1920]{1,0:T(8,128)(2,1)}, bf16[1536,640]{1,0:T(8,128)(2,1)}, f32[1536,640]{1,0:T(8,128)}) custom-call(bf16[1536,640]{1,0:T(8,128)(2,1)} %bitcast.94, f32[16,640]{1,0:T(8,128)} %get-tuple-element.159.rows_ref, bf16[368,640]{1,0:T(8,128)(2,1)} %pack.6.refs_0_, ...), custom_call_target="tpu_custom_call" | custom-call | flops 6039797760 | bytes 20000000 | tf_op jit(solution)/shard_map/pallas_call | solution.py:669
  156.5 19.5 %shard_map.187 = (bf16[1536,640]{1,0:T(8,128)(2,1)}, bf16[1536,640]{1,0:T(8,128)(2,1)}, bf16[480,1280]{1,0:T(8,128)(2,1)}, bf16[1536,640]{1,0:T(8,128)(2,1)}, f32[1536,640]{1,0:T(8,128)}) custom-call(f32[1536,640]{1,0:T(8,128)} %get-tuple-element.85.h_ref, f32[16,640]{1,0:T(8,128)} %get-tuple-element.159.rows_ref, ...), custom_call_target="tpu_custom_call" | custom-call | flops 5536481280 | bytes 20000000 | tf_op jit(solution)/shard_map/pallas_call | solution.py:681
  177.5 30.1 %shard_map.188 = (bf16[1536,640]{1,0:T(8,128)(2,1)}, bf16[1536,2560]{1,0:T(8,128)(2,1)}, f32[1536,2560]{1,0:T(8,128)}, f32[1536,2560]{1,0:T(8,128)}, f32[1536,640]{1,0:T(8,128)}) custom-call(f32[1536,640]{1,0:T(8,128)} %get-tuple-element.90.h_ref, f32[16,640]{1,0:T(8,128)} %get-tuple-element.159.rows_ref, f32[1,5120]{1,0:T(1,128)} %bitcast.89, ...), custom_call_target="tpu_custom_call" | custom-call | flops 15099494400 | bytes 60000000 | tf_op jit(solution)/shard_map/pallas_call | solution.py:711
  208.0 1.9 collective-permute-start.37
  210.4 37.5 %shard_map.189 = (bf16[1536,640]{1,0:T(8,128)(2,1)}, bf16[1536,1920]{1,0:T(8,128)(2,1)}, bf16[1536,640]{1,0:T(8,128)(2,1)}, f32[1536,640]{1,0:T(8,128)}, bf16[15...) custom-call(f32[1536,640]{1,0:T(8,128)} %get-tuple-element.93.h_ref,, ...), custom_call_target="tpu_custom_call" | custom-call | flops 11576279040 | bytes 40000000 | tf_op jit(solution)/shard_map/pallas_call | solution.py:698
  249.8 39.2 %shard_map.190 = (bf16[1536,640]{1,0:T(8,128)(2,1)}, bf16[1536,2560]{1,0:T(8,128)(2,1)}, f32[1536,2560]{1,0:T(8,128)}, f32[1536,2560]{1,0:T(8,128)}, f32[640,640]{1,0:T(8,128)}, /*index=5*/f32[640,640]{1,0:T(8,128)}) custom-call(f32[1536,640]{1,0:T(8,128)} %get-tuple-element.94.h_ref, f32[16,640]{1,0:T(8,128)} %get-tuple-element.158.rows_ref, ...), custom_call_target="tpu_custom_call" | custom-call | flops 15099494400 | bytes 50000000 | tf_op jit(solution)/shard_map/pallas_call | solution.py:725
  290.0 47.9 %shard_map.192 = (f32[1536,640]{1,0:T(8,128)}, f32[8,640]{1,0:T(8,128)}, f32[8,5120]{1,0:T(8,128)}, f32[1280,640]{1,0:T(8,128)}, f32[1280,640]{1,0:T(8,128)}) custom-call(bf16[1536,640]{1,0:T(8,128)(2,1)} %bitcast.92, bf16[1536,640]{1,0:T(8,128)(2,1)} %bitcast.93, f32[1536,2560]{1,0:T(8,128)} %get-tuple-element.96.save_a, ...), custom_call_target="tpu_custom_call" | custom-call | flops 25165824000 | bytes 60000000 | tf_op jit(solution)/shard_map/pallas_call | solution.py:1112
  338.0 28.4 %shard_map.193 = (f32[1536,640]{1,0:T(8,128)}, f32[8,640]{1,0:T(8,128)}, f32[1344,640]{1,0:T(8,128)}, f32[1344,640]{1,0:T(8,128)}) custom-call(f32[1536,640]{1,0:T(8,128)} %get-tuple-element.99.grad_ref, bf16[1536,640]{1,0:T(8,128)(2,1)} %get-tuple-element.100.query_ref, bf16[480,1280]{1,0:T(8,128)(2,1)} %get-tuple-element.101.kv_ref, ...), custom_call_target="tpu_custom_call" | custom-call | flops 8975810560 | bytes 20000000 | tf_op jit(solution)/shard_map/pallas_call | solution.py:756
  366.4 40.0 %shard_map.194 = (f32[1536,640]{1,0:T(8,128)}, bf16[1536,640]{1,0:T(8,128)(2,1)}, f32[8,640]{1,0:T(8,128)}, f32[640,640]{1,0:T(8,128)}, f32[640,640]{1,0:T(8,128)}) custom-call(f32[1536,640]{1,0:T(8,128)} %get-tuple-element.107.grad_ref, bf16[1536,1920]{1,0:T(8,128)(2,1)} %get-tuple-element.108.qkv_ref, f32[1536,640]{1,0:T(8,128)} %get-tuple-element.93.h_ref, ...), custom_call_target="tpu_custom_call" | custom-call | flops 12582912000 | bytes 30000000 | tf_op jit(solution)/shard_map/pallas_call | solution.py:774
  406.4 47.8 %shard_map.195 = (f32[1536,640]{1,0:T(8,128)}, f32[8,640]{1,0:T(8,128)}, f32[8,5120]{1,0:T(8,128)}, f32[1280,640]{1,0:T(8,128)}, f32[1280,640]{1,0:T(8,128)}) custom-call(bf16[1536,640]{1,0:T(8,128)(2,1)} %get-tuple-element.111.rounded_ref.refs_1_, f32[1536,640]{1,0:T(8,128)} %get-tuple-element.112.grad_ref, f32[1536,2560]{1,0:T(8,128)} %get-tuple-element.113.save_a, ...), custom_call_target="tpu_custom_call" | custom-call | flops 25165824000 | bytes 60000000 | tf_op jit(solution)/shard_map/pallas_call | solution.py:1112
  454.2 28.4 %shard_map.196 = (f32[1536,640]{1,0:T(8,128)}, f32[8,640]{1,0:T(8,128)}, f32[1344,640]{1,0:T(8,128)}, f32[1344,640]{1,0:T(8,128)}) custom-call(f32[1536,640]{1,0:T(8,128)} %get-tuple-element.116.grad_ref, bf16[1536,640]{1,0:T(8,128)(2,1)} %get-tuple-element.117.query_ref, bf16[480,1280]{1,0:T(8,128)(2,1)} %get-tuple-element.118.kv_ref, ...), custom_call_target="tpu_custom_call" | custom-call | flops 8975810560 | bytes 20000000 | tf_op jit(solution)/shard_map/pallas_call | solution.py:756
  482.6 40.3 %shard_map.197 = (f32[1536,640]{1,0:T(8,128)}, bf16[1536,640]{1,0:T(8,128)(2,1)}, f32[8,640]{1,0:T(8,128)}, f32[640,640]{1,0:T(8,128)}, f32[640,640]{1,0:T(8,128)}) custom-call(f32[1536,640]{1,0:T(8,128)} %get-tuple-element.121.grad_ref, bf16[1536,1920]{1,0:T(8,128)(2,1)} %get-tuple-element.122.qkv_ref, bf16[1536,640]{1,0:T(8,128)(2,1)} %bitcast.95, ...), custom_call_target="tpu_custom_call" | custom-call | flops 12582912000 | bytes 30000000 | tf_op jit(solution)/shard_map/pallas_call | solution.py:774
  523.1 1.9 collective-permute-start.45
  525.2 1.8 vec_pack.1
  527.0 1.5 collective-permute-done.59
  529.4 1.9 collective-permute-start.60
  531.5 66.8 %collective-permute-done.60 = f32[48,640]{1,0:T(8,128)S(1)} collective-permute-done((f32[48,640]{1,0:T(8,128)S(1)}, f32[48,640]{1,0:T(8,128)S(1)}, u32[]{:S(2)}, u32[]{:S(2)}) %collective-permute-start.60) | collective-permute-done | bytes 122912 | tf_op jit(solution)/shard_map/ppermute | solution.py:80
  598.5 17.0 %shard_map.198 = (f32[640,640]{1,0:T(8,128)}, f32[640,640]{1,0:T(8,128)}) custom-call(bf16[1536,2560]{1,0:T(8,128)(2,1)} %get-tuple-element.143.refs_0_, bf16[1536,640]{1,0:T(8,128)(2,1)} %get-tuple-element.111.rounded_ref.refs_1_), custom_call_target="tpu_custom_call" | custom-call | flops 5033164800 | bytes 20000000 | tf_op jit(solution)/shard_map/pallas_call | solution.py:872
  615.5 1.9 collective-permute-start.55
  617.6 72.0 %collective-permute-done.55.refs_1_ = f32[640,640]{1,0:T(8,128)S(1)} collective-permute-done((f32[640,640]{1,0:T(8,128)}, f32[640,640]{1,0:T(8,128)S(1)}, u32[]{:S(2)}, u32[]{:S(2)}) %collective-permute-start.55) | collective-permute-done | bytes 1638432 | tf_op jit(solution)/shard_map/ppermute | solution.py:80
  689.7 1.9 slice_add_fusion.7
  691.7 1.4 slice_add_fusion.6
  694.4 3.0 slice_add_fusion.3
  698.5 1.4 slice_add_fusion.1
  701.2 3.0 slice_add_fusion
  704.2 30.6 %collective-permute-done.61 = f32[48,640]{1,0:T(8,128)S(1)} collective-permute-done((f32[48,640]{1,0:T(8,128)S(1)}, f32[48,640]{1,0:T(8,128)S(1)}, u32[]{:S(2)}, u32[]{:S(2)}) %collective-permute-start.61) | collective-permute-done | bytes 122912 | tf_op jit(solution)/shard_map/ppermute | solution.py:80
  735.7 34.2 %collective-permute-done.57.refs_4_ = f32[640,640]{1,0:T(8,128)S(1)} collective-permute-done((f32[640,640]{1,0:T(8,128)}, f32[640,640]{1,0:T(8,128)S(1)}, u32[]{:S(2)}, u32[]{:S(2)}) %collective-permute-start.57) | collective-permute-done | bytes 1638432 | tf_op jit(solution)/shard_map/ppermute | solution.py:80
  770.5 1.4 collective-permute-start.50
  771.9 1.3 slice_add_fusion.2
  777.3 12.2 %shard_map.191 = bf16[1536,640]{1,0:T(8,128)(2,1)} custom-call(f32[1536,640]{1,0:T(8,128)} %get-tuple-element.94.h_ref, f32[16,640]{1,0:T(8,128)} %get-tuple-element.158.rows_ref, bf16[1536,2560]{1,0:T(8,128)(2,1)} %get-tuple-element.95.gated_ref, bf16[320,640]{1,0:T(8,128)(2,1)} %pack.11.refs_0_.refs_8_, ...), custom_call_target="tpu_custom_call" | custom-call | flops 5033164800 | bytes 20000000 | tf_op jit(solution)/shard_map/pallas_call | solution.py:740
  790.3 3.8 totals.4
  794.1 60.4 %collective-permute-done.58.refs_5_ = f32[320,640]{1,0:T(8,128)} collective-permute-done((f32[320,640]{1,0:T(8,128)}, f32[320,640]{1,0:T(8,128)}, u32[]{:S(2)}, u32[]{:S(2)}) %collective-permute-start.58) | collective-permute-done | bytes 819232 | tf_op jit(solution)/shard_map/ppermute | solution.py:80
  854.5 3.8 totals.7
  858.3 7.4 totals.6
  867.0 6.3 totals.5
  873.3 1.3 copy.58
  (197 shorter events, 29.8 us)
Async XLA Ops:
  6.2 13.4 %collective-permute-start.36 = (bf16[320,640]{1,0:T(8,128)(2,1)}, bf16[320,640]{1,0:T(8,128)(2,1)}, u32[]{:S(2)}, u32[]{:S(2)}) collective-permute-start(bf16[320,640]{1,0:T(8,128)(2,1)} %pack.11.refs_0_.refs_8_), channel_id=1, source_target_pairs={{0,2},{1,5},{2,0},{3,7},{4,6},{5,1},{6,4},{7,3}} | collective-permute-start | bytes 1228808 | tf_op jit(solution)/shard_map/ppermute | solution.py:80
  9.5 12.6 %collective-permute-start.35 = (bf16[320,640]{1,0:T(8,128)(2,1)}, bf16[320,640]{1,0:T(8,128)(2,1)}, u32[]{:S(2)}, u32[]{:S(2)}) collective-permute-start(bf16[320,640]{1,0:T(8,128)(2,1)} %pack.11.refs_0_.refs_8_), channel_id=1, source_target_pairs={{0,4},{1,3},{2,6},{3,1},{4,0},{5,7},{6,2},{7,5}} | collective-permute-start | bytes 1228808 | tf_op jit(solution)/shard_map/ppermute | solution.py:80
  15.7 11.0 %collective-permute-start.3 = (bf16[368,640]{1,0:T(8,128)(2,1)}, bf16[368,640]{1,0:T(8,128)(2,1)S(1)}, u32[]{:S(2)}, u32[]{:S(2)}) collective-permute-start(bf16[368,640]{1,0:T(8,128)(2,1)} %pack.6.refs_0_), channel_id=1, source_target_pairs={{0,1},{1,0},{2,3},{3,2},{4,5},{5,4},{6,7},{7,6}} | collective-permute-start | bytes 1413128 | tf_op jit(solution)/shard_map/ppermute | solution.py:80
  15.7 14.0 %collective-permute-start.1 = (bf16[368,640]{1,0:T(8,128)(2,1)}, bf16[368,640]{1,0:T(8,128)(2,1)S(1)}, u32[]{:S(2)}, u32[]{:S(2)}) collective-permute-start(bf16[368,640]{1,0:T(8,128)(2,1)} %pack.6.refs_0_), channel_id=1, source_target_pairs={{0,2},{1,5},{2,0},{3,7},{4,6},{5,1},{6,4},{7,3}} | collective-permute-start | bytes 1413128 | tf_op jit(solution)/shard_map/ppermute | solution.py:80
  16.4 15.7 %collective-permute-start = (bf16[368,640]{1,0:T(8,128)(2,1)}, bf16[368,640]{1,0:T(8,128)(2,1)}, u32[]{:S(2)}, u32[]{:S(2)}) collective-permute-start(bf16[368,640]{1,0:T(8,128)(2,1)} %pack.6.refs_0_), channel_id=1, source_target_pairs={{0,4},{1,3},{2,6},{3,1},{4,0},{5,7},{6,2},{7,5}} | collective-permute-start | bytes 1413128 | tf_op jit(solution)/shard_map/ppermute | solution.py:80
  19.8 27.4 %collective-permute-start.29 = (bf16[640,640]{1,0:T(8,128)(2,1)S(1)}, bf16[640,640]{1,0:T(8,128)(2,1)}, u32[]{:S(2)}, u32[]{:S(2)}) collective-permute-start(bf16[640,640]{1,0:T(8,128)(2,1)S(1)} %copy-done.17), channel_id=1, source_target_pairs={{0,2},{1,5},{2,0},{3,7},{4,6},{5,1},{6,4},{7,3}} | collective-permute-start | bytes 2457608 | tf_op jit(solution)/shard_map/ppermute | solution.py:80
  22.1 25.8 %collective-permute-start.28 = (bf16[640,640]{1,0:T(8,128)(2,1)S(1)}, bf16[640,640]{1,0:T(8,128)(2,1)}, u32[]{:S(2)}, u32[]{:S(2)}) collective-permute-start(bf16[640,640]{1,0:T(8,128)(2,1)S(1)} %copy-done.17), channel_id=1, source_target_pairs={{0,4},{1,3},{2,6},{3,1},{4,0},{5,7},{6,2},{7,5}} | collective-permute-start | bytes 2457608 | tf_op jit(solution)/shard_map/ppermute | solution.py:80
  26.7 23.4 %collective-permute-start.10 = (bf16[672,640]{1,0:T(8,128)(2,1)}, bf16[672,640]{1,0:T(8,128)(2,1)S(1)}, u32[]{:S(2)}, u32[]{:S(2)}) collective-permute-start(bf16[672,640]{1,0:T(8,128)(2,1)} %pack.7.refs_0_), channel_id=1, source_target_pairs={{0,1},{1,0},{2,3},{3,2},{4,5},{5,4},{6,7},{7,6}} | collective-permute-start | bytes 2580488 | tf_op jit(solution)/shard_map/ppermute | solution.py:80
  29.7 36.0 %collective-permute-start.8 = (bf16[672,640]{1,0:T(8,128)(2,1)}, bf16[672,640]{1,0:T(8,128)(2,1)}, u32[]{:S(2)}, u32[]{:S(2)}) collective-permute-start(bf16[672,640]{1,0:T(8,128)(2,1)} %pack.7.refs_0_), channel_id=1, source_target_pairs={{0,2},{1,5},{2,0},{3,7},{4,6},{5,1},{6,4},{7,3}} | collective-permute-start | bytes 2580488 | tf_op jit(solution)/shard_map/ppermute | solution.py:80
  32.1 33.6 %collective-permute-start.7 = (bf16[672,640]{1,0:T(8,128)(2,1)}, bf16[672,640]{1,0:T(8,128)(2,1)}, u32[]{:S(2)}, u32[]{:S(2)}) collective-permute-start(bf16[672,640]{1,0:T(8,128)(2,1)} %pack.7.refs_0_), channel_id=1, source_target_pairs={{0,4},{1,3},{2,6},{3,1},{4,0},{5,7},{6,2},{7,5}} | collective-permute-start | bytes 2580488 | tf_op jit(solution)/shard_map/ppermute | solution.py:80
  47.2 53.0 %collective-permute-start.17 = (bf16[960,640]{1,0:T(8,128)(2,1)}, bf16[960,640]{1,0:T(8,128)(2,1)}, u32[]{:S(2)}, u32[]{:S(2)}) collective-permute-start(bf16[960,640]{1,0:T(8,128)(2,1)} %pack.8.refs_0_.refs_8_), channel_id=1, source_target_pairs={{0,1},{1,0},{2,3},{3,2},{4,5},{5,4},{6,7},{7,6}} | collective-permute-start | bytes 3686408 | tf_op jit(solution)/shard_map/ppermute | solution.py:80
  47.9 53.2 %collective-permute-start.14 = (bf16[960,640]{1,0:T(8,128)(2,1)}, bf16[960,640]{1,0:T(8,128)(2,1)}, u32[]{:S(2)}, u32[]{:S(2)}) collective-permute-start(bf16[960,640]{1,0:T(8,128)(2,1)} %pack.8.refs_0_.refs_8_), channel_id=1, source_target_pairs={{0,4},{1,3},{2,6},{3,1},{4,0},{5,7},{6,2},{7,5}} | collective-permute-start | bytes 3686408 | tf_op jit(solution)/shard_map/ppermute | solution.py:80
  50.1 18.1 %collective-permute-start.5 = (bf16[368,640]{1,0:T(8,128)(2,1)S(1)}, bf16[368,640]{1,0:T(8,128)(2,1)S(1)}, u32[]{:S(2)}, u32[]{:S(2)}) collective-permute-start(bf16[368,640]{1,0:T(8,128)(2,1)S(1)} %collective-permute-done.1.refs_2_), channel_id=1, source_target_pairs={{0,1},{1,0},{2,3},{3,2},{4,5},{5,4},{6,7},{7,6}} | collective-permute-start | bytes 1413128 | tf_op jit(solution)/shard_map/ppermute | solution.py:80
  65.7 2.5 collective-permute-start.4
  65.7 37.1 %collective-permute-start.15 = (bf16[960,640]{1,0:T(8,128)(2,1)}, bf16[960,640]{1,0:T(8,128)(2,1)}, u32[]{:S(2)}, u32[]{:S(2)}) collective-permute-start(bf16[960,640]{1,0:T(8,128)(2,1)} %pack.8.refs_0_.refs_8_), channel_id=1, source_target_pairs={{0,2},{1,5},{2,0},{3,7},{4,6},{5,1},{6,4},{7,3}} | collective-permute-start | bytes 3686408 | tf_op jit(solution)/shard_map/ppermute | solution.py:80
  68.2 29.3 %collective-permute-start.2 = (bf16[368,640]{1,0:T(8,128)(2,1)}, bf16[368,640]{1,0:T(8,128)(2,1)S(1)}, u32[]{:S(2)}, u32[]{:S(2)}) collective-permute-start(bf16[368,640]{1,0:T(8,128)(2,1)} %collective-permute-done.refs_1_), channel_id=1, source_target_pairs={{0,2},{1,5},{2,0},{3,7},{4,6},{5,1},{6,4},{7,3}} | collective-permute-start | bytes 1413128 | tf_op jit(solution)/shard_map/ppermute | solution.py:80
  68.2 41.8 %collective-permute-start.9 = (bf16[672,640]{1,0:T(8,128)(2,1)}, bf16[672,640]{1,0:T(8,128)(2,1)}, u32[]{:S(2)}, u32[]{:S(2)}) collective-permute-start(bf16[672,640]{1,0:T(8,128)(2,1)} %collective-permute-done.7.refs_1_), channel_id=1, source_target_pairs={{0,2},{1,5},{2,0},{3,7},{4,6},{5,1},{6,4},{7,3}} | collective-permute-start | bytes 2580488 | tf_op jit(solution)/shard_map/ppermute | solution.py:80
  97.5 5.3 collective-permute-start.6
  100.1 31.1 %collective-permute-start.21 = (bf16[992,640]{1,0:T(8,128)(2,1)}, bf16[992,640]{1,0:T(8,128)(2,1)}, u32[]{:S(2)}, u32[]{:S(2)}) collective-permute-start(bf16[992,640]{1,0:T(8,128)(2,1)} %pack.9.refs_0_), channel_id=1, source_target_pairs={{0,4},{1,3},{2,6},{3,1},{4,0},{5,7},{6,2},{7,5}} | collective-permute-start | bytes 3809288 | tf_op jit(solution)/shard_map/ppermute | solution.py:80
  101.1 32.7 %collective-permute-start.16 = (bf16[960,640]{1,0:T(8,128)(2,1)}, bf16[960,640]{1,0:T(8,128)(2,1)}, u32[]{:S(2)}, u32[]{:S(2)}) collective-permute-start(bf16[960,640]{1,0:T(8,128)(2,1)} %collective-permute-done.14.refs_1_.refs_9_), channel_id=1, source_target_pairs={{0,2},{1,5},{2,0},{3,7},{4,6},{5,1},{6,4},{7,3}} | collective-permute-start | bytes 3686408 | tf_op jit(solution)/shard_map/ppermute | solution.py:80
  102.8 30.5 %collective-permute-start.12 = (bf16[672,640]{1,0:T(8,128)(2,1)}, bf16[672,640]{1,0:T(8,128)(2,1)}, u32[]{:S(2)}, u32[]{:S(2)}) collective-permute-start(bf16[672,640]{1,0:T(8,128)(2,1)} %collective-permute-done.8.refs_2_), channel_id=1, source_target_pairs={{0,1},{1,0},{2,3},{3,2},{4,5},{5,4},{6,7},{7,6}} | collective-permute-start | bytes 2580488 | tf_op jit(solution)/shard_map/ppermute | solution.py:80
  102.8 30.5 %collective-permute-start.11 = (bf16[672,640]{1,0:T(8,128)(2,1)}, bf16[672,640]{1,0:T(8,128)(2,1)}, u32[]{:S(2)}, u32[]{:S(2)}) collective-permute-start(bf16[672,640]{1,0:T(8,128)(2,1)} %collective-permute-done.7.refs_1_), channel_id=1, source_target_pairs={{0,1},{1,0},{2,3},{3,2},{4,5},{5,4},{6,7},{7,6}} | collective-permute-start | bytes 2580488 | tf_op jit(solution)/shard_map/ppermute | solution.py:80
  110.0 25.6 %collective-permute-start.13 = (bf16[672,640]{1,0:T(8,128)(2,1)}, bf16[672,640]{1,0:T(8,128)(2,1)}, u32[]{:S(2)}, u32[]{:S(2)}) collective-permute-start(bf16[672,640]{1,0:T(8,128)(2,1)} %collective-permute-done.9.refs_3_), channel_id=1, source_target_pairs={{0,1},{1,0},{2,3},{3,2},{4,5},{5,4},{6,7},{7,6}} | collective-permute-start | bytes 2580488 | tf_op jit(solution)/shard_map/ppermute | solution.py:80
  131.3 44.8 %collective-permute-start.22 = (bf16[992,640]{1,0:T(8,128)(2,1)S(1)}, bf16[992,640]{1,0:T(8,128)(2,1)S(1)}, u32[]{:S(2)}, u32[]{:S(2)}) collective-permute-start(bf16[992,640]{1,0:T(8,128)(2,1)S(1)} %copy-done.15), channel_id=1, source_target_pairs={{0,2},{1,5},{2,0},{3,7},{4,6},{5,1},{6,4},{7,3}} | collective-permute-start | bytes 3809288 | tf_op jit(solution)/shard_map/ppermute | solution.py:80
  133.3 43.5 %collective-permute-start.18 = (bf16[960,640]{1,0:T(8,128)(2,1)}, bf16[960,640]{1,0:T(8,128)(2,1)}, u32[]{:S(2)}, u32[]{:S(2)}) collective-permute-start(bf16[960,640]{1,0:T(8,128)(2,1)} %collective-permute-done.14.refs_1_.refs_9_), channel_id=1, source_target_pairs={{0,1},{1,0},{2,3},{3,2},{4,5},{5,4},{6,7},{7,6}} | collective-permute-start | bytes 3686408 | tf_op jit(solution)/shard_map/ppermute | solution.py:80
  133.3 43.3 %collective-permute-start.19 = (bf16[960,640]{1,0:T(8,128)(2,1)}, bf16[960,640]{1,0:T(8,128)(2,1)}, u32[]{:S(2)}, u32[]{:S(2)}) collective-permute-start(bf16[960,640]{1,0:T(8,128)(2,1)} %collective-permute-done.15.refs_2_.refs_10_), channel_id=1, source_target_pairs={{0,1},{1,0},{2,3},{3,2},{4,5},{5,4},{6,7},{7,6}} | collective-permute-start | bytes 3686408 | tf_op jit(solution)/shard_map/ppermute | solution.py:80
  133.8 43.1 %collective-permute-start.23 = (bf16[992,640]{1,0:T(8,128)(2,1)}, bf16[992,640]{1,0:T(8,128)(2,1)}, u32[]{:S(2)}, u32[]{:S(2)}) collective-permute-start(bf16[992,640]{1,0:T(8,128)(2,1)} %collective-permute-done.21.refs_1_), channel_id=1, source_target_pairs={{0,2},{1,5},{2,0},{3,7},{4,6},{5,1},{6,4},{7,3}} | collective-permute-start | bytes 3809288 | tf_op jit(solution)/shard_map/ppermute | solution.py:80
  135.7 41.6 %collective-permute-start.20 = (bf16[960,640]{1,0:T(8,128)(2,1)}, bf16[960,640]{1,0:T(8,128)(2,1)}, u32[]{:S(2)}, u32[]{:S(2)}) collective-permute-start(bf16[960,640]{1,0:T(8,128)(2,1)} %collective-permute-done.16.refs_3_.refs_11_), channel_id=1, source_target_pairs={{0,1},{1,0},{2,3},{3,2},{4,5},{5,4},{6,7},{7,6}} | collective-permute-start | bytes 3686408 | tf_op jit(solution)/shard_map/ppermute | solution.py:80
  176.0 31.6 %collective-permute-start.24 = (bf16[992,640]{1,0:T(8,128)(2,1)S(1)}, bf16[992,640]{1,0:T(8,128)(2,1)}, u32[]{:S(2)}, u32[]{:S(2)}) collective-permute-start(bf16[992,640]{1,0:T(8,128)(2,1)S(1)} %copy-done.15), channel_id=1, source_target_pairs={{0,1},{1,0},{2,3},{3,2},{4,5},{5,4},{6,7},{7,6}} | collective-permute-start | bytes 3809288 | tf_op jit(solution)/shard_map/ppermute | solution.py:80
  176.6 31.4 %collective-permute-start.30 = (bf16[640,640]{1,0:T(8,128)(2,1)}, bf16[640,640]{1,0:T(8,128)(2,1)}, u32[]{:S(2)}, u32[]{:S(2)}) collective-permute-start(bf16[640,640]{1,0:T(8,128)(2,1)} %collective-permute-done.28.refs_1_), channel_id=1, source_target_pairs={{0,2},{1,5},{2,0},{3,7},{4,6},{5,1},{6,4},{7,3}} | collective-permute-start | bytes 2457608 | tf_op jit(solution)/shard_map/ppermute | solution.py:80
  176.7 33.1 %collective-permute-start.25 = (bf16[992,640]{1,0:T(8,128)(2,1)}, bf16[992,640]{1,0:T(8,128)(2,1)}, u32[]{:S(2)}, u32[]{:S(2)}) collective-permute-start(bf16[992,640]{1,0:T(8,128)(2,1)} %collective-permute-done.21.refs_1_), channel_id=1, source_target_pairs={{0,1},{1,0},{2,3},{3,2},{4,5},{5,4},{6,7},{7,6}} | collective-permute-start | bytes 3809288 | tf_op jit(solution)/shard_map/ppermute | solution.py:80
  176.9 32.9 %collective-permute-start.26 = (bf16[992,640]{1,0:T(8,128)(2,1)S(1)}, bf16[992,640]{1,0:T(8,128)(2,1)}, u32[]{:S(2)}, u32[]{:S(2)}) collective-permute-start(bf16[992,640]{1,0:T(8,128)(2,1)S(1)} %collective-permute-done.22.refs_2_), channel_id=1, source_target_pairs={{0,1},{1,0},{2,3},{3,2},{4,5},{5,4},{6,7},{7,6}} | collective-permute-start | bytes 3809288 | tf_op jit(solution)/shard_map/ppermute | solution.py:80
  177.3 33.1 %collective-permute-start.27 = (bf16[992,640]{1,0:T(8,128)(2,1)}, bf16[992,640]{1,0:T(8,128)(2,1)}, u32[]{:S(2)}, u32[]{:S(2)}) collective-permute-start(bf16[992,640]{1,0:T(8,128)(2,1)} %collective-permute-done.23.refs_3_), channel_id=1, source_target_pairs={{0,1},{1,0},{2,3},{3,2},{4,5},{5,4},{6,7},{7,6}} | collective-permute-start | bytes 3809288 | tf_op jit(solution)/shard_map/ppermute | solution.py:80
  207.6 40.8 %collective-permute-start.31 = (bf16[640,640]{1,0:T(8,128)(2,1)S(1)}, bf16[640,640]{1,0:T(8,128)(2,1)S(1)}, u32[]{:S(2)}, u32[]{:S(2)}) collective-permute-start(bf16[640,640]{1,0:T(8,128)(2,1)S(1)} %copy-done.17), channel_id=1, source_target_pairs={{0,1},{1,0},{2,3},{3,2},{4,5},{5,4},{6,7},{7,6}} | collective-permute-start | bytes 2457608 | tf_op jit(solution)/shard_map/ppermute | solution.py:80
  208.0 39.9 %collective-permute-start.37 = (bf16[320,640]{1,0:T(8,128)(2,1)}, bf16[320,640]{1,0:T(8,128)(2,1)S(1)}, u32[]{:S(2)}, u32[]{:S(2)}) collective-permute-start(bf16[320,640]{1,0:T(8,128)(2,1)} %collective-permute-done.35.refs_1_.refs_9_), channel_id=1, source_target_pairs={{0,2},{1,5},{2,0},{3,7},{4,6},{5,1},{6,4},{7,3}} | collective-permute-start | bytes 1228808 | tf_op jit(solution)/shard_map/ppermute | solution.py:80
  209.8 39.1 %collective-permute-start.32 = (bf16[640,640]{1,0:T(8,128)(2,1)}, bf16[640,640]{1,0:T(8,128)(2,1)S(1)}, u32[]{:S(2)}, u32[]{:S(2)}) collective-permute-start(bf16[640,640]{1,0:T(8,128)(2,1)} %collective-permute-done.28.refs_1_), channel_id=1, source_target_pairs={{0,1},{1,0},{2,3},{3,2},{4,5},{5,4},{6,7},{7,6}} | collective-permute-start | bytes 2457608 | tf_op jit(solution)/shard_map/ppermute | solution.py:80
  209.8 38.6 %collective-permute-start.33 = (bf16[640,640]{1,0:T(8,128)(2,1)}, bf16[640,640]{1,0:T(8,128)(2,1)}, u32[]{:S(2)}, u32[]{:S(2)}) collective-permute-start(bf16[640,640]{1,0:T(8,128)(2,1)} %collective-permute-done.29.refs_2_), channel_id=1, source_target_pairs={{0,1},{1,0},{2,3},{3,2},{4,5},{5,4},{6,7},{7,6}} | collective-permute-start | bytes 2457608 | tf_op jit(solution)/shard_map/ppermute | solution.py:80
  210.3 38.6 %collective-permute-start.34 = (bf16[640,640]{1,0:T(8,128)(2,1)}, bf16[640,640]{1,0:T(8,128)(2,1)}, u32[]{:S(2)}, u32[]{:S(2)}) collective-permute-start(bf16[640,640]{1,0:T(8,128)(2,1)} %collective-permute-done.30.refs_3_), channel_id=1, source_target_pairs={{0,1},{1,0},{2,3},{3,2},{4,5},{5,4},{6,7},{7,6}} | collective-permute-start | bytes 2457608 | tf_op jit(solution)/shard_map/ppermute | solution.py:80
  247.9 41.1 %collective-permute-start.38 = (bf16[320,640]{1,0:T(8,128)(2,1)S(1)}, bf16[320,640]{1,0:T(8,128)(2,1)S(1)}, u32[]{:S(2)}, u32[]{:S(2)}) collective-permute-start(bf16[320,640]{1,0:T(8,128)(2,1)S(1)} %copy-done.26), channel_id=1, source_target_pairs={{0,1},{1,0},{2,3},{3,2},{4,5},{5,4},{6,7},{7,6}} | collective-permute-start | bytes 1228808 | tf_op jit(solution)/shard_map/ppermute | solution.py:80
  248.4 89.6 %collective-permute-start.42 = (bf16[1024,512]{1,0:T(8,128)(2,1)}, bf16[1024,512]{1,0:T(8,128)(2,1)}, u32[]{:S(2)}, u32[]{:S(2)}) collective-permute-start(bf16[1024,512]{1,0:T(8,128)(2,1)} %get-tuple-element.106), channel_id=1, source_target_pairs={{0,1},{1,0},{2,3},{3,2},{4,5},{5,4},{6,7},{7,6}} | collective-permute-start | bytes 3145736 | tf_op jit(solution)/shard_map/ppermute | solution.py:80
  248.5 40.6 %collective-permute-start.39 = (bf16[320,640]{1,0:T(8,128)(2,1)}, bf16[320,640]{1,0:T(8,128)(2,1)S(1)}, u32[]{:S(2)}, u32[]{:S(2)}) collective-permute-start(bf16[320,640]{1,0:T(8,128)(2,1)} %collective-permute-done.35.refs_1_.refs_9_), channel_id=1, source_target_pairs={{0,1},{1,0},{2,3},{3,2},{4,5},{5,4},{6,7},{7,6}} | collective-permute-start | bytes 1228808 | tf_op jit(solution)/shard_map/ppermute | solution.py:80
  248.9 40.1 %collective-permute-start.40 = (bf16[320,640]{1,0:T(8,128)(2,1)}, bf16[320,640]{1,0:T(8,128)(2,1)S(1)}, u32[]{:S(2)}, u32[]{:S(2)}) collective-permute-start(bf16[320,640]{1,0:T(8,128)(2,1)} %collective-permute-done.36.refs_2_.refs_10_), channel_id=1, source_target_pairs={{0,1},{1,0},{2,3},{3,2},{4,5},{5,4},{6,7},{7,6}} | collective-permute-start | bytes 1228808 | tf_op jit(solution)/shard_map/ppermute | solution.py:80
  249.0 40.1 %collective-permute-start.41 = (bf16[320,640]{1,0:T(8,128)(2,1)S(1)}, bf16[320,640]{1,0:T(8,128)(2,1)}, u32[]{:S(2)}, u32[]{:S(2)}) collective-permute-start(bf16[320,640]{1,0:T(8,128)(2,1)S(1)} %collective-permute-done.37.refs_3_.refs_11_), channel_id=1, source_target_pairs={{0,1},{1,0},{2,3},{3,2},{4,5},{5,4},{6,7},{7,6}} | collective-permute-start | bytes 1228808 | tf_op jit(solution)/shard_map/ppermute | solution.py:80
  522.9 92.6 %collective-permute-start.43 = (f32[640,640]{1,0:T(8,128)}, f32[640,640]{1,0:T(8,128)}, u32[]{:S(2)}, u32[]{:S(2)}) collective-permute-start(f32[640,640]{1,0:T(8,128)} %get-tuple-element.127), channel_id=1, source_target_pairs={{0,2},{1,5},{2,0},{3,7},{4,6},{5,1},{6,4},{7,3}} | collective-permute-start | bytes 4915208 | tf_op jit(solution)/shard_map/ppermute | solution.py:80
  523.1 94.2 %collective-permute-start.45 = (f32[640,640]{1,0:T(8,128)}, f32[640,640]{1,0:T(8,128)}, u32[]{:S(2)}, u32[]{:S(2)}) collective-permute-start(f32[640,640]{1,0:T(8,128)} %get-tuple-element.129), channel_id=1, source_target_pairs={{0,2},{1,5},{2,0},{3,7},{4,6},{5,1},{6,4},{7,3}} | collective-permute-start | bytes 4915208 | tf_op jit(solution)/shard_map/ppermute | solution.py:80
  525.0 168.4 %collective-permute-start.51 = (f32[1280,640]{1,0:T(8,128)}, f32[1280,640]{1,0:T(8,128)}, u32[]{:S(2)}, u32[]{:S(2)}) collective-permute-start(f32[1280,640]{1,0:T(8,128)} %get-tuple-element.140), channel_id=1, source_target_pairs={{0,2},{1,5},{2,0},{3,7},{4,6},{5,1},{6,4},{7,3}} | collective-permute-start | bytes 9830408 | tf_op jit(solution)/shard_map/ppermute | solution.py:80
  527.0 1.5 collective-permute-start.59
  529.4 68.9 %collective-permute-start.60 = (f32[48,640]{1,0:T(8,128)S(1)}, f32[48,640]{1,0:T(8,128)S(1)}, u32[]{:S(2)}, u32[]{:S(2)}) collective-permute-start(f32[48,640]{1,0:T(8,128)S(1)} %add.48), channel_id=1, source_target_pairs={{0,2},{1,5},{2,0},{3,7},{4,6},{5,1},{6,4},{7,3}} | collective-permute-start | bytes 368648 | tf_op jit(solution)/shard_map/ppermute | solution.py:80
  531.3 166.1 %collective-permute-start.47 = (f32[1344,640]{1,0:T(8,128)}, f32[1344,640]{1,0:T(8,128)S(1)}, u32[]{:S(2)}, u32[]{:S(2)}) collective-permute-start(f32[1344,640]{1,0:T(8,128)} %get-tuple-element.133), channel_id=1, source_target_pairs={{0,2},{1,5},{2,0},{3,7},{4,6},{5,1},{6,4},{7,3}} | collective-permute-start | bytes 10321928 | tf_op jit(solution)/shard_map/ppermute | solution.py:80
  598.3 101.6 %collective-permute-start.49 = (f32[1344,640]{1,0:T(8,128)}, f32[1344,640]{1,0:T(8,128)}, u32[]{:S(2)}, u32[]{:S(2)}) collective-permute-start(f32[1344,640]{1,0:T(8,128)} %get-tuple-element.135), channel_id=1, source_target_pairs={{0,2},{1,5},{2,0},{3,7},{4,6},{5,1},{6,4},{7,3}} | collective-permute-start | bytes 10321928 | tf_op jit(solution)/shard_map/ppermute | solution.py:80
  615.5 76.2 %copy-start.10 = (f32[640,640]{1,0:T(8,128)S(1)}, f32[640,640]{1,0:T(8,128)}, u32[]{:S(2)}) copy-start(f32[640,640]{1,0:T(8,128)} %get-tuple-element.128.refs_3_) | copy-start | bytes 4915204
  615.5 74.1 %collective-permute-start.55 = (f32[640,640]{1,0:T(8,128)}, f32[640,640]{1,0:T(8,128)S(1)}, u32[]{:S(2)}, u32[]{:S(2)}) collective-permute-start(f32[640,640]{1,0:T(8,128)} %get-tuple-element.145), channel_id=1, source_target_pairs={{0,2},{1,5},{2,0},{3,7},{4,6},{5,1},{6,4},{7,3}} | collective-permute-start | bytes 4915208 | tf_op jit(solution)/shard_map/ppermute | solution.py:80
  617.4 153.1 %collective-permute-start.53 = (f32[1280,640]{1,0:T(8,128)}, f32[1280,640]{1,0:T(8,128)S(1)}, u32[]{:S(2)}, u32[]{:S(2)}) collective-permute-start(f32[1280,640]{1,0:T(8,128)} %get-tuple-element.142), channel_id=1, source_target_pairs={{0,2},{1,5},{2,0},{3,7},{4,6},{5,1},{6,4},{7,3}} | collective-permute-start | bytes 9830408 | tf_op jit(solution)/shard_map/ppermute | solution.py:80
  689.6 80.3 %collective-permute-start.57 = (f32[640,640]{1,0:T(8,128)}, f32[640,640]{1,0:T(8,128)S(1)}, u32[]{:S(2)}, u32[]{:S(2)}) collective-permute-start(f32[640,640]{1,0:T(8,128)} %get-tuple-element.147), channel_id=1, source_target_pairs={{0,2},{1,5},{2,0},{3,7},{4,6},{5,1},{6,4},{7,3}} | collective-permute-start | bytes 4915208 | tf_op jit(solution)/shard_map/ppermute | solution.py:80
  693.4 79.8 %collective-permute-start.44 = (f32[320,640]{1,0:T(8,128)S(1)}, f32[320,640]{1,0:T(8,128)S(1)}, u32[]{:S(2)}, u32[]{:S(2)}) collective-permute-start(f32[320,640]{1,0:T(8,128)S(1)} %slice_add_fusion.7), channel_id=1, source_target_pairs={{0,4},{1,3},{2,6},{3,1},{4,0},{5,7},{6,2},{7,5}} | collective-permute-start | bytes 2457608 | tf_op jit(solution)/shard_map/ppermute | solution.py:80
  697.4 76.9 %collective-permute-start.46 = (f32[320,640]{1,0:T(8,128)S(1)}, f32[320,640]{1,0:T(8,128)S(1)}, u32[]{:S(2)}, u32[]{:S(2)}) collective-permute-start(f32[320,640]{1,0:T(8,128)S(1)} %slice_add_fusion.6), channel_id=1, source_target_pairs={{0,4},{1,3},{2,6},{3,1},{4,0},{5,7},{6,2},{7,5}} | collective-permute-start | bytes 2457608 | tf_op jit(solution)/shard_map/ppermute | solution.py:80
  699.9 34.9 %collective-permute-start.61 = (f32[48,640]{1,0:T(8,128)S(1)}, f32[48,640]{1,0:T(8,128)S(1)}, u32[]{:S(2)}, u32[]{:S(2)}) collective-permute-start(f32[48,640]{1,0:T(8,128)S(1)} %add.49), channel_id=1, source_target_pairs={{0,4},{1,3},{2,6},{3,1},{4,0},{5,7},{6,2},{7,5}} | collective-permute-start | bytes 368648 | tf_op jit(solution)/shard_map/ppermute | solution.py:80
  701.2 70.8 %copy-start.3 = (f32[1280,640]{1,0:T(8,128)S(1)}, f32[1280,640]{1,0:T(8,128)}, u32[]{:S(2)}) copy-start(f32[1280,640]{1,0:T(8,128)} %get-tuple-element.141.refs_3_) | copy-start | bytes 9830404
  734.8 41.5 %collective-permute-start.56 = (f32[320,640]{1,0:T(8,128)S(1)}, f32[320,640]{1,0:T(8,128)S(1)}, u32[]{:S(2)}, u32[]{:S(2)}) collective-permute-start(f32[320,640]{1,0:T(8,128)S(1)} %slice_add_fusion.5), channel_id=1, source_target_pairs={{0,4},{1,3},{2,6},{3,1},{4,0},{5,7},{6,2},{7,5}} | collective-permute-start | bytes 2457608 | tf_op jit(solution)/shard_map/ppermute | solution.py:80
  769.9 95.9 %collective-permute-start.48 = (f32[672,640]{1,0:T(8,128)}, f32[672,640]{1,0:T(8,128)S(1)}, u32[]{:S(2)}, u32[]{:S(2)}) collective-permute-start(f32[672,640]{1,0:T(8,128)} %slice_add_fusion.1), channel_id=1, source_target_pairs={{0,4},{1,3},{2,6},{3,1},{4,0},{5,7},{6,2},{7,5}} | collective-permute-start | bytes 5160968 | tf_op jit(solution)/shard_map/ppermute | solution.py:80
  770.5 95.3 %collective-permute-start.50 = (f32[672,640]{1,0:T(8,128)}, f32[672,640]{1,0:T(8,128)}, u32[]{:S(2)}, u32[]{:S(2)}) collective-permute-start(f32[672,640]{1,0:T(8,128)} %slice_add_fusion), channel_id=1, source_target_pairs={{0,4},{1,3},{2,6},{3,1},{4,0},{5,7},{6,2},{7,5}} | collective-permute-start | bytes 5160968 | tf_op jit(solution)/shard_map/ppermute | solution.py:80
  773.3 85.1 %collective-permute-start.52 = (f32[640,640]{1,0:T(8,128)}, f32[640,640]{1,0:T(8,128)}, u32[]{:S(2)}, u32[]{:S(2)}) collective-permute-start(f32[640,640]{1,0:T(8,128)} %slice_add_fusion.3), channel_id=1, source_target_pairs={{0,4},{1,3},{2,6},{3,1},{4,0},{5,7},{6,2},{7,5}} | collective-permute-start | bytes 4915208 | tf_op jit(solution)/shard_map/ppermute | solution.py:80
  774.3 84.1 %collective-permute-start.54 = (f32[640,640]{1,0:T(8,128)}, f32[640,640]{1,0:T(8,128)}, u32[]{:S(2)}, u32[]{:S(2)}) collective-permute-start(f32[640,640]{1,0:T(8,128)} %slice_add_fusion.2), channel_id=1, source_target_pairs={{0,4},{1,3},{2,6},{3,1},{4,0},{5,7},{6,2},{7,5}} | collective-permute-start | bytes 4915208 | tf_op jit(solution)/shard_map/ppermute | solution.py:80
  776.3 78.2 %collective-permute-start.58 = (f32[320,640]{1,0:T(8,128)}, f32[320,640]{1,0:T(8,128)}, u32[]{:S(2)}, u32[]{:S(2)}) collective-permute-start(f32[320,640]{1,0:T(8,128)} %slice_add_fusion.4), channel_id=1, source_target_pairs={{0,4},{1,3},{2,6},{3,1},{4,0},{5,7},{6,2},{7,5}} | collective-permute-start | bytes 2457608 | tf_op jit(solution)/shard_map/ppermute | solution.py:80
  (38 other events, 334.1 us)
